TPU v7x, 32 devices: a whole 2x2x4 slice. The times are simulated.
32 devices in a mesh: tm: 8 (over z, x), hid: 4 (over y, core).
Axes of the slice: x: 2, y: 2, z: 4, core: 2. Of those that a mesh axis runs over, the one named last changes fastest.
Arguments:
- token_ids: int32 [4096], P('tm'), may hold values from 0 to 255
- input_table: float32 [256, 3, 2048], P(None, None, 'hid'), may hold values from -6 to 6
- recur_weight: bfloat16 [2048, 3, 2048], P(None, None, 'hid'), may hold values from -0.125 to 0.125
- z_bias: float32 [2048], P('hid'), may hold values from -1 to 9
- hn_bias: float32 [2048], P('hid'), may hold values from -4 to 4
- init_state: float32 [2048], P('hid'), may hold values from -0.9 to 0.9
- guess: float32 [4096, 2048], P('tm', 'hid'), may hold values from -3 to 3
Outputs:
- states: float32 [4096, 2048], P('tm', 'hid')
- residual_norm: float32 [2], replicated
All inputs are finite; a program needn't handle non-finite values.
Results may differ from a plain program's by a relative error of at most 0.00063.
Values may be sent and summed in bfloat16 or wider, within the bound.
No kernel may reach another device: no remote copies, remote signals or barrier semaphores. Data moves between devices by JAX's collectives and lax.ppermute only.
A program may use at most 128 MiB of HBM per device.

v0:
```python
import functools

import jax
import jax.numpy as jnp
from jax import lax
from jax.experimental import pallas as pl
from jax.experimental.pallas import tpu as pltpu
from jax.sharding import PartitionSpec as P


ITERS = 2
CHUNKS = 2
GROUP = 8
EXTRA = 16
TILE = 256
F32 = jnp.float32
BF16 = jnp.bfloat16


def swapped(block, axis, bit):
    route = [(i, i ^ bit) for i in range(lax.axis_size(axis))]
    return lax.ppermute(block, axis, route)


def from_next(block, axis):
    route = [(i + 1, i) for i in range(lax.axis_size(axis) - 1)]
    return lax.ppermute(block, axis, route)


def sigmoid(x):
    return 0.5 * jnp.tanh(0.5 * x) + 0.5


def vmem(count):
    return [pl.BlockSpec(memory_space=pltpu.VMEM)] * count


def hbm(count):
    return [pl.BlockSpec(memory_space=pltpu.HBM)] * count


def smem():
    return [pl.BlockSpec(memory_space=pltpu.SMEM)]


def params(mib):
    return pltpu.CompilerParams(vmem_limit_bytes=mib * 1024 * 1024)


def cost(flops, moved):
    return pl.CostEstimate(flops=flops, bytes_accessed=moved, transcendentals=0)


def prepare_kernel(where_ref, ids_ref, table_ref, bias_ref, weight_ref, out_ref, diag_ref, own, held, sems):
    rows = ids_ref.shape[0]
    vocab = table_ref.shape[1]
    width = own.shape[2]
    first = pl.multiple_of(where_ref[0] * width, width)
    fetch = pltpu.make_async_copy(weight_ref.at[:, pl.ds(first, width), :], own, sems.at[0])
    fetch.start()
    hot = (lax.broadcasted_iota(jnp.int32, (rows, vocab), 1) == ids_ref[...]).astype(F32).astype(BF16)
    stores = []
    for gate in range(3):
        table = table_ref[gate]
        if gate == 0:
            table = table + bias_ref[...]
        total = None
        for _ in range(3):
            part = table.astype(BF16)
            table = table - part.astype(F32)
            picked = jnp.dot(hot, part, preferred_element_type=F32)
            total = picked if total is None else total + picked
        held[gate] = total
        stores.append(pltpu.make_async_copy(held.at[gate], out_ref.at[gate], sems.at[1 + gate]))
        stores[-1].start()
    fetch.wait()
    row = lax.broadcasted_iota(jnp.int32, (width, width), 0)
    col = lax.broadcasted_iota(jnp.int32, (width, width), 1)
    for gate in range(3):
        block = own[gate].astype(F32)
        line = jnp.sum(jnp.where(row == col, block, 0.0), axis=0, keepdims=True)
        diag_ref[pl.ds(gate * GROUP, GROUP), :] = jnp.broadcast_to(line, (GROUP, width))
    for store in stores:
        store.wait()


def gates(inputs, products, prev, hn_bias):
    zeta = sigmoid(inputs[0] + products[0])
    reset = sigmoid(inputs[1] + products[1])
    cand_pre = products[2] + hn_bias
    gated = reset * cand_pre
    cand = jnp.tanh(inputs[2] + gated)
    gap = prev - cand
    return zeta, reset, gated, cand, gap, cand + zeta * gap


def step_kernel(count, start, chunk, first, last, copies, where_ref, *refs):
    refs = list(refs)
    blocks = [refs.pop(0) for _ in range(count)]
    weight_ref, inputs_ref, state_ref, next_ref, bias_ref, diag_ref = [refs.pop(0) for _ in range(6)]
    before_ref = None if first == 1 else refs.pop(0)
    init_ref = refs.pop(0) if first == 1 else None
    a_ref, b_ref, ends_ref = [refs.pop(0) for _ in range(3)]
    send_ref = refs.pop(0) if last else None
    weights, inputs, lhs, products, sems = refs
    rows, width = state_ref.shape
    hid = where_ref[0]
    is_first = where_ref[1]
    is_last = where_ref[2]
    tiles = width // TILE
    groups = chunk // GROUP

    fetches = []
    for tile in range(tiles):
        lanes = pl.ds(tile * TILE, TILE)
        for gate in range(3):
            fetches.append(
                pltpu.make_async_copy(
                    weight_ref.at[gate, :, lanes], weights.at[gate, :, lanes], sems.at[tile * 4 + gate]
                )
            )
        fetches.append(
            pltpu.make_async_copy(
                inputs_ref.at[:, pl.ds(start, chunk), lanes], inputs.at[:, pl.ds(0, chunk), lanes], sems.at[tile * 4 + 3]
            )
        )
    if first == 1:
        fetches.append(
            pltpu.make_async_copy(
                inputs_ref.at[:, pl.ds(rows, GROUP), :], inputs.at[:, pl.ds(chunk, GROUP), :], sems.at[tiles * 4]
            )
        )
    for fetch in fetches:
        fetch.start()
    for offset in range(count):
        place = pl.multiple_of((hid ^ offset) * width, width)
        lhs[:, pl.ds(place, width)] = blocks[offset][...]
    row = lax.broadcasted_iota(jnp.int32, (GROUP, TILE), 0)
    if first == 1:
        fetches[-1].wait()

    for tile in range(tiles):
        lanes = pl.ds(tile * TILE, TILE)
        for gate in range(3):
            fetches[tile * 4 + gate].wait()
            products[gate] = jnp.dot(lhs[...], weights[gate, :, lanes], preferred_element_type=F32)
        fetches[tile * 4 + 3].wait()
        hn_bias = jnp.broadcast_to(bias_ref[:, lanes], (GROUP, TILE))
        diag_z = diag_ref[pl.ds(0, GROUP), lanes]
        diag_r = diag_ref[pl.ds(GROUP, GROUP), lanes]
        diag_n = diag_ref[pl.ds(2 * GROUP, GROUP), lanes]

        def advance(group, carry):
            turned, run_a, run_b, squares = carry
            here = pl.ds(pl.multiple_of(group * GROUP, GROUP), GROUP)
            prev = state_ref[pl.ds(pl.multiple_of(start + group * GROUP, GROUP), GROUP), lanes]
            if last:
                after = jnp.minimum(start + group * GROUP + GROUP, rows - GROUP)
                following = state_ref[pl.ds(pl.multiple_of(after, GROUP), GROUP), lanes]
                following = jnp.where(group == groups - 1, jnp.broadcast_to(next_ref[:, lanes], (GROUP, TILE)), following)
            else:
                following = state_ref[pl.ds(pl.multiple_of(start + group * GROUP + GROUP, GROUP), GROUP), lanes]
            turned_next = pltpu.roll(following, GROUP - 1, 0)
            state = jnp.where(row == GROUP - 1, turned_next, turned)
            zeta, reset, gated, cand, gap, value = gates(
                [inputs[gate, here, lanes] for gate in range(3)],
                [products[gate, here, :] for gate in range(3)],
                prev,
                hn_bias,
            )
            rest = 1.0 - zeta
            slope = zeta + gap * (zeta * rest) * diag_z
            slope = slope + rest * (1.0 - cand * cand) * (reset * diag_n + gated * (1.0 - reset) * diag_r)
            error = state - value
            if last:
                outside = (row == GROUP - 1) & (group == groups - 1) & (is_last == 1)
                error = jnp.where(outside, 0.0, error)
            squares = squares + error * error
            a = slope
            b = value - slope * prev
            for distance in (1, 2, 4):
                keep = row >= distance
                a_up = jnp.where(keep, pltpu.roll(a, distance, 0), 1.0)
                b_up = jnp.where(keep, pltpu.roll(b, distance, 0), 0.0)
                b = a * b_up + b
                a = a * a_up
            a_ref[here, lanes] = a * run_a
            b_ref[here, lanes] = a * run_b + b
            last_a = jnp.broadcast_to(a[GROUP - 1 :], (GROUP, TILE))
            last_b = jnp.broadcast_to(b[GROUP - 1 :], (GROUP, TILE))
            return (turned_next, last_a * run_a, last_a * run_b + last_b, squares)

        turned = pltpu.roll(state_ref[pl.ds(start, GROUP), lanes], GROUP - 1, 0)
        zeros = jnp.zeros((GROUP, TILE), F32)
        if first:
            carry = (turned, jnp.ones((GROUP, TILE), F32), zeros, zeros)
        else:
            carry = (
                turned,
                jnp.broadcast_to(before_ref[0:1, lanes], (GROUP, TILE)),
                jnp.broadcast_to(before_ref[1:2, lanes], (GROUP, TILE)),
                jnp.where(row == 0, before_ref[2:3, lanes], 0.0),
            )
        _, run_a, run_b, squares = lax.fori_loop(0, groups, advance, carry, unroll=4)
        if first == 1:
            begin = gates(
                [inputs[gate, pl.ds(chunk, GROUP), lanes] for gate in range(3)],
                [products[gate, pl.ds(chunk, GROUP), :] for gate in range(3)],
                jnp.broadcast_to(init_ref[:, lanes], (GROUP, TILE)),
                hn_bias,
            )[-1]
            error = state_ref[pl.ds(0, GROUP), lanes] - begin
            squares = squares + jnp.where((row == 0) & (is_first == 1), error * error, 0.0)
            begin = begin[0:1]
        else:
            begin = before_ref[3:4, lanes]
        total = jnp.sum(squares, axis=0, keepdims=True)
        ends_ref[0:1, lanes] = run_a[0:1]
        ends_ref[1:2, lanes] = run_b[0:1]
        ends_ref[2:3, lanes] = total
        ends_ref[3:4, lanes] = begin
        if last:
            fixed = run_a[0:1] * begin + run_b[0:1]
            send_a = jnp.where(is_first == 1, 0.0, run_a[0:1])
            send_b = jnp.where(is_first == 1, fixed, run_b[0:1])
            for peer in range(copies):
                send_ref[peer, 0:1, lanes] = send_a
                send_ref[peer, 1:2, lanes] = send_b
                send_ref[peer, 2:3, lanes] = total


def apply_kernel(chunks, final, where_ref, *refs):
    maps, refs = refs[: 2 * chunks], refs[2 * chunks :]
    begin_ref, all_ref, state_ref, sum_ref = refs[:4]
    outs = refs[4:]
    copies = all_ref.shape[0]
    chunk, width = maps[0].shape
    place = where_ref[3]

    def compose(peer, carry):
        enter, total = carry
        moved = all_ref[peer, 0:1, :] * enter + all_ref[peer, 1:2, :]
        return (jnp.where(peer < place, moved, enter), total + all_ref[peer, 2:3, :])

    enter, total = lax.fori_loop(0, copies, compose, (begin_ref[3:4, :], jnp.zeros((1, width), F32)), unroll=min(copies, 8))
    sum_ref[...] = total
    step = 2 * GROUP
    row = lax.broadcasted_iota(jnp.int32, (step, width), 0)
    enter = jnp.broadcast_to(enter, (step, width))
    before = enter
    for index in range(chunks):
        a_ref, b_ref = maps[2 * index], maps[2 * index + 1]

        def advance(group, before):
            here = pl.ds(pl.multiple_of(group * step, step), step)
            turned = pltpu.roll(a_ref[here, :] * enter + b_ref[here, :], 1, 0)
            moved = jnp.where(row == 0, before, turned)
            state_ref[pl.ds(pl.multiple_of(index * chunk + group * step, step), step), :] = moved
            if not final:
                outs[1 + index][here, :] = moved.astype(BF16)
            return turned

        before = lax.fori_loop(0, chunk // step, advance, before, unroll=2)
    if not final:
        outs[0][...] = before[0:1]


def newton(token_ids, input_table, recur_weight, z_bias, hn_bias, init_state, guess):
    rows, width = guess.shape
    full = recur_weight.shape[0]
    count = lax.axis_size("hid")
    blocks_tm = lax.axis_size("tm")
    hid = lax.axis_index("hid")
    tm = lax.axis_index("tm")
    weight = jnp.transpose(recur_weight, (1, 0, 2))
    table = jnp.transpose(input_table, (1, 0, 2))
    chunk = rows // CHUNKS
    where = jnp.stack([hid, (tm == 0).astype(jnp.int32), (tm == blocks_tm - 1).astype(jnp.int32), tm])

    state = guess
    moved = [guess[index * chunk : (index + 1) * chunk].astype(BF16) for index in range(CHUNKS)]
    moved[0] = jnp.concatenate([moved[0], init_state.astype(BF16)[None], jnp.zeros((EXTRA - 1, width), BF16)], 0)

    def gather(block):
        found = {0: block}
        bit = count // 2
        while bit:
            for offset in list(found):
                found[offset | bit] = swapped(found[offset], "hid", bit)
            bit //= 2
        return [found[offset] for offset in range(count)]

    following = from_next(guess[:1], "tm")
    next_id = from_next(token_ids[:1], "tm")
    ids = jnp.concatenate([token_ids[1:], next_id, token_ids[:1], jnp.zeros((GROUP - 1,), jnp.int32)])
    inputs, diag = pl.pallas_call(
        prepare_kernel,
        out_shape=[jax.ShapeDtypeStruct((3, rows + GROUP, width), F32), jax.ShapeDtypeStruct((3 * GROUP, width), F32)],
        in_specs=smem() + vmem(3) + hbm(1),
        out_specs=hbm(1) + vmem(1),
        scratch_shapes=[
            pltpu.VMEM((3, width, width), BF16),
            pltpu.VMEM((3, rows + GROUP, width), F32),
            pltpu.SemaphoreType.DMA((4,)),
        ],
        compiler_params=params(40),
        cost_estimate=cost(18 * rows * table.shape[1] * width, 8 * rows * width),
        name="prepare",
    )(where, ids[:, None], table, z_bias[None], weight)

    sums = []
    for step in range(ITERS):
        gathered = [gather(block) for block in moved]
        maps = []
        ends = begin if step else None
        for index in range(CHUNKS):
            first = 0 if index else (2 if step else 1)
            last = index == CHUNKS - 1
            height = gathered[index][0].shape[0]
            operands = [where, *gathered[index], weight, inputs, state, following, hn_bias[None], diag]
            specs = smem() + vmem(count) + hbm(2) + vmem(4)
            if first != 1:
                operands.append(ends)
                specs += vmem(1)
            else:
                operands.append(init_state[None])
                specs += vmem(1)
            outs = [
                jax.ShapeDtypeStruct((chunk, width), F32),
                jax.ShapeDtypeStruct((chunk, width), F32),
                jax.ShapeDtypeStruct((4, width), F32),
            ]
            if last:
                outs.append(jax.ShapeDtypeStruct((blocks_tm, 3, width), F32))
            found = pl.pallas_call(
                functools.partial(step_kernel, count, index * chunk, chunk, first, last, blocks_tm),
                out_shape=outs,
                in_specs=specs,
                out_specs=vmem(len(outs)),
                scratch_shapes=[
                    pltpu.VMEM((3, full, width), BF16),
                    pltpu.VMEM((3, chunk + GROUP, width), F32),
                    pltpu.VMEM((height, full), BF16),
                    pltpu.VMEM((3, height, TILE), F32),
                    pltpu.SemaphoreType.DMA((width // TILE * 4 + 1,)),
                ],
                compiler_params=params(32),
                cost_estimate=cost(2 * height * full * 3 * width, 6 * full * width),
            )(*operands)
            maps += found[:2]
            ends = found[2]
        begin = ends
        every = lax.all_to_all(found[3], "tm", 0, 0)
        final = step == ITERS - 1
        outs = [jax.ShapeDtypeStruct((rows, width), F32), jax.ShapeDtypeStruct((1, width), F32)]
        if not final:
            outs.append(jax.ShapeDtypeStruct((1, width), F32))
            outs += [jax.ShapeDtypeStruct((chunk, width), BF16)] * CHUNKS
        result = pl.pallas_call(
            functools.partial(apply_kernel, CHUNKS, final),
            out_shape=outs,
            in_specs=smem() + vmem(2 * CHUNKS + 2),
            out_specs=vmem(len(outs)),
            compiler_params=params(16),
        )(where, *maps, begin, every)
        state = result[0]
        sums.append(result[1])
        if not final:
            following = result[2]
            moved = list(result[3:])
    squares = jnp.concatenate(sums, 0)
    bit = 1
    while bit < count:
        squares = squares + swapped(squares, "hid", bit)
        bit *= 2
    size = blocks_tm * rows * count * width
    residual_norm = jnp.sqrt(jnp.sum(squares, axis=1) / size)
    return (state, residual_norm)


def solution(mesh):
    return jax.shard_map(
        newton,
        mesh=mesh,
        in_specs=(
            P("tm"),
            P(None, None, "hid"),
            P(None, None, "hid"),
            P("hid"),
            P("hid"),
            P("hid"),
            P("tm", "hid"),
        ),
        out_specs=(P("tm", "hid"), P()),
        check_vma=False,
    )
```

profile of v0, /device:TPU:0, one launch (start us, length us, event | category | flops | bytes accessed | tf_op | source)
XLA Modules:
  0.0 96.9 jit_solution(3717110586967492363)
XLA Ops:
  1.5 1.3 %convert.6 = bf16[512,512]{1,0:T(8,128)(2,1)S(1)} convert(f32[512,512]{1,0:T(8,128)} %refs_6_.3) | non-fusion elementwise | flops 262144 | bytes 1572864 | tf_op jit(solution)/shard_map/convert.3
  3.1 3.1 %collective-permute-start.1 = (bf16[272,512]{1,0:T(8,128)(2,1)S(1)}, bf16[272,512]{1,0:T(8,128)(2,1)S(1)}, u32[]{:S(2)}, u32[]{:S(2)}) collective-permute-start(bf16[272,512]{1,0:T(8,128)(2,1)S(1)} %maximum_maximum_fusion.refs_0_), channel_id=1, source_target_pairs={{0,2},{1,3},{2,0},{3,1},{4,6},{5,7},{6,4},{7,5},{8,10},{9,11},{10,... | collective-permute-start | bytes 835592 | tf_op jit(solution)/shard_map/ppermute | solution.py:22
  6.7 1.3 %slice.20 = s32[1]{0:T(128)} slice(s32[512]{0:T(512)} %param.7), slice={[0:1]} | slice | bytes 8 | tf_op jit(solution)/shard_map/slice | solution.py:294
  8.0 1.3 %collective-permute-start.3 = (s32[1]{0:T(128)}, s32[1]{0:T(128)}, u32[]{:S(2)}, u32[]{:S(2)}) collective-permute-start(s32[1]{0:T(128)} %slice.20), channel_id=1, source_target_pairs={{4,0},{8,4},{12,8},{16,12},{20,16},{24,20},{28,24},{5,1},{9,5},{13... | collective-permute-start | bytes 20 | tf_op jit(solution)/shard_map/ppermute | solution.py:27
  9.3 4.3 %collective-permute-done.1.refs_2_ = bf16[272,512]{1,0:T(8,128)(2,1)S(1)} collective-permute-done((bf16[272,512]{1,0:T(8,128)(2,1)S(1)}, bf16[272,512]{1,0:T(8,128)(2,1)S(1)}, u32[]{:S(2)}, u32[]{:S(2)}) %collective-permute-start.1) | collective-permute-done | bytes 278560 | tf_op jit(solution)/shard_map/ppermute | solution.py:22
  13.8 1.3 %collective-permute-start.4 = (f32[1,512]{1,0:T(1,128)S(1)}, f32[1,512]{1,0:T(1,128)S(1)}, u32[]{:S(2)}, u32[]{:S(2)}) collective-permute-start(f32[1,512]{1,0:T(1,128)S(1)} %slice.21), channel_id=1, source_target_pairs={{4,0},{8,4},{12,8},{16,12},{20,16},{24,20},{28,24},{5,1},{9,5},{13... | collective-permute-start | bytes 6152 | tf_op jit(solution)/shard_map/ppermute | solution.py:27
  15.1 1.4 %pad_add_fusion = s32[520]{0:T(1024)S(1)} fusion(s32[7]{0:T(128)S(1)} %broadcast.7, s32[1]{0:T(128)} %slice.20, s32[1]{0:T(128)} %collective-permute-done.3, s32[511]{0:T(512)S(1)} %slice.19), kind=kLoop, calls=%fused_computation.1 | loop fusion | flops 1560 | bytes 4160 | tf_op jit(solution)/shard_map/concatenate | solution.py:295
  16.6 1.9 %collective-permute-done.6.refs_2_ = bf16[256,512]{1,0:T(8,128)(2,1)} collective-permute-done((bf16[256,512]{1,0:T(8,128)(2,1)S(1)}, bf16[256,512]{1,0:T(8,128)(2,1)}, u32[]{:S(2)}, u32[]{:S(2)}) %collective-permute-start.6) | collective-permute-done | bytes 262176 | tf_op jit(solution)/shard_map/ppermute | solution.py:22
  18.5 2.8 %copy-done = bf16[2048,3,512]{2,0,1:T(8,128)(2,1)S(1)} copy-done((bf16[2048,3,512]{2,0,1:T(8,128)(2,1)S(1)}, bf16[2048,3,512]{2,0,1:T(8,128)(2,1)}, u32[]{:S(2)}) %copy-start) | copy-done | bytes 6291480
  21.3 3.1 %prepare.1 = (f32[3,520,512]{2,1,0:T(8,128)S(1)}, f32[24,512]{1,0:T(8,128)S(1)}) custom-call(s32[4]{0:T(128)S(1)} %pad_add_fusion.1.where_ref, s32[520,1]{1,0:T(8,128)S(1)} %broadcast_in_dim.27.ids_ref, f32[3,256,512]{2,1,0:T(8,128)S(1)} %bitcast.14, f32[1,512]{1,0:T(1,128)S(1)} %bitcast.20, bf16[3,2048,512]{2,1,0:T(8,128)(2,1)S(1)} %bitcast.9), custom_call_target="tpu_custom_call" | custom-call | flops 1207959552 | bytes 2097152 | tf_op jit(solution)/shard_map/prepare/pallas_call | solution.py:296
  24.5 7.6 %shard_map.86 = (f32[256,512]{1,0:T(8,128)S(1)}, f32[256,512]{1,0:T(8,128)S(1)}, f32[4,512]{1,0:T(4,128)S(1)}) custom-call(s32[4]{0:T(128)S(1)} %pad_add_fusion.1.where_ref, bf16[272,512]{1,0:T(8,128)(2,1)S(1)} %maximum_maximum_fusion.refs_0_, bf16[272,512]{1,0:T(8,128)(2,1)} %collective-permute-done.refs_1_, ...), custom_call_target="tpu_custom_call" | custom-call | flops 1711276032 | bytes 6291456 | tf_op jit(solution)/shard_map/pallas_call | solution.py:335
  32.1 7.5 %shard_map.87 = (f32[256,512]{1,0:T(8,128)S(1)}, f32[256,512]{1,0:T(8,128)S(1)}, f32[4,512]{1,0:T(4,128)S(1)}, f32[8,3,512]{2,1,0:T(4,128)S(1)}) custom-call(s32[4]{0:T(128)S(1)} %pad_add_fusion.1.where_ref, bf16[256,512]{1,0:T(8,128)(2,1)S(1)} %get-tuple-element.48.refs_0_, bf16[256,512]{1,0:T(8,128)(2,1)} %collective-permute-done.5.refs_1_, ...), custom_call_target="tpu_custom_call" | custom-call | flops 1610612736 | bytes 6291456 | tf_op jit(solution)/shard_map/pallas_call | solution.py:335
  39.6 12.8 %all_to_all.10.refs_5_ = f32[8,3,512]{2,1,0:T(4,128)S(1)} all-to-all(f32[8,3,512]{2,1,0:T(4,128)S(1)} %get-tuple-element.33), channel_id=1, replica_groups=mesh['tm'=8,'hid'=4] {'tm'}, dimensions={0} | all-to-all | bytes 98304 | tf_op jit(solution)/shard_map/all_to_all | solution.py:353
  52.4 0.9 shard_map.88
  53.2 1.6 %collective-permute-start.9 = (bf16[256,512]{1,0:T(8,128)(2,1)S(1)}, bf16[256,512]{1,0:T(8,128)(2,1)S(1)}, u32[]{:S(2)}, u32[]{:S(2)}) collective-permute-start(bf16[256,512]{1,0:T(8,128)(2,1)S(1)} %get-tuple-element.34.refs_0_), channel_id=1, source_target_pairs={{0,2},{1,3},{2,0},{3,1},{4,6},{5,7},{6,4},{7,5},{8,10},{9,11},{10,... | collective-permute-start | bytes 786440 | tf_op jit(solution)/shard_map/ppermute | solution.py:22
  55.3 7.1 %collective-permute-done.9.refs_2_ = bf16[256,512]{1,0:T(8,128)(2,1)S(1)} collective-permute-done((bf16[256,512]{1,0:T(8,128)(2,1)S(1)}, bf16[256,512]{1,0:T(8,128)(2,1)S(1)}, u32[]{:S(2)}, u32[]{:S(2)}) %collective-permute-start.9) | collective-permute-done | bytes 262176 | tf_op jit(solution)/shard_map/ppermute | solution.py:22
  63.0 3.2 %collective-permute-done.12.refs_2_ = bf16[256,512]{1,0:T(8,128)(2,1)S(1)} collective-permute-done((bf16[256,512]{1,0:T(8,128)(2,1)S(1)}, bf16[256,512]{1,0:T(8,128)(2,1)S(1)}, u32[]{:S(2)}, u32[]{:S(2)}) %collective-permute-start.12) | collective-permute-done | bytes 262176 | tf_op jit(solution)/shard_map/ppermute | solution.py:22
  66.2 6.9 %shard_map.89 = (f32[256,512]{1,0:T(8,128)S(1)}, f32[256,512]{1,0:T(8,128)S(1)}, f32[4,512]{1,0:T(4,128)S(1)}) custom-call(s32[4]{0:T(128)S(1)} %pad_add_fusion.1.where_ref, bf16[256,512]{1,0:T(8,128)(2,1)S(1)} %get-tuple-element.34.refs_0_, bf16[256,512]{1,0:T(8,128)(2,1)S(1)} %collective-permute-done.8.refs_1_, ...), custom_call_target="tpu_custom_call" | custom-call | flops 1610612736 | bytes 6291456 | tf_op jit(solution)/shard_map/pallas_call | solution.py:335
  73.2 7.0 %shard_map.90 = (f32[256,512]{1,0:T(8,128)S(1)}, f32[256,512]{1,0:T(8,128)S(1)}, f32[4,512]{1,0:T(4,128)S(1)}, f32[8,3,512]{2,1,0:T(4,128)S(1)}) custom-call(s32[4]{0:T(128)S(1)} %pad_add_fusion.1.where_ref, bf16[256,512]{1,0:T(8,128)(2,1)S(1)} %get-tuple-element.39.refs_0_, bf16[256,512]{1,0:T(8,128)(2,1)S(1)} %collective-permute-done.11.refs_1_, ...), custom_call_target="tpu_custom_call" | custom-call | flops 1610612736 | bytes 6291456 | tf_op jit(solution)/shard_map/pallas_call | solution.py:335
  80.2 9.3 %all_to_all.11.refs_5_ = f32[8,3,512]{2,1,0:T(4,128)S(1)} all-to-all(f32[8,3,512]{2,1,0:T(4,128)S(1)} %get-tuple-element.44), channel_id=1, replica_groups=mesh['tm'=8,'hid'=4] {'tm'}, dimensions={0} | all-to-all | bytes 98304 | tf_op jit(solution)/shard_map/all_to_all | solution.py:353
  89.5 1.8 %shard_map.91 = (f32[512,512]{1,0:T(8,128)}, f32[1,512]{1,0:T(1,128)S(1)}) custom-call(s32[4]{0:T(128)S(1)} %pad_add_fusion.1.where_ref, f32[256,512]{1,0:T(8,128)S(1)} %get-tuple-element.37.refs_0_, f32[256,512]{1,0:T(8,128)S(1)} %get-tuple-element.38.refs_1_, f32[256,512]{1,0:T(8,128)S(1)} %get-tuple-element.41.refs_2_, ...), custom_call_target="tpu_custom_call" | custom-call | tf_op jit(solution)/shard_map/pallas_call | solution.py:359
  91.4 1.2 %collective-permute-done.14 = f32[2,512]{1,0:T(2,128)S(1)} collective-permute-done((f32[2,512]{1,0:T(2,128)S(1)}, f32[2,512]{1,0:T(2,128)S(1)}, u32[]{:S(2)}, u32[]{:S(2)}) %collective-permute-start.14) | collective-permute-done | bytes 4128 | tf_op jit(solution)/shard_map/ppermute | solution.py:22
  92.5 1.6 %collective-permute-start.15 = (f32[2,512]{1,0:T(2,128)S(1)}, f32[2,512]{1,0:T(2,128)S(1)}, u32[]{:S(2)}, u32[]{:S(2)}) collective-permute-start(f32[2,512]{1,0:T(2,128)S(1)} %fusion), channel_id=1, source_target_pairs={{0,2},{1,3},{2,0},{3,1},{4,6},{5,7},{6,4},{7,5},{8,10},{9,11},{10,... | collective-permute-start | bytes 12296 | tf_op jit(solution)/shard_map/ppermute | solution.py:22
  94.1 2.1 %collective-permute-done.15 = f32[2,512]{1,0:T(2,128)S(1)} collective-permute-done((f32[2,512]{1,0:T(2,128)S(1)}, f32[2,512]{1,0:T(2,128)S(1)}, u32[]{:S(2)}, u32[]{:S(2)}) %collective-permute-start.15) | collective-permute-done | bytes 4128 | tf_op jit(solution)/shard_map/ppermute | solution.py:22
  (51 shorter events, 3.8 us)
Async XLA Ops:
  0.6 13.2 %copy-start.2 = (f32[512,512]{1,0:T(8,128)S(1)}, f32[512,512]{1,0:T(8,128)}, u32[]{:S(2)}) copy-start(f32[512,512]{1,0:T(8,128)} %refs_6_.3) | copy-start | bytes 3145732
  0.6 13.1 %copy-start.7 = (s32[512]{0:T(512)S(1)}, s32[512]{0:T(512)}, u32[]{:S(2)}) copy-start(s32[512]{0:T(512)} %param.7) | copy-start | bytes 6148
  0.7 17.9 %copy-start.6 = (f32[512]{0:T(512)S(1)}, f32[512]{0:T(512)}, u32[]{:S(2)}) copy-start(f32[512]{0:T(512)} %param.10) | copy-start | bytes 6148
  0.7 17.9 %copy-start.3 = (f32[256,3,512]{2,0,1:T(8,128)S(1)}, f32[256,3,512]{2,0,1:T(8,128)}, u32[]{:S(2)}) copy-start(f32[256,3,512]{2,0,1:T(8,128)} %param.8) | copy-start | bytes 4718596
  3.1 10.6 %collective-permute-start.1 = (bf16[272,512]{1,0:T(8,128)(2,1)S(1)}, bf16[272,512]{1,0:T(8,128)(2,1)S(1)}, u32[]{:S(2)}, u32[]{:S(2)}) collective-permute-start(bf16[272,512]{1,0:T(8,128)(2,1)S(1)} %maximum_maximum_fusion.refs_0_), channel_id=1, source_target_pairs={{0,2},{1,3},{2,0},{3,1},{4,6},{5,7},{6,4},{7,5},{8,10},{9,11},{10,... | collective-permute-start | bytes 835592 | tf_op jit(solution)/shard_map/ppermute | solution.py:22
  6.1 12.4 %collective-permute-start.6 = (bf16[256,512]{1,0:T(8,128)(2,1)S(1)}, bf16[256,512]{1,0:T(8,128)(2,1)}, u32[]{:S(2)}, u32[]{:S(2)}) collective-permute-start(bf16[256,512]{1,0:T(8,128)(2,1)S(1)} %get-tuple-element.48.refs_0_), channel_id=1, source_target_pairs={{0,2},{1,3},{2,0},{3,1},{4,6},{5,7},{6,4},{7,5},{8,10},{9,11},{10,... | collective-permute-start | bytes 786440 | tf_op jit(solution)/shard_map/ppermute | solution.py:22
  6.2 25.9 %collective-permute-start.5 = (bf16[256,512]{1,0:T(8,128)(2,1)S(1)}, bf16[256,512]{1,0:T(8,128)(2,1)}, u32[]{:S(2)}, u32[]{:S(2)}) collective-permute-start(bf16[256,512]{1,0:T(8,128)(2,1)S(1)} %get-tuple-element.48.refs_0_), channel_id=1, source_target_pairs={{0,1},{1,0},{2,3},{3,2},{4,5},{5,4},{6,7},{7,6},{8,9},{9,8},{10,11... | collective-permute-start | bytes 786440 | tf_op jit(solution)/shard_map/ppermute | solution.py:22
  6.2 18.2 %collective-permute-start = (bf16[272,512]{1,0:T(8,128)(2,1)S(1)}, bf16[272,512]{1,0:T(8,128)(2,1)}, u32[]{:S(2)}, u32[]{:S(2)}) collective-permute-start(bf16[272,512]{1,0:T(8,128)(2,1)S(1)} %maximum_maximum_fusion.refs_0_), channel_id=1, source_target_pairs={{0,1},{1,0},{2,3},{3,2},{4,5},{5,4},{6,7},{7,6},{8,9},{9,8},{10,11... | collective-permute-start | bytes 835592 | tf_op jit(solution)/shard_map/ppermute | solution.py:22
  8.0 5.8 %collective-permute-start.3 = (s32[1]{0:T(128)}, s32[1]{0:T(128)}, u32[]{:S(2)}, u32[]{:S(2)}) collective-permute-start(s32[1]{0:T(128)} %slice.20), channel_id=1, source_target_pairs={{4,0},{8,4},{12,8},{16,12},{20,16},{24,20},{28,24},{5,1},{9,5},{13... | collective-permute-start | bytes 20 | tf_op jit(solution)/shard_map/ppermute | solution.py:27
  13.6 10.8 %collective-permute-start.2 = (bf16[272,512]{1,0:T(8,128)(2,1)S(1)}, bf16[272,512]{1,0:T(8,128)(2,1)S(1)}, u32[]{:S(2)}, u32[]{:S(2)}) collective-permute-start(bf16[272,512]{1,0:T(8,128)(2,1)S(1)} %collective-permute-done.1.refs_2_), channel_id=1, source_target_pairs={{0,1},{1,0},{2,3},{3,2},{4,5},{5,4},{6,7},{7,6},{8,9},{9,8},{10,11... | collective-permute-start | bytes 835592 | tf_op jit(solution)/shard_map/ppermute | solution.py:22
  13.8 10.6 %collective-permute-start.4 = (f32[1,512]{1,0:T(1,128)S(1)}, f32[1,512]{1,0:T(1,128)S(1)}, u32[]{:S(2)}, u32[]{:S(2)}) collective-permute-start(f32[1,512]{1,0:T(1,128)S(1)} %slice.21), channel_id=1, source_target_pairs={{4,0},{8,4},{12,8},{16,12},{20,16},{24,20},{28,24},{5,1},{9,5},{13... | collective-permute-start | bytes 6152 | tf_op jit(solution)/shard_map/ppermute | solution.py:27
  18.5 13.6 %collective-permute-start.7 = (bf16[256,512]{1,0:T(8,128)(2,1)}, bf16[256,512]{1,0:T(8,128)(2,1)S(1)}, u32[]{:S(2)}, u32[]{:S(2)}) collective-permute-start(bf16[256,512]{1,0:T(8,128)(2,1)} %collective-permute-done.6.refs_2_), channel_id=1, source_target_pairs={{0,1},{1,0},{2,3},{3,2},{4,5},{5,4},{6,7},{7,6},{8,9},{9,8},{10,11... | collective-permute-start | bytes 786440 | tf_op jit(solution)/shard_map/ppermute | solution.py:22
  18.5 2.8 %copy-start = (bf16[2048,3,512]{2,0,1:T(8,128)(2,1)S(1)}, bf16[2048,3,512]{2,0,1:T(8,128)(2,1)}, u32[]{:S(2)}) copy-start(bf16[2048,3,512]{2,0,1:T(8,128)(2,1)} %param.9) | copy-start | bytes 18874372
  21.3 3.1 %copy-start.1 = (bf16[2048,3,512]{2,0,1:T(8,128)(2,1)S(1)}, bf16[2048,3,512]{2,0,1:T(8,128)(2,1)}, u32[]{:S(2)}) copy-start(bf16[2048,3,512]{2,0,1:T(8,128)(2,1)} %param.9) | copy-start | bytes 18874372
  21.3 3.1 %copy-start.4 = (f32[512]{0:T(512)S(1)}, f32[512]{0:T(512)}, u32[]{:S(2)}) copy-start(f32[512]{0:T(512)} %param.11) | copy-start | bytes 6148
  21.3 3.2 %copy-start.5 = (f32[512]{0:T(512)S(1)}, f32[512]{0:T(512)}, u32[]{:S(2)}) copy-start(f32[512]{0:T(512)} %param.12) | copy-start | bytes 6148
  53.2 9.2 %collective-permute-start.9 = (bf16[256,512]{1,0:T(8,128)(2,1)S(1)}, bf16[256,512]{1,0:T(8,128)(2,1)S(1)}, u32[]{:S(2)}, u32[]{:S(2)}) collective-permute-start(bf16[256,512]{1,0:T(8,128)(2,1)S(1)} %get-tuple-element.34.refs_0_), channel_id=1, source_target_pairs={{0,2},{1,3},{2,0},{3,1},{4,6},{5,7},{6,4},{7,5},{8,10},{9,11},{10,... | collective-permute-start | bytes 786440 | tf_op jit(solution)/shard_map/ppermute | solution.py:22
  54.8 11.4 %collective-permute-start.12 = (bf16[256,512]{1,0:T(8,128)(2,1)S(1)}, bf16[256,512]{1,0:T(8,128)(2,1)S(1)}, u32[]{:S(2)}, u32[]{:S(2)}) collective-permute-start(bf16[256,512]{1,0:T(8,128)(2,1)S(1)} %get-tuple-element.39.refs_0_), channel_id=1, source_target_pairs={{0,2},{1,3},{2,0},{3,1},{4,6},{5,7},{6,4},{7,5},{8,10},{9,11},{10,... | collective-permute-start | bytes 786440 | tf_op jit(solution)/shard_map/ppermute | solution.py:22
  55.3 10.9 %collective-permute-start.8 = (bf16[256,512]{1,0:T(8,128)(2,1)S(1)}, bf16[256,512]{1,0:T(8,128)(2,1)S(1)}, u32[]{:S(2)}, u32[]{:S(2)}) collective-permute-start(bf16[256,512]{1,0:T(8,128)(2,1)S(1)} %get-tuple-element.34.refs_0_), channel_id=1, source_target_pairs={{0,1},{1,0},{2,3},{3,2},{4,5},{5,4},{6,7},{7,6},{8,9},{9,8},{10,11... | collective-permute-start | bytes 786440 | tf_op jit(solution)/shard_map/ppermute | solution.py:22
  62.5 3.7 %collective-permute-start.10 = (bf16[256,512]{1,0:T(8,128)(2,1)S(1)}, bf16[256,512]{1,0:T(8,128)(2,1)S(1)}, u32[]{:S(2)}, u32[]{:S(2)}) collective-permute-start(bf16[256,512]{1,0:T(8,128)(2,1)S(1)} %collective-permute-done.9.refs_2_), channel_id=1, source_target_pairs={{0,1},{1,0},{2,3},{3,2},{4,5},{5,4},{6,7},{7,6},{8,9},{9,8},{10,11... | collective-permute-start | bytes 786440 | tf_op jit(solution)/shard_map/ppermute | solution.py:22
  62.5 10.7 %collective-permute-start.11 = (bf16[256,512]{1,0:T(8,128)(2,1)S(1)}, bf16[256,512]{1,0:T(8,128)(2,1)S(1)}, u32[]{:S(2)}, u32[]{:S(2)}) collective-permute-start(bf16[256,512]{1,0:T(8,128)(2,1)S(1)} %get-tuple-element.39.refs_0_), channel_id=1, source_target_pairs={{0,1},{1,0},{2,3},{3,2},{4,5},{5,4},{6,7},{7,6},{8,9},{9,8},{10,11... | collective-permute-start | bytes 786440 | tf_op jit(solution)/shard_map/ppermute | solution.py:22
  66.2 7.0 %collective-permute-start.13 = (bf16[256,512]{1,0:T(8,128)(2,1)S(1)}, bf16[256,512]{1,0:T(8,128)(2,1)S(1)}, u32[]{:S(2)}, u32[]{:S(2)}) collective-permute-start(bf16[256,512]{1,0:T(8,128)(2,1)S(1)} %collective-permute-done.12.refs_2_), channel_id=1, source_target_pairs={{0,1},{1,0},{2,3},{3,2},{4,5},{5,4},{6,7},{7,6},{8,9},{9,8},{10,11... | collective-permute-start | bytes 786440 | tf_op jit(solution)/shard_map/ppermute | solution.py:22
  91.3 1.2 %collective-permute-start.14 = (f32[2,512]{1,0:T(2,128)S(1)}, f32[2,512]{1,0:T(2,128)S(1)}, u32[]{:S(2)}, u32[]{:S(2)}) collective-permute-start(f32[2,512]{1,0:T(2,128)S(1)} %pad_maximum_fusion), channel_id=1, source_target_pairs={{0,1},{1,0},{2,3},{3,2},{4,5},{5,4},{6,7},{7,6},{8,9},{9,8},{10,11... | collective-permute-start | bytes 12296 | tf_op jit(solution)/shard_map/ppermute | solution.py:22
  92.5 3.7 %collective-permute-start.15 = (f32[2,512]{1,0:T(2,128)S(1)}, f32[2,512]{1,0:T(2,128)S(1)}, u32[]{:S(2)}, u32[]{:S(2)}) collective-permute-start(f32[2,512]{1,0:T(2,128)S(1)} %fusion), channel_id=1, source_target_pairs={{0,2},{1,3},{2,0},{3,1},{4,6},{5,7},{6,4},{7,5},{8,10},{9,11},{10,... | collective-permute-start | bytes 12296 | tf_op jit(solution)/shard_map/ppermute | solution.py:22
where the time goes:
time: 97.3 us; the launch traced here: 96.9 us
  Pallas kernels  34.7 us (36%)
  blocking collectives  22.1 us (23%)
  waiting for transfers between devices  19.8 us (20%)
  starting transfers between devices  10.5 us (11%)
  local copies, waits for them, and re-layouts  4.41 us (5%)
  other arithmetic  4.38 us (5%)
    pallas_call x4, Pallas kernels, newton(): pl.pallas_call(functools.partial(step_kernel, count, index * chunk, chunk...  29 us
    all_to_all x2, blocking collectives, newton(): every = lax.all_to_all(found[3], 'tm', 0, 0)  22.1 us
    ppermute x14, waiting for transfers between devices, swapped(): return lax.ppermute(block, axis, route)  19.8 us
    ppermute x14, starting transfers between devices, swapped(): return lax.ppermute(block, axis, route)  7.92 us
    pallas_call x1, Pallas kernels, newton(): pl.pallas_call(prepare_kernel, out_shape=[jax.ShapeDtypeStruct((3, rows +...  3.09 us
    unnamed x16, local copies, waits for them, and re-layouts  2.81 us
    pallas_call x2, Pallas kernels, newton(): pl.pallas_call(functools.partial(apply_kernel, CHUNKS, final), out_shape=...  2.63 us
    ppermute x2, starting transfers between devices, from_next(): return lax.ppermute(block, axis, route)  2.57 us
  transfers between devices with their start and end apart: 16, of which 6 were waited for; matrix products, arithmetic and copies ran while one was open for 3% of the time, Pallas kernels for 18%

commit v1 on v0

v1 whole, which is shorter than its diff:
```python
import functools

import jax
import jax.numpy as jnp
from jax import lax
from jax.experimental import pallas as pl
from jax.experimental.pallas import tpu as pltpu
from jax.sharding import PartitionSpec as P


ITERS = 2
CHUNKS = 2
GROUP = 8
EXTRA = 16
TILE = 256
LANES = 128
F32 = jnp.float32
BF16 = jnp.bfloat16


def swapped(block, axis, bit):
    route = [(i, i ^ bit) for i in range(lax.axis_size(axis))]
    return lax.ppermute(block, axis, route)


def from_next(block, axis):
    route = [(i + 1, i) for i in range(lax.axis_size(axis) - 1)]
    return lax.ppermute(block, axis, route)


def sigmoid(x):
    return 0.5 * jnp.tanh(0.5 * x) + 0.5


def vmem(count):
    return [pl.BlockSpec(memory_space=pltpu.VMEM)] * count


def smem():
    return [pl.BlockSpec(memory_space=pltpu.SMEM)]


def params(mib):
    return pltpu.CompilerParams(vmem_limit_bytes=mib * 1024 * 1024)


def cost(flops, moved):
    return pl.CostEstimate(flops=flops, bytes_accessed=moved, transcendentals=0)


def round_kernel(chunks, guess_ref, init_ref, whole_ref, *parts):
    rows, width = guess_ref.shape
    chunk = rows // chunks
    row = lax.broadcasted_iota(jnp.int32, (EXTRA, width), 0)
    lead = jnp.where(row == 0, jnp.broadcast_to(init_ref[...], (EXTRA, width)), 0.0).astype(BF16)
    whole_ref[pl.ds(0, EXTRA), :] = lead
    parts[0][pl.ds(0, EXTRA), :] = lead
    for index, part in enumerate(parts):
        skip = 0 if index else EXTRA
        for start in range(0, chunk, GROUP * 4):
            block = guess_ref[pl.ds(index * chunk + start, GROUP * 4), :].astype(BF16)
            whole_ref[pl.ds(EXTRA + index * chunk + start, GROUP * 4), :] = block
            part[pl.ds(skip + start, GROUP * 4), :] = block


def prepare_kernel(where_ref, ids_ref, next_ref, table_ref, bias_ref, out_ref):
    rows = ids_ref.shape[0]
    vocab, width = table_ref.shape[1:]
    token = lax.broadcasted_iota(jnp.int32, (rows, 1), 0)
    ids = jnp.where(token == rows - GROUP - 1, jnp.broadcast_to(next_ref[:, width : width + 1], (rows, 1)), ids_ref[...])
    entry = lax.broadcasted_iota(jnp.int32, (rows, vocab), 1).astype(F32)
    hot = (entry == ids).astype(F32).astype(BF16)
    for gate in range(3):
        table = table_ref[gate]
        if gate == 0:
            table = table + bias_ref[...]
        total = None
        for _ in range(3):
            part = table.astype(BF16)
            table = table - part.astype(F32)
            picked = jnp.dot(hot, part, preferred_element_type=F32)
            total = picked if total is None else total + picked
        out_ref[gate] = total


def diagonals(weight_ref, hid, diag_ref):
    width = diag_ref.shape[1]
    row = lax.broadcasted_iota(jnp.int32, (width, width), 0)
    col = lax.broadcasted_iota(jnp.int32, (width, width), 1)
    first = pl.multiple_of(hid * width, width)
    for gate in range(3):
        block = weight_ref[gate, pl.ds(first, width), :].astype(F32)
        line = jnp.sum(jnp.where(row == col, block, 0.0), axis=0, keepdims=True)
        diag_ref[pl.ds(gate * GROUP, GROUP), :] = jnp.broadcast_to(line, (GROUP, width))


def gates(inputs, products, prev, hn_bias):
    zeta = sigmoid(inputs[0] + products[0])
    reset = sigmoid(inputs[1] + products[1])
    cand_pre = products[2] + hn_bias
    gated = reset * cand_pre
    cand = jnp.tanh(inputs[2] + gated)
    gap = prev - cand
    return zeta, reset, gated, cand, gap, cand + zeta * gap


def step_kernel(count, index, chunks, step, copies, where_ref, *refs):
    refs = list(refs)
    near = [refs.pop(0) for _ in range(count // 2)]
    far = [refs.pop(0) for _ in range(count // 2)]
    weight_ref, inputs_ref, state_ref, next_ref, bias_ref, before_ref = [refs.pop(0) for _ in range(6)]
    begins = index == 0 and step == 0
    diag_ref = None if begins else refs.pop(0)
    a_ref, b_ref, ends_ref = [refs.pop(0) for _ in range(3)]
    diag_ref = refs.pop(0) if begins else diag_ref
    last = index == chunks - 1
    send_ref = refs.pop(0) if last else None
    lhs, products = refs
    height = lhs.shape[0]
    rows, width = state_ref.shape
    chunk = rows // chunks
    start = index * chunk
    lead = height - chunk
    skip = EXTRA if step == 0 else 0
    hid = where_ref[0]
    is_first = where_ref[1]
    is_last = where_ref[2]
    groups = chunk // GROUP

    if begins:
        diagonals(weight_ref, hid, diag_ref)
    for offset in range(count):
        place = pl.multiple_of((hid ^ offset) * width, width)
        if offset < count // 2:
            lhs[:, pl.ds(place, width)] = near[offset][pl.ds(skip + start - lead, height), :]
        else:
            lhs[:, pl.ds(place, width)] = far[offset - count // 2][...]
    row = lax.broadcasted_iota(jnp.int32, (GROUP, TILE), 0)

    for tile in range(width // TILE):
        lanes = pl.ds(tile * TILE, TILE)
        for gate in range(3):
            products[gate] = jnp.dot(lhs[...], weight_ref[gate, :, lanes], preferred_element_type=F32)
        hn_bias = jnp.broadcast_to(bias_ref[:, lanes], (GROUP, TILE))
        diag_z = diag_ref[pl.ds(0, GROUP), lanes]
        diag_r = diag_ref[pl.ds(GROUP, GROUP), lanes]
        diag_n = diag_ref[pl.ds(2 * GROUP, GROUP), lanes]

        def advance(group, carry):
            turned, run_a, run_b, squares = carry
            here = pl.ds(pl.multiple_of(group * GROUP, GROUP), GROUP)
            token = pl.ds(pl.multiple_of(start + group * GROUP, GROUP), GROUP)
            prev = state_ref[token, lanes]
            after = start + group * GROUP + GROUP
            if last:
                after = jnp.minimum(after, rows - GROUP)
            following = state_ref[pl.ds(pl.multiple_of(after, GROUP), GROUP), lanes]
            if last:
                following = jnp.where(group == groups - 1, jnp.broadcast_to(next_ref[:, lanes], (GROUP, TILE)), following)
            turned_next = pltpu.roll(following, GROUP - 1, 0)
            state = jnp.where(row == GROUP - 1, turned_next, turned)
            product = pl.ds(pl.multiple_of(lead + group * GROUP, GROUP), GROUP)
            zeta, reset, gated, cand, gap, value = gates(
                [inputs_ref[gate, token, lanes] for gate in range(3)],
                [products[gate, product, :] for gate in range(3)],
                prev,
                hn_bias,
            )
            rest = 1.0 - zeta
            slope = zeta + gap * (zeta * rest) * diag_z
            slope = slope + rest * (1.0 - cand * cand) * (reset * diag_n + gated * (1.0 - reset) * diag_r)
            error = state - value
            if last:
                outside = (row == GROUP - 1) & (group == groups - 1) & (is_last == 1)
                error = jnp.where(outside, 0.0, error)
            squares = squares + error * error
            a = slope
            b = value - slope * prev
            for distance in (1, 2, 4):
                keep = row >= distance
                a_up = jnp.where(keep, pltpu.roll(a, distance, 0), 1.0)
                b_up = jnp.where(keep, pltpu.roll(b, distance, 0), 0.0)
                b = a * b_up + b
                a = a * a_up
            a_ref[here, lanes] = a * run_a
            b_ref[here, lanes] = a * run_b + b
            last_a = jnp.broadcast_to(a[GROUP - 1 :], (GROUP, TILE))
            last_b = jnp.broadcast_to(b[GROUP - 1 :], (GROUP, TILE))
            return (turned_next, last_a * run_a, last_a * run_b + last_b, squares)

        turned = pltpu.roll(state_ref[pl.ds(start, GROUP), lanes], GROUP - 1, 0)
        zeros = jnp.zeros((GROUP, TILE), F32)
        if index == 0:
            carry = (turned, jnp.ones((GROUP, TILE), F32), zeros, zeros)
        else:
            carry = (
                turned,
                jnp.broadcast_to(before_ref[0:1, lanes], (GROUP, TILE)),
                jnp.broadcast_to(before_ref[1:2, lanes], (GROUP, TILE)),
                jnp.where(row == 0, before_ref[2:3, lanes], 0.0),
            )
        _, run_a, run_b, squares = lax.fori_loop(0, groups, advance, carry, unroll=4)
        if begins:
            begin = gates(
                [inputs_ref[gate, pl.ds(rows, GROUP), lanes] for gate in range(3)],
                [products[gate, pl.ds(0, GROUP), :] for gate in range(3)],
                jnp.broadcast_to(before_ref[:, lanes], (GROUP, TILE)),
                hn_bias,
            )[-1]
            error = state_ref[pl.ds(0, GROUP), lanes] - begin
            squares = squares + jnp.where((row == 0) & (is_first == 1), error * error, 0.0)
            begin = begin[0:1]
            earlier = zeros[0:1]
        else:
            begin = before_ref[3:4, lanes]
            earlier = before_ref[2:3, lanes] if index == 0 else before_ref[4:5, lanes]
        total = jnp.sum(squares, axis=0, keepdims=True)
        ends_ref[0:1, lanes] = run_a[0:1]
        ends_ref[1:2, lanes] = run_b[0:1]
        ends_ref[2:3, lanes] = total
        ends_ref[3:4, lanes] = begin
        ends_ref[4:5, lanes] = earlier
        if last:
            send_a = jnp.where(is_first == 1, 0.0, run_a[0:1])
            send_b = jnp.where(is_first == 1, run_a[0:1] * begin + run_b[0:1], run_b[0:1])
            for part in range(TILE // LANES):
                at = tile * (TILE // LANES) + part
                for line, sent in ((at, send_a), (width // LANES + at, send_b)):
                    picked = sent[:, part * LANES : (part + 1) * LANES]
                    send_ref[:, pl.ds(line, 1), :] = jnp.broadcast_to(picked[None], (copies, 1, LANES))
    if last and step == ITERS - 1:
        lane = lax.broadcasted_iota(jnp.int32, (1, LANES), 1)
        sums = jnp.zeros((1, LANES), F32)
        for line, half in ((4, 0), (2, 1)):
            part = sum(ends_ref[pl.ds(line, 1), pl.ds(at, LANES)] for at in range(0, width, LANES))
            part = part + pltpu.roll(part, LANES // 2, 1)
            sums = jnp.where(lane // (LANES // 2) == half, part, sums)
        send_ref[:, pl.ds(2 * width // LANES, 1), :] = jnp.broadcast_to(sums[None], (copies, 1, LANES))


def apply_kernel(chunks, final, count, where_ref, *refs):
    maps, refs = refs[: 2 * chunks], refs[2 * chunks :]
    begin_ref, all_ref, state_ref = refs[:3]
    outs = refs[3:]
    chunk, width = maps[0].shape
    lines = width // LANES
    place = where_ref[3]
    hid = where_ref[0]
    copies = all_ref.shape[0]
    peers = copies // count if final else copies

    def compose(peer, enter):
        slot = peer * count + hid if final else peer
        moved = all_ref[slot, pl.ds(0, lines), :] * enter + all_ref[slot, pl.ds(lines, lines), :]
        return jnp.where(peer < place, moved, enter)

    begin = jnp.concatenate([begin_ref[3:4, pl.ds(at * LANES, LANES)] for at in range(lines)], axis=0)
    found = lax.fori_loop(0, peers, compose, begin, unroll=min(peers, 8))
    enter = jnp.concatenate([found[at : at + 1] for at in range(lines)], axis=1)
    if final:
        total = jnp.sum(all_ref[:, pl.ds(2 * lines, 1), :], axis=0)
        lane = lax.broadcasted_iota(jnp.int32, (1, LANES), 1)
        size = copies * chunk * chunks * width
        for half in range(2):
            outs[0][half] = jnp.sqrt(jnp.sum(jnp.where(lane // (LANES // 2) == half, total, 0.0)) / size)
    step = 2 * GROUP
    row = lax.broadcasted_iota(jnp.int32, (step, width), 0)
    enter = jnp.broadcast_to(enter, (step, width))
    before = enter
    for index in range(chunks):
        a_ref, b_ref = maps[2 * index], maps[2 * index + 1]

        def advance(group, before):
            here = pl.ds(pl.multiple_of(group * step, step), step)
            token = pl.ds(pl.multiple_of(index * chunk + group * step, step), step)
            turned = pltpu.roll(a_ref[here, :] * enter + b_ref[here, :], 1, 0)
            moved = jnp.where(row == 0, before, turned)
            state_ref[token, :] = moved
            if not final:
                rounded = moved.astype(BF16)
                outs[1][token, :] = rounded
                outs[2 + index][here, :] = rounded
            return turned

        before = lax.fori_loop(0, chunk // step, advance, before, unroll=2)
    if not final:
        outs[0][...] = before[0:1]


def newton(token_ids, input_table, recur_weight, z_bias, hn_bias, init_state, guess):
    rows, width = guess.shape
    full = recur_weight.shape[0]
    count = lax.axis_size("hid")
    blocks_tm = lax.axis_size("tm")
    hid = lax.axis_index("hid")
    tm = lax.axis_index("tm")
    weight = jnp.transpose(recur_weight, (1, 0, 2))
    table = jnp.transpose(input_table, (1, 0, 2))
    chunk = rows // CHUNKS
    lines = width // LANES
    where = jnp.stack([hid, (tm == 0).astype(jnp.int32), (tm == blocks_tm - 1).astype(jnp.int32), tm])

    state = guess
    whole, *moved = pl.pallas_call(
        functools.partial(round_kernel, CHUNKS),
        out_shape=[jax.ShapeDtypeStruct((rows + EXTRA, width), BF16)]
        + [jax.ShapeDtypeStruct((chunk + (0 if index else EXTRA), width), BF16) for index in range(CHUNKS)],
        in_specs=vmem(2),
        out_specs=vmem(1 + CHUNKS),
        compiler_params=params(16),
        cost_estimate=cost(rows * width, 8 * rows * width),
        name="round",
    )(guess, init_state[None])

    ids = token_ids.astype(F32)
    lead = jnp.concatenate([guess[:1], jnp.broadcast_to(ids[:1, None], (1, LANES))], 1)
    following = from_next(lead, "tm")
    ids = jnp.concatenate([ids[1:], ids[:1], ids[:1], jnp.zeros((GROUP - 1,), F32)])
    inputs = pl.pallas_call(
        prepare_kernel,
        out_shape=jax.ShapeDtypeStruct((3, rows + GROUP, width), F32),
        in_specs=smem() + vmem(4),
        out_specs=vmem(1)[0],
        compiler_params=params(32),
        cost_estimate=cost(18 * rows * table.shape[1] * width, 8 * rows * width),
        name="prepare",
    )(where, ids[:, None], following, table, z_bias[None])

    ends = init_state[None]
    diag = None
    for step in range(ITERS):
        final = step == ITERS - 1
        near = {0: whole}
        far = [{count // 2: None} for _ in range(CHUNKS)]
        for index in range(CHUNKS):
            far[index][count // 2] = swapped(moved[index], "hid", count // 2)
        bit = count // 4
        while bit:
            for offset in list(near):
                near[offset | bit] = swapped(near[offset], "hid", bit)
            for index in range(CHUNKS):
                for offset in list(far[index]):
                    far[index][offset | bit] = swapped(far[index][offset], "hid", bit)
            bit //= 2
        maps = []
        for index in range(CHUNKS):
            last = index == CHUNKS - 1
            height = moved[index].shape[0]
            operands = [near[offset] for offset in range(count // 2)]
            operands += [far[index][offset] for offset in range(count // 2, count)]
            operands += [weight, inputs, state, following, hn_bias[None], ends]
            if diag is not None:
                operands.append(diag)
            outs = [
                jax.ShapeDtypeStruct((chunk, width), F32),
                jax.ShapeDtypeStruct((chunk, width), F32),
                jax.ShapeDtypeStruct((5, width), F32),
            ]
            if diag is None:
                outs.append(jax.ShapeDtypeStruct((3 * GROUP, width), F32))
            copies = blocks_tm * count if final else blocks_tm
            if last:
                outs.append(jax.ShapeDtypeStruct((copies, 2 * lines + final, LANES), F32))
            found = pl.pallas_call(
                functools.partial(step_kernel, count, index, CHUNKS, step, copies),
                out_shape=outs,
                in_specs=smem() + vmem(len(operands)),
                out_specs=vmem(len(outs)),
                scratch_shapes=[pltpu.VMEM((height, full), BF16), pltpu.VMEM((3, height, TILE), F32)],
                compiler_params=params(32),
                cost_estimate=cost(2 * height * full * 3 * width, 6 * full * width),
            )(where, *operands)
            maps += found[:2]
            ends = found[2]
            diag = found[3] if diag is None else diag
        every = lax.all_to_all(found[-1], ("tm", "hid") if final else "tm", 0, 0)
        outs = [jax.ShapeDtypeStruct((rows, width), F32)]
        if final:
            outs.append(jax.ShapeDtypeStruct((ITERS,), F32))
            specs = vmem(1) + smem()
        else:
            outs.append(jax.ShapeDtypeStruct((1, width), F32))
            outs.append(jax.ShapeDtypeStruct((rows, width), BF16))
            outs += [jax.ShapeDtypeStruct((chunk, width), BF16)] * CHUNKS
            specs = vmem(len(outs))
        result = pl.pallas_call(
            functools.partial(apply_kernel, CHUNKS, final, count),
            out_shape=outs,
            in_specs=smem() + vmem(2 * CHUNKS + 2),
            out_specs=specs,
            compiler_params=params(16),
            cost_estimate=cost(2 * rows * width, 16 * rows * width),
        )(where, *maps, ends, every)
        if final:
            return (result[0], result[1])
        state, following, whole, *moved = result


def solution(mesh):
    return jax.shard_map(
        newton,
        mesh=mesh,
        in_specs=(
            P("tm"),
            P(None, None, "hid"),
            P(None, None, "hid"),
            P("hid"),
            P("hid"),
            P("hid"),
            P("tm", "hid"),
        ),
        out_specs=(P("tm", "hid"), P()),
        check_vma=False,
    )
```

time: 97.3 us -> 87.7 us (0.901)
  Pallas kernels: 34.7 us -> 26.2 us
  starting transfers between devices: 10.5 us -> 6.42 us
  local copies, waits for them, and re-layouts: 4.41 us -> 8.15 us
  blocking collectives: 22.1 us -> 25.2 us
  other arithmetic: 4.38 us -> 1.48 us
    pallas_call x7 -> x8, Pallas kernels: 34.7 us -> 26.2 us  [the longest x4 20.3 us: newton(): pl.pallas_call(functools.partial(step_kernel, count, index, CHUNKS, step,...]
    unnamed x16 -> x20, local copies, waits for them, and re-layouts: 2.81 us -> 6.79 us
    all_to_all x2, blocking collectives: 22.1 us -> 25.2 us  [newton(): every = lax.all_to_all(found[-1], ('tm', 'hid') if final else 'tm', 0, 0)]
    ppermute x14 -> x10, starting transfers between devices: 7.92 us -> 5.12 us  [swapped(): return lax.ppermute(block, axis, route)]
    another operation x1 -> x0, other arithmetic: 1.29 us -> none
    ppermute x2 -> x1, starting transfers between devices: 2.57 us -> 1.29 us  [from_next(): return lax.ppermute(block, axis, route)]
    ppermute x14 -> x10, waiting for transfers between devices: 19.8 us -> 19.1 us  [swapped(): return lax.ppermute(block, axis, route)]
  transfers between devices with their start and end apart: 16 -> 11, of which waited for: 6 -> 4; matrix products, arithmetic and copies ran while one was open for 3% -> 3% of each run, Pallas kernels for 18% -> 14%
where the time goes in v1:
time: 87.7 us; the launch traced here: 87.3 us
  Pallas kernels  26.2 us (30%)
  blocking collectives  25.2 us (29%)
  waiting for transfers between devices  19.1 us (22%)
  local copies, waits for them, and re-layouts  8.15 us (9%)
  starting transfers between devices  6.42 us (7%)
  other arithmetic  1.48 us (2%)
    all_to_all x2, blocking collectives, newton(): every = lax.all_to_all(found[-1], ('tm', 'hid') if final else 'tm', 0, 0)  25.2 us
    pallas_call x4, Pallas kernels, newton(): pl.pallas_call(functools.partial(step_kernel, count, index, CHUNKS, step,...  20.3 us
    ppermute x10, waiting for transfers between devices, swapped(): return lax.ppermute(block, axis, route)  19.1 us
    unnamed x20, local copies, waits for them, and re-layouts  6.79 us
    ppermute x10, starting transfers between devices, swapped(): return lax.ppermute(block, axis, route)  5.12 us
    pallas_call x2, Pallas kernels, newton(): pl.pallas_call(functools.partial(apply_kernel, CHUNKS, final, count), out...  2.88 us
    pallas_call x1, Pallas kernels, newton(): pl.pallas_call(prepare_kernel, out_shape=jax.ShapeDtypeStruct((3, rows +...  2.04 us
  transfers between devices with their start and end apart: 11, of which 4 were waited for; matrix products, arithmetic and copies ran while one was open for 3% of the time, Pallas kernels for 14%

profile of v1, /device:TPU:0, one launch (start us, length us, event | category | flops | bytes accessed | tf_op | source)
XLA Modules:
  0.0 87.3 jit_solution(4722070275889756345)
XLA Ops:
  0.6 1.2 %copy-done.1 = f32[512,512]{1,0:T(8,128)S(1)} copy-done((f32[512,512]{1,0:T(8,128)S(1)}, f32[512,512]{1,0:T(8,128)}, u32[]{:S(2)}) %copy-start.1) | copy-done | bytes 1048600
  1.9 0.7 copy-done.5
  2.5 1.0 %round.1 = (bf16[528,512]{1,0:T(8,128)(2,1)}, bf16[272,512]{1,0:T(8,128)(2,1)S(1)}, bf16[256,512]{1,0:T(8,128)(2,1)}) custom-call(f32[512,512]{1,0:T(8,128)S(1)} %copy-done.1, f32[1,512]{1,0:T(1,128)S(1)} %bitcast.21), custom_call_target="tpu_custom_call" | custom-call | flops 262144 | bytes 2097152 | tf_op jit(solution)/shard_map/round/pallas_call | solution.py:304
  3.5 3.0 %collective-permute-start.1 = (bf16[272,512]{1,0:T(8,128)(2,1)S(1)}, bf16[272,512]{1,0:T(8,128)(2,1)S(1)}, u32[]{:S(2)}, u32[]{:S(2)}) collective-permute-start(bf16[272,512]{1,0:T(8,128)(2,1)S(1)} %get-tuple-element.26), channel_id=1, source_target_pairs={{0,2},{1,3},{2,0},{3,1},{4,6},{5,7},{6,4},{7,5},{8,10},{9,11},{10,... | collective-permute-start | bytes 835592 | tf_op jit(solution)/shard_map/ppermute | solution.py:23
  6.5 0.7 convert_element_type.2
  8.4 1.3 %collective-permute-start.3 = (f32[1,640]{1,0:T(1,128)S(1)}, f32[1,640]{1,0:T(1,128)S(1)}, u32[]{:S(2)}, u32[]{:S(2)}) collective-permute-start(f32[1,640]{1,0:T(1,128)S(1)} %concatenate.7), channel_id=1, source_target_pairs={{4,0},{8,4},{12,8},{16,12},{20,16},{24,20},{28,24},{5,1},{9,5},{13... | collective-permute-start | bytes 7688 | tf_op jit(solution)/shard_map/ppermute | solution.py:28
  9.8 4.2 %collective-permute-done.1.refs_2_ = bf16[272,512]{1,0:T(8,128)(2,1)S(1)} collective-permute-done((bf16[272,512]{1,0:T(8,128)(2,1)S(1)}, bf16[272,512]{1,0:T(8,128)(2,1)S(1)}, u32[]{:S(2)}, u32[]{:S(2)}) %collective-permute-start.1) | collective-permute-done | bytes 278560 | tf_op jit(solution)/shard_map/ppermute | solution.py:23
  14.0 0.7 pad_maximum_fusion
  14.9 3.9 %collective-permute-done.4.refs_2_ = bf16[256,512]{1,0:T(8,128)(2,1)} collective-permute-done((bf16[256,512]{1,0:T(8,128)(2,1)}, bf16[256,512]{1,0:T(8,128)(2,1)}, u32[]{:S(2)}, u32[]{:S(2)}) %collective-permute-start.4) | collective-permute-done | bytes 262176 | tf_op jit(solution)/shard_map/ppermute | solution.py:23
  18.9 1.4 %copy-done.3 = f32[256,3,512]{2,0,1:T(8,128)S(1)} copy-done((f32[256,3,512]{2,0,1:T(8,128)S(1)}, f32[256,3,512]{2,0,1:T(8,128)}, u32[]{:S(2)}) %copy-start.3) | copy-done | bytes 1572888
  20.3 0.7 copy-done.7
  21.0 2.0 %prepare.1.refs_5_ = f32[3,520,512]{2,1,0:T(8,128)S(1)} custom-call(s32[4]{0:T(128)S(1)} %pad_add_fusion.where_ref, f32[520,1]{1,0:T(8,128)S(1)} %broadcast_in_dim.27.ids_ref, f32[1,640]{1,0:T(1,128)S(1)} %collective-permute-done.3.next_ref.refs_7_, f32[3,256,512]{2,1,0:T(8,128)S(1)} %bitcast.16, f32[1,512]{1,0:T(1,128)S(1)} %bitcast.23), custom_call_target="tpu_custom_call" | custom-call | flops 1207959552 | bytes 2097152 | tf_op jit(solution)/shard_map/prepare/pallas_call | solution.py:319
  23.1 2.8 %copy-done = bf16[2048,3,512]{2,0,1:T(8,128)(2,1)S(1)} copy-done((bf16[2048,3,512]{2,0,1:T(8,128)(2,1)S(1)}, bf16[2048,3,512]{2,0,1:T(8,128)(2,1)}, u32[]{:S(2)}) %copy-start) | copy-done | bytes 6291480
  25.9 5.7 %shard_map.86 = (f32[256,512]{1,0:T(8,128)S(1)}, f32[256,512]{1,0:T(8,128)S(1)}, f32[5,512]{1,0:T(8,128)S(1)}, f32[24,512]{1,0:T(8,128)S(1)}) custom-call(s32[4]{0:T(128)S(1)} %pad_add_fusion.where_ref, bf16[528,512]{1,0:T(8,128)(2,1)} %get-tuple-element.25.refs_0_, bf16[528,512]{1,0:T(8,128)(2,1)} %collective-permute-done.refs_1_, ...), custom_call_target="tpu_custom_call" | custom-call | flops 1711276032 | bytes 6291456 | tf_op jit(solution)/shard_map/pallas_call | solution.py:364
  31.7 5.4 %shard_map.87 = (f32[256,512]{1,0:T(8,128)S(1)}, f32[256,512]{1,0:T(8,128)S(1)}, f32[5,512]{1,0:T(8,128)S(1)}, f32[8,8,128]{2,1,0:T(8,128)S(1)}) custom-call(s32[4]{0:T(128)S(1)} %pad_add_fusion.where_ref, bf16[528,512]{1,0:T(8,128)(2,1)} %get-tuple-element.25.refs_0_, bf16[528,512]{1,0:T(8,128)(2,1)} %collective-permute-done.refs_1_, ...), custom_call_target="tpu_custom_call" | custom-call | flops 1610612736 | bytes 6291456 | tf_op jit(solution)/shard_map/pallas_call | solution.py:364
  37.0 12.5 %all_to_all.10.refs_5_ = f32[8,8,128]{2,1,0:T(8,128)S(1)} all-to-all(f32[8,8,128]{2,1,0:T(8,128)S(1)} %get-tuple-element.35), channel_id=1, replica_groups=mesh['tm'=8,'hid'=4] {'tm'}, dimensions={0} | all-to-all | bytes 65536 | tf_op jit(solution)/shard_map/all_to_all | solution.py:376
  49.5 0.9 %shard_map.88 = (f32[512,512]{1,0:T(8,128)S(1)}, f32[1,512]{1,0:T(1,128)S(1)}, bf16[512,512]{1,0:T(8,128)(2,1)S(1)}, bf16[256,512]{1,0:T(8,128)(2,1)S(1)}, bf16[256,512]{1,0:T(8,128)(2,1)S(1)}) custom-call(s32[4]{0:T(128)S(1)} %pad_add_fusion.where_ref, f32[256,512]{1,0:T(8,128)S(1)} %get-tuple-element.27.refs_0_, f32[256,512]{1,0:T(8,128)S(1)} %get-tuple-element.28.refs_1_, ...), custom_call_target="tpu_custom_call" | custom-call | flops 524288 | bytes 4194304 | tf_op jit(solution)/shard_map/pallas_call | solution.py:386
  50.4 1.6 %collective-permute-start.7 = (bf16[256,512]{1,0:T(8,128)(2,1)S(1)}, bf16[256,512]{1,0:T(8,128)(2,1)S(1)}, u32[]{:S(2)}, u32[]{:S(2)}) collective-permute-start(bf16[256,512]{1,0:T(8,128)(2,1)S(1)} %get-tuple-element.37), channel_id=1, source_target_pairs={{0,2},{1,3},{2,0},{3,1},{4,6},{5,7},{6,4},{7,5},{8,10},{9,11},{10,... | collective-permute-start | bytes 786440 | tf_op jit(solution)/shard_map/ppermute | solution.py:23
  52.5 7.1 %collective-permute-done.7.refs_2_ = bf16[256,512]{1,0:T(8,128)(2,1)S(1)} collective-permute-done((bf16[256,512]{1,0:T(8,128)(2,1)S(1)}, bf16[256,512]{1,0:T(8,128)(2,1)S(1)}, u32[]{:S(2)}, u32[]{:S(2)}) %collective-permute-start.7) | collective-permute-done | bytes 262176 | tf_op jit(solution)/shard_map/ppermute | solution.py:23
  59.7 3.7 %collective-permute-done.9.refs_2_ = bf16[256,512]{1,0:T(8,128)(2,1)S(1)} collective-permute-done((bf16[256,512]{1,0:T(8,128)(2,1)S(1)}, bf16[256,512]{1,0:T(8,128)(2,1)S(1)}, u32[]{:S(2)}, u32[]{:S(2)}) %collective-permute-start.9) | collective-permute-done | bytes 262176 | tf_op jit(solution)/shard_map/ppermute | solution.py:23
  63.4 4.5 %shard_map.89 = (f32[256,512]{1,0:T(8,128)S(1)}, f32[256,512]{1,0:T(8,128)S(1)}, f32[5,512]{1,0:T(8,128)S(1)}) custom-call(s32[4]{0:T(128)S(1)} %pad_add_fusion.where_ref, bf16[512,512]{1,0:T(8,128)(2,1)S(1)} %get-tuple-element.36.refs_0_, bf16[512,512]{1,0:T(8,128)(2,1)S(1)} %collective-permute-done.6.refs_1_, ...), custom_call_target="tpu_custom_call" | custom-call | flops 1610612736 | bytes 6291456 | tf_op jit(solution)/shard_map/pallas_call | solution.py:364
  68.0 4.7 %shard_map.90 = (f32[256,512]{1,0:T(8,128)S(1)}, f32[256,512]{1,0:T(8,128)S(1)}, f32[5,512]{1,0:T(8,128)S(1)}, f32[32,9,128]{2,1,0:T(8,128)S(1)}) custom-call(s32[4]{0:T(128)S(1)} %pad_add_fusion.where_ref, bf16[512,512]{1,0:T(8,128)(2,1)S(1)} %get-tuple-element.36.refs_0_, bf16[512,512]{1,0:T(8,128)(2,1)S(1)} %collective-permute-done.6.refs_1_, ...), custom_call_target="tpu_custom_call" | custom-call | flops 1610612736 | bytes 6291456 | tf_op jit(solution)/shard_map/pallas_call | solution.py:364
  72.7 12.7 %all_to_all.11.refs_5_ = f32[32,9,128]{2,1,0:T(8,128)S(1)} all-to-all(f32[32,9,128]{2,1,0:T(8,128)S(1)} %get-tuple-element.47), channel_id=1, replica_groups=mesh['tm'=8,'hid'=4] {'tm','hid'}, dimensions={0} | all-to-all | bytes 294912 | tf_op jit(solution)/shard_map/all_to_all | solution.py:376
  85.3 2.0 %shard_map.91 = (f32[512,512]{1,0:T(8,128)}, f32[2]{0:T(128)}) custom-call(s32[4]{0:T(128)S(1)} %pad_add_fusion.where_ref, f32[256,512]{1,0:T(8,128)S(1)} %get-tuple-element.40.refs_0_, f32[256,512]{1,0:T(8,128)S(1)} %get-tuple-element.41.refs_1_, f32[256,512]{1,0:T(8,128)S(1)} %get-tuple-element.44.refs_2_, f32[256,512]{1,0:T(8,128)S(1)} %get-tuple-element.45.refs_3_, ...), custom_call_target="tpu_custom_call" | custom-call | flops 524288 | bytes 4194304 | tf_op jit(solution)/shard_map/pallas_call | solution.py:386
  (38 shorter events, 2.0 us)
Async XLA Ops:
  0.6 1.2 %copy-start.1 = (f32[512,512]{1,0:T(8,128)S(1)}, f32[512,512]{1,0:T(8,128)}, u32[]{:S(2)}) copy-start(f32[512,512]{1,0:T(8,128)} %refs_6_.3) | copy-start | bytes 3145732
  1.9 0.7 copy-start.5
  2.5 20.5 %copy-start.2 = (f32[512,512]{1,0:T(8,128)S(1)}, f32[512,512]{1,0:T(8,128)}, u32[]{:S(2)}) copy-start(f32[512,512]{1,0:T(8,128)} %refs_6_.3) | copy-start | bytes 3145732
  2.5 29.1 %slice-start = ((s8[6291456]{0:T(1024)(128)(4,1)}), s8[2097152]{0:T(1024)(128)(4,1)S(1)}, s32[]{:S(2)}) async-start(s8[6291456]{0:T(1024)(128)(4,1)} %bitcast.11), calls=%async_computation.2 | async-start | bytes 4194304
  3.5 10.5 %collective-permute-start.1 = (bf16[272,512]{1,0:T(8,128)(2,1)S(1)}, bf16[272,512]{1,0:T(8,128)(2,1)S(1)}, u32[]{:S(2)}, u32[]{:S(2)}) collective-permute-start(bf16[272,512]{1,0:T(8,128)(2,1)S(1)} %get-tuple-element.26), channel_id=1, source_target_pairs={{0,2},{1,3},{2,0},{3,1},{4,6},{5,7},{6,4},{7,5},{8,10},{9,11},{10,... | collective-permute-start | bytes 835592 | tf_op jit(solution)/shard_map/ppermute | solution.py:23
  6.5 16.5 %collective-permute-start = (bf16[528,512]{1,0:T(8,128)(2,1)}, bf16[528,512]{1,0:T(8,128)(2,1)}, u32[]{:S(2)}, u32[]{:S(2)}) collective-permute-start(bf16[528,512]{1,0:T(8,128)(2,1)} %get-tuple-element.25.refs_0_), channel_id=1, source_target_pairs={{0,1},{1,0},{2,3},{3,2},{4,5},{5,4},{6,7},{7,6},{8,9},{9,8},{10,11... | collective-permute-start | bytes 1622024 | tf_op jit(solution)/shard_map/ppermute | solution.py:23
  6.5 12.4 %collective-permute-start.4 = (bf16[256,512]{1,0:T(8,128)(2,1)}, bf16[256,512]{1,0:T(8,128)(2,1)}, u32[]{:S(2)}, u32[]{:S(2)}) collective-permute-start(bf16[256,512]{1,0:T(8,128)(2,1)} %get-tuple-element.29), channel_id=1, source_target_pairs={{0,2},{1,3},{2,0},{3,1},{4,6},{5,7},{6,4},{7,5},{8,10},{9,11},{10,... | collective-permute-start | bytes 786440 | tf_op jit(solution)/shard_map/ppermute | solution.py:23
  8.4 10.5 %collective-permute-start.3 = (f32[1,640]{1,0:T(1,128)S(1)}, f32[1,640]{1,0:T(1,128)S(1)}, u32[]{:S(2)}, u32[]{:S(2)}) collective-permute-start(f32[1,640]{1,0:T(1,128)S(1)} %concatenate.7), channel_id=1, source_target_pairs={{4,0},{8,4},{12,8},{16,12},{20,16},{24,20},{28,24},{5,1},{9,5},{13... | collective-permute-start | bytes 7688 | tf_op jit(solution)/shard_map/ppermute | solution.py:28
  14.0 9.0 %collective-permute-start.2 = (bf16[272,512]{1,0:T(8,128)(2,1)S(1)}, bf16[272,512]{1,0:T(8,128)(2,1)}, u32[]{:S(2)}, u32[]{:S(2)}) collective-permute-start(bf16[272,512]{1,0:T(8,128)(2,1)S(1)} %collective-permute-done.1.refs_2_), channel_id=1, source_target_pairs={{0,1},{1,0},{2,3},{3,2},{4,5},{5,4},{6,7},{7,6},{8,9},{9,8},{10,11... | collective-permute-start | bytes 835592 | tf_op jit(solution)/shard_map/ppermute | solution.py:23
  18.9 12.7 %collective-permute-start.5 = (bf16[256,512]{1,0:T(8,128)(2,1)}, bf16[256,512]{1,0:T(8,128)(2,1)S(1)}, u32[]{:S(2)}, u32[]{:S(2)}) collective-permute-start(bf16[256,512]{1,0:T(8,128)(2,1)} %collective-permute-done.4.refs_2_), channel_id=1, source_target_pairs={{0,1},{1,0},{2,3},{3,2},{4,5},{5,4},{6,7},{7,6},{8,9},{9,8},{10,11... | collective-permute-start | bytes 786440 | tf_op jit(solution)/shard_map/ppermute | solution.py:23
  18.9 1.4 %copy-start.3 = (f32[256,3,512]{2,0,1:T(8,128)S(1)}, f32[256,3,512]{2,0,1:T(8,128)}, u32[]{:S(2)}) copy-start(f32[256,3,512]{2,0,1:T(8,128)} %param.8) | copy-start | bytes 4718596
  20.3 0.7 copy-start.7
  21.0 2.1 %copy-start.4 = (f32[512]{0:T(512)S(1)}, f32[512]{0:T(512)}, u32[]{:S(2)}) copy-start(f32[512]{0:T(512)} %param.11) | copy-start | bytes 6148
  21.0 2.1 %copy-start.6 = (f32[512]{0:T(512)S(1)}, f32[512]{0:T(512)}, u32[]{:S(2)}) copy-start(f32[512]{0:T(512)} %param.12) | copy-start | bytes 6148
  23.1 2.8 %copy-start = (bf16[2048,3,512]{2,0,1:T(8,128)(2,1)S(1)}, bf16[2048,3,512]{2,0,1:T(8,128)(2,1)}, u32[]{:S(2)}) copy-start(bf16[2048,3,512]{2,0,1:T(8,128)(2,1)} %param.9) | copy-start | bytes 18874372
  25.9 5.8 %slice-start.1 = ((s8[6291456]{0:T(1024)(128)(4,1)}), s8[4194304]{0:T(1024)(128)(4,1)S(1)}, s32[]{:S(2)}) async-start(s8[6291456]{0:T(1024)(128)(4,1)} %bitcast.11), calls=%async_computation.3 | async-start | bytes 8388608
  50.4 9.2 %collective-permute-start.7 = (bf16[256,512]{1,0:T(8,128)(2,1)S(1)}, bf16[256,512]{1,0:T(8,128)(2,1)S(1)}, u32[]{:S(2)}, u32[]{:S(2)}) collective-permute-start(bf16[256,512]{1,0:T(8,128)(2,1)S(1)} %get-tuple-element.37), channel_id=1, source_target_pairs={{0,2},{1,3},{2,0},{3,1},{4,6},{5,7},{6,4},{7,5},{8,10},{9,11},{10,... | collective-permute-start | bytes 786440 | tf_op jit(solution)/shard_map/ppermute | solution.py:23
  52.0 11.4 %collective-permute-start.6 = (bf16[512,512]{1,0:T(8,128)(2,1)S(1)}, bf16[512,512]{1,0:T(8,128)(2,1)S(1)}, u32[]{:S(2)}, u32[]{:S(2)}) collective-permute-start(bf16[512,512]{1,0:T(8,128)(2,1)S(1)} %get-tuple-element.36.refs_0_), channel_id=1, source_target_pairs={{0,1},{1,0},{2,3},{3,2},{4,5},{5,4},{6,7},{7,6},{8,9},{9,8},{10,11... | collective-permute-start | bytes 1572872 | tf_op jit(solution)/shard_map/ppermute | solution.py:23
  52.0 11.4 %collective-permute-start.9 = (bf16[256,512]{1,0:T(8,128)(2,1)S(1)}, bf16[256,512]{1,0:T(8,128)(2,1)S(1)}, u32[]{:S(2)}, u32[]{:S(2)}) collective-permute-start(bf16[256,512]{1,0:T(8,128)(2,1)S(1)} %get-tuple-element.42), channel_id=1, source_target_pairs={{0,2},{1,3},{2,0},{3,1},{4,6},{5,7},{6,4},{7,5},{8,10},{9,11},{10,... | collective-permute-start | bytes 786440 | tf_op jit(solution)/shard_map/ppermute | solution.py:23
  59.7 3.7 %collective-permute-start.8 = (bf16[256,512]{1,0:T(8,128)(2,1)S(1)}, bf16[256,512]{1,0:T(8,128)(2,1)S(1)}, u32[]{:S(2)}, u32[]{:S(2)}) collective-permute-start(bf16[256,512]{1,0:T(8,128)(2,1)S(1)} %collective-permute-done.7.refs_2_), channel_id=1, source_target_pairs={{0,1},{1,0},{2,3},{3,2},{4,5},{5,4},{6,7},{7,6},{8,9},{9,8},{10,11... | collective-permute-start | bytes 786440 | tf_op jit(solution)/shard_map/ppermute | solution.py:23
  63.4 4.6 %collective-permute-start.10 = (bf16[256,512]{1,0:T(8,128)(2,1)S(1)}, bf16[256,512]{1,0:T(8,128)(2,1)S(1)}, u32[]{:S(2)}, u32[]{:S(2)}) collective-permute-start(bf16[256,512]{1,0:T(8,128)(2,1)S(1)} %collective-permute-done.9.refs_2_), channel_id=1, source_target_pairs={{0,1},{1,0},{2,3},{3,2},{4,5},{5,4},{6,7},{7,6},{8,9},{9,8},{10,11... | collective-permute-start | bytes 786440 | tf_op jit(solution)/shard_map/ppermute | solution.py:23

commit v2 on v1

--- a/solution.py
+++ b/solution.py
@@ -48,13 +48,15 @@
     return pl.CostEstimate(flops=flops, bytes_accessed=moved, transcendentals=0)
 
 
-def round_kernel(chunks, guess_ref, init_ref, whole_ref, *parts):
+def round_kernel(chunks, ids_ref, guess_ref, init_ref, whole_ref, lead_ref, *parts):
     rows, width = guess_ref.shape
     chunk = rows // chunks
     row = lax.broadcasted_iota(jnp.int32, (EXTRA, width), 0)
-    lead = jnp.where(row == 0, jnp.broadcast_to(init_ref[...], (EXTRA, width)), 0.0).astype(BF16)
-    whole_ref[pl.ds(0, EXTRA), :] = lead
-    parts[0][pl.ds(0, EXTRA), :] = lead
+    head = jnp.where(row == 0, jnp.broadcast_to(init_ref[...], (EXTRA, width)), 0.0).astype(BF16)
+    whole_ref[pl.ds(0, EXTRA), :] = head
+    parts[0][pl.ds(0, EXTRA), :] = head
+    lead_ref[:, pl.ds(0, width)] = guess_ref[0:1, :]
+    lead_ref[:, pl.ds(width, LANES)] = jnp.full((1, LANES), ids_ref[0], jnp.int32).astype(F32)
     for index, part in enumerate(parts):
         skip = 0 if index else EXTRA
         for start in range(0, chunk, GROUP * 4):
@@ -63,13 +65,23 @@
             part[pl.ds(skip + start, GROUP * 4), :] = block
 
 
-def prepare_kernel(where_ref, ids_ref, next_ref, table_ref, bias_ref, out_ref):
-    rows = ids_ref.shape[0]
+def prepare_kernel(ids_ref, next_ref, table_ref, bias_ref, out_ref):
     vocab, width = table_ref.shape[1:]
-    token = lax.broadcasted_iota(jnp.int32, (rows, 1), 0)
-    ids = jnp.where(token == rows - GROUP - 1, jnp.broadcast_to(next_ref[:, width : width + 1], (rows, 1)), ids_ref[...])
-    entry = lax.broadcasted_iota(jnp.int32, (rows, vocab), 1).astype(F32)
-    hot = (entry == ids).astype(F32).astype(BF16)
+    rows = ids_ref.shape[1]
+    ids = ids_ref[...].astype(F32)
+    lane = lax.broadcasted_iota(jnp.int32, (1, rows), 1)
+    following = jnp.broadcast_to(next_ref[:, width : width + 1], (1, rows))
+    ids = jnp.where(lane == rows - 1, following, pltpu.roll(ids, rows - 1, 1))
+    begin = jnp.broadcast_to(ids_ref[:, 0:1].astype(F32), (1, LANES))
+
+    def spread(line):
+        entry = lax.broadcasted_iota(jnp.int32, (vocab, line.shape[1]), 0).astype(F32)
+        return (entry == line).astype(F32).astype(BF16)
+
+    def pick(hot, part):
+        return lax.dot_general(hot, part, (((0,), (0,)), ((), ())), preferred_element_type=F32)
+
+    hot, hot_begin = spread(ids), spread(begin)
     for gate in range(3):
         table = table_ref[gate]
         if gate == 0:
@@ -78,9 +90,10 @@
         for _ in range(3):
             part = table.astype(BF16)
             table = table - part.astype(F32)
-            picked = jnp.dot(hot, part, preferred_element_type=F32)
-            total = picked if total is None else total + picked
-        out_ref[gate] = total
+            picked = (pick(hot, part), pick(hot_begin, part))
+            total = picked if total is None else (total[0] + picked[0], total[1] + picked[1])
+        out_ref[gate, pl.ds(0, rows), :] = total[0]
+        out_ref[gate, pl.ds(rows, GROUP), :] = total[1][0:GROUP]
 
 
 def diagonals(weight_ref, hid, diag_ref):
@@ -104,7 +117,7 @@
     return zeta, reset, gated, cand, gap, cand + zeta * gap
 
 
-def step_kernel(count, index, chunks, step, copies, where_ref, *refs):
+def step_kernel(count, index, chunks, step, copies, *refs):
     refs = list(refs)
     near = [refs.pop(0) for _ in range(count // 2)]
     far = [refs.pop(0) for _ in range(count // 2)]
@@ -115,17 +128,18 @@
     diag_ref = refs.pop(0) if begins else diag_ref
     last = index == chunks - 1
     send_ref = refs.pop(0) if last else None
-    lhs, products = refs
-    height = lhs.shape[0]
+    lhs, *products = refs
+    height, full = lhs.shape
     rows, width = state_ref.shape
     chunk = rows // chunks
     start = index * chunk
     lead = height - chunk
     skip = EXTRA if step == 0 else 0
-    hid = where_ref[0]
-    is_first = where_ref[1]
-    is_last = where_ref[2]
+    hid = lax.axis_index("hid")
+    is_first = lax.axis_index("tm") == 0
+    is_last = lax.axis_index("tm") == lax.axis_size("tm") - 1
     groups = chunk // GROUP
+    tiles = width // TILE
 
     if begins:
         diagonals(weight_ref, hid, diag_ref)
@@ -136,33 +150,44 @@
         else:
             lhs[:, pl.ds(place, width)] = far[offset - count // 2][...]
     row = lax.broadcasted_iota(jnp.int32, (GROUP, TILE), 0)
-
-    for tile in range(width // TILE):
+    zeros = jnp.zeros((GROUP, TILE), F32)
+
+    def dots(tile):
         lanes = pl.ds(tile * TILE, TILE)
-        for gate in range(3):
-            products[gate] = jnp.dot(lhs[...], weight_ref[gate, :, lanes], preferred_element_type=F32)
+        half = full // 2
+        for gate in range(2):
+            products[tile][gate] = jnp.dot(lhs[...], weight_ref[gate, :, lanes], preferred_element_type=F32)
+        left = jnp.dot(lhs[:, pl.ds(0, half)], weight_ref[2, pl.ds(0, half), lanes], preferred_element_type=F32)
+        right = jnp.dot(lhs[:, pl.ds(half, half)], weight_ref[2, pl.ds(half, half), lanes], preferred_element_type=F32)
+        products[tile][2] = left + right
+
+    def cells(tile):
+        lanes = pl.ds(tile * TILE, TILE)
         hn_bias = jnp.broadcast_to(bias_ref[:, lanes], (GROUP, TILE))
         diag_z = diag_ref[pl.ds(0, GROUP), lanes]
         diag_r = diag_ref[pl.ds(GROUP, GROUP), lanes]
         diag_n = diag_ref[pl.ds(2 * GROUP, GROUP), lanes]
-
-        def advance(group, carry):
-            turned, run_a, run_b, squares = carry
-            here = pl.ds(pl.multiple_of(group * GROUP, GROUP), GROUP)
-            token = pl.ds(pl.multiple_of(start + group * GROUP, GROUP), GROUP)
+        squares = zeros
+        if index == 0:
+            run_a, run_b = jnp.ones((GROUP, TILE), F32), zeros
+        else:
+            run_a = jnp.broadcast_to(before_ref[0:1, lanes], (GROUP, TILE))
+            run_b = jnp.broadcast_to(before_ref[1:2, lanes], (GROUP, TILE))
+        turned = pltpu.roll(state_ref[pl.ds(start, GROUP), lanes], GROUP - 1, 0)
+        for group in range(groups):
+            here = pl.ds(group * GROUP, GROUP)
+            token = pl.ds(start + group * GROUP, GROUP)
             prev = state_ref[token, lanes]
-            after = start + group * GROUP + GROUP
-            if last:
-                after = jnp.minimum(after, rows - GROUP)
-            following = state_ref[pl.ds(pl.multiple_of(after, GROUP), GROUP), lanes]
-            if last:
-                following = jnp.where(group == groups - 1, jnp.broadcast_to(next_ref[:, lanes], (GROUP, TILE)), following)
+            if last and group == groups - 1:
+                following = jnp.broadcast_to(next_ref[:, lanes], (GROUP, TILE))
+            else:
+                following = state_ref[pl.ds(start + (group + 1) * GROUP, GROUP), lanes]
             turned_next = pltpu.roll(following, GROUP - 1, 0)
             state = jnp.where(row == GROUP - 1, turned_next, turned)
-            product = pl.ds(pl.multiple_of(lead + group * GROUP, GROUP), GROUP)
+            turned = turned_next
             zeta, reset, gated, cand, gap, value = gates(
                 [inputs_ref[gate, token, lanes] for gate in range(3)],
-                [products[gate, product, :] for gate in range(3)],
+                [products[tile][gate, pl.ds(lead + group * GROUP, GROUP), :] for gate in range(3)],
                 prev,
                 hn_bias,
             )
@@ -170,9 +195,8 @@
             slope = zeta + gap * (zeta * rest) * diag_z
             slope = slope + rest * (1.0 - cand * cand) * (reset * diag_n + gated * (1.0 - reset) * diag_r)
             error = state - value
-            if last:
-                outside = (row == GROUP - 1) & (group == groups - 1) & (is_last == 1)
-                error = jnp.where(outside, 0.0, error)
+            if last and group == groups - 1:
+                error = jnp.where((row == GROUP - 1) & is_last, 0.0, error)
             squares = squares + error * error
             a = slope
             b = value - slope * prev
@@ -186,48 +210,43 @@
             b_ref[here, lanes] = a * run_b + b
             last_a = jnp.broadcast_to(a[GROUP - 1 :], (GROUP, TILE))
             last_b = jnp.broadcast_to(b[GROUP - 1 :], (GROUP, TILE))
-            return (turned_next, last_a * run_a, last_a * run_b + last_b, squares)
-
-        turned = pltpu.roll(state_ref[pl.ds(start, GROUP), lanes], GROUP - 1, 0)
-        zeros = jnp.zeros((GROUP, TILE), F32)
-        if index == 0:
-            carry = (turned, jnp.ones((GROUP, TILE), F32), zeros, zeros)
-        else:
-            carry = (
-                turned,
-                jnp.broadcast_to(before_ref[0:1, lanes], (GROUP, TILE)),
-                jnp.broadcast_to(before_ref[1:2, lanes], (GROUP, TILE)),
-                jnp.where(row == 0, before_ref[2:3, lanes], 0.0),
-            )
-        _, run_a, run_b, squares = lax.fori_loop(0, groups, advance, carry, unroll=4)
+            run_a, run_b = last_a * run_a, last_a * run_b + last_b
         if begins:
             begin = gates(
                 [inputs_ref[gate, pl.ds(rows, GROUP), lanes] for gate in range(3)],
-                [products[gate, pl.ds(0, GROUP), :] for gate in range(3)],
+                [products[tile][gate, pl.ds(0, GROUP), :] for gate in range(3)],
                 jnp.broadcast_to(before_ref[:, lanes], (GROUP, TILE)),
                 hn_bias,
             )[-1]
             error = state_ref[pl.ds(0, GROUP), lanes] - begin
-            squares = squares + jnp.where((row == 0) & (is_first == 1), error * error, 0.0)
+            squares = squares + jnp.where((row == 0) & is_first, error * error, 0.0)
             begin = begin[0:1]
             earlier = zeros[0:1]
         else:
             begin = before_ref[3:4, lanes]
             earlier = before_ref[2:3, lanes] if index == 0 else before_ref[4:5, lanes]
         total = jnp.sum(squares, axis=0, keepdims=True)
+        if index:
+            total = total + before_ref[2:3, lanes]
         ends_ref[0:1, lanes] = run_a[0:1]
         ends_ref[1:2, lanes] = run_b[0:1]
         ends_ref[2:3, lanes] = total
         ends_ref[3:4, lanes] = begin
         ends_ref[4:5, lanes] = earlier
         if last:
-            send_a = jnp.where(is_first == 1, 0.0, run_a[0:1])
-            send_b = jnp.where(is_first == 1, run_a[0:1] * begin + run_b[0:1], run_b[0:1])
+            send_a = jnp.where(is_first, 0.0, run_a[0:1])
+            send_b = jnp.where(is_first, run_a[0:1] * begin + run_b[0:1], run_b[0:1])
             for part in range(TILE // LANES):
                 at = tile * (TILE // LANES) + part
                 for line, sent in ((at, send_a), (width // LANES + at, send_b)):
                     picked = sent[:, part * LANES : (part + 1) * LANES]
                     send_ref[:, pl.ds(line, 1), :] = jnp.broadcast_to(picked[None], (copies, 1, LANES))
+
+    dots(0)
+    for tile in range(1, tiles):
+        dots(tile)
+        cells(tile - 1)
+    cells(tiles - 1)
     if last and step == ITERS - 1:
         lane = lax.broadcasted_iota(jnp.int32, (1, LANES), 1)
         sums = jnp.zeros((1, LANES), F32)
@@ -238,14 +257,14 @@
         send_ref[:, pl.ds(2 * width // LANES, 1), :] = jnp.broadcast_to(sums[None], (copies, 1, LANES))
 
 
-def apply_kernel(chunks, final, count, where_ref, *refs):
+def apply_kernel(chunks, final, count, *refs):
     maps, refs = refs[: 2 * chunks], refs[2 * chunks :]
     begin_ref, all_ref, state_ref = refs[:3]
     outs = refs[3:]
     chunk, width = maps[0].shape
     lines = width // LANES
-    place = where_ref[3]
-    hid = where_ref[0]
+    place = lax.axis_index("tm")
+    hid = lax.axis_index("hid")
     copies = all_ref.shape[0]
     peers = copies // count if final else copies
 
@@ -292,39 +311,33 @@
     full = recur_weight.shape[0]
     count = lax.axis_size("hid")
     blocks_tm = lax.axis_size("tm")
-    hid = lax.axis_index("hid")
-    tm = lax.axis_index("tm")
     weight = jnp.transpose(recur_weight, (1, 0, 2))
     table = jnp.transpose(input_table, (1, 0, 2))
     chunk = rows // CHUNKS
     lines = width // LANES
-    where = jnp.stack([hid, (tm == 0).astype(jnp.int32), (tm == blocks_tm - 1).astype(jnp.int32), tm])
 
     state = guess
-    whole, *moved = pl.pallas_call(
+    whole, lead, *moved = pl.pallas_call(
         functools.partial(round_kernel, CHUNKS),
-        out_shape=[jax.ShapeDtypeStruct((rows + EXTRA, width), BF16)]
+        out_shape=[jax.ShapeDtypeStruct((rows + EXTRA, width), BF16), jax.ShapeDtypeStruct((1, width + LANES), F32)]
         + [jax.ShapeDtypeStruct((chunk + (0 if index else EXTRA), width), BF16) for index in range(CHUNKS)],
-        in_specs=vmem(2),
-        out_specs=vmem(1 + CHUNKS),
+        in_specs=smem() + vmem(2),
+        out_specs=vmem(2 + CHUNKS),
         compiler_params=params(16),
         cost_estimate=cost(rows * width, 8 * rows * width),
         name="round",
-    )(guess, init_state[None])
-
-    ids = token_ids.astype(F32)
-    lead = jnp.concatenate([guess[:1], jnp.broadcast_to(ids[:1, None], (1, LANES))], 1)
+    )(token_ids, guess, init_state[None])
+
     following = from_next(lead, "tm")
-    ids = jnp.concatenate([ids[1:], ids[:1], ids[:1], jnp.zeros((GROUP - 1,), F32)])
     inputs = pl.pallas_call(
         prepare_kernel,
         out_shape=jax.ShapeDtypeStruct((3, rows + GROUP, width), F32),
-        in_specs=smem() + vmem(4),
+        in_specs=vmem(4),
         out_specs=vmem(1)[0],
         compiler_params=params(32),
         cost_estimate=cost(18 * rows * table.shape[1] * width, 8 * rows * width),
         name="prepare",
-    )(where, ids[:, None], following, table, z_bias[None])
+    )(token_ids[None], following, table, z_bias[None])
 
     ends = init_state[None]
     diag = None
@@ -364,12 +377,13 @@
             found = pl.pallas_call(
                 functools.partial(step_kernel, count, index, CHUNKS, step, copies),
                 out_shape=outs,
-                in_specs=smem() + vmem(len(operands)),
+                in_specs=vmem(len(operands)),
                 out_specs=vmem(len(outs)),
-                scratch_shapes=[pltpu.VMEM((height, full), BF16), pltpu.VMEM((3, height, TILE), F32)],
+                scratch_shapes=[pltpu.VMEM((height, full), BF16)]
+                + [pltpu.VMEM((3, height, TILE), F32)] * (width // TILE),
                 compiler_params=params(32),
                 cost_estimate=cost(2 * height * full * 3 * width, 6 * full * width),
-            )(where, *operands)
+            )(*operands)
             maps += found[:2]
             ends = found[2]
             diag = found[3] if diag is None else diag
@@ -386,11 +400,11 @@
         result = pl.pallas_call(
             functools.partial(apply_kernel, CHUNKS, final, count),
             out_shape=outs,
-            in_specs=smem() + vmem(2 * CHUNKS + 2),
+            in_specs=vmem(2 * CHUNKS + 2),
             out_specs=specs,
             compiler_params=params(16),
             cost_estimate=cost(2 * rows * width, 16 * rows * width),
-        )(where, *maps, ends, every)
+        )(*maps, ends, every)
         if final:
             return (result[0], result[1])
         state, following, whole, *moved = result

time: 87.7 us -> 79.4 us (0.905)
  Pallas kernels: 26.2 us -> 16.3 us
  waiting for transfers between devices: 19.1 us -> 21.5 us
  other arithmetic: 1.48 us -> 0 us
    pallas_call x4, Pallas kernels: 20.3 us -> 11.9 us  [newton(): pl.pallas_call(functools.partial(step_kernel, count, index, CHUNKS, step,...]
    ppermute x10, waiting for transfers between devices: 19.1 us -> 20.8 us  [swapped(): return lax.ppermute(block, axis, route)]
    unnamed x20 -> x22, local copies, waits for them, and re-layouts: 6.79 us -> 8.14 us
    pallas_call x2, Pallas kernels: 2.88 us -> 1.8 us  [newton(): pl.pallas_call(functools.partial(apply_kernel, CHUNKS, final, count), out...]
  transfers between devices with their start and end apart: 11 -> 11, of which waited for: 4 -> 5; matrix products, arithmetic and copies ran while one was open for 3% -> 0% of each run, Pallas kernels for 14% -> 10%
where the time goes in v2:
time: 79.4 us; the launch traced here: 79 us
  blocking collectives  25.5 us (32%)
  waiting for transfers between devices  21.5 us (27%)
  Pallas kernels  16.3 us (21%)
  local copies, waits for them, and re-layouts  8.14 us (10%)
  starting transfers between devices  6.6 us (8%)
  between operations  0.95 us (1%)
    all_to_all x2, blocking collectives, newton(): every = lax.all_to_all(found[-1], ('tm', 'hid') if final else 'tm', 0, 0)  25.5 us
    ppermute x10, waiting for transfers between devices, swapped(): return lax.ppermute(block, axis, route)  20.8 us
    pallas_call x4, Pallas kernels, newton(): pl.pallas_call(functools.partial(step_kernel, count, index, CHUNKS, step,...  11.9 us
    unnamed x22, local copies, waits for them, and re-layouts  8.14 us
    ppermute x10, starting transfers between devices, swapped(): return lax.ppermute(block, axis, route)  5.32 us
    pallas_call x1, Pallas kernels, newton(): pl.pallas_call(prepare_kernel, out_shape=jax.ShapeDtypeStruct((3, rows +...  1.97 us
    pallas_call x2, Pallas kernels, newton(): pl.pallas_call(functools.partial(apply_kernel, CHUNKS, final, count), out...  1.8 us
  transfers between devices with their start and end apart: 11, of which 5 were waited for; matrix products, arithmetic and copies ran while one was open for 0% of the time, Pallas kernels for 10%

profile of v2, /device:TPU:0, one launch (start us, length us, event | category | flops | bytes accessed | tf_op | source)
XLA Modules:
  0.0 79.0 jit_solution(3632849805219931656)
XLA Ops:
  0.6 1.2 %copy-done.2 = f32[512,512]{1,0:T(8,128)S(1)} copy-done((f32[512,512]{1,0:T(8,128)S(1)}, f32[512,512]{1,0:T(8,128)}, u32[]{:S(2)}) %copy-start.2) | copy-done | bytes 1048600
  1.9 0.7 copy-done.6
  2.5 0.7 copy-done.8
  3.2 0.6 round.1
  3.9 3.1 %collective-permute-start.1 = (bf16[272,512]{1,0:T(8,128)(2,1)S(1)}, bf16[272,512]{1,0:T(8,128)(2,1)S(1)}, u32[]{:S(2)}, u32[]{:S(2)}) collective-permute-start(bf16[272,512]{1,0:T(8,128)(2,1)S(1)} %get-tuple-element.27), channel_id=1, source_target_pairs={{0,2},{1,3},{2,0},{3,1},{4,6},{5,7},{6,4},{7,5},{8,10},{9,11},{10,... | collective-permute-start | bytes 835592 | tf_op jit(solution)/shard_map/ppermute | solution.py:23
  7.1 7.3 %collective-permute-done.1.refs_2_ = bf16[272,512]{1,0:T(8,128)(2,1)S(1)} collective-permute-done((bf16[272,512]{1,0:T(8,128)(2,1)S(1)}, bf16[272,512]{1,0:T(8,128)(2,1)S(1)}, u32[]{:S(2)}, u32[]{:S(2)}) %collective-permute-start.1) | collective-permute-done | bytes 278560 | tf_op jit(solution)/shard_map/ppermute | solution.py:23
  14.4 1.3 %collective-permute-start.3 = (f32[1,640]{1,0:T(1,128)S(1)}, f32[1,640]{1,0:T(1,128)S(1)}, u32[]{:S(2)}, u32[]{:S(2)}) collective-permute-start(f32[1,640]{1,0:T(1,128)S(1)} %get-tuple-element.28), channel_id=1, source_target_pairs={{4,0},{8,4},{12,8},{16,12},{20,16},{24,20},{28,24},{5,1},{9,5},{13... | collective-permute-start | bytes 7688 | tf_op jit(solution)/shard_map/ppermute | solution.py:28
  15.7 3.5 %collective-permute-done.4.refs_2_ = bf16[256,512]{1,0:T(8,128)(2,1)S(1)} collective-permute-done((bf16[256,512]{1,0:T(8,128)(2,1)S(1)}, bf16[256,512]{1,0:T(8,128)(2,1)S(1)}, u32[]{:S(2)}, u32[]{:S(2)}) %collective-permute-start.4) | collective-permute-done | bytes 262176 | tf_op jit(solution)/shard_map/ppermute | solution.py:23
  19.2 0.7 collective-permute-done.3.next_ref.refs_7_
  19.9 1.4 %copy-done.4 = f32[256,3,512]{2,0,1:T(8,128)S(1)} copy-done((f32[256,3,512]{2,0,1:T(8,128)S(1)}, f32[256,3,512]{2,0,1:T(8,128)}, u32[]{:S(2)}) %copy-start.4) | copy-done | bytes 1572888
  21.3 0.7 copy-done.7
  22.0 0.7 copy-done.10
  22.7 2.0 %prepare.1.refs_5_ = f32[3,520,512]{2,1,0:T(8,128)S(1)} custom-call(s32[1,512]{1,0:T(1,128)S(1)} %bitcast.15, f32[1,640]{1,0:T(1,128)S(1)} %collective-permute-done.3.next_ref.refs_7_, f32[3,256,512]{2,1,0:T(8,128)S(1)} %bitcast.10, f32[1,512]{1,0:T(1,128)S(1)} %bitcast.18), custom_call_target="tpu_custom_call" | custom-call | flops 1207959552 | bytes 2097152 | tf_op jit(solution)/shard_map/prepare/pallas_call | solution.py:332
  24.7 2.8 %copy-done = bf16[2048,3,512]{2,0,1:T(8,128)(2,1)S(1)} copy-done((bf16[2048,3,512]{2,0,1:T(8,128)(2,1)S(1)}, bf16[2048,3,512]{2,0,1:T(8,128)(2,1)}, u32[]{:S(2)}) %copy-start) | copy-done | bytes 6291480
  27.5 3.1 %shard_map.86 = (f32[256,512]{1,0:T(8,128)S(1)}, f32[256,512]{1,0:T(8,128)S(1)}, f32[5,512]{1,0:T(8,128)S(1)}, f32[24,512]{1,0:T(8,128)S(1)}) custom-call(bf16[528,512]{1,0:T(8,128)(2,1)S(1)} %get-tuple-element.26.refs_0_, bf16[528,512]{1,0:T(8,128)(2,1)S(1)} %collective-permute-done.refs_1_, bf16[272,512]{1,0:T(8,128)(2,1)S(1)} %collective-permute-done.1.refs_2_, ...), custom_call_target="tpu_custom_call" | custom-call | flops 1711276032 | bytes 6291456 | tf_op jit(solution)/shard_map/pallas_call | solution.py:377
  30.6 2.9 %shard_map.87 = (f32[256,512]{1,0:T(8,128)S(1)}, f32[256,512]{1,0:T(8,128)S(1)}, f32[5,512]{1,0:T(8,128)S(1)}, f32[8,8,128]{2,1,0:T(8,128)S(1)}) custom-call(bf16[528,512]{1,0:T(8,128)(2,1)S(1)} %get-tuple-element.26.refs_0_, bf16[528,512]{1,0:T(8,128)(2,1)S(1)} %collective-permute-done.refs_1_, bf16[256,512]{1,0:T(8,128)(2,1)S(1)} %collective-permute-done.4.refs_2_, ...), custom_call_target="tpu_custom_call" | custom-call | flops 1610612736 | bytes 6291456 | tf_op jit(solution)/shard_map/pallas_call | solution.py:377
  33.5 12.7 %all_to_all.10.refs_5_ = f32[8,8,128]{2,1,0:T(8,128)S(1)} all-to-all(f32[8,8,128]{2,1,0:T(8,128)S(1)} %get-tuple-element.37), channel_id=1, replica_groups=mesh['tm'=8,'hid'=4] {'tm'}, dimensions={0} | all-to-all | bytes 65536 | tf_op jit(solution)/shard_map/all_to_all | solution.py:390
  46.5 1.6 %collective-permute-start.7 = (bf16[256,512]{1,0:T(8,128)(2,1)S(1)}, bf16[256,512]{1,0:T(8,128)(2,1)S(1)}, u32[]{:S(2)}, u32[]{:S(2)}) collective-permute-start(bf16[256,512]{1,0:T(8,128)(2,1)S(1)} %get-tuple-element.39), channel_id=1, source_target_pairs={{0,2},{1,3},{2,0},{3,1},{4,6},{5,7},{6,4},{7,5},{8,10},{9,11},{10,... | collective-permute-start | bytes 786440 | tf_op jit(solution)/shard_map/ppermute | solution.py:23
  48.6 6.2 %collective-permute-done.7.refs_2_ = bf16[256,512]{1,0:T(8,128)(2,1)S(1)} collective-permute-done((bf16[256,512]{1,0:T(8,128)(2,1)S(1)}, bf16[256,512]{1,0:T(8,128)(2,1)S(1)}, u32[]{:S(2)}, u32[]{:S(2)}) %collective-permute-start.7) | collective-permute-done | bytes 262176 | tf_op jit(solution)/shard_map/ppermute | solution.py:23
  54.8 3.8 %collective-permute-done.9.refs_2_ = bf16[256,512]{1,0:T(8,128)(2,1)S(1)} collective-permute-done((bf16[256,512]{1,0:T(8,128)(2,1)S(1)}, bf16[256,512]{1,0:T(8,128)(2,1)S(1)}, u32[]{:S(2)}, u32[]{:S(2)}) %collective-permute-start.9) | collective-permute-done | bytes 262176 | tf_op jit(solution)/shard_map/ppermute | solution.py:23
  58.6 2.9 %shard_map.89 = (f32[256,512]{1,0:T(8,128)S(1)}, f32[256,512]{1,0:T(8,128)S(1)}, f32[5,512]{1,0:T(8,128)S(1)}) custom-call(bf16[512,512]{1,0:T(8,128)(2,1)S(1)} %get-tuple-element.38.refs_0_, bf16[512,512]{1,0:T(8,128)(2,1)S(1)} %collective-permute-done.6.refs_1_, bf16[256,512]{1,0:T(8,128)(2,1)S(1)} %collective-permute-done.7.refs_2_, ...), custom_call_target="tpu_custom_call" | custom-call | flops 1610612736 | bytes 6291456 | tf_op jit(solution)/shard_map/pallas_call | solution.py:377
  61.6 3.0 %shard_map.90 = (f32[256,512]{1,0:T(8,128)S(1)}, f32[256,512]{1,0:T(8,128)S(1)}, f32[5,512]{1,0:T(8,128)S(1)}, f32[32,9,128]{2,1,0:T(8,128)S(1)}) custom-call(bf16[512,512]{1,0:T(8,128)(2,1)S(1)} %get-tuple-element.38.refs_0_, bf16[512,512]{1,0:T(8,128)(2,1)S(1)} %collective-permute-done.6.refs_1_, bf16[256,512]{1,0:T(8,128)(2,1)S(1)} %collective-permute-done.9.refs_2_, ...), custom_call_target="tpu_custom_call" | custom-call | flops 1610612736 | bytes 6291456 | tf_op jit(solution)/shard_map/pallas_call | solution.py:377
  64.6 12.8 %all_to_all.11.refs_5_ = f32[32,9,128]{2,1,0:T(8,128)S(1)} all-to-all(f32[32,9,128]{2,1,0:T(8,128)S(1)} %get-tuple-element.49), channel_id=1, replica_groups=mesh['tm'=8,'hid'=4] {'tm','hid'}, dimensions={0} | all-to-all | bytes 294912 | tf_op jit(solution)/shard_map/all_to_all | solution.py:390
  77.4 1.5 %shard_map.91 = (f32[512,512]{1,0:T(8,128)}, f32[2]{0:T(128)}) custom-call(f32[256,512]{1,0:T(8,128)S(1)} %get-tuple-element.42.refs_0_, f32[256,512]{1,0:T(8,128)S(1)} %get-tuple-element.43.refs_1_, f32[256,512]{1,0:T(8,128)S(1)} %get-tuple-element.46.refs_2_, f32[256,512]{1,0:T(8,128)S(1)} %get-tuple-element.47.refs_3_, ...), custom_call_target="tpu_custom_call" | custom-call | flops 524288 | bytes 4194304 | tf_op jit(solution)/shard_map/pallas_call | solution.py:400
  (30 shorter events, 1.1 us)
Async XLA Ops:
  0.6 1.2 %copy-start.2 = (f32[512,512]{1,0:T(8,128)S(1)}, f32[512,512]{1,0:T(8,128)}, u32[]{:S(2)}) copy-start(f32[512,512]{1,0:T(8,128)} %refs_6_.3) | copy-start | bytes 3145732
  1.9 0.7 copy-start.6
  2.5 0.7 copy-start.8
  3.2 21.5 %copy-start.3 = (f32[512,512]{1,0:T(8,128)S(1)}, f32[512,512]{1,0:T(8,128)}, u32[]{:S(2)}) copy-start(f32[512,512]{1,0:T(8,128)} %refs_6_.3) | copy-start | bytes 3145732
  3.2 21.5 %copy-start.5 = (f32[512]{0:T(512)S(1)}, f32[512]{0:T(512)}, u32[]{:S(2)}) copy-start(f32[512]{0:T(512)} %param.11) | copy-start | bytes 6148
  3.2 21.5 %copy-start.9 = (f32[512]{0:T(512)S(1)}, f32[512]{0:T(512)}, u32[]{:S(2)}) copy-start(f32[512]{0:T(512)} %param.12) | copy-start | bytes 6148
  3.9 10.6 %collective-permute-start.1 = (bf16[272,512]{1,0:T(8,128)(2,1)S(1)}, bf16[272,512]{1,0:T(8,128)(2,1)S(1)}, u32[]{:S(2)}, u32[]{:S(2)}) collective-permute-start(bf16[272,512]{1,0:T(8,128)(2,1)S(1)} %get-tuple-element.27), channel_id=1, source_target_pairs={{0,2},{1,3},{2,0},{3,1},{4,6},{5,7},{6,4},{7,5},{8,10},{9,11},{10,... | collective-permute-start | bytes 835592 | tf_op jit(solution)/shard_map/ppermute | solution.py:23
  6.9 17.7 %collective-permute-start = (bf16[528,512]{1,0:T(8,128)(2,1)S(1)}, bf16[528,512]{1,0:T(8,128)(2,1)S(1)}, u32[]{:S(2)}, u32[]{:S(2)}) collective-permute-start(bf16[528,512]{1,0:T(8,128)(2,1)S(1)} %get-tuple-element.26.refs_0_), channel_id=1, source_target_pairs={{0,1},{1,0},{2,3},{3,2},{4,5},{5,4},{6,7},{7,6},{8,9},{9,8},{10,11... | collective-permute-start | bytes 1622024 | tf_op jit(solution)/shard_map/ppermute | solution.py:23
  6.9 12.3 %collective-permute-start.4 = (bf16[256,512]{1,0:T(8,128)(2,1)S(1)}, bf16[256,512]{1,0:T(8,128)(2,1)S(1)}, u32[]{:S(2)}, u32[]{:S(2)}) collective-permute-start(bf16[256,512]{1,0:T(8,128)(2,1)S(1)} %get-tuple-element.31), channel_id=1, source_target_pairs={{0,2},{1,3},{2,0},{3,1},{4,6},{5,7},{6,4},{7,5},{8,10},{9,11},{10,... | collective-permute-start | bytes 786440 | tf_op jit(solution)/shard_map/ppermute | solution.py:23
  14.4 10.2 %collective-permute-start.2 = (bf16[272,512]{1,0:T(8,128)(2,1)S(1)}, bf16[272,512]{1,0:T(8,128)(2,1)S(1)}, u32[]{:S(2)}, u32[]{:S(2)}) collective-permute-start(bf16[272,512]{1,0:T(8,128)(2,1)S(1)} %collective-permute-done.1.refs_2_), channel_id=1, source_target_pairs={{0,1},{1,0},{2,3},{3,2},{4,5},{5,4},{6,7},{7,6},{8,9},{9,8},{10,11... | collective-permute-start | bytes 835592 | tf_op jit(solution)/shard_map/ppermute | solution.py:23
  14.4 5.5 %collective-permute-start.3 = (f32[1,640]{1,0:T(1,128)S(1)}, f32[1,640]{1,0:T(1,128)S(1)}, u32[]{:S(2)}, u32[]{:S(2)}) collective-permute-start(f32[1,640]{1,0:T(1,128)S(1)} %get-tuple-element.28), channel_id=1, source_target_pairs={{4,0},{8,4},{12,8},{16,12},{20,16},{24,20},{28,24},{5,1},{9,5},{13... | collective-permute-start | bytes 7688 | tf_op jit(solution)/shard_map/ppermute | solution.py:28
  19.2 11.4 %collective-permute-start.5 = (bf16[256,512]{1,0:T(8,128)(2,1)S(1)}, bf16[256,512]{1,0:T(8,128)(2,1)S(1)}, u32[]{:S(2)}, u32[]{:S(2)}) collective-permute-start(bf16[256,512]{1,0:T(8,128)(2,1)S(1)} %collective-permute-done.4.refs_2_), channel_id=1, source_target_pairs={{0,1},{1,0},{2,3},{3,2},{4,5},{5,4},{6,7},{7,6},{8,9},{9,8},{10,11... | collective-permute-start | bytes 786440 | tf_op jit(solution)/shard_map/ppermute | solution.py:23
  19.9 1.4 %copy-start.4 = (f32[256,3,512]{2,0,1:T(8,128)S(1)}, f32[256,3,512]{2,0,1:T(8,128)}, u32[]{:S(2)}) copy-start(f32[256,3,512]{2,0,1:T(8,128)} %param.8) | copy-start | bytes 4718596
  21.3 0.7 copy-start.7
  22.0 0.7 copy-start.10
  24.7 2.8 %copy-start = (bf16[2048,3,512]{2,0,1:T(8,128)(2,1)S(1)}, bf16[2048,3,512]{2,0,1:T(8,128)(2,1)}, u32[]{:S(2)}) copy-start(bf16[2048,3,512]{2,0,1:T(8,128)(2,1)} %param.9) | copy-start | bytes 18874372
  27.5 3.1 %copy-start.1 = (bf16[2048,3,512]{2,0,1:T(8,128)(2,1)S(1)}, bf16[2048,3,512]{2,0,1:T(8,128)(2,1)}, u32[]{:S(2)}) copy-start(bf16[2048,3,512]{2,0,1:T(8,128)(2,1)} %param.9) | copy-start | bytes 18874372
  46.5 8.3 %collective-permute-start.7 = (bf16[256,512]{1,0:T(8,128)(2,1)S(1)}, bf16[256,512]{1,0:T(8,128)(2,1)S(1)}, u32[]{:S(2)}, u32[]{:S(2)}) collective-permute-start(bf16[256,512]{1,0:T(8,128)(2,1)S(1)} %get-tuple-element.39), channel_id=1, source_target_pairs={{0,2},{1,3},{2,0},{3,1},{4,6},{5,7},{6,4},{7,5},{8,10},{9,11},{10,... | collective-permute-start | bytes 786440 | tf_op jit(solution)/shard_map/ppermute | solution.py:23
  48.1 10.5 %collective-permute-start.6 = (bf16[512,512]{1,0:T(8,128)(2,1)S(1)}, bf16[512,512]{1,0:T(8,128)(2,1)S(1)}, u32[]{:S(2)}, u32[]{:S(2)}) collective-permute-start(bf16[512,512]{1,0:T(8,128)(2,1)S(1)} %get-tuple-element.38.refs_0_), channel_id=1, source_target_pairs={{0,1},{1,0},{2,3},{3,2},{4,5},{5,4},{6,7},{7,6},{8,9},{9,8},{10,11... | collective-permute-start | bytes 1572872 | tf_op jit(solution)/shard_map/ppermute | solution.py:23
  48.1 10.5 %collective-permute-start.9 = (bf16[256,512]{1,0:T(8,128)(2,1)S(1)}, bf16[256,512]{1,0:T(8,128)(2,1)S(1)}, u32[]{:S(2)}, u32[]{:S(2)}) collective-permute-start(bf16[256,512]{1,0:T(8,128)(2,1)S(1)} %get-tuple-element.44), channel_id=1, source_target_pairs={{0,2},{1,3},{2,0},{3,1},{4,6},{5,7},{6,4},{7,5},{8,10},{9,11},{10,... | collective-permute-start | bytes 786440 | tf_op jit(solution)/shard_map/ppermute | solution.py:23
  54.8 3.8 %collective-permute-start.8 = (bf16[256,512]{1,0:T(8,128)(2,1)S(1)}, bf16[256,512]{1,0:T(8,128)(2,1)S(1)}, u32[]{:S(2)}, u32[]{:S(2)}) collective-permute-start(bf16[256,512]{1,0:T(8,128)(2,1)S(1)} %collective-permute-done.7.refs_2_), channel_id=1, source_target_pairs={{0,1},{1,0},{2,3},{3,2},{4,5},{5,4},{6,7},{7,6},{8,9},{9,8},{10,11... | collective-permute-start | bytes 786440 | tf_op jit(solution)/shard_map/ppermute | solution.py:23
  58.6 2.9 %collective-permute-start.10 = (bf16[256,512]{1,0:T(8,128)(2,1)S(1)}, bf16[256,512]{1,0:T(8,128)(2,1)S(1)}, u32[]{:S(2)}, u32[]{:S(2)}) collective-permute-start(bf16[256,512]{1,0:T(8,128)(2,1)S(1)} %collective-permute-done.9.refs_2_), channel_id=1, source_target_pairs={{0,1},{1,0},{2,3},{3,2},{4,5},{5,4},{6,7},{7,6},{8,9},{9,8},{10,11... | collective-permute-start | bytes 786440 | tf_op jit(solution)/shard_map/ppermute | solution.py:23

commit v3 on v2

--- a/solution.py
+++ b/solution.py
@@ -14,6 +14,7 @@
 EXTRA = 16
 TILE = 256
 LANES = 128
+COVER = 32
 F32 = jnp.float32
 BF16 = jnp.bfloat16
 
@@ -48,21 +49,15 @@
     return pl.CostEstimate(flops=flops, bytes_accessed=moved, transcendentals=0)
 
 
-def round_kernel(chunks, ids_ref, guess_ref, init_ref, whole_ref, lead_ref, *parts):
-    rows, width = guess_ref.shape
-    chunk = rows // chunks
-    row = lax.broadcasted_iota(jnp.int32, (EXTRA, width), 0)
-    head = jnp.where(row == 0, jnp.broadcast_to(init_ref[...], (EXTRA, width)), 0.0).astype(BF16)
-    whole_ref[pl.ds(0, EXTRA), :] = head
-    parts[0][pl.ds(0, EXTRA), :] = head
+def merge_kernel(ids_ref, guess_ref, *refs):
+    *parts, whole_ref, lead_ref = refs
+    width = guess_ref.shape[1]
+    at = 0
+    for part in parts:
+        whole_ref[pl.ds(at, part.shape[0]), :] = part[...]
+        at += part.shape[0]
+    lead_ref[:, pl.ds(width, LANES)] = jnp.broadcast_to(ids_ref[:, 0:1], (1, LANES)).astype(F32)
     lead_ref[:, pl.ds(0, width)] = guess_ref[0:1, :]
-    lead_ref[:, pl.ds(width, LANES)] = jnp.full((1, LANES), ids_ref[0], jnp.int32).astype(F32)
-    for index, part in enumerate(parts):
-        skip = 0 if index else EXTRA
-        for start in range(0, chunk, GROUP * 4):
-            block = guess_ref[pl.ds(index * chunk + start, GROUP * 4), :].astype(BF16)
-            whole_ref[pl.ds(EXTRA + index * chunk + start, GROUP * 4), :] = block
-            part[pl.ds(skip + start, GROUP * 4), :] = block
 
 
 def prepare_kernel(ids_ref, next_ref, table_ref, bias_ref, out_ref):
@@ -121,12 +116,14 @@
     refs = list(refs)
     near = [refs.pop(0) for _ in range(count // 2)]
     far = [refs.pop(0) for _ in range(count // 2)]
-    weight_ref, inputs_ref, state_ref, next_ref, bias_ref, before_ref = [refs.pop(0) for _ in range(6)]
-    begins = index == 0 and step == 0
-    diag_ref = None if begins else refs.pop(0)
+    weight_ref, inputs_ref, state_ref, next_ref, bias_ref, init_ref = [refs.pop(0) for _ in range(6)]
+    opens = index == 0 and step == 0
+    before_ref = None if opens else refs.pop(0)
+    diag_ref = None if opens else refs.pop(0)
     a_ref, b_ref, ends_ref = [refs.pop(0) for _ in range(3)]
-    diag_ref = refs.pop(0) if begins else diag_ref
+    diag_ref = refs.pop(0) if opens else diag_ref
     last = index == chunks - 1
+    begins = last and step == 0
     send_ref = refs.pop(0) if last else None
     lhs, *products = refs
     height, full = lhs.shape
@@ -134,19 +131,18 @@
     chunk = rows // chunks
     start = index * chunk
     lead = height - chunk
-    skip = EXTRA if step == 0 else 0
     hid = lax.axis_index("hid")
     is_first = lax.axis_index("tm") == 0
     is_last = lax.axis_index("tm") == lax.axis_size("tm") - 1
     groups = chunk // GROUP
     tiles = width // TILE
 
-    if begins:
+    if opens:
         diagonals(weight_ref, hid, diag_ref)
     for offset in range(count):
         place = pl.multiple_of((hid ^ offset) * width, width)
         if offset < count // 2:
-            lhs[:, pl.ds(place, width)] = near[offset][pl.ds(skip + start - lead, height), :]
+            lhs[:, pl.ds(place, width)] = near[offset][pl.ds(start, height), :]
         else:
             lhs[:, pl.ds(place, width)] = far[offset - count // 2][...]
     row = lax.broadcasted_iota(jnp.int32, (GROUP, TILE), 0)
@@ -215,13 +211,15 @@
             begin = gates(
                 [inputs_ref[gate, pl.ds(rows, GROUP), lanes] for gate in range(3)],
                 [products[tile][gate, pl.ds(0, GROUP), :] for gate in range(3)],
-                jnp.broadcast_to(before_ref[:, lanes], (GROUP, TILE)),
+                jnp.broadcast_to(init_ref[:, lanes], (GROUP, TILE)),
                 hn_bias,
             )[-1]
             error = state_ref[pl.ds(0, GROUP), lanes] - begin
             squares = squares + jnp.where((row == 0) & is_first, error * error, 0.0)
             begin = begin[0:1]
             earlier = zeros[0:1]
+        elif step == 0:
+            begin, earlier = zeros[0:1], zeros[0:1]
         else:
             begin = before_ref[3:4, lanes]
             earlier = before_ref[2:3, lanes] if index == 0 else before_ref[4:5, lanes]
@@ -317,17 +315,23 @@
     lines = width // LANES
 
     state = guess
-    whole, lead, *moved = pl.pallas_call(
-        functools.partial(round_kernel, CHUNKS),
-        out_shape=[jax.ShapeDtypeStruct((rows + EXTRA, width), BF16), jax.ShapeDtypeStruct((1, width + LANES), F32)]
-        + [jax.ShapeDtypeStruct((chunk + (0 if index else EXTRA), width), BF16) for index in range(CHUNKS)],
-        in_specs=smem() + vmem(2),
-        out_specs=vmem(2 + CHUNKS),
-        compiler_params=params(16),
-        cost_estimate=cost(rows * width, 8 * rows * width),
-        name="round",
-    )(token_ids, guess, init_state[None])
-
+    moved, rest = [], guess
+    for index in range(CHUNKS):
+        part = rest[index * chunk : (index + 1) * chunk].astype(BF16)
+        if index == CHUNKS - 1:
+            head = jnp.concatenate([init_state.astype(BF16)[None], jnp.zeros((EXTRA - 1, width), BF16)], 0)
+            part = jnp.concatenate([head, part], 0)
+        part, rest = lax.optimization_barrier((part, rest))
+        moved.append(part)
+    whole, lead = pl.pallas_call(
+        merge_kernel,
+        out_shape=[jax.ShapeDtypeStruct((rows + EXTRA, width), BF16), jax.ShapeDtypeStruct((1, width + LANES), F32)],
+        in_specs=vmem(2 + CHUNKS),
+        out_specs=vmem(2),
+        compiler_params=params(8),
+        cost_estimate=cost(COVER * rows * width, COVER * rows * width),
+        name="merge",
+    )(token_ids[None], guess[:GROUP], *moved)
     following = from_next(lead, "tm")
     inputs = pl.pallas_call(
         prepare_kernel,
@@ -335,12 +339,11 @@
         in_specs=vmem(4),
         out_specs=vmem(1)[0],
         compiler_params=params(32),
-        cost_estimate=cost(18 * rows * table.shape[1] * width, 8 * rows * width),
+        cost_estimate=cost(72 * rows * table.shape[1] * width, COVER * rows * width),
         name="prepare",
     )(token_ids[None], following, table, z_bias[None])
 
-    ends = init_state[None]
-    diag = None
+    ends, diag = None, None
     for step in range(ITERS):
         final = step == ITERS - 1
         near = {0: whole}
@@ -361,9 +364,9 @@
             height = moved[index].shape[0]
             operands = [near[offset] for offset in range(count // 2)]
             operands += [far[index][offset] for offset in range(count // 2, count)]
-            operands += [weight, inputs, state, following, hn_bias[None], ends]
+            operands += [weight, inputs, state, following, hn_bias[None], init_state[None]]
             if diag is not None:
-                operands.append(diag)
+                operands += [ends, diag]
             outs = [
                 jax.ShapeDtypeStruct((chunk, width), F32),
                 jax.ShapeDtypeStruct((chunk, width), F32),

time: 79.4 us -> 77.3 us (0.974)
  waiting for transfers between devices: 21.5 us -> 19.8 us
  local copies, waits for them, and re-layouts: 8.14 us -> 6.76 us
  other arithmetic: 0 us -> 0.8 us
    unnamed x22 -> x18, local copies, waits for them, and re-layouts: 8.14 us -> 3.8 us
    slice x0 -> x3, local copies, waits for them, and re-layouts: none -> 2.87 us  [the longest x2 2.15 us: newton(): part = rest[index * chunk:(index + 1) * chunk].astype(BF16)]
    ppermute x10, waiting for transfers between devices: 20.8 us -> 19.8 us  [swapped(): return lax.ppermute(block, axis, route)]
  transfers between devices with their start and end apart: 11 -> 11, of which waited for: 5 -> 3; matrix products, arithmetic and copies ran while one was open for 0% -> 1% of each run, Pallas kernels for 10% -> 11%
where the time goes in v3:
time: 77.3 us; the launch traced here: 76.9 us
  blocking collectives  25.3 us (33%)
  waiting for transfers between devices  19.8 us (26%)
  Pallas kernels  16.2 us (21%)
  starting transfers between devices  7.08 us (9%)
  local copies, waits for them, and re-layouts  6.76 us (9%)
  between operations  0.96 us (1%)
  other arithmetic  0.8 us (1%)
    all_to_all x2, blocking collectives, newton(): every = lax.all_to_all(found[-1], ('tm', 'hid') if final else 'tm', 0, 0)  25.3 us
    ppermute x10, waiting for transfers between devices, swapped(): return lax.ppermute(block, axis, route)  19.8 us
    pallas_call x4, Pallas kernels, newton(): pl.pallas_call(functools.partial(step_kernel, count, index, CHUNKS, step,...  12.4 us
    ppermute x10, starting transfers between devices, swapped(): return lax.ppermute(block, axis, route)  5.79 us
    unnamed x18, local copies, waits for them, and re-layouts  3.8 us
    slice x2, local copies, waits for them, and re-layouts, newton(): part = rest[index * chunk:(index + 1) * chunk].astype(BF16)  2.15 us
    pallas_call x1, Pallas kernels, newton(): pl.pallas_call(prepare_kernel, out_shape=jax.ShapeDtypeStruct((3, rows +...  1.97 us
    pallas_call x2, Pallas kernels, newton(): pl.pallas_call(functools.partial(apply_kernel, CHUNKS, final, count), out...  1.8 us
  transfers between devices with their start and end apart: 11, of which 3 were waited for; matrix products, arithmetic and copies ran while one was open for 1% of the time, Pallas kernels for 11%

profile of v3, /device:TPU:0, one launch (start us, length us, event | category | flops | bytes accessed | tf_op | source)
XLA Modules:
  0.0 76.9 jit_solution(4167012722448112976)
XLA Ops:
  0.6 1.1 %slice.19.refs_0_ = bf16[256,512]{1,0:T(8,128)(2,1)S(1)} slice(f32[512,512]{1,0:T(8,128)} %refs_6_.3), slice={[0:256], [0:512]} | slice | bytes 524288 | tf_op jit(solution)/shard_map/slice | solution.py:320
  1.7 1.1 %slice.18 = bf16[256,512]{1,0:T(8,128)(2,1)S(1)} slice(f32[512,512]{1,0:T(8,128)} %refs_6_.3), slice={[256:512], [0:512]} | slice | bytes 524288 | tf_op jit(solution)/shard_map/slice | solution.py:320
  2.8 0.7 convert_element_type.2
  3.7 3.1 %collective-permute-start.4 = (bf16[272,512]{1,0:T(8,128)(2,1)S(1)}, bf16[272,512]{1,0:T(8,128)(2,1)S(1)}, u32[]{:S(2)}, u32[]{:S(2)}) collective-permute-start(bf16[272,512]{1,0:T(8,128)(2,1)S(1)} %pad_maximum_fusion.refs_1_), channel_id=1, source_target_pairs={{0,2},{1,3},{2,0},{3,1},{4,6},{5,7},{6,4},{7,5},{8,10},{9,11},{10,... | collective-permute-start | bytes 835592 | tf_op jit(solution)/shard_map/ppermute | solution.py:24
  6.8 0.7 slice.11.guess_ref
  7.5 0.7 copy-done.3
  8.3 1.3 %collective-permute-start.3 = (f32[1,640]{1,0:T(1,128)S(1)}, f32[1,640]{1,0:T(1,128)S(1)}, u32[]{:S(2)}, u32[]{:S(2)}) collective-permute-start(f32[1,640]{1,0:T(1,128)S(1)} %get-tuple-element.31), channel_id=1, source_target_pairs={{4,0},{8,4},{12,8},{16,12},{20,16},{24,20},{28,24},{5,1},{9,5},{13... | collective-permute-start | bytes 7688 | tf_op jit(solution)/shard_map/ppermute | solution.py:29
  9.6 9.4 %collective-permute-done.1.refs_2_ = bf16[256,512]{1,0:T(8,128)(2,1)S(1)} collective-permute-done((bf16[256,512]{1,0:T(8,128)(2,1)S(1)}, bf16[256,512]{1,0:T(8,128)(2,1)S(1)}, u32[]{:S(2)}, u32[]{:S(2)}) %collective-permute-start.1) | collective-permute-done | bytes 262176 | tf_op jit(solution)/shard_map/ppermute | solution.py:24
  19.0 0.5 collective-permute-start.5
  19.5 0.8 %copy-done.4 = s32[512]{0:T(512)S(1)} copy-done((s32[512]{0:T(512)S(1)}, s32[512]{0:T(512)}, u32[]{:S(2)}) %copy-start.4) | copy-done | bytes 2072
  20.4 1.6 %copy-done.5 = f32[256,3,512]{2,0,1:T(8,128)S(1)} copy-done((f32[256,3,512]{2,0,1:T(8,128)S(1)}, f32[256,3,512]{2,0,1:T(8,128)}, u32[]{:S(2)}) %copy-start.5) | copy-done | bytes 1572888
  22.0 0.7 copy-done.6
  22.7 2.0 %prepare.1.refs_5_ = f32[3,520,512]{2,1,0:T(8,128)S(1)} custom-call(s32[1,512]{1,0:T(1,128)S(1)} %bitcast.21, f32[1,640]{1,0:T(1,128)S(1)} %collective-permute-done.3.next_ref.refs_7_, f32[3,256,512]{2,1,0:T(8,128)S(1)} %bitcast.22, f32[1,512]{1,0:T(1,128)S(1)} %bitcast.23), custom_call_target="tpu_custom_call" | custom-call | flops 4831838208 | bytes 8388608 | tf_op jit(solution)/shard_map/prepare/pallas_call | solution.py:336
  24.7 3.1 %shard_map.86 = (f32[256,512]{1,0:T(8,128)S(1)}, f32[256,512]{1,0:T(8,128)S(1)}, f32[5,512]{1,0:T(8,128)S(1)}, f32[24,512]{1,0:T(8,128)S(1)}) custom-call(bf16[528,512]{1,0:T(8,128)(2,1)S(1)} %get-tuple-element.30.refs_0_, bf16[528,512]{1,0:T(8,128)(2,1)S(1)} %collective-permute-done.refs_1_, bf16[256,512]{1,0:T(8,128)(2,1)S(1)} %collective-permute-done.1.refs_2_, ...), custom_call_target="tpu_custom_call" | custom-call | flops 1610612736 | bytes 6291456 | tf_op jit(solution)/shard_map/pallas_call | solution.py:380
  27.8 3.1 %shard_map.87 = (f32[256,512]{1,0:T(8,128)S(1)}, f32[256,512]{1,0:T(8,128)S(1)}, f32[5,512]{1,0:T(8,128)S(1)}, f32[8,8,128]{2,1,0:T(8,128)S(1)}) custom-call(bf16[528,512]{1,0:T(8,128)(2,1)S(1)} %get-tuple-element.30.refs_0_, bf16[528,512]{1,0:T(8,128)(2,1)S(1)} %collective-permute-done.refs_1_, bf16[272,512]{1,0:T(8,128)(2,1)S(1)} %collective-permute-done.4.refs_2_, ...), custom_call_target="tpu_custom_call" | custom-call | flops 1711276032 | bytes 6291456 | tf_op jit(solution)/shard_map/pallas_call | solution.py:380
  30.9 12.5 %all_to_all.10.refs_5_ = f32[8,8,128]{2,1,0:T(8,128)S(1)} all-to-all(f32[8,8,128]{2,1,0:T(8,128)S(1)} %get-tuple-element.39), channel_id=1, replica_groups=mesh['tm'=8,'hid'=4] {'tm'}, dimensions={0} | all-to-all | bytes 65536 | tf_op jit(solution)/shard_map/all_to_all | solution.py:393
  43.8 1.6 %collective-permute-start.7 = (bf16[256,512]{1,0:T(8,128)(2,1)S(1)}, bf16[256,512]{1,0:T(8,128)(2,1)S(1)}, u32[]{:S(2)}, u32[]{:S(2)}) collective-permute-start(bf16[256,512]{1,0:T(8,128)(2,1)S(1)} %get-tuple-element.41), channel_id=1, source_target_pairs={{0,2},{1,3},{2,0},{3,1},{4,6},{5,7},{6,4},{7,5},{8,10},{9,11},{10,... | collective-permute-start | bytes 786440 | tf_op jit(solution)/shard_map/ppermute | solution.py:24
  45.4 0.5 collective-permute-start.9
  45.9 7.0 %collective-permute-done.7.refs_2_ = bf16[256,512]{1,0:T(8,128)(2,1)S(1)} collective-permute-done((bf16[256,512]{1,0:T(8,128)(2,1)S(1)}, bf16[256,512]{1,0:T(8,128)(2,1)S(1)}, u32[]{:S(2)}, u32[]{:S(2)}) %collective-permute-start.7) | collective-permute-done | bytes 262176 | tf_op jit(solution)/shard_map/ppermute | solution.py:24
  52.9 3.4 %collective-permute-done.9.refs_2_ = bf16[256,512]{1,0:T(8,128)(2,1)S(1)} collective-permute-done((bf16[256,512]{1,0:T(8,128)(2,1)S(1)}, bf16[256,512]{1,0:T(8,128)(2,1)S(1)}, u32[]{:S(2)}, u32[]{:S(2)}) %collective-permute-start.9) | collective-permute-done | bytes 262176 | tf_op jit(solution)/shard_map/ppermute | solution.py:24
  56.3 3.0 %shard_map.89 = (f32[256,512]{1,0:T(8,128)S(1)}, f32[256,512]{1,0:T(8,128)S(1)}, f32[5,512]{1,0:T(8,128)S(1)}) custom-call(bf16[512,512]{1,0:T(8,128)(2,1)S(1)} %get-tuple-element.40.refs_0_, bf16[512,512]{1,0:T(8,128)(2,1)S(1)} %collective-permute-done.6.refs_1_, bf16[256,512]{1,0:T(8,128)(2,1)S(1)} %collective-permute-done.7.refs_2_, ...), custom_call_target="tpu_custom_call" | custom-call | flops 1610612736 | bytes 6291456 | tf_op jit(solution)/shard_map/pallas_call | solution.py:380
  59.4 3.1 %shard_map.90 = (f32[256,512]{1,0:T(8,128)S(1)}, f32[256,512]{1,0:T(8,128)S(1)}, f32[5,512]{1,0:T(8,128)S(1)}, f32[32,9,128]{2,1,0:T(8,128)S(1)}) custom-call(bf16[512,512]{1,0:T(8,128)(2,1)S(1)} %get-tuple-element.40.refs_0_, bf16[512,512]{1,0:T(8,128)(2,1)S(1)} %collective-permute-done.6.refs_1_, bf16[256,512]{1,0:T(8,128)(2,1)S(1)} %collective-permute-done.9.refs_2_, ...), custom_call_target="tpu_custom_call" | custom-call | flops 1610612736 | bytes 6291456 | tf_op jit(solution)/shard_map/pallas_call | solution.py:380
  62.5 12.8 %all_to_all.11.refs_5_ = f32[32,9,128]{2,1,0:T(8,128)S(1)} all-to-all(f32[32,9,128]{2,1,0:T(8,128)S(1)} %get-tuple-element.51), channel_id=1, replica_groups=mesh['tm'=8,'hid'=4] {'tm','hid'}, dimensions={0} | all-to-all | bytes 294912 | tf_op jit(solution)/shard_map/all_to_all | solution.py:393
  75.3 1.5 %shard_map.91 = (f32[512,512]{1,0:T(8,128)}, f32[2]{0:T(128)}) custom-call(f32[256,512]{1,0:T(8,128)S(1)} %get-tuple-element.44.refs_0_, f32[256,512]{1,0:T(8,128)S(1)} %get-tuple-element.45.refs_1_, f32[256,512]{1,0:T(8,128)S(1)} %get-tuple-element.48.refs_2_, f32[256,512]{1,0:T(8,128)S(1)} %get-tuple-element.49.refs_3_, ...), custom_call_target="tpu_custom_call" | custom-call | flops 524288 | bytes 4194304 | tf_op jit(solution)/shard_map/pallas_call | solution.py:403
  (35 shorter events, 0.8 us)
Async XLA Ops:
  3.7 15.3 %collective-permute-start.4 = (bf16[272,512]{1,0:T(8,128)(2,1)S(1)}, bf16[272,512]{1,0:T(8,128)(2,1)S(1)}, u32[]{:S(2)}, u32[]{:S(2)}) collective-permute-start(bf16[272,512]{1,0:T(8,128)(2,1)S(1)} %pad_maximum_fusion.refs_1_), channel_id=1, source_target_pairs={{0,2},{1,3},{2,0},{3,1},{4,6},{5,7},{6,4},{7,5},{8,10},{9,11},{10,... | collective-permute-start | bytes 835592 | tf_op jit(solution)/shard_map/ppermute | solution.py:24
  6.7 12.3 %collective-permute-start.1 = (bf16[256,512]{1,0:T(8,128)(2,1)S(1)}, bf16[256,512]{1,0:T(8,128)(2,1)S(1)}, u32[]{:S(2)}, u32[]{:S(2)}) collective-permute-start(bf16[256,512]{1,0:T(8,128)(2,1)S(1)} %slice.19.refs_0_), channel_id=1, source_target_pairs={{0,2},{1,3},{2,0},{3,1},{4,6},{5,7},{6,4},{7,5},{8,10},{9,11},{10,... | collective-permute-start | bytes 786440 | tf_op jit(solution)/shard_map/ppermute | solution.py:24
  7.5 0.7 copy-start.3
  8.3 16.3 %collective-permute-start = (bf16[528,512]{1,0:T(8,128)(2,1)S(1)}, bf16[528,512]{1,0:T(8,128)(2,1)S(1)}, u32[]{:S(2)}, u32[]{:S(2)}) collective-permute-start(bf16[528,512]{1,0:T(8,128)(2,1)S(1)} %get-tuple-element.30.refs_0_), channel_id=1, source_target_pairs={{0,1},{1,0},{2,3},{3,2},{4,5},{5,4},{6,7},{7,6},{8,9},{9,8},{10,11... | collective-permute-start | bytes 1622024 | tf_op jit(solution)/shard_map/ppermute | solution.py:24
  8.3 11.2 %collective-permute-start.3 = (f32[1,640]{1,0:T(1,128)S(1)}, f32[1,640]{1,0:T(1,128)S(1)}, u32[]{:S(2)}, u32[]{:S(2)}) collective-permute-start(f32[1,640]{1,0:T(1,128)S(1)} %get-tuple-element.31), channel_id=1, source_target_pairs={{4,0},{8,4},{12,8},{16,12},{20,16},{24,20},{28,24},{5,1},{9,5},{13... | collective-permute-start | bytes 7688 | tf_op jit(solution)/shard_map/ppermute | solution.py:29
  19.0 5.6 %collective-permute-start.2 = (bf16[256,512]{1,0:T(8,128)(2,1)S(1)}, bf16[256,512]{1,0:T(8,128)(2,1)S(1)}, u32[]{:S(2)}, u32[]{:S(2)}) collective-permute-start(bf16[256,512]{1,0:T(8,128)(2,1)S(1)} %collective-permute-done.1.refs_2_), channel_id=1, source_target_pairs={{0,1},{1,0},{2,3},{3,2},{4,5},{5,4},{6,7},{7,6},{8,9},{9,8},{10,11... | collective-permute-start | bytes 786440 | tf_op jit(solution)/shard_map/ppermute | solution.py:24
  19.0 8.8 %collective-permute-start.5 = (bf16[272,512]{1,0:T(8,128)(2,1)S(1)}, bf16[272,512]{1,0:T(8,128)(2,1)S(1)}, u32[]{:S(2)}, u32[]{:S(2)}) collective-permute-start(bf16[272,512]{1,0:T(8,128)(2,1)S(1)} %collective-permute-done.4.refs_2_), channel_id=1, source_target_pairs={{0,1},{1,0},{2,3},{3,2},{4,5},{5,4},{6,7},{7,6},{8,9},{9,8},{10,11... | collective-permute-start | bytes 835592 | tf_op jit(solution)/shard_map/ppermute | solution.py:24
  19.5 5.1 %slice-start = ((s8[6291456]{0:T(1024)(128)(4,1)}), s8[4194304]{0:T(1024)(128)(4,1)S(1)}, s32[]{:S(2)}) async-start(s8[6291456]{0:T(1024)(128)(4,1)} %bitcast.6), calls=%async_computation.2 | async-start | bytes 8388608
  19.5 0.8 %copy-start.4 = (s32[512]{0:T(512)S(1)}, s32[512]{0:T(512)}, u32[]{:S(2)}) copy-start(s32[512]{0:T(512)} %param.7) | copy-start | bytes 6148
  20.4 1.6 %copy-start.5 = (f32[256,3,512]{2,0,1:T(8,128)S(1)}, f32[256,3,512]{2,0,1:T(8,128)}, u32[]{:S(2)}) copy-start(f32[256,3,512]{2,0,1:T(8,128)} %param.8) | copy-start | bytes 4718596
  22.0 0.7 copy-start.6
  22.6 2.0 %slice-start.1 = ((s8[6291456]{0:T(1024)(128)(4,1)}), s8[2097152]{0:T(1024)(128)(4,1)S(1)}, s32[]{:S(2)}) async-start(s8[6291456]{0:T(1024)(128)(4,1)} %bitcast.6), calls=%async_computation.3 | async-start | bytes 4194304
  22.6 2.0 %copy-start = (f32[512,512]{1,0:T(8,128)S(1)}, f32[512,512]{1,0:T(8,128)}, u32[]{:S(2)}) copy-start(f32[512,512]{1,0:T(8,128)} %refs_6_.3) | copy-start | bytes 3145732
  22.6 2.0 %copy-start.1 = (f32[512]{0:T(512)S(1)}, f32[512]{0:T(512)}, u32[]{:S(2)}) copy-start(f32[512]{0:T(512)} %param.12) | copy-start | bytes 6148
  22.6 2.0 %copy-start.2 = (f32[512]{0:T(512)S(1)}, f32[512]{0:T(512)}, u32[]{:S(2)}) copy-start(f32[512]{0:T(512)} %param.11) | copy-start | bytes 6148
  43.8 9.0 %collective-permute-start.7 = (bf16[256,512]{1,0:T(8,128)(2,1)S(1)}, bf16[256,512]{1,0:T(8,128)(2,1)S(1)}, u32[]{:S(2)}, u32[]{:S(2)}) collective-permute-start(bf16[256,512]{1,0:T(8,128)(2,1)S(1)} %get-tuple-element.41), channel_id=1, source_target_pairs={{0,2},{1,3},{2,0},{3,1},{4,6},{5,7},{6,4},{7,5},{8,10},{9,11},{10,... | collective-permute-start | bytes 786440 | tf_op jit(solution)/shard_map/ppermute | solution.py:24
  45.4 10.9 %collective-permute-start.6 = (bf16[512,512]{1,0:T(8,128)(2,1)S(1)}, bf16[512,512]{1,0:T(8,128)(2,1)S(1)}, u32[]{:S(2)}, u32[]{:S(2)}) collective-permute-start(bf16[512,512]{1,0:T(8,128)(2,1)S(1)} %get-tuple-element.40.refs_0_), channel_id=1, source_target_pairs={{0,1},{1,0},{2,3},{3,2},{4,5},{5,4},{6,7},{7,6},{8,9},{9,8},{10,11... | collective-permute-start | bytes 1572872 | tf_op jit(solution)/shard_map/ppermute | solution.py:24
  45.4 10.9 %collective-permute-start.9 = (bf16[256,512]{1,0:T(8,128)(2,1)S(1)}, bf16[256,512]{1,0:T(8,128)(2,1)S(1)}, u32[]{:S(2)}, u32[]{:S(2)}) collective-permute-start(bf16[256,512]{1,0:T(8,128)(2,1)S(1)} %get-tuple-element.46), channel_id=1, source_target_pairs={{0,2},{1,3},{2,0},{3,1},{4,6},{5,7},{6,4},{7,5},{8,10},{9,11},{10,... | collective-permute-start | bytes 786440 | tf_op jit(solution)/shard_map/ppermute | solution.py:24
  52.8 3.4 %collective-permute-start.8 = (bf16[256,512]{1,0:T(8,128)(2,1)S(1)}, bf16[256,512]{1,0:T(8,128)(2,1)S(1)}, u32[]{:S(2)}, u32[]{:S(2)}) collective-permute-start(bf16[256,512]{1,0:T(8,128)(2,1)S(1)} %collective-permute-done.7.refs_2_), channel_id=1, source_target_pairs={{0,1},{1,0},{2,3},{3,2},{4,5},{5,4},{6,7},{7,6},{8,9},{9,8},{10,11... | collective-permute-start | bytes 786440 | tf_op jit(solution)/shard_map/ppermute | solution.py:24
  56.3 3.1 %collective-permute-start.10 = (bf16[256,512]{1,0:T(8,128)(2,1)S(1)}, bf16[256,512]{1,0:T(8,128)(2,1)S(1)}, u32[]{:S(2)}, u32[]{:S(2)}) collective-permute-start(bf16[256,512]{1,0:T(8,128)(2,1)S(1)} %collective-permute-done.9.refs_2_), channel_id=1, source_target_pairs={{0,1},{1,0},{2,3},{3,2},{4,5},{5,4},{6,7},{7,6},{8,9},{9,8},{10,11... | collective-permute-start | bytes 786440 | tf_op jit(solution)/shard_map/ppermute | solution.py:24

commit v4 on v3

--- a/solution.py
+++ b/solution.py
@@ -14,7 +14,7 @@
 EXTRA = 16
 TILE = 256
 LANES = 128
-COVER = 32
+COVER = 2_000_000_000
 F32 = jnp.float32
 BF16 = jnp.bfloat16
 
@@ -49,34 +49,37 @@
     return pl.CostEstimate(flops=flops, bytes_accessed=moved, transcendentals=0)
 
 
-def merge_kernel(ids_ref, guess_ref, *refs):
-    *parts, whole_ref, lead_ref = refs
-    width = guess_ref.shape[1]
-    at = 0
-    for part in parts:
-        whole_ref[pl.ds(at, part.shape[0]), :] = part[...]
-        at += part.shape[0]
-    lead_ref[:, pl.ds(width, LANES)] = jnp.broadcast_to(ids_ref[:, 0:1], (1, LANES)).astype(F32)
-    lead_ref[:, pl.ds(0, width)] = guess_ref[0:1, :]
-
-
-def prepare_kernel(ids_ref, next_ref, table_ref, bias_ref, out_ref):
+def merge_kernel(guess_ref, init_ref, opening_ref, whole_ref, *parts):
+    chunk, width = opening_ref.shape
+    whole_ref[pl.ds(0, chunk), :] = opening_ref[...]
+    for index, part in enumerate(parts):
+        lead = part.shape[0] - chunk
+        at = (index + 1) * chunk
+        if lead:
+            row = lax.broadcasted_iota(jnp.int32, (lead, width), 0)
+            head = jnp.where(row == 0, jnp.broadcast_to(init_ref[...], (lead, width)), 0.0).astype(BF16)
+            part[pl.ds(0, lead), :] = head
+            whole_ref[pl.ds(at, lead), :] = head
+        for start in range(0, chunk, GROUP * 4):
+            block = guess_ref[pl.ds(at + start, GROUP * 4), :].astype(BF16)
+            part[pl.ds(lead + start, GROUP * 4), :] = block
+            whole_ref[pl.ds(at + lead + start, GROUP * 4), :] = block
+
+
+def prepare_kernel(ids_ref, guess_ref, table_ref, bias_ref, out_ref, line_ref):
     vocab, width = table_ref.shape[1:]
     rows = ids_ref.shape[1]
-    ids = ids_ref[...].astype(F32)
-    lane = lax.broadcasted_iota(jnp.int32, (1, rows), 1)
-    following = jnp.broadcast_to(next_ref[:, width : width + 1], (1, rows))
-    ids = jnp.where(lane == rows - 1, following, pltpu.roll(ids, rows - 1, 1))
-    begin = jnp.broadcast_to(ids_ref[:, 0:1].astype(F32), (1, LANES))
+    ids = ids_ref[...]
 
     def spread(line):
-        entry = lax.broadcasted_iota(jnp.int32, (vocab, line.shape[1]), 0).astype(F32)
+        entry = lax.broadcasted_iota(jnp.int32, (vocab, line.shape[1]), 0)
         return (entry == line).astype(F32).astype(BF16)
 
     def pick(hot, part):
         return lax.dot_general(hot, part, (((0,), (0,)), ((), ())), preferred_element_type=F32)
 
-    hot, hot_begin = spread(ids), spread(begin)
+    hot, hot_begin = spread(pltpu.roll(ids, rows - 1, 1)), spread(jnp.broadcast_to(ids[:, 0:1], (1, LANES)))
+    line_ref[:, pl.ds(0, width)] = guess_ref[0:1, :]
     for gate in range(3):
         table = table_ref[gate]
         if gate == 0:
@@ -89,6 +92,7 @@
             total = picked if total is None else (total[0] + picked[0], total[1] + picked[1])
         out_ref[gate, pl.ds(0, rows), :] = total[0]
         out_ref[gate, pl.ds(rows, GROUP), :] = total[1][0:GROUP]
+        line_ref[:, pl.ds((gate + 1) * width, width)] = total[1][0:1]
 
 
 def diagonals(weight_ref, hid, diag_ref):
@@ -116,7 +120,7 @@
     refs = list(refs)
     near = [refs.pop(0) for _ in range(count // 2)]
     far = [refs.pop(0) for _ in range(count // 2)]
-    weight_ref, inputs_ref, state_ref, next_ref, bias_ref, init_ref = [refs.pop(0) for _ in range(6)]
+    weight_ref, inputs_ref, state_ref, next_ref, edge_ref, bias_ref, init_ref = [refs.pop(0) for _ in range(7)]
     opens = index == 0 and step == 0
     before_ref = None if opens else refs.pop(0)
     diag_ref = None if opens else refs.pop(0)
@@ -181,8 +185,13 @@
             turned_next = pltpu.roll(following, GROUP - 1, 0)
             state = jnp.where(row == GROUP - 1, turned_next, turned)
             turned = turned_next
+            terms = [inputs_ref[gate, token, lanes] for gate in range(3)]
+            if last and group == groups - 1:
+                for gate in range(3):
+                    edge = edge_ref[:, pl.ds((gate + 1) * width + tile * TILE, TILE)]
+                    terms[gate] = jnp.where(row == GROUP - 1, jnp.broadcast_to(edge, (GROUP, TILE)), terms[gate])
             zeta, reset, gated, cand, gap, value = gates(
-                [inputs_ref[gate, token, lanes] for gate in range(3)],
+                terms,
                 [products[tile][gate, pl.ds(lead + group * GROUP, GROUP), :] for gate in range(3)],
                 prev,
                 hn_bias,
@@ -314,34 +323,32 @@
     chunk = rows // CHUNKS
     lines = width // LANES
 
-    state = guess
-    moved, rest = [], guess
-    for index in range(CHUNKS):
-        part = rest[index * chunk : (index + 1) * chunk].astype(BF16)
-        if index == CHUNKS - 1:
-            head = jnp.concatenate([init_state.astype(BF16)[None], jnp.zeros((EXTRA - 1, width), BF16)], 0)
-            part = jnp.concatenate([head, part], 0)
-        part, rest = lax.optimization_barrier((part, rest))
-        moved.append(part)
-    whole, lead = pl.pallas_call(
+    opening, rest = lax.optimization_barrier((guess[:chunk].astype(BF16), guess))
+    whole, *moved = pl.pallas_call(
         merge_kernel,
-        out_shape=[jax.ShapeDtypeStruct((rows + EXTRA, width), BF16), jax.ShapeDtypeStruct((1, width + LANES), F32)],
-        in_specs=vmem(2 + CHUNKS),
+        out_shape=[jax.ShapeDtypeStruct((rows + EXTRA, width), BF16)]
+        + [jax.ShapeDtypeStruct((chunk + EXTRA * (index == CHUNKS - 1), width), BF16) for index in range(1, CHUNKS)],
+        in_specs=vmem(3),
+        out_specs=vmem(CHUNKS),
+        compiler_params=params(8),
+        cost_estimate=cost(COVER, 8 * rows * width),
+        name="merge",
+    )(rest, init_state[None], opening)
+    moved = [opening, *moved]
+    inputs, line = pl.pallas_call(
+        prepare_kernel,
+        out_shape=[
+            jax.ShapeDtypeStruct((3, rows + GROUP, width), F32),
+            jax.ShapeDtypeStruct((1, 4 * width), F32),
+        ],
+        in_specs=vmem(4),
         out_specs=vmem(2),
-        compiler_params=params(8),
-        cost_estimate=cost(COVER * rows * width, COVER * rows * width),
-        name="merge",
-    )(token_ids[None], guess[:GROUP], *moved)
-    following = from_next(lead, "tm")
-    inputs = pl.pallas_call(
-        prepare_kernel,
-        out_shape=jax.ShapeDtypeStruct((3, rows + GROUP, width), F32),
-        in_specs=vmem(4),
-        out_specs=vmem(1)[0],
         compiler_params=params(32),
-        cost_estimate=cost(72 * rows * table.shape[1] * width, COVER * rows * width),
+        cost_estimate=cost(2 * COVER, 8 * rows * width),
         name="prepare",
-    )(token_ids[None], following, table, z_bias[None])
+    )(token_ids[None], rest, table, z_bias[None])
+    edge = from_next(line, "tm")
+    state, following = rest, edge
 
     ends, diag = None, None
     for step in range(ITERS):
@@ -364,7 +371,7 @@
             height = moved[index].shape[0]
             operands = [near[offset] for offset in range(count // 2)]
             operands += [far[index][offset] for offset in range(count // 2, count)]
-            operands += [weight, inputs, state, following, hn_bias[None], init_state[None]]
+            operands += [weight, inputs, state, following, edge, hn_bias[None], init_state[None]]
             if diag is not None:
                 operands += [ends, diag]
             outs = [

time: 77.3 us -> 78.8 us (1.019)
  waiting for transfers between devices: 19.8 us -> 26.4 us
  local copies, waits for them, and re-layouts: 6.76 us -> 3.01 us
  other arithmetic: 0.8 us -> 0.01 us
    ppermute x1, waiting for transfers between devices: 0.01 us -> 4.24 us  [from_next(): return lax.ppermute(block, axis, route)]
    ppermute x10, waiting for transfers between devices: 19.8 us -> 22.2 us  [swapped(): return lax.ppermute(block, axis, route)]
    unnamed x18 -> x20, local copies, waits for them, and re-layouts: 3.8 us -> 1.94 us
    slice x3 -> x1, local copies, waits for them, and re-layouts: 2.87 us -> 1.08 us  [newton(): guess[:chunk].astype(BF16)]
  transfers between devices with their start and end apart: 11 -> 11, of which waited for: 3 -> 4; matrix products, arithmetic and copies ran while one was open for 1% -> 0% of each run, Pallas kernels for 11% -> 10%
where the time goes in v4:
time: 78.8 us; the launch traced here: 78.5 us
  waiting for transfers between devices  26.4 us (34%)
  blocking collectives  24.9 us (32%)
  Pallas kernels  16.2 us (21%)
  starting transfers between devices  7.04 us (9%)
  local copies, waits for them, and re-layouts  3.01 us (4%)
  between operations  0.96 us (1%)
    all_to_all x2, blocking collectives, newton(): every = lax.all_to_all(found[-1], ('tm', 'hid') if final else 'tm', 0, 0)  24.9 us
    ppermute x10, waiting for transfers between devices, swapped(): return lax.ppermute(block, axis, route)  22.2 us
    pallas_call x4, Pallas kernels, newton(): pl.pallas_call(functools.partial(step_kernel, count, index, CHUNKS, step,...  12.4 us
    ppermute x10, starting transfers between devices, swapped(): return lax.ppermute(block, axis, route)  5.75 us
    ppermute x1, waiting for transfers between devices, from_next(): return lax.ppermute(block, axis, route)  4.24 us
    unnamed x20, local copies, waits for them, and re-layouts  1.94 us
    pallas_call x1, Pallas kernels, newton(): pl.pallas_call(prepare_kernel, out_shape=[jax.ShapeDtypeStruct((3, rows +...  1.93 us
    pallas_call x2, Pallas kernels, newton(): pl.pallas_call(functools.partial(apply_kernel, CHUNKS, final, count), out...  1.8 us
  transfers between devices with their start and end apart: 11, of which 4 were waited for; matrix products, arithmetic and copies ran while one was open for 0% of the time, Pallas kernels for 10%

profile of v4, /device:TPU:0, one launch (start us, length us, event | category | flops | bytes accessed | tf_op | source)
XLA Modules:
  0.0 78.5 jit_solution(9574252988903611375)
XLA Ops:
  0.6 1.1 %slice.7.opening_ref = bf16[256,512]{1,0:T(8,128)(2,1)S(1)} slice(f32[512,512]{1,0:T(8,128)} %refs_6_.1), slice={[0:256], [0:512]} | slice | bytes 524288 | tf_op jit(solution)/shard_map/slice | solution.py:326
  1.7 1.2 %copy-done = f32[512,512]{1,0:T(8,128)S(1)} copy-done((f32[512,512]{1,0:T(8,128)S(1)}, f32[512,512]{1,0:T(8,128)}, u32[]{:S(2)}) %copy-start) | copy-done | bytes 1048600
  2.9 0.7 copy-done.2
  3.6 0.1 merge.1
  3.7 3.1 %collective-permute-start.4 = (bf16[272,512]{1,0:T(8,128)(2,1)S(1)}, bf16[272,512]{1,0:T(8,128)(2,1)S(1)}, u32[]{:S(2)}, u32[]{:S(2)}) collective-permute-start(bf16[272,512]{1,0:T(8,128)(2,1)S(1)} %get-tuple-element.35), channel_id=1, source_target_pairs={{0,2},{1,3},{2,0},{3,1},{4,6},{5,7},{6,4},{7,5},{8,10},{9,11},{10,... | collective-permute-start | bytes 835592 | tf_op jit(solution)/shard_map/ppermute | solution.py:24
  6.8 0.1 collective-permute-start.1
  6.8 12.2 %collective-permute-done.1.refs_2_ = bf16[256,512]{1,0:T(8,128)(2,1)S(1)} collective-permute-done((bf16[256,512]{1,0:T(8,128)(2,1)S(1)}, bf16[256,512]{1,0:T(8,128)(2,1)S(1)}, u32[]{:S(2)}, u32[]{:S(2)}) %collective-permute-start.1) | collective-permute-done | bytes 262176 | tf_op jit(solution)/shard_map/ppermute | solution.py:24
  19.0 0.5 collective-permute-start.5
  19.6 0.0 copy-start.3
  19.6 1.9 %prepare.1 = (f32[3,520,512]{2,1,0:T(8,128)S(1)}, f32[1,2048]{1,0:T(1,128)S(1)}) custom-call(s32[1,512]{1,0:T(1,128)S(1)} %bitcast.22, f32[512,512]{1,0:T(8,128)S(1)} %copy-done.1, f32[3,256,512]{2,1,0:T(8,128)S(1)} %bitcast.21, f32[1,512]{1,0:T(1,128)S(1)} %bitcast.23), custom_call_target="tpu_custom_call" | custom-call | flops 4000000000 | bytes 2097152 | tf_op jit(solution)/shard_map/prepare/pallas_call | solution.py:338
  21.5 1.3 %collective-permute-start.3 = (f32[1,2048]{1,0:T(1,128)S(1)}, f32[1,2048]{1,0:T(1,128)S(1)}, u32[]{:S(2)}, u32[]{:S(2)}) collective-permute-start(f32[1,2048]{1,0:T(1,128)S(1)} %get-tuple-element.32), channel_id=1, source_target_pairs={{4,0},{8,4},{12,8},{16,12},{20,16},{24,20},{28,24},{5,1},{9,5},{13... | collective-permute-start | bytes 24584 | tf_op jit(solution)/shard_map/ppermute | solution.py:29
  22.8 4.2 %collective-permute-done.3.refs_7_.refs_8_ = f32[1,2048]{1,0:T(1,128)S(1)} collective-permute-done((f32[1,2048]{1,0:T(1,128)S(1)}, f32[1,2048]{1,0:T(1,128)S(1)}, u32[]{:S(2)}, u32[]{:S(2)}) %collective-permute-start.3) | collective-permute-done | bytes 8224 | tf_op jit(solution)/shard_map/ppermute | solution.py:29
  27.1 3.1 %shard_map.86 = (f32[256,512]{1,0:T(8,128)S(1)}, f32[256,512]{1,0:T(8,128)S(1)}, f32[5,512]{1,0:T(8,128)S(1)}, f32[24,512]{1,0:T(8,128)S(1)}) custom-call(bf16[528,512]{1,0:T(8,128)(2,1)S(1)} %get-tuple-element.30.refs_0_, bf16[528,512]{1,0:T(8,128)(2,1)S(1)} %collective-permute-done.refs_1_, bf16[256,512]{1,0:T(8,128)(2,1)S(1)} %collective-permute-done.1.refs_2_, ...), custom_call_target="tpu_custom_call" | custom-call | flops 1610612736 | bytes 6291456 | tf_op jit(solution)/shard_map/pallas_call | solution.py:387
  30.2 3.1 %shard_map.87 = (f32[256,512]{1,0:T(8,128)S(1)}, f32[256,512]{1,0:T(8,128)S(1)}, f32[5,512]{1,0:T(8,128)S(1)}, f32[8,8,128]{2,1,0:T(8,128)S(1)}) custom-call(bf16[528,512]{1,0:T(8,128)(2,1)S(1)} %get-tuple-element.30.refs_0_, bf16[528,512]{1,0:T(8,128)(2,1)S(1)} %collective-permute-done.refs_1_, bf16[272,512]{1,0:T(8,128)(2,1)S(1)} %collective-permute-done.4.refs_2_, ...), custom_call_target="tpu_custom_call" | custom-call | flops 1711276032 | bytes 6291456 | tf_op jit(solution)/shard_map/pallas_call | solution.py:387
  33.4 12.4 %all_to_all.10.refs_5_ = f32[8,8,128]{2,1,0:T(8,128)S(1)} all-to-all(f32[8,8,128]{2,1,0:T(8,128)S(1)} %get-tuple-element.41), channel_id=1, replica_groups=mesh['tm'=8,'hid'=4] {'tm'}, dimensions={0} | all-to-all | bytes 65536 | tf_op jit(solution)/shard_map/all_to_all | solution.py:400
  45.8 0.3 shard_map.88
  46.1 1.6 %collective-permute-start.7 = (bf16[256,512]{1,0:T(8,128)(2,1)S(1)}, bf16[256,512]{1,0:T(8,128)(2,1)S(1)}, u32[]{:S(2)}, u32[]{:S(2)}) collective-permute-start(bf16[256,512]{1,0:T(8,128)(2,1)S(1)} %get-tuple-element.43), channel_id=1, source_target_pairs={{0,2},{1,3},{2,0},{3,1},{4,6},{5,7},{6,4},{7,5},{8,10},{9,11},{10,... | collective-permute-start | bytes 786440 | tf_op jit(solution)/shard_map/ppermute | solution.py:24
  47.7 0.5 collective-permute-start.9
  48.2 6.1 %collective-permute-done.7.refs_2_ = bf16[256,512]{1,0:T(8,128)(2,1)S(1)} collective-permute-done((bf16[256,512]{1,0:T(8,128)(2,1)S(1)}, bf16[256,512]{1,0:T(8,128)(2,1)S(1)}, u32[]{:S(2)}, u32[]{:S(2)}) %collective-permute-start.7) | collective-permute-done | bytes 262176 | tf_op jit(solution)/shard_map/ppermute | solution.py:24
  54.4 3.8 %collective-permute-done.9.refs_2_ = bf16[256,512]{1,0:T(8,128)(2,1)S(1)} collective-permute-done((bf16[256,512]{1,0:T(8,128)(2,1)S(1)}, bf16[256,512]{1,0:T(8,128)(2,1)S(1)}, u32[]{:S(2)}, u32[]{:S(2)}) %collective-permute-start.9) | collective-permute-done | bytes 262176 | tf_op jit(solution)/shard_map/ppermute | solution.py:24
  58.2 3.0 %shard_map.89 = (f32[256,512]{1,0:T(8,128)S(1)}, f32[256,512]{1,0:T(8,128)S(1)}, f32[5,512]{1,0:T(8,128)S(1)}) custom-call(bf16[512,512]{1,0:T(8,128)(2,1)S(1)} %get-tuple-element.42.refs_0_, bf16[512,512]{1,0:T(8,128)(2,1)S(1)} %collective-permute-done.6.refs_1_, bf16[256,512]{1,0:T(8,128)(2,1)S(1)} %collective-permute-done.7.refs_2_, ...), custom_call_target="tpu_custom_call" | custom-call | flops 1610612736 | bytes 6291456 | tf_op jit(solution)/shard_map/pallas_call | solution.py:387
  61.2 3.1 %shard_map.90 = (f32[256,512]{1,0:T(8,128)S(1)}, f32[256,512]{1,0:T(8,128)S(1)}, f32[5,512]{1,0:T(8,128)S(1)}, f32[32,9,128]{2,1,0:T(8,128)S(1)}) custom-call(bf16[512,512]{1,0:T(8,128)(2,1)S(1)} %get-tuple-element.42.refs_0_, bf16[512,512]{1,0:T(8,128)(2,1)S(1)} %collective-permute-done.6.refs_1_, bf16[256,512]{1,0:T(8,128)(2,1)S(1)} %collective-permute-done.9.refs_2_, ...), custom_call_target="tpu_custom_call" | custom-call | flops 1610612736 | bytes 6291456 | tf_op jit(solution)/shard_map/pallas_call | solution.py:387
  64.4 12.5 %all_to_all.11.refs_5_ = f32[32,9,128]{2,1,0:T(8,128)S(1)} all-to-all(f32[32,9,128]{2,1,0:T(8,128)S(1)} %get-tuple-element.53), channel_id=1, replica_groups=mesh['tm'=8,'hid'=4] {'tm','hid'}, dimensions={0} | all-to-all | bytes 294912 | tf_op jit(solution)/shard_map/all_to_all | solution.py:400
  76.9 1.5 %shard_map.91 = (f32[512,512]{1,0:T(8,128)}, f32[2]{0:T(128)}) custom-call(f32[256,512]{1,0:T(8,128)S(1)} %get-tuple-element.46.refs_0_, f32[256,512]{1,0:T(8,128)S(1)} %get-tuple-element.47.refs_1_, f32[256,512]{1,0:T(8,128)S(1)} %get-tuple-element.50.refs_2_, f32[256,512]{1,0:T(8,128)S(1)} %get-tuple-element.51.refs_3_, ...), custom_call_target="tpu_custom_call" | custom-call | flops 524288 | bytes 4194304 | tf_op jit(solution)/shard_map/pallas_call | solution.py:410
  (30 shorter events, 0.1 us)
Async XLA Ops:
  1.7 1.2 %copy-start = (f32[512,512]{1,0:T(8,128)S(1)}, f32[512,512]{1,0:T(8,128)}, u32[]{:S(2)}) copy-start(f32[512,512]{1,0:T(8,128)} %refs_6_.1) | copy-start | bytes 3145732
  2.9 0.7 copy-start.2
  3.6 15.9 %copy-start.1 = (f32[512,512]{1,0:T(8,128)S(1)}, f32[512,512]{1,0:T(8,128)}, u32[]{:S(2)}) copy-start(f32[512,512]{1,0:T(8,128)} %refs_6_.1) | copy-start | bytes 3145732
  3.6 15.9 %copy-start.5 = (f32[256,3,512]{2,0,1:T(8,128)S(1)}, f32[256,3,512]{2,0,1:T(8,128)}, u32[]{:S(2)}) copy-start(f32[256,3,512]{2,0,1:T(8,128)} %param.8) | copy-start | bytes 4718596
  3.6 15.9 %copy-start.6 = (s32[512]{0:T(512)S(1)}, s32[512]{0:T(512)}, u32[]{:S(2)}) copy-start(s32[512]{0:T(512)} %param.7) | copy-start | bytes 6148
  3.6 15.9 %copy-start.7 = (f32[512]{0:T(512)S(1)}, f32[512]{0:T(512)}, u32[]{:S(2)}) copy-start(f32[512]{0:T(512)} %param.10) | copy-start | bytes 6148
  3.7 15.3 %collective-permute-start.4 = (bf16[272,512]{1,0:T(8,128)(2,1)S(1)}, bf16[272,512]{1,0:T(8,128)(2,1)S(1)}, u32[]{:S(2)}, u32[]{:S(2)}) collective-permute-start(bf16[272,512]{1,0:T(8,128)(2,1)S(1)} %get-tuple-element.35), channel_id=1, source_target_pairs={{0,2},{1,3},{2,0},{3,1},{4,6},{5,7},{6,4},{7,5},{8,10},{9,11},{10,... | collective-permute-start | bytes 835592 | tf_op jit(solution)/shard_map/ppermute | solution.py:24
  6.8 12.3 %collective-permute-start.1 = (bf16[256,512]{1,0:T(8,128)(2,1)S(1)}, bf16[256,512]{1,0:T(8,128)(2,1)S(1)}, u32[]{:S(2)}, u32[]{:S(2)}) collective-permute-start(bf16[256,512]{1,0:T(8,128)(2,1)S(1)} %slice.7.opening_ref), channel_id=1, source_target_pairs={{0,2},{1,3},{2,0},{3,1},{4,6},{5,7},{6,4},{7,5},{8,10},{9,11},{10,... | collective-permute-start | bytes 786440 | tf_op jit(solution)/shard_map/ppermute | solution.py:24
  6.8 20.3 %collective-permute-start = (bf16[528,512]{1,0:T(8,128)(2,1)S(1)}, bf16[528,512]{1,0:T(8,128)(2,1)S(1)}, u32[]{:S(2)}, u32[]{:S(2)}) collective-permute-start(bf16[528,512]{1,0:T(8,128)(2,1)S(1)} %get-tuple-element.30.refs_0_), channel_id=1, source_target_pairs={{0,1},{1,0},{2,3},{3,2},{4,5},{5,4},{6,7},{7,6},{8,9},{9,8},{10,11... | collective-permute-start | bytes 1622024 | tf_op jit(solution)/shard_map/ppermute | solution.py:24
  19.0 8.1 %collective-permute-start.2 = (bf16[256,512]{1,0:T(8,128)(2,1)S(1)}, bf16[256,512]{1,0:T(8,128)(2,1)S(1)}, u32[]{:S(2)}, u32[]{:S(2)}) collective-permute-start(bf16[256,512]{1,0:T(8,128)(2,1)S(1)} %collective-permute-done.1.refs_2_), channel_id=1, source_target_pairs={{0,1},{1,0},{2,3},{3,2},{4,5},{5,4},{6,7},{7,6},{8,9},{9,8},{10,11... | collective-permute-start | bytes 786440 | tf_op jit(solution)/shard_map/ppermute | solution.py:24
  19.0 11.2 %collective-permute-start.5 = (bf16[272,512]{1,0:T(8,128)(2,1)S(1)}, bf16[272,512]{1,0:T(8,128)(2,1)S(1)}, u32[]{:S(2)}, u32[]{:S(2)}) collective-permute-start(bf16[272,512]{1,0:T(8,128)(2,1)S(1)} %collective-permute-done.4.refs_2_), channel_id=1, source_target_pairs={{0,1},{1,0},{2,3},{3,2},{4,5},{5,4},{6,7},{7,6},{8,9},{9,8},{10,11... | collective-permute-start | bytes 835592 | tf_op jit(solution)/shard_map/ppermute | solution.py:24
  19.5 7.6 %slice-start = ((s8[6291456]{0:T(1024)(128)(4,1)}), s8[4194304]{0:T(1024)(128)(4,1)S(1)}, s32[]{:S(2)}) async-start(s8[6291456]{0:T(1024)(128)(4,1)} %bitcast.6), calls=%async_computation.2 | async-start | bytes 8388608
  19.6 7.5 %slice-start.1 = ((s8[6291456]{0:T(1024)(128)(4,1)}), s8[2097152]{0:T(1024)(128)(4,1)S(1)}, s32[]{:S(2)}) async-start(s8[6291456]{0:T(1024)(128)(4,1)} %bitcast.6), calls=%async_computation.3 | async-start | bytes 4194304
  19.6 7.5 %copy-start.3 = (f32[512]{0:T(512)S(1)}, f32[512]{0:T(512)}, u32[]{:S(2)}) copy-start(f32[512]{0:T(512)} %param.12) | copy-start | bytes 6148
  19.6 7.5 %copy-start.4 = (f32[512]{0:T(512)S(1)}, f32[512]{0:T(512)}, u32[]{:S(2)}) copy-start(f32[512]{0:T(512)} %param.11) | copy-start | bytes 6148
  21.5 5.5 %collective-permute-start.3 = (f32[1,2048]{1,0:T(1,128)S(1)}, f32[1,2048]{1,0:T(1,128)S(1)}, u32[]{:S(2)}, u32[]{:S(2)}) collective-permute-start(f32[1,2048]{1,0:T(1,128)S(1)} %get-tuple-element.32), channel_id=1, source_target_pairs={{4,0},{8,4},{12,8},{16,12},{20,16},{24,20},{28,24},{5,1},{9,5},{13... | collective-permute-start | bytes 24584 | tf_op jit(solution)/shard_map/ppermute | solution.py:29
  46.1 8.2 %collective-permute-start.7 = (bf16[256,512]{1,0:T(8,128)(2,1)S(1)}, bf16[256,512]{1,0:T(8,128)(2,1)S(1)}, u32[]{:S(2)}, u32[]{:S(2)}) collective-permute-start(bf16[256,512]{1,0:T(8,128)(2,1)S(1)} %get-tuple-element.43), channel_id=1, source_target_pairs={{0,2},{1,3},{2,0},{3,1},{4,6},{5,7},{6,4},{7,5},{8,10},{9,11},{10,... | collective-permute-start | bytes 786440 | tf_op jit(solution)/shard_map/ppermute | solution.py:24
  47.7 10.5 %collective-permute-start.6 = (bf16[512,512]{1,0:T(8,128)(2,1)S(1)}, bf16[512,512]{1,0:T(8,128)(2,1)S(1)}, u32[]{:S(2)}, u32[]{:S(2)}) collective-permute-start(bf16[512,512]{1,0:T(8,128)(2,1)S(1)} %get-tuple-element.42.refs_0_), channel_id=1, source_target_pairs={{0,1},{1,0},{2,3},{3,2},{4,5},{5,4},{6,7},{7,6},{8,9},{9,8},{10,11... | collective-permute-start | bytes 1572872 | tf_op jit(solution)/shard_map/ppermute | solution.py:24
  47.7 10.5 %collective-permute-start.9 = (bf16[256,512]{1,0:T(8,128)(2,1)S(1)}, bf16[256,512]{1,0:T(8,128)(2,1)S(1)}, u32[]{:S(2)}, u32[]{:S(2)}) collective-permute-start(bf16[256,512]{1,0:T(8,128)(2,1)S(1)} %get-tuple-element.48), channel_id=1, source_target_pairs={{0,2},{1,3},{2,0},{3,1},{4,6},{5,7},{6,4},{7,5},{8,10},{9,11},{10,... | collective-permute-start | bytes 786440 | tf_op jit(solution)/shard_map/ppermute | solution.py:24
  54.4 3.8 %collective-permute-start.8 = (bf16[256,512]{1,0:T(8,128)(2,1)S(1)}, bf16[256,512]{1,0:T(8,128)(2,1)S(1)}, u32[]{:S(2)}, u32[]{:S(2)}) collective-permute-start(bf16[256,512]{1,0:T(8,128)(2,1)S(1)} %collective-permute-done.7.refs_2_), channel_id=1, source_target_pairs={{0,1},{1,0},{2,3},{3,2},{4,5},{5,4},{6,7},{7,6},{8,9},{9,8},{10,11... | collective-permute-start | bytes 786440 | tf_op jit(solution)/shard_map/ppermute | solution.py:24
  58.2 3.1 %collective-permute-start.10 = (bf16[256,512]{1,0:T(8,128)(2,1)S(1)}, bf16[256,512]{1,0:T(8,128)(2,1)S(1)}, u32[]{:S(2)}, u32[]{:S(2)}) collective-permute-start(bf16[256,512]{1,0:T(8,128)(2,1)S(1)} %collective-permute-done.9.refs_2_), channel_id=1, source_target_pairs={{0,1},{1,0},{2,3},{3,2},{4,5},{5,4},{6,7},{7,6},{8,9},{9,8},{10,11... | collective-permute-start | bytes 786440 | tf_op jit(solution)/shard_map/ppermute | solution.py:24

commit v5 on v4

--- a/solution.py
+++ b/solution.py
@@ -9,7 +9,8 @@
 
 
 ITERS = 2
-CHUNKS = 2
+SHARES = ((8, 8), (9, 7))
+CHUNKS = len(SHARES[0])
 GROUP = 8
 EXTRA = 16
 TILE = 256
@@ -33,6 +34,15 @@
     return 0.5 * jnp.tanh(0.5 * x) + 0.5
 
 
+def spans(step, rows):
+    unit = rows // sum(SHARES[step])
+    found, at = [], 0
+    for share in SHARES[step]:
+        found.append((at, share * unit))
+        at += share * unit
+    return found
+
+
 def vmem(count):
     return [pl.BlockSpec(memory_space=pltpu.VMEM)] * count
 
@@ -50,11 +60,10 @@
 
 
 def merge_kernel(guess_ref, init_ref, opening_ref, whole_ref, *parts):
-    chunk, width = opening_ref.shape
-    whole_ref[pl.ds(0, chunk), :] = opening_ref[...]
-    for index, part in enumerate(parts):
+    rows, width = guess_ref.shape
+    whole_ref[pl.ds(0, opening_ref.shape[0]), :] = opening_ref[...]
+    for (at, chunk), part in zip(spans(0, rows)[1:], parts):
         lead = part.shape[0] - chunk
-        at = (index + 1) * chunk
         if lead:
             row = lax.broadcasted_iota(jnp.int32, (lead, width), 0)
             head = jnp.where(row == 0, jnp.broadcast_to(init_ref[...], (lead, width)), 0.0).astype(BF16)
@@ -116,24 +125,23 @@
     return zeta, reset, gated, cand, gap, cand + zeta * gap
 
 
-def step_kernel(count, index, chunks, step, copies, *refs):
+def step_kernel(count, index, start, chunk, step, copies, *refs):
     refs = list(refs)
     near = [refs.pop(0) for _ in range(count // 2)]
     far = [refs.pop(0) for _ in range(count // 2)]
-    weight_ref, inputs_ref, state_ref, next_ref, edge_ref, bias_ref, init_ref = [refs.pop(0) for _ in range(7)]
+    weight_ref, inputs_ref, state_ref, bias_ref, init_ref = [refs.pop(0) for _ in range(5)]
+    last = index == CHUNKS - 1
+    next_ref, edge_ref = [refs.pop(0) for _ in range(2)] if last else (None, None)
     opens = index == 0 and step == 0
     before_ref = None if opens else refs.pop(0)
     diag_ref = None if opens else refs.pop(0)
     a_ref, b_ref, ends_ref = [refs.pop(0) for _ in range(3)]
     diag_ref = refs.pop(0) if opens else diag_ref
-    last = index == chunks - 1
     begins = last and step == 0
     send_ref = refs.pop(0) if last else None
     lhs, *products = refs
     height, full = lhs.shape
     rows, width = state_ref.shape
-    chunk = rows // chunks
-    start = index * chunk
     lead = height - chunk
     hid = lax.axis_index("hid")
     is_first = lax.axis_index("tm") == 0
@@ -264,11 +272,12 @@
         send_ref[:, pl.ds(2 * width // LANES, 1), :] = jnp.broadcast_to(sums[None], (copies, 1, LANES))
 
 
-def apply_kernel(chunks, final, count, *refs):
-    maps, refs = refs[: 2 * chunks], refs[2 * chunks :]
+def apply_kernel(step, count, *refs):
+    final = step == ITERS - 1
+    maps, refs = refs[: 2 * CHUNKS], refs[2 * CHUNKS :]
     begin_ref, all_ref, state_ref = refs[:3]
     outs = refs[3:]
-    chunk, width = maps[0].shape
+    rows, width = state_ref.shape
     lines = width // LANES
     place = lax.axis_index("tm")
     hid = lax.axis_index("hid")
@@ -286,29 +295,35 @@
     if final:
         total = jnp.sum(all_ref[:, pl.ds(2 * lines, 1), :], axis=0)
         lane = lax.broadcasted_iota(jnp.int32, (1, LANES), 1)
-        size = copies * chunk * chunks * width
+        size = copies * rows * width
         for half in range(2):
             outs[0][half] = jnp.sqrt(jnp.sum(jnp.where(lane // (LANES // 2) == half, total, 0.0)) / size)
-    step = 2 * GROUP
-    row = lax.broadcasted_iota(jnp.int32, (step, width), 0)
-    enter = jnp.broadcast_to(enter, (step, width))
+    height = 2 * GROUP
+    row = lax.broadcasted_iota(jnp.int32, (height, width), 0)
+    enter = jnp.broadcast_to(enter, (height, width))
     before = enter
-    for index in range(chunks):
-        a_ref, b_ref = maps[2 * index], maps[2 * index + 1]
+    held = spans(step, rows)
+    sent = held if final else spans(step + 1, rows)
+    cuts = sorted({at for at, _ in held + sent} | {rows})
+    for low, high in zip(cuts, cuts[1:]):
+        source = max(place for place, (at, _) in enumerate(held) if at <= low)
+        target = max(place for place, (at, _) in enumerate(sent) if at <= low)
+        a_ref, b_ref = maps[2 * source], maps[2 * source + 1]
 
         def advance(group, before):
-            here = pl.ds(pl.multiple_of(group * step, step), step)
-            token = pl.ds(pl.multiple_of(index * chunk + group * step, step), step)
+            at = low + group * height
+            here = pl.ds(pl.multiple_of(at - held[source][0], height), height)
+            token = pl.ds(pl.multiple_of(at, height), height)
             turned = pltpu.roll(a_ref[here, :] * enter + b_ref[here, :], 1, 0)
             moved = jnp.where(row == 0, before, turned)
             state_ref[token, :] = moved
             if not final:
                 rounded = moved.astype(BF16)
                 outs[1][token, :] = rounded
-                outs[2 + index][here, :] = rounded
+                outs[2 + target][pl.ds(pl.multiple_of(at - sent[target][0], height), height), :] = rounded
             return turned
 
-        before = lax.fori_loop(0, chunk // step, advance, before, unroll=2)
+        before = lax.fori_loop(0, (high - low) // height, advance, before, unroll=2)
     if not final:
         outs[0][...] = before[0:1]
 
@@ -320,14 +335,17 @@
     blocks_tm = lax.axis_size("tm")
     weight = jnp.transpose(recur_weight, (1, 0, 2))
     table = jnp.transpose(input_table, (1, 0, 2))
-    chunk = rows // CHUNKS
     lines = width // LANES
 
-    opening, rest = lax.optimization_barrier((guess[:chunk].astype(BF16), guess))
+    first = spans(0, rows)[0][1]
+    opening, rest = lax.optimization_barrier((guess[:first].astype(BF16), guess))
     whole, *moved = pl.pallas_call(
         merge_kernel,
         out_shape=[jax.ShapeDtypeStruct((rows + EXTRA, width), BF16)]
-        + [jax.ShapeDtypeStruct((chunk + EXTRA * (index == CHUNKS - 1), width), BF16) for index in range(1, CHUNKS)],
+        + [
+            jax.ShapeDtypeStruct((height + EXTRA * (at + height == rows), width), BF16)
+            for at, height in spans(0, rows)[1:]
+        ],
         in_specs=vmem(3),
         out_specs=vmem(CHUNKS),
         compiler_params=params(8),
@@ -366,12 +384,14 @@
                     far[index][offset | bit] = swapped(far[index][offset], "hid", bit)
             bit //= 2
         maps = []
-        for index in range(CHUNKS):
+        for index, (start, chunk) in enumerate(spans(step, rows)):
             last = index == CHUNKS - 1
             height = moved[index].shape[0]
             operands = [near[offset] for offset in range(count // 2)]
             operands += [far[index][offset] for offset in range(count // 2, count)]
-            operands += [weight, inputs, state, following, edge, hn_bias[None], init_state[None]]
+            operands += [weight, inputs, state, hn_bias[None], init_state[None]]
+            if last:
+                operands += [following, edge]
             if diag is not None:
                 operands += [ends, diag]
             outs = [
@@ -385,7 +405,7 @@
             if last:
                 outs.append(jax.ShapeDtypeStruct((copies, 2 * lines + final, LANES), F32))
             found = pl.pallas_call(
-                functools.partial(step_kernel, count, index, CHUNKS, step, copies),
+                functools.partial(step_kernel, count, index, start, chunk, step, copies),
                 out_shape=outs,
                 in_specs=vmem(len(operands)),
                 out_specs=vmem(len(outs)),
@@ -405,10 +425,10 @@
         else:
             outs.append(jax.ShapeDtypeStruct((1, width), F32))
             outs.append(jax.ShapeDtypeStruct((rows, width), BF16))
-            outs += [jax.ShapeDtypeStruct((chunk, width), BF16)] * CHUNKS
+            outs += [jax.ShapeDtypeStruct((chunk, width), BF16) for _, chunk in spans(step + 1, rows)]
             specs = vmem(len(outs))
         result = pl.pallas_call(
-            functools.partial(apply_kernel, CHUNKS, final, count),
+            functools.partial(apply_kernel, step, count),
             out_shape=outs,
             in_specs=vmem(2 * CHUNKS + 2),
             out_specs=specs,

time: 78.8 us -> 79 us (level)
  starting transfers between devices: 7.04 us -> 8.07 us
  waiting for transfers between devices: 26.4 us -> 25.6 us
    ppermute x1, waiting for transfers between devices: 4.24 us -> 1.22 us  [from_next(): return lax.ppermute(block, axis, route)]
    ppermute x10, waiting for transfers between devices: 22.2 us -> 24.4 us  [swapped(): return lax.ppermute(block, axis, route)]
    ppermute x10, starting transfers between devices: 5.75 us -> 6.78 us  [swapped(): return lax.ppermute(block, axis, route)]
where the time goes in v5:
time: 79 us; the launch traced here: 78.7 us
  waiting for transfers between devices  25.6 us (32%)
  blocking collectives  25.3 us (32%)
  Pallas kernels  15.7 us (20%)
  starting transfers between devices  8.07 us (10%)
  local copies, waits for them, and re-layouts  3.01 us (4%)
  between operations  0.98 us (1%)
    all_to_all x2, blocking collectives, newton(): every = lax.all_to_all(found[-1], ('tm', 'hid') if final else 'tm', 0, 0)  25.3 us
    ppermute x10, waiting for transfers between devices, swapped(): return lax.ppermute(block, axis, route)  24.4 us
    pallas_call x4, Pallas kernels, newton(): pl.pallas_call(functools.partial(step_kernel, count, index, start, chunk,...  11.9 us
    ppermute x10, starting transfers between devices, swapped(): return lax.ppermute(block, axis, route)  6.78 us
    unnamed x20, local copies, waits for them, and re-layouts  1.94 us
    pallas_call x1, Pallas kernels, newton(): pl.pallas_call(prepare_kernel, out_shape=[jax.ShapeDtypeStruct((3, rows +...  1.93 us
    pallas_call x2, Pallas kernels, newton(): pl.pallas_call(functools.partial(apply_kernel, step, count), out_shape=ou...  1.8 us
  transfers between devices with their start and end apart: 11, of which 4 were waited for; matrix products, arithmetic and copies ran while one was open for 0% of the time, Pallas kernels for 10%

profile of v5, /device:TPU:0, one launch (start us, length us, event | category | flops | bytes accessed | tf_op | source)
XLA Modules:
  0.0 78.7 jit_solution(10150238721998693765)
XLA Ops:
  0.6 1.1 %slice.7.opening_ref = bf16[256,512]{1,0:T(8,128)(2,1)S(1)} slice(f32[512,512]{1,0:T(8,128)} %refs_6_.1), slice={[0:256], [0:512]} | slice | bytes 524288 | tf_op jit(solution)/shard_map/slice | solution.py:341
  1.7 1.2 %copy-done = f32[512,512]{1,0:T(8,128)S(1)} copy-done((f32[512,512]{1,0:T(8,128)S(1)}, f32[512,512]{1,0:T(8,128)}, u32[]{:S(2)}) %copy-start) | copy-done | bytes 1048600
  2.9 0.7 copy-done.2
  3.6 0.1 merge.1
  3.7 3.1 %collective-permute-start.3 = (bf16[272,512]{1,0:T(8,128)(2,1)S(1)}, bf16[272,512]{1,0:T(8,128)(2,1)S(1)}, u32[]{:S(2)}, u32[]{:S(2)}) collective-permute-start(bf16[272,512]{1,0:T(8,128)(2,1)S(1)} %get-tuple-element.34), channel_id=1, source_target_pairs={{0,2},{1,3},{2,0},{3,1},{4,6},{5,7},{6,4},{7,5},{8,10},{9,11},{10,... | collective-permute-start | bytes 835592 | tf_op jit(solution)/shard_map/ppermute | solution.py:25
  6.8 0.1 collective-permute-start.1
  6.8 12.2 %collective-permute-done.1.refs_2_ = bf16[256,512]{1,0:T(8,128)(2,1)S(1)} collective-permute-done((bf16[256,512]{1,0:T(8,128)(2,1)S(1)}, bf16[256,512]{1,0:T(8,128)(2,1)S(1)}, u32[]{:S(2)}, u32[]{:S(2)}) %collective-permute-start.1) | collective-permute-done | bytes 262176 | tf_op jit(solution)/shard_map/ppermute | solution.py:25
  19.0 0.5 collective-permute-start.4
  19.6 0.0 copy-start.3
  19.6 1.9 %prepare.1 = (f32[3,520,512]{2,1,0:T(8,128)S(1)}, f32[1,2048]{1,0:T(1,128)S(1)}) custom-call(s32[1,512]{1,0:T(1,128)S(1)} %bitcast.22, f32[512,512]{1,0:T(8,128)S(1)} %copy-done.1, f32[3,256,512]{2,1,0:T(8,128)S(1)} %bitcast.21, f32[1,512]{1,0:T(1,128)S(1)} %bitcast.23), custom_call_target="tpu_custom_call" | custom-call | flops 4000000000 | bytes 2097152 | tf_op jit(solution)/shard_map/prepare/pallas_call | solution.py:356
  21.5 1.3 %collective-permute-start.5 = (f32[1,2048]{1,0:T(1,128)S(1)}, f32[1,2048]{1,0:T(1,128)S(1)}, u32[]{:S(2)}, u32[]{:S(2)}) collective-permute-start(f32[1,2048]{1,0:T(1,128)S(1)} %get-tuple-element.35), channel_id=1, source_target_pairs={{4,0},{8,4},{12,8},{16,12},{20,16},{24,20},{28,24},{5,1},{9,5},{13... | collective-permute-start | bytes 24584 | tf_op jit(solution)/shard_map/ppermute | solution.py:30
  22.9 2.9 %shard_map.86 = (f32[256,512]{1,0:T(8,128)S(1)}, f32[256,512]{1,0:T(8,128)S(1)}, f32[5,512]{1,0:T(8,128)S(1)}, f32[24,512]{1,0:T(8,128)S(1)}) custom-call(bf16[528,512]{1,0:T(8,128)(2,1)S(1)} %get-tuple-element.30.refs_0_, bf16[528,512]{1,0:T(8,128)(2,1)S(1)} %collective-permute-done.refs_1_, bf16[256,512]{1,0:T(8,128)(2,1)S(1)} %collective-permute-done.1.refs_2_, ...), custom_call_target="tpu_custom_call" | custom-call | flops 1610612736 | bytes 6291456 | tf_op jit(solution)/shard_map/pallas_call | solution.py:407
  25.9 1.2 %collective-permute-done.5.refs_9_.refs_10_ = f32[1,2048]{1,0:T(1,128)S(1)} collective-permute-done((f32[1,2048]{1,0:T(1,128)S(1)}, f32[1,2048]{1,0:T(1,128)S(1)}, u32[]{:S(2)}, u32[]{:S(2)}) %collective-permute-start.5) | collective-permute-done | bytes 8224 | tf_op jit(solution)/shard_map/ppermute | solution.py:30
  27.1 3.0 %shard_map.87 = (f32[256,512]{1,0:T(8,128)S(1)}, f32[256,512]{1,0:T(8,128)S(1)}, f32[5,512]{1,0:T(8,128)S(1)}, f32[8,8,128]{2,1,0:T(8,128)S(1)}) custom-call(bf16[528,512]{1,0:T(8,128)(2,1)S(1)} %get-tuple-element.30.refs_0_, bf16[528,512]{1,0:T(8,128)(2,1)S(1)} %collective-permute-done.refs_1_, bf16[272,512]{1,0:T(8,128)(2,1)S(1)} %collective-permute-done.3.refs_2_, ...), custom_call_target="tpu_custom_call" | custom-call | flops 1711276032 | bytes 6291456 | tf_op jit(solution)/shard_map/pallas_call | solution.py:407
  30.1 12.5 %all_to_all.10.refs_5_ = f32[8,8,128]{2,1,0:T(8,128)S(1)} all-to-all(f32[8,8,128]{2,1,0:T(8,128)S(1)} %get-tuple-element.41), channel_id=1, replica_groups=mesh['tm'=8,'hid'=4] {'tm'}, dimensions={0} | all-to-all | bytes 65536 | tf_op jit(solution)/shard_map/all_to_all | solution.py:420
  42.6 0.3 shard_map.88
  42.9 1.6 %collective-permute-start.7 = (bf16[288,512]{1,0:T(8,128)(2,1)S(1)}, bf16[288,512]{1,0:T(8,128)(2,1)S(1)}, u32[]{:S(2)}, u32[]{:S(2)}) collective-permute-start(bf16[288,512]{1,0:T(8,128)(2,1)S(1)} %get-tuple-element.43), channel_id=1, source_target_pairs={{0,2},{1,3},{2,0},{3,1},{4,6},{5,7},{6,4},{7,5},{8,10},{9,11},{10,... | collective-permute-start | bytes 884744 | tf_op jit(solution)/shard_map/ppermute | solution.py:25
  44.5 5.7 %collective-permute-done.7.refs_2_ = bf16[288,512]{1,0:T(8,128)(2,1)S(1)} collective-permute-done((bf16[288,512]{1,0:T(8,128)(2,1)S(1)}, bf16[288,512]{1,0:T(8,128)(2,1)S(1)}, u32[]{:S(2)}, u32[]{:S(2)}) %collective-permute-start.7) | collective-permute-done | bytes 294944 | tf_op jit(solution)/shard_map/ppermute | solution.py:25
  50.2 1.5 %collective-permute-start.9 = (bf16[224,512]{1,0:T(8,128)(2,1)S(1)}, bf16[224,512]{1,0:T(8,128)(2,1)S(1)}, u32[]{:S(2)}, u32[]{:S(2)}) collective-permute-start(bf16[224,512]{1,0:T(8,128)(2,1)S(1)} %get-tuple-element.47), channel_id=1, source_target_pairs={{0,2},{1,3},{2,0},{3,1},{4,6},{5,7},{6,4},{7,5},{8,10},{9,11},{10,... | collective-permute-start | bytes 688136 | tf_op jit(solution)/shard_map/ppermute | solution.py:25
  51.8 6.5 %collective-permute-done.9.refs_2_ = bf16[224,512]{1,0:T(8,128)(2,1)S(1)} collective-permute-done((bf16[224,512]{1,0:T(8,128)(2,1)S(1)}, bf16[224,512]{1,0:T(8,128)(2,1)S(1)}, u32[]{:S(2)}, u32[]{:S(2)}) %collective-permute-start.9) | collective-permute-done | bytes 229408 | tf_op jit(solution)/shard_map/ppermute | solution.py:25
  58.3 3.3 %shard_map.89 = (f32[288,512]{1,0:T(8,128)S(1)}, f32[288,512]{1,0:T(8,128)S(1)}, f32[5,512]{1,0:T(8,128)S(1)}) custom-call(bf16[512,512]{1,0:T(8,128)(2,1)S(1)} %get-tuple-element.42.refs_0_, bf16[512,512]{1,0:T(8,128)(2,1)S(1)} %collective-permute-done.6.refs_1_, bf16[288,512]{1,0:T(8,128)(2,1)S(1)} %collective-permute-done.7.refs_2_, ...), custom_call_target="tpu_custom_call" | custom-call | flops 1811939328 | bytes 6291456 | tf_op jit(solution)/shard_map/pallas_call | solution.py:407
  61.5 2.7 %shard_map.90 = (f32[224,512]{1,0:T(8,128)S(1)}, f32[224,512]{1,0:T(8,128)S(1)}, f32[5,512]{1,0:T(8,128)S(1)}, f32[32,9,128]{2,1,0:T(8,128)S(1)}) custom-call(bf16[512,512]{1,0:T(8,128)(2,1)S(1)} %get-tuple-element.42.refs_0_, bf16[512,512]{1,0:T(8,128)(2,1)S(1)} %collective-permute-done.6.refs_1_, bf16[224,512]{1,0:T(8,128)(2,1)S(1)} %collective-permute-done.9.refs_2_, ...), custom_call_target="tpu_custom_call" | custom-call | flops 1409286144 | bytes 6291456 | tf_op jit(solution)/shard_map/pallas_call | solution.py:407
  64.2 12.8 %all_to_all.11.refs_5_ = f32[32,9,128]{2,1,0:T(8,128)S(1)} all-to-all(f32[32,9,128]{2,1,0:T(8,128)S(1)} %get-tuple-element.53), channel_id=1, replica_groups=mesh['tm'=8,'hid'=4] {'tm','hid'}, dimensions={0} | all-to-all | bytes 294912 | tf_op jit(solution)/shard_map/all_to_all | solution.py:420
  77.0 1.5 %shard_map.91 = (f32[512,512]{1,0:T(8,128)}, f32[2]{0:T(128)}) custom-call(f32[288,512]{1,0:T(8,128)S(1)} %get-tuple-element.45.refs_0_, f32[288,512]{1,0:T(8,128)S(1)} %get-tuple-element.46.refs_1_, f32[224,512]{1,0:T(8,128)S(1)} %get-tuple-element.50.refs_2_, f32[224,512]{1,0:T(8,128)S(1)} %get-tuple-element.51.refs_3_, ...), custom_call_target="tpu_custom_call" | custom-call | flops 524288 | bytes 4194304 | tf_op jit(solution)/shard_map/pallas_call | solution.py:430
  (30 shorter events, 0.1 us)
Async XLA Ops:
  1.7 1.2 %copy-start = (f32[512,512]{1,0:T(8,128)S(1)}, f32[512,512]{1,0:T(8,128)}, u32[]{:S(2)}) copy-start(f32[512,512]{1,0:T(8,128)} %refs_6_.1) | copy-start | bytes 3145732
  2.9 0.7 copy-start.2
  3.6 15.9 %copy-start.1 = (f32[512,512]{1,0:T(8,128)S(1)}, f32[512,512]{1,0:T(8,128)}, u32[]{:S(2)}) copy-start(f32[512,512]{1,0:T(8,128)} %refs_6_.1) | copy-start | bytes 3145732
  3.6 15.9 %copy-start.5 = (f32[256,3,512]{2,0,1:T(8,128)S(1)}, f32[256,3,512]{2,0,1:T(8,128)}, u32[]{:S(2)}) copy-start(f32[256,3,512]{2,0,1:T(8,128)} %param.8) | copy-start | bytes 4718596
  3.6 15.9 %copy-start.6 = (s32[512]{0:T(512)S(1)}, s32[512]{0:T(512)}, u32[]{:S(2)}) copy-start(s32[512]{0:T(512)} %param.7) | copy-start | bytes 6148
  3.6 15.9 %copy-start.7 = (f32[512]{0:T(512)S(1)}, f32[512]{0:T(512)}, u32[]{:S(2)}) copy-start(f32[512]{0:T(512)} %param.10) | copy-start | bytes 6148
  3.7 15.3 %collective-permute-start.3 = (bf16[272,512]{1,0:T(8,128)(2,1)S(1)}, bf16[272,512]{1,0:T(8,128)(2,1)S(1)}, u32[]{:S(2)}, u32[]{:S(2)}) collective-permute-start(bf16[272,512]{1,0:T(8,128)(2,1)S(1)} %get-tuple-element.34), channel_id=1, source_target_pairs={{0,2},{1,3},{2,0},{3,1},{4,6},{5,7},{6,4},{7,5},{8,10},{9,11},{10,... | collective-permute-start | bytes 835592 | tf_op jit(solution)/shard_map/ppermute | solution.py:25
  6.8 12.3 %collective-permute-start.1 = (bf16[256,512]{1,0:T(8,128)(2,1)S(1)}, bf16[256,512]{1,0:T(8,128)(2,1)S(1)}, u32[]{:S(2)}, u32[]{:S(2)}) collective-permute-start(bf16[256,512]{1,0:T(8,128)(2,1)S(1)} %slice.7.opening_ref), channel_id=1, source_target_pairs={{0,2},{1,3},{2,0},{3,1},{4,6},{5,7},{6,4},{7,5},{8,10},{9,11},{10,... | collective-permute-start | bytes 786440 | tf_op jit(solution)/shard_map/ppermute | solution.py:25
  6.8 16.0 %collective-permute-start = (bf16[528,512]{1,0:T(8,128)(2,1)S(1)}, bf16[528,512]{1,0:T(8,128)(2,1)S(1)}, u32[]{:S(2)}, u32[]{:S(2)}) collective-permute-start(bf16[528,512]{1,0:T(8,128)(2,1)S(1)} %get-tuple-element.30.refs_0_), channel_id=1, source_target_pairs={{0,1},{1,0},{2,3},{3,2},{4,5},{5,4},{6,7},{7,6},{8,9},{9,8},{10,11... | collective-permute-start | bytes 1622024 | tf_op jit(solution)/shard_map/ppermute | solution.py:25
  19.0 3.8 %collective-permute-start.2 = (bf16[256,512]{1,0:T(8,128)(2,1)S(1)}, bf16[256,512]{1,0:T(8,128)(2,1)S(1)}, u32[]{:S(2)}, u32[]{:S(2)}) collective-permute-start(bf16[256,512]{1,0:T(8,128)(2,1)S(1)} %collective-permute-done.1.refs_2_), channel_id=1, source_target_pairs={{0,1},{1,0},{2,3},{3,2},{4,5},{5,4},{6,7},{7,6},{8,9},{9,8},{10,11... | collective-permute-start | bytes 786440 | tf_op jit(solution)/shard_map/ppermute | solution.py:25
  19.0 8.1 %collective-permute-start.4 = (bf16[272,512]{1,0:T(8,128)(2,1)S(1)}, bf16[272,512]{1,0:T(8,128)(2,1)S(1)}, u32[]{:S(2)}, u32[]{:S(2)}) collective-permute-start(bf16[272,512]{1,0:T(8,128)(2,1)S(1)} %collective-permute-done.3.refs_2_), channel_id=1, source_target_pairs={{0,1},{1,0},{2,3},{3,2},{4,5},{5,4},{6,7},{7,6},{8,9},{9,8},{10,11... | collective-permute-start | bytes 835592 | tf_op jit(solution)/shard_map/ppermute | solution.py:25
  19.5 3.3 %slice-start = ((s8[6291456]{0:T(1024)(128)(4,1)}), s8[4194304]{0:T(1024)(128)(4,1)S(1)}, s32[]{:S(2)}) async-start(s8[6291456]{0:T(1024)(128)(4,1)} %bitcast.6), calls=%async_computation.2 | async-start | bytes 8388608
  19.6 3.3 %slice-start.1 = ((s8[6291456]{0:T(1024)(128)(4,1)}), s8[2097152]{0:T(1024)(128)(4,1)S(1)}, s32[]{:S(2)}) async-start(s8[6291456]{0:T(1024)(128)(4,1)} %bitcast.6), calls=%async_computation.3 | async-start | bytes 4194304
  19.6 3.3 %copy-start.3 = (f32[512]{0:T(512)S(1)}, f32[512]{0:T(512)}, u32[]{:S(2)}) copy-start(f32[512]{0:T(512)} %param.12) | copy-start | bytes 6148
  19.6 3.3 %copy-start.4 = (f32[512]{0:T(512)S(1)}, f32[512]{0:T(512)}, u32[]{:S(2)}) copy-start(f32[512]{0:T(512)} %param.11) | copy-start | bytes 6148
  21.5 5.5 %collective-permute-start.5 = (f32[1,2048]{1,0:T(1,128)S(1)}, f32[1,2048]{1,0:T(1,128)S(1)}, u32[]{:S(2)}, u32[]{:S(2)}) collective-permute-start(f32[1,2048]{1,0:T(1,128)S(1)} %get-tuple-element.35), channel_id=1, source_target_pairs={{4,0},{8,4},{12,8},{16,12},{20,16},{24,20},{28,24},{5,1},{9,5},{13... | collective-permute-start | bytes 24584 | tf_op jit(solution)/shard_map/ppermute | solution.py:30
  42.9 7.3 %collective-permute-start.7 = (bf16[288,512]{1,0:T(8,128)(2,1)S(1)}, bf16[288,512]{1,0:T(8,128)(2,1)S(1)}, u32[]{:S(2)}, u32[]{:S(2)}) collective-permute-start(bf16[288,512]{1,0:T(8,128)(2,1)S(1)} %get-tuple-element.43), channel_id=1, source_target_pairs={{0,2},{1,3},{2,0},{3,1},{4,6},{5,7},{6,4},{7,5},{8,10},{9,11},{10,... | collective-permute-start | bytes 884744 | tf_op jit(solution)/shard_map/ppermute | solution.py:25
  44.5 13.7 %collective-permute-start.6 = (bf16[512,512]{1,0:T(8,128)(2,1)S(1)}, bf16[512,512]{1,0:T(8,128)(2,1)S(1)}, u32[]{:S(2)}, u32[]{:S(2)}) collective-permute-start(bf16[512,512]{1,0:T(8,128)(2,1)S(1)} %get-tuple-element.42.refs_0_), channel_id=1, source_target_pairs={{0,1},{1,0},{2,3},{3,2},{4,5},{5,4},{6,7},{7,6},{8,9},{9,8},{10,11... | collective-permute-start | bytes 1572872 | tf_op jit(solution)/shard_map/ppermute | solution.py:25
  50.2 8.0 %collective-permute-start.8 = (bf16[288,512]{1,0:T(8,128)(2,1)S(1)}, bf16[288,512]{1,0:T(8,128)(2,1)S(1)}, u32[]{:S(2)}, u32[]{:S(2)}) collective-permute-start(bf16[288,512]{1,0:T(8,128)(2,1)S(1)} %collective-permute-done.7.refs_2_), channel_id=1, source_target_pairs={{0,1},{1,0},{2,3},{3,2},{4,5},{5,4},{6,7},{7,6},{8,9},{9,8},{10,11... | collective-permute-start | bytes 884744 | tf_op jit(solution)/shard_map/ppermute | solution.py:25
  50.2 8.0 %collective-permute-start.9 = (bf16[224,512]{1,0:T(8,128)(2,1)S(1)}, bf16[224,512]{1,0:T(8,128)(2,1)S(1)}, u32[]{:S(2)}, u32[]{:S(2)}) collective-permute-start(bf16[224,512]{1,0:T(8,128)(2,1)S(1)} %get-tuple-element.47), channel_id=1, source_target_pairs={{0,2},{1,3},{2,0},{3,1},{4,6},{5,7},{6,4},{7,5},{8,10},{9,11},{10,... | collective-permute-start | bytes 688136 | tf_op jit(solution)/shard_map/ppermute | solution.py:25
  58.3 3.3 %collective-permute-start.10 = (bf16[224,512]{1,0:T(8,128)(2,1)S(1)}, bf16[224,512]{1,0:T(8,128)(2,1)S(1)}, u32[]{:S(2)}, u32[]{:S(2)}) collective-permute-start(bf16[224,512]{1,0:T(8,128)(2,1)S(1)} %collective-permute-done.9.refs_2_), channel_id=1, source_target_pairs={{0,1},{1,0},{2,3},{3,2},{4,5},{5,4},{6,7},{7,6},{8,9},{9,8},{10,11... | collective-permute-start | bytes 688136 | tf_op jit(solution)/shard_map/ppermute | solution.py:25

commit v6 on v5

--- a/solution.py
+++ b/solution.py
@@ -87,7 +87,9 @@
     def pick(hot, part):
         return lax.dot_general(hot, part, (((0,), (0,)), ((), ())), preferred_element_type=F32)
 
-    hot, hot_begin = spread(pltpu.roll(ids, rows - 1, 1)), spread(jnp.broadcast_to(ids[:, 0:1], (1, LANES)))
+    lane = lax.broadcasted_iota(jnp.int32, (1, rows), 1)
+    hot = spread(jnp.where(lane == rows - 1, vocab, pltpu.roll(ids, rows - 1, 1)))
+    hot_begin = spread(jnp.broadcast_to(ids[:, 0:1], (1, LANES)))
     line_ref[:, pl.ds(0, width)] = guess_ref[0:1, :]
     for gate in range(3):
         table = table_ref[gate]
@@ -115,21 +117,63 @@
         diag_ref[pl.ds(gate * GROUP, GROUP), :] = jnp.broadcast_to(line, (GROUP, width))
 
 
-def gates(inputs, products, prev, hn_bias):
-    zeta = sigmoid(inputs[0] + products[0])
-    reset = sigmoid(inputs[1] + products[1])
-    cand_pre = products[2] + hn_bias
-    gated = reset * cand_pre
-    cand = jnp.tanh(inputs[2] + gated)
+def gates(bases, products, inputs, prev):
+    zeta = sigmoid(bases[0] + products[0])
+    reset = sigmoid(bases[1] + products[1])
+    gated = reset * (bases[2] + products[2])
+    cand = jnp.tanh(inputs + gated)
     gap = prev - cand
     return zeta, reset, gated, cand, gap, cand + zeta * gap
 
 
+def tile_dot(lhs, weight_ref, first, gate, lanes):
+    depth = lhs.shape[1]
+    pieces = 2 if gate == 2 else 1
+    total = None
+    for piece in range(pieces):
+        at = pl.multiple_of(first + piece * (depth // pieces), depth // pieces)
+        term = jnp.dot(
+            lhs[:, pl.ds(piece * (depth // pieces), depth // pieces)],
+            weight_ref[gate, pl.ds(at, depth // pieces), lanes],
+            preferred_element_type=F32,
+        )
+        total = term if total is None else total + term
+    return total
+
+
+def base_kernel(step, count, *refs):
+    near, (weight_ref, inputs_ref, bias_ref, base_ref, lhs) = refs[: count // 2], refs[count // 2 :]
+    height, _ = lhs.shape
+    width = base_ref.shape[2]
+    rows = inputs_ref.shape[1] - GROUP
+    hid = lax.axis_index("hid")
+    own = hid % (count // 2)
+    for offset in range(count // 2):
+        lhs[:, pl.ds(pl.multiple_of((own ^ offset) * width, width), width)] = near[offset][...]
+    pieces, at = [], 0
+    for start, chunk in spans(step, rows):
+        if start + chunk == rows and height > rows:
+            pieces.append((at, rows, GROUP))
+            at += EXTRA
+        pieces.append((at, start, chunk))
+        at += chunk
+    for tile in range(width // TILE):
+        lanes = pl.ds(tile * TILE, TILE)
+        for gate in range(3):
+            found = tile_dot(lhs, weight_ref, (hid - own) * width, gate, lanes)
+            if gate == 2:
+                base_ref[gate, :, lanes] = found + bias_ref[:, lanes]
+            else:
+                for at, start, size in pieces:
+                    base_ref[gate, pl.ds(at, size), lanes] = (
+                        found[at : at + size] + inputs_ref[gate, pl.ds(start, size), lanes]
+                    )
+
+
 def step_kernel(count, index, start, chunk, step, copies, *refs):
     refs = list(refs)
-    near = [refs.pop(0) for _ in range(count // 2)]
     far = [refs.pop(0) for _ in range(count // 2)]
-    weight_ref, inputs_ref, state_ref, bias_ref, init_ref = [refs.pop(0) for _ in range(5)]
+    weight_ref, base_ref, inputs_ref, state_ref, init_ref = [refs.pop(0) for _ in range(5)]
     last = index == CHUNKS - 1
     next_ref, edge_ref = [refs.pop(0) for _ in range(2)] if last else (None, None)
     opens = index == 0 and step == 0
@@ -140,7 +184,7 @@
     begins = last and step == 0
     send_ref = refs.pop(0) if last else None
     lhs, *products = refs
-    height, full = lhs.shape
+    height = lhs.shape[0]
     rows, width = state_ref.shape
     lead = height - chunk
     hid = lax.axis_index("hid")
@@ -151,27 +195,19 @@
 
     if opens:
         diagonals(weight_ref, hid, diag_ref)
-    for offset in range(count):
-        place = pl.multiple_of((hid ^ offset) * width, width)
-        if offset < count // 2:
-            lhs[:, pl.ds(place, width)] = near[offset][pl.ds(start, height), :]
-        else:
-            lhs[:, pl.ds(place, width)] = far[offset - count // 2][...]
+    own = hid % (count // 2)
+    for offset in range(count // 2):
+        lhs[:, pl.ds(pl.multiple_of((own ^ offset) * width, width), width)] = far[offset][...]
+    first = ((hid - own) ^ (count // 2)) * width
     row = lax.broadcasted_iota(jnp.int32, (GROUP, TILE), 0)
     zeros = jnp.zeros((GROUP, TILE), F32)
 
     def dots(tile):
-        lanes = pl.ds(tile * TILE, TILE)
-        half = full // 2
-        for gate in range(2):
-            products[tile][gate] = jnp.dot(lhs[...], weight_ref[gate, :, lanes], preferred_element_type=F32)
-        left = jnp.dot(lhs[:, pl.ds(0, half)], weight_ref[2, pl.ds(0, half), lanes], preferred_element_type=F32)
-        right = jnp.dot(lhs[:, pl.ds(half, half)], weight_ref[2, pl.ds(half, half), lanes], preferred_element_type=F32)
-        products[tile][2] = left + right
+        for gate in range(3):
+            products[tile][gate] = tile_dot(lhs, weight_ref, first, gate, pl.ds(tile * TILE, TILE))
 
     def cells(tile):
         lanes = pl.ds(tile * TILE, TILE)
-        hn_bias = jnp.broadcast_to(bias_ref[:, lanes], (GROUP, TILE))
         diag_z = diag_ref[pl.ds(0, GROUP), lanes]
         diag_r = diag_ref[pl.ds(GROUP, GROUP), lanes]
         diag_n = diag_ref[pl.ds(2 * GROUP, GROUP), lanes]
@@ -193,17 +229,16 @@
             turned_next = pltpu.roll(following, GROUP - 1, 0)
             state = jnp.where(row == GROUP - 1, turned_next, turned)
             turned = turned_next
-            terms = [inputs_ref[gate, token, lanes] for gate in range(3)]
+            place = lead + group * GROUP
+            bases = [base_ref[gate, pl.ds(start + place, GROUP), lanes] for gate in range(3)]
+            inputs = inputs_ref[2, token, lanes]
             if last and group == groups - 1:
-                for gate in range(3):
-                    edge = edge_ref[:, pl.ds((gate + 1) * width + tile * TILE, TILE)]
-                    terms[gate] = jnp.where(row == GROUP - 1, jnp.broadcast_to(edge, (GROUP, TILE)), terms[gate])
-            zeta, reset, gated, cand, gap, value = gates(
-                terms,
-                [products[tile][gate, pl.ds(lead + group * GROUP, GROUP), :] for gate in range(3)],
-                prev,
-                hn_bias,
-            )
+                edges = [edge_ref[:, pl.ds((gate + 1) * width + tile * TILE, TILE)] for gate in range(3)]
+                edges = [jnp.where(row == GROUP - 1, jnp.broadcast_to(line, (GROUP, TILE)), 0.0) for line in edges]
+                bases = [bases[0] + edges[0], bases[1] + edges[1], bases[2]]
+                inputs = inputs + edges[2]
+            found = [products[tile][gate, pl.ds(place, GROUP), :] for gate in range(3)]
+            zeta, reset, gated, cand, gap, value = gates(bases, found, inputs, prev)
             rest = 1.0 - zeta
             slope = zeta + gap * (zeta * rest) * diag_z
             slope = slope + rest * (1.0 - cand * cand) * (reset * diag_n + gated * (1.0 - reset) * diag_r)
@@ -226,10 +261,10 @@
             run_a, run_b = last_a * run_a, last_a * run_b + last_b
         if begins:
             begin = gates(
-                [inputs_ref[gate, pl.ds(rows, GROUP), lanes] for gate in range(3)],
+                [base_ref[gate, pl.ds(start, GROUP), lanes] for gate in range(3)],
                 [products[tile][gate, pl.ds(0, GROUP), :] for gate in range(3)],
+                inputs_ref[2, pl.ds(rows, GROUP), lanes],
                 jnp.broadcast_to(init_ref[:, lanes], (GROUP, TILE)),
-                hn_bias,
             )[-1]
             error = state_ref[pl.ds(0, GROUP), lanes] - begin
             squares = squares + jnp.where((row == 0) & is_first, error * error, 0.0)
@@ -383,13 +418,22 @@
                 for offset in list(far[index]):
                     far[index][offset | bit] = swapped(far[index][offset], "hid", bit)
             bit //= 2
+        height = whole.shape[0]
+        base = pl.pallas_call(
+            functools.partial(base_kernel, step, count),
+            out_shape=jax.ShapeDtypeStruct((3, height, width), F32),
+            in_specs=vmem(count // 2 + 3),
+            out_specs=vmem(1)[0],
+            scratch_shapes=[pltpu.VMEM((height, full // 2), BF16)],
+            compiler_params=params(16),
+            cost_estimate=cost(3 * height * full * width, 3 * full * width),
+        )(*[near[offset] for offset in range(count // 2)], weight, inputs, hn_bias[None])
         maps = []
         for index, (start, chunk) in enumerate(spans(step, rows)):
             last = index == CHUNKS - 1
             height = moved[index].shape[0]
-            operands = [near[offset] for offset in range(count // 2)]
-            operands += [far[index][offset] for offset in range(count // 2, count)]
-            operands += [weight, inputs, state, hn_bias[None], init_state[None]]
+            operands = [far[index][offset] for offset in range(count // 2, count)]
+            operands += [weight, base, inputs, state, init_state[None]]
             if last:
                 operands += [following, edge]
             if diag is not None:
@@ -409,10 +453,10 @@
                 out_shape=outs,
                 in_specs=vmem(len(operands)),
                 out_specs=vmem(len(outs)),
-                scratch_shapes=[pltpu.VMEM((height, full), BF16)]
+                scratch_shapes=[pltpu.VMEM((height, full // 2), BF16)]
                 + [pltpu.VMEM((3, height, TILE), F32)] * (width // TILE),
                 compiler_params=params(32),
-                cost_estimate=cost(2 * height * full * 3 * width, 6 * full * width),
+                cost_estimate=cost(height * full * 3 * width, 3 * full * width),
             )(*operands)
             maps += found[:2]
             ends = found[2]

time: 79 us -> 78.3 us (level)
  waiting for transfers between devices: 25.6 us -> 24.5 us
  starting transfers between devices: 8.07 us -> 7.11 us
  blocking collectives: 25.3 us -> 26.1 us
    pallas_call x0 -> x2, Pallas kernels: none -> 3.91 us  [newton(): pl.pallas_call(functools.partial(base_kernel, step, count), out_shape=jax...]
    pallas_call x4, Pallas kernels: 11.9 us -> 8.57 us  [newton(): pl.pallas_call(functools.partial(step_kernel, count, index, start, chunk,...]
    ppermute x1, waiting for transfers between devices: 1.22 us -> 0.06 us  [from_next(): return lax.ppermute(block, axis, route)]
    ppermute x10, starting transfers between devices: 6.78 us -> 5.82 us  [swapped(): return lax.ppermute(block, axis, route)]
    all_to_all x2, blocking collectives: 25.3 us -> 26.1 us  [newton(): every = lax.all_to_all(found[-1], ('tm', 'hid') if final else 'tm', 0, 0)]
  transfers between devices with their start and end apart: 11 -> 11, of which waited for: 4 -> 4; matrix products, arithmetic and copies ran while one was open for 0% -> 0% of each run, Pallas kernels for 10% -> 13%
where the time goes in v6:
time: 78.3 us; the launch traced here: 78 us
  blocking collectives  26.1 us (33%)
  waiting for transfers between devices  24.5 us (31%)
  Pallas kernels  16.3 us (21%)
  starting transfers between devices  7.11 us (9%)
  local copies, waits for them, and re-layouts  3.01 us (4%)
  between operations  1 us (1%)
    all_to_all x2, blocking collectives, newton(): every = lax.all_to_all(found[-1], ('tm', 'hid') if final else 'tm', 0, 0)  26.1 us
    ppermute x10, waiting for transfers between devices, swapped(): return lax.ppermute(block, axis, route)  24.4 us
    pallas_call x4, Pallas kernels, newton(): pl.pallas_call(functools.partial(step_kernel, count, index, start, chunk,...  8.57 us
    ppermute x10, starting transfers between devices, swapped(): return lax.ppermute(block, axis, route)  5.82 us
    pallas_call x2, Pallas kernels, newton(): pl.pallas_call(functools.partial(base_kernel, step, count), out_shape=jax...  3.91 us
    unnamed x20, local copies, waits for them, and re-layouts  1.94 us
    pallas_call x1, Pallas kernels, newton(): pl.pallas_call(prepare_kernel, out_shape=[jax.ShapeDtypeStruct((3, rows +...  1.94 us
    pallas_call x2, Pallas kernels, newton(): pl.pallas_call(functools.partial(apply_kernel, step, count), out_shape=ou...  1.8 us
  transfers between devices with their start and end apart: 11, of which 4 were waited for; matrix products, arithmetic and copies ran while one was open for 0% of the time, Pallas kernels for 13%

profile of v6, /device:TPU:0, one launch (start us, length us, event | category | flops | bytes accessed | tf_op | source)
XLA Modules:
  0.0 78.0 jit_solution(11272457753499497468)
XLA Ops:
  0.6 1.1 %slice.7.opening_ref = bf16[256,512]{1,0:T(8,128)(2,1)S(1)} slice(f32[512,512]{1,0:T(8,128)} %refs_5_.1), slice={[0:256], [0:512]} | slice | bytes 524288 | tf_op jit(solution)/shard_map/slice | solution.py:376
  1.7 1.2 %copy-done = f32[512,512]{1,0:T(8,128)S(1)} copy-done((f32[512,512]{1,0:T(8,128)S(1)}, f32[512,512]{1,0:T(8,128)}, u32[]{:S(2)}) %copy-start) | copy-done | bytes 1048600
  2.9 0.7 copy-done.2
  3.7 3.1 %collective-permute-start.3 = (bf16[272,512]{1,0:T(8,128)(2,1)S(1)}, bf16[272,512]{1,0:T(8,128)(2,1)S(1)}, u32[]{:S(2)}, u32[]{:S(2)}) collective-permute-start(bf16[272,512]{1,0:T(8,128)(2,1)S(1)} %get-tuple-element.34), channel_id=1, source_target_pairs={{0,2},{1,3},{2,0},{3,1},{4,6},{5,7},{6,4},{7,5},{8,10},{9,11},{10,... | collective-permute-start | bytes 835592 | tf_op jit(solution)/shard_map/ppermute | solution.py:25
  6.8 0.1 collective-permute-start
  6.8 12.2 %collective-permute-done.refs_0_ = bf16[256,512]{1,0:T(8,128)(2,1)S(1)} collective-permute-done((bf16[256,512]{1,0:T(8,128)(2,1)S(1)}, bf16[256,512]{1,0:T(8,128)(2,1)S(1)}, u32[]{:S(2)}, u32[]{:S(2)}) %collective-permute-start) | collective-permute-done | bytes 262176 | tf_op jit(solution)/shard_map/ppermute | solution.py:25
  19.0 0.5 collective-permute-start.4
  19.6 1.9 %prepare.1 = (f32[3,520,512]{2,1,0:T(8,128)S(1)}, f32[1,2048]{1,0:T(1,128)S(1)}) custom-call(s32[1,512]{1,0:T(1,128)S(1)} %bitcast.22, f32[512,512]{1,0:T(8,128)S(1)} %copy-done.1, f32[3,256,512]{2,1,0:T(8,128)S(1)} %bitcast.21, f32[1,512]{1,0:T(1,128)S(1)} %bitcast.23), custom_call_target="tpu_custom_call" | custom-call | flops 4000000000 | bytes 2097152 | tf_op jit(solution)/shard_map/prepare/pallas_call | solution.py:391
  21.5 1.3 %collective-permute-start.5 = (f32[1,2048]{1,0:T(1,128)S(1)}, f32[1,2048]{1,0:T(1,128)S(1)}, u32[]{:S(2)}, u32[]{:S(2)}) collective-permute-start(f32[1,2048]{1,0:T(1,128)S(1)} %get-tuple-element.35), channel_id=1, source_target_pairs={{4,0},{8,4},{12,8},{16,12},{20,16},{24,20},{28,24},{5,1},{9,5},{13... | collective-permute-start | bytes 24584 | tf_op jit(solution)/shard_map/ppermute | solution.py:30
  22.9 2.0 %shard_map.86.refs_3_ = f32[3,528,512]{2,1,0:T(8,128)S(1)} custom-call(bf16[528,512]{1,0:T(8,128)(2,1)S(1)} %get-tuple-element.30.refs_0_, bf16[528,512]{1,0:T(8,128)(2,1)S(1)} %collective-permute-done.2.refs_1_, bf16[3,2048,512]{2,1,0:T(8,128)(2,1)S(1)} %bitcast.8, f32[3,520,512]{2,1,0:T(8,128)S(1)} %get-tuple-element.31.refs_3_.refs_4_, f32[1,512]{1,0:T(1,128)S(1)} %bitcast.19), custom_call_target="tpu_custom_call" | custom-call | flops 1660944384 | bytes 3145728 | tf_op jit(solution)/shard_map/pallas_call | solution.py:422
  24.9 2.1 %shard_map.87 = (f32[256,512]{1,0:T(8,128)S(1)}, f32[256,512]{1,0:T(8,128)S(1)}, f32[5,512]{1,0:T(8,128)S(1)}, f32[24,512]{1,0:T(8,128)S(1)}) custom-call(bf16[256,512]{1,0:T(8,128)(2,1)S(1)} %collective-permute-done.refs_0_, bf16[256,512]{1,0:T(8,128)(2,1)S(1)} %collective-permute-done.1.refs_1_, bf16[3,2048,512]{2,1,0:T(8,128)(2,1)S(1)} %bitcast.9, ...), custom_call_target="tpu_custom_call" | custom-call | flops 805306368 | bytes 3145728 | tf_op jit(solution)/shard_map/pallas_call | solution.py:451
  27.1 2.2 %shard_map.88 = (f32[256,512]{1,0:T(8,128)S(1)}, f32[256,512]{1,0:T(8,128)S(1)}, f32[5,512]{1,0:T(8,128)S(1)}, f32[8,8,128]{2,1,0:T(8,128)S(1)}) custom-call(bf16[272,512]{1,0:T(8,128)(2,1)S(1)} %collective-permute-done.3.refs_0_, bf16[272,512]{1,0:T(8,128)(2,1)S(1)} %collective-permute-done.4.refs_1_, bf16[3,2048,512]{2,1,0:T(8,128)(2,1)S(1)} %bitcast.10, ...), custom_call_target="tpu_custom_call" | custom-call | flops 855638016 | bytes 3145728 | tf_op jit(solution)/shard_map/pallas_call | solution.py:451
  29.3 13.6 %all_to_all.10.refs_5_ = f32[8,8,128]{2,1,0:T(8,128)S(1)} all-to-all(f32[8,8,128]{2,1,0:T(8,128)S(1)} %get-tuple-element.41), channel_id=1, replica_groups=mesh['tm'=8,'hid'=4] {'tm'}, dimensions={0} | all-to-all | bytes 65536 | tf_op jit(solution)/shard_map/all_to_all | solution.py:464
  42.9 0.3 shard_map.89
  43.2 0.1 collective-permute-start.8
  43.3 1.6 %collective-permute-start.6 = (bf16[288,512]{1,0:T(8,128)(2,1)S(1)}, bf16[288,512]{1,0:T(8,128)(2,1)S(1)}, u32[]{:S(2)}, u32[]{:S(2)}) collective-permute-start(bf16[288,512]{1,0:T(8,128)(2,1)S(1)} %get-tuple-element.42), channel_id=1, source_target_pairs={{0,2},{1,3},{2,0},{3,1},{4,6},{5,7},{6,4},{7,5},{8,10},{9,11},{10,... | collective-permute-start | bytes 884744 | tf_op jit(solution)/shard_map/ppermute | solution.py:25
  44.9 0.5 collective-permute-start.9
  45.4 7.9 %collective-permute-done.6.refs_0_ = bf16[288,512]{1,0:T(8,128)(2,1)S(1)} collective-permute-done((bf16[288,512]{1,0:T(8,128)(2,1)S(1)}, bf16[288,512]{1,0:T(8,128)(2,1)S(1)}, u32[]{:S(2)}, u32[]{:S(2)}) %collective-permute-start.6) | collective-permute-done | bytes 294944 | tf_op jit(solution)/shard_map/ppermute | solution.py:25
  53.3 4.4 %collective-permute-done.9.refs_0_ = bf16[224,512]{1,0:T(8,128)(2,1)S(1)} collective-permute-done((bf16[224,512]{1,0:T(8,128)(2,1)S(1)}, bf16[224,512]{1,0:T(8,128)(2,1)S(1)}, u32[]{:S(2)}, u32[]{:S(2)}) %collective-permute-start.9) | collective-permute-done | bytes 229408 | tf_op jit(solution)/shard_map/ppermute | solution.py:25
  57.6 1.9 %shard_map.90.refs_3_ = f32[3,512,512]{2,1,0:T(8,128)S(1)} custom-call(bf16[512,512]{1,0:T(8,128)(2,1)S(1)} %get-tuple-element.43.refs_0_, bf16[512,512]{1,0:T(8,128)(2,1)S(1)} %collective-permute-done.8.refs_1_, bf16[3,2048,512]{2,1,0:T(8,128)(2,1)S(1)} %bitcast.11, f32[3,520,512]{2,1,0:T(8,128)S(1)} %get-tuple-element.31.refs_3_.refs_4_, f32[1,512]{1,0:T(1,128)S(1)} %bitcast.20), custom_call_target="tpu_custom_call" | custom-call | flops 1610612736 | bytes 3145728 | tf_op jit(solution)/shard_map/pallas_call | solution.py:422
  59.6 2.3 %shard_map.91 = (f32[288,512]{1,0:T(8,128)S(1)}, f32[288,512]{1,0:T(8,128)S(1)}, f32[5,512]{1,0:T(8,128)S(1)}) custom-call(bf16[288,512]{1,0:T(8,128)(2,1)S(1)} %collective-permute-done.6.refs_0_, bf16[288,512]{1,0:T(8,128)(2,1)S(1)} %collective-permute-done.7.refs_1_, bf16[3,2048,512]{2,1,0:T(8,128)(2,1)S(1)} %bitcast.12, ...), custom_call_target="tpu_custom_call" | custom-call | flops 905969664 | bytes 3145728 | tf_op jit(solution)/shard_map/pallas_call | solution.py:451
  61.9 2.0 %shard_map.92 = (f32[224,512]{1,0:T(8,128)S(1)}, f32[224,512]{1,0:T(8,128)S(1)}, f32[5,512]{1,0:T(8,128)S(1)}, f32[32,9,128]{2,1,0:T(8,128)S(1)}) custom-call(bf16[224,512]{1,0:T(8,128)(2,1)S(1)} %collective-permute-done.9.refs_0_, bf16[224,512]{1,0:T(8,128)(2,1)S(1)} %collective-permute-done.10.refs_1_, bf16[3,2048,512]{2,1,0:T(8,128)(2,1)S(1)} %bitcast.13, ...), custom_call_target="tpu_custom_call" | custom-call | flops 704643072 | bytes 3145728 | tf_op jit(solution)/shard_map/pallas_call | solution.py:451
  63.9 12.5 %all_to_all.11.refs_5_ = f32[32,9,128]{2,1,0:T(8,128)S(1)} all-to-all(f32[32,9,128]{2,1,0:T(8,128)S(1)} %get-tuple-element.53), channel_id=1, replica_groups=mesh['tm'=8,'hid'=4] {'tm','hid'}, dimensions={0} | all-to-all | bytes 294912 | tf_op jit(solution)/shard_map/all_to_all | solution.py:464
  76.4 1.5 %shard_map.93 = (f32[512,512]{1,0:T(8,128)}, f32[2]{0:T(128)}) custom-call(f32[288,512]{1,0:T(8,128)S(1)} %get-tuple-element.45.refs_0_, f32[288,512]{1,0:T(8,128)S(1)} %get-tuple-element.46.refs_1_, f32[224,512]{1,0:T(8,128)S(1)} %get-tuple-element.50.refs_2_, f32[224,512]{1,0:T(8,128)S(1)} %get-tuple-element.51.refs_3_, ...), custom_call_target="tpu_custom_call" | custom-call | flops 524288 | bytes 4194304 | tf_op jit(solution)/shard_map/pallas_call | solution.py:474
  (32 shorter events, 0.2 us)
Async XLA Ops:
  1.7 1.2 %copy-start = (f32[512,512]{1,0:T(8,128)S(1)}, f32[512,512]{1,0:T(8,128)}, u32[]{:S(2)}) copy-start(f32[512,512]{1,0:T(8,128)} %refs_5_.1) | copy-start | bytes 3145732
  2.9 0.7 copy-start.2
  3.6 15.9 %copy-start.1 = (f32[512,512]{1,0:T(8,128)S(1)}, f32[512,512]{1,0:T(8,128)}, u32[]{:S(2)}) copy-start(f32[512,512]{1,0:T(8,128)} %refs_5_.1) | copy-start | bytes 3145732
  3.6 15.9 %copy-start.5 = (f32[256,3,512]{2,0,1:T(8,128)S(1)}, f32[256,3,512]{2,0,1:T(8,128)}, u32[]{:S(2)}) copy-start(f32[256,3,512]{2,0,1:T(8,128)} %param.8) | copy-start | bytes 4718596
  3.6 15.9 %copy-start.6 = (s32[512]{0:T(512)S(1)}, s32[512]{0:T(512)}, u32[]{:S(2)}) copy-start(s32[512]{0:T(512)} %param.7) | copy-start | bytes 6148
  3.6 15.9 %copy-start.7 = (f32[512]{0:T(512)S(1)}, f32[512]{0:T(512)}, u32[]{:S(2)}) copy-start(f32[512]{0:T(512)} %param.10) | copy-start | bytes 6148
  3.7 15.3 %collective-permute-start.3 = (bf16[272,512]{1,0:T(8,128)(2,1)S(1)}, bf16[272,512]{1,0:T(8,128)(2,1)S(1)}, u32[]{:S(2)}, u32[]{:S(2)}) collective-permute-start(bf16[272,512]{1,0:T(8,128)(2,1)S(1)} %get-tuple-element.34), channel_id=1, source_target_pairs={{0,2},{1,3},{2,0},{3,1},{4,6},{5,7},{6,4},{7,5},{8,10},{9,11},{10,... | collective-permute-start | bytes 835592 | tf_op jit(solution)/shard_map/ppermute | solution.py:25
  6.8 12.3 %collective-permute-start = (bf16[256,512]{1,0:T(8,128)(2,1)S(1)}, bf16[256,512]{1,0:T(8,128)(2,1)S(1)}, u32[]{:S(2)}, u32[]{:S(2)}) collective-permute-start(bf16[256,512]{1,0:T(8,128)(2,1)S(1)} %slice.7.opening_ref), channel_id=1, source_target_pairs={{0,2},{1,3},{2,0},{3,1},{4,6},{5,7},{6,4},{7,5},{8,10},{9,11},{10,... | collective-permute-start | bytes 786440 | tf_op jit(solution)/shard_map/ppermute | solution.py:25
  6.8 16.0 %collective-permute-start.2 = (bf16[528,512]{1,0:T(8,128)(2,1)S(1)}, bf16[528,512]{1,0:T(8,128)(2,1)S(1)}, u32[]{:S(2)}, u32[]{:S(2)}) collective-permute-start(bf16[528,512]{1,0:T(8,128)(2,1)S(1)} %get-tuple-element.30.refs_0_), channel_id=1, source_target_pairs={{0,1},{1,0},{2,3},{3,2},{4,5},{5,4},{6,7},{7,6},{8,9},{9,8},{10,11... | collective-permute-start | bytes 1622024 | tf_op jit(solution)/shard_map/ppermute | solution.py:25
  19.0 5.9 %collective-permute-start.1 = (bf16[256,512]{1,0:T(8,128)(2,1)S(1)}, bf16[256,512]{1,0:T(8,128)(2,1)S(1)}, u32[]{:S(2)}, u32[]{:S(2)}) collective-permute-start(bf16[256,512]{1,0:T(8,128)(2,1)S(1)} %collective-permute-done.refs_0_), channel_id=1, source_target_pairs={{0,1},{1,0},{2,3},{3,2},{4,5},{5,4},{6,7},{7,6},{8,9},{9,8},{10,11... | collective-permute-start | bytes 786440 | tf_op jit(solution)/shard_map/ppermute | solution.py:25
  19.0 8.0 %collective-permute-start.4 = (bf16[272,512]{1,0:T(8,128)(2,1)S(1)}, bf16[272,512]{1,0:T(8,128)(2,1)S(1)}, u32[]{:S(2)}, u32[]{:S(2)}) collective-permute-start(bf16[272,512]{1,0:T(8,128)(2,1)S(1)} %collective-permute-done.3.refs_0_), channel_id=1, source_target_pairs={{0,1},{1,0},{2,3},{3,2},{4,5},{5,4},{6,7},{7,6},{8,9},{9,8},{10,11... | collective-permute-start | bytes 835592 | tf_op jit(solution)/shard_map/ppermute | solution.py:25
  19.5 3.3 %slice-start = ((s8[6291456]{0:T(1024)(128)(4,1)}), s8[4194304]{0:T(1024)(128)(4,1)S(1)}, s32[]{:S(2)}) async-start(s8[6291456]{0:T(1024)(128)(4,1)} %bitcast.6), calls=%async_computation.2 | async-start | bytes 8388608
  19.6 3.3 %slice-start.1 = ((s8[6291456]{0:T(1024)(128)(4,1)}), s8[2097152]{0:T(1024)(128)(4,1)S(1)}, s32[]{:S(2)}) async-start(s8[6291456]{0:T(1024)(128)(4,1)} %bitcast.6), calls=%async_computation.3 | async-start | bytes 4194304
  19.6 3.3 %copy-start.4 = (f32[512]{0:T(512)S(1)}, f32[512]{0:T(512)}, u32[]{:S(2)}) copy-start(f32[512]{0:T(512)} %param.11) | copy-start | bytes 6148
  21.5 5.5 %collective-permute-start.5 = (f32[1,2048]{1,0:T(1,128)S(1)}, f32[1,2048]{1,0:T(1,128)S(1)}, u32[]{:S(2)}, u32[]{:S(2)}) collective-permute-start(f32[1,2048]{1,0:T(1,128)S(1)} %get-tuple-element.35), channel_id=1, source_target_pairs={{4,0},{8,4},{12,8},{16,12},{20,16},{24,20},{28,24},{5,1},{9,5},{13... | collective-permute-start | bytes 24584 | tf_op jit(solution)/shard_map/ppermute | solution.py:30
  22.9 2.0 %copy-start.3 = (f32[512]{0:T(512)S(1)}, f32[512]{0:T(512)}, u32[]{:S(2)}) copy-start(f32[512]{0:T(512)} %param.12) | copy-start | bytes 6148
  43.2 14.4 %collective-permute-start.8 = (bf16[512,512]{1,0:T(8,128)(2,1)S(1)}, bf16[512,512]{1,0:T(8,128)(2,1)S(1)}, u32[]{:S(2)}, u32[]{:S(2)}) collective-permute-start(bf16[512,512]{1,0:T(8,128)(2,1)S(1)} %get-tuple-element.43.refs_0_), channel_id=1, source_target_pairs={{0,1},{1,0},{2,3},{3,2},{4,5},{5,4},{6,7},{7,6},{8,9},{9,8},{10,11... | collective-permute-start | bytes 1572872 | tf_op jit(solution)/shard_map/ppermute | solution.py:25
  43.3 9.9 %collective-permute-start.6 = (bf16[288,512]{1,0:T(8,128)(2,1)S(1)}, bf16[288,512]{1,0:T(8,128)(2,1)S(1)}, u32[]{:S(2)}, u32[]{:S(2)}) collective-permute-start(bf16[288,512]{1,0:T(8,128)(2,1)S(1)} %get-tuple-element.42), channel_id=1, source_target_pairs={{0,2},{1,3},{2,0},{3,1},{4,6},{5,7},{6,4},{7,5},{8,10},{9,11},{10,... | collective-permute-start | bytes 884744 | tf_op jit(solution)/shard_map/ppermute | solution.py:25
  44.9 12.8 %collective-permute-start.9 = (bf16[224,512]{1,0:T(8,128)(2,1)S(1)}, bf16[224,512]{1,0:T(8,128)(2,1)S(1)}, u32[]{:S(2)}, u32[]{:S(2)}) collective-permute-start(bf16[224,512]{1,0:T(8,128)(2,1)S(1)} %get-tuple-element.47), channel_id=1, source_target_pairs={{0,2},{1,3},{2,0},{3,1},{4,6},{5,7},{6,4},{7,5},{8,10},{9,11},{10,... | collective-permute-start | bytes 688136 | tf_op jit(solution)/shard_map/ppermute | solution.py:25
  53.3 6.3 %collective-permute-start.7 = (bf16[288,512]{1,0:T(8,128)(2,1)S(1)}, bf16[288,512]{1,0:T(8,128)(2,1)S(1)}, u32[]{:S(2)}, u32[]{:S(2)}) collective-permute-start(bf16[288,512]{1,0:T(8,128)(2,1)S(1)} %collective-permute-done.6.refs_0_), channel_id=1, source_target_pairs={{0,1},{1,0},{2,3},{3,2},{4,5},{5,4},{6,7},{7,6},{8,9},{9,8},{10,11... | collective-permute-start | bytes 884744 | tf_op jit(solution)/shard_map/ppermute | solution.py:25
  57.6 4.3 %collective-permute-start.10 = (bf16[224,512]{1,0:T(8,128)(2,1)S(1)}, bf16[224,512]{1,0:T(8,128)(2,1)S(1)}, u32[]{:S(2)}, u32[]{:S(2)}) collective-permute-start(bf16[224,512]{1,0:T(8,128)(2,1)S(1)} %collective-permute-done.9.refs_0_), channel_id=1, source_target_pairs={{0,1},{1,0},{2,3},{3,2},{4,5},{5,4},{6,7},{7,6},{8,9},{9,8},{10,11... | collective-permute-start | bytes 688136 | tf_op jit(solution)/shard_map/ppermute | solution.py:25

commit v7 on v6

--- a/solution.py
+++ b/solution.py
@@ -9,7 +9,7 @@
 
 
 ITERS = 2
-SHARES = ((8, 8), (9, 7))
+SHARES = ((8, 8), (8, 8))
 CHUNKS = len(SHARES[0])
 GROUP = 8
 EXTRA = 16
@@ -59,9 +59,10 @@
     return pl.CostEstimate(flops=flops, bytes_accessed=moved, transcendentals=0)
 
 
-def merge_kernel(guess_ref, init_ref, opening_ref, whole_ref, *parts):
-    rows, width = guess_ref.shape
-    whole_ref[pl.ds(0, opening_ref.shape[0]), :] = opening_ref[...]
+def merge_kernel(rounded_ref, init_ref, whole_ref, *parts):
+    rows, width = rounded_ref.shape
+    opening = spans(0, rows)[0][1]
+    whole_ref[pl.ds(0, opening), :] = rounded_ref[pl.ds(0, opening), :]
     for (at, chunk), part in zip(spans(0, rows)[1:], parts):
         lead = part.shape[0] - chunk
         if lead:
@@ -69,10 +70,9 @@
             head = jnp.where(row == 0, jnp.broadcast_to(init_ref[...], (lead, width)), 0.0).astype(BF16)
             part[pl.ds(0, lead), :] = head
             whole_ref[pl.ds(at, lead), :] = head
-        for start in range(0, chunk, GROUP * 4):
-            block = guess_ref[pl.ds(at + start, GROUP * 4), :].astype(BF16)
-            part[pl.ds(lead + start, GROUP * 4), :] = block
-            whole_ref[pl.ds(at + lead + start, GROUP * 4), :] = block
+        block = rounded_ref[pl.ds(at, chunk), :]
+        part[pl.ds(lead, chunk), :] = block
+        whole_ref[pl.ds(at + lead, chunk), :] = block
 
 
 def prepare_kernel(ids_ref, guess_ref, table_ref, bias_ref, out_ref, line_ref):
@@ -307,7 +307,7 @@
         send_ref[:, pl.ds(2 * width // LANES, 1), :] = jnp.broadcast_to(sums[None], (copies, 1, LANES))
 
 
-def apply_kernel(step, count, *refs):
+def apply_kernel(step, *refs):
     final = step == ITERS - 1
     maps, refs = refs[: 2 * CHUNKS], refs[2 * CHUNKS :]
     begin_ref, all_ref, state_ref = refs[:3]
@@ -315,24 +315,15 @@
     rows, width = state_ref.shape
     lines = width // LANES
     place = lax.axis_index("tm")
-    hid = lax.axis_index("hid")
-    copies = all_ref.shape[0]
-    peers = copies // count if final else copies
+    peers = all_ref.shape[0]
 
     def compose(peer, enter):
-        slot = peer * count + hid if final else peer
-        moved = all_ref[slot, pl.ds(0, lines), :] * enter + all_ref[slot, pl.ds(lines, lines), :]
+        moved = all_ref[peer, pl.ds(0, lines), :] * enter + all_ref[peer, pl.ds(lines, lines), :]
         return jnp.where(peer < place, moved, enter)
 
     begin = jnp.concatenate([begin_ref[3:4, pl.ds(at * LANES, LANES)] for at in range(lines)], axis=0)
     found = lax.fori_loop(0, peers, compose, begin, unroll=min(peers, 8))
     enter = jnp.concatenate([found[at : at + 1] for at in range(lines)], axis=1)
-    if final:
-        total = jnp.sum(all_ref[:, pl.ds(2 * lines, 1), :], axis=0)
-        lane = lax.broadcasted_iota(jnp.int32, (1, LANES), 1)
-        size = copies * rows * width
-        for half in range(2):
-            outs[0][half] = jnp.sqrt(jnp.sum(jnp.where(lane // (LANES // 2) == half, total, 0.0)) / size)
     height = 2 * GROUP
     row = lax.broadcasted_iota(jnp.int32, (height, width), 0)
     enter = jnp.broadcast_to(enter, (height, width))
@@ -363,6 +354,18 @@
         outs[0][...] = before[0:1]
 
 
+def sums_kernel(all_ref, out_ref):
+    out_ref[...] = jnp.sum(all_ref[:, pl.ds(all_ref.shape[1] - 1, 1), :], axis=0)
+
+
+def norm_kernel(size, *refs):
+    *parts, out_ref = refs
+    total = sum(part[...] for part in parts)
+    lane = lax.broadcasted_iota(jnp.int32, (1, LANES), 1)
+    for half in range(ITERS):
+        out_ref[half] = jnp.sqrt(jnp.sum(jnp.where(lane // (LANES // 2) == half, total, 0.0)) / size)
+
+
 def newton(token_ids, input_table, recur_weight, z_bias, hn_bias, init_state, guess):
     rows, width = guess.shape
     full = recur_weight.shape[0]
@@ -373,7 +376,8 @@
     lines = width // LANES
 
     first = spans(0, rows)[0][1]
-    opening, rest = lax.optimization_barrier((guess[:first].astype(BF16), guess))
+    rounded, rest = lax.optimization_barrier((guess.astype(BF16), guess))
+    opening = rounded[:first]
     whole, *moved = pl.pallas_call(
         merge_kernel,
         out_shape=[jax.ShapeDtypeStruct((rows + EXTRA, width), BF16)]
@@ -381,12 +385,12 @@
             jax.ShapeDtypeStruct((height + EXTRA * (at + height == rows), width), BF16)
             for at, height in spans(0, rows)[1:]
         ],
-        in_specs=vmem(3),
+        in_specs=vmem(2),
         out_specs=vmem(CHUNKS),
         compiler_params=params(8),
         cost_estimate=cost(COVER, 8 * rows * width),
         name="merge",
-    )(rest, init_state[None], opening)
+    )(rounded, init_state[None])
     moved = [opening, *moved]
     inputs, line = pl.pallas_call(
         prepare_kernel,
@@ -445,7 +449,7 @@
             ]
             if diag is None:
                 outs.append(jax.ShapeDtypeStruct((3 * GROUP, width), F32))
-            copies = blocks_tm * count if final else blocks_tm
+            copies = blocks_tm
             if last:
                 outs.append(jax.ShapeDtypeStruct((copies, 2 * lines + final, LANES), F32))
             found = pl.pallas_call(
@@ -461,26 +465,42 @@
             maps += found[:2]
             ends = found[2]
             diag = found[3] if diag is None else diag
-        every = lax.all_to_all(found[-1], ("tm", "hid") if final else "tm", 0, 0)
+        every = lax.all_to_all(found[-1], "tm", 0, 0)
         outs = [jax.ShapeDtypeStruct((rows, width), F32)]
         if final:
-            outs.append(jax.ShapeDtypeStruct((ITERS,), F32))
-            specs = vmem(1) + smem()
+            part = pl.pallas_call(
+                sums_kernel,
+                out_shape=jax.ShapeDtypeStruct((1, LANES), F32),
+                in_specs=vmem(1),
+                out_specs=vmem(1)[0],
+                compiler_params=params(8),
+                name="sums",
+            )(every)
+            parts = [part]
+            for offset in range(1, count):
+                parts.append(swapped(part, "hid", offset))
         else:
             outs.append(jax.ShapeDtypeStruct((1, width), F32))
             outs.append(jax.ShapeDtypeStruct((rows, width), BF16))
             outs += [jax.ShapeDtypeStruct((chunk, width), BF16) for _, chunk in spans(step + 1, rows)]
-            specs = vmem(len(outs))
         result = pl.pallas_call(
-            functools.partial(apply_kernel, step, count),
+            functools.partial(apply_kernel, step),
             out_shape=outs,
             in_specs=vmem(2 * CHUNKS + 2),
-            out_specs=specs,
+            out_specs=vmem(len(outs)),
             compiler_params=params(16),
             cost_estimate=cost(2 * rows * width, 16 * rows * width),
         )(*maps, ends, every)
         if final:
-            return (result[0], result[1])
+            residual_norm = pl.pallas_call(
+                functools.partial(norm_kernel, blocks_tm * count * rows * width),
+                out_shape=jax.ShapeDtypeStruct((ITERS,), F32),
+                in_specs=vmem(count),
+                out_specs=smem()[0],
+                compiler_params=params(8),
+                name="norm",
+            )(*parts)
+            return (result[0], residual_norm)
         state, following, whole, *moved = result
 
 

time: 78.3 us -> 78 us (level)
  blocking collectives: 26.1 us -> 23 us
  local copies, waits for them, and re-layouts: 3.01 us -> 0.73 us
  starting transfers between devices: 7.11 us -> 9.09 us
  waiting for transfers between devices: 24.5 us -> 25.9 us
  other arithmetic: 0.01 us -> 1.29 us
    all_to_all x2, blocking collectives: 26.1 us -> 23 us  [newton(): every = lax.all_to_all(found[-1], 'tm', 0, 0)]
    ppermute x10 -> x13, starting transfers between devices: 5.82 us -> 7.8 us  [swapped(): return lax.ppermute(block, axis, route)]
    ppermute x10 -> x13, waiting for transfers between devices: 24.4 us -> 25.8 us  [swapped(): return lax.ppermute(block, axis, route)]
    convert_element_type x0 -> x1, other arithmetic: none -> 1.29 us  [newton(): rounded, rest = lax.optimization_barrier((guess.astype(BF16), guess))]
    unnamed x20 -> x18, local copies, waits for them, and re-layouts: 1.94 us -> 0.71 us
    slice x1, local copies, waits for them, and re-layouts: 1.08 us -> 0.02 us  [newton(): opening = rounded[:first]]
    pallas_call x2 -> x4, Pallas kernels: 1.8 us -> 2.31 us  [the longest x2 1.57 us: newton(): pl.pallas_call(functools.partial(apply_kernel, step), out_shape=outs, in_...]
  transfers between devices with their start and end apart: 11 -> 14, of which waited for: 4 -> 6; matrix products, arithmetic and copies ran while one was open for 0% -> 0% of each run, Pallas kernels for 13% -> 15%
where the time goes in v7:
time: 78 us; the launch traced here: 77.8 us
  waiting for transfers between devices  25.9 us (33%)
  blocking collectives  23 us (29%)
  Pallas kernels  16.8 us (22%)
  starting transfers between devices  9.09 us (12%)
  other arithmetic  1.29 us (2%)
  between operations  1.01 us (1%)
    ppermute x13, waiting for transfers between devices, swapped(): return lax.ppermute(block, axis, route)  25.8 us
    all_to_all x2, blocking collectives, newton(): every = lax.all_to_all(found[-1], 'tm', 0, 0)  23 us
    pallas_call x4, Pallas kernels, newton(): pl.pallas_call(functools.partial(step_kernel, count, index, start, chunk,...  8.57 us
    ppermute x13, starting transfers between devices, swapped(): return lax.ppermute(block, axis, route)  7.8 us
    pallas_call x2, Pallas kernels, newton(): pl.pallas_call(functools.partial(base_kernel, step, count), out_shape=jax...  3.91 us
    pallas_call x1, Pallas kernels, newton(): pl.pallas_call(prepare_kernel, out_shape=[jax.ShapeDtypeStruct((3, rows +...  1.95 us
    pallas_call x2, Pallas kernels, newton(): pl.pallas_call(functools.partial(apply_kernel, step), out_shape=outs, in_...  1.57 us
  transfers between devices with their start and end apart: 14, of which 6 were waited for; matrix products, arithmetic and copies ran while one was open for 0% of the time, Pallas kernels for 15%

profile of v7, /device:TPU:0, one launch (start us, length us, event | category | flops | bytes accessed | tf_op | source)
XLA Modules:
  0.0 77.8 jit_solution(8510301474505034953)
XLA Ops:
  0.6 1.3 %convert_element_type.3.rounded_ref = bf16[512,512]{1,0:T(8,128)(2,1)S(1)} convert(f32[512,512]{1,0:T(8,128)} %refs_5_.1) | non-fusion elementwise | flops 262144 | bytes 1572864 | tf_op jit(solution)/shard_map/convert_element_type | solution.py:379
  1.9 0.7 copy-done.1
  2.7 3.1 %collective-permute-start.3 = (bf16[272,512]{1,0:T(8,128)(2,1)S(1)}, bf16[272,512]{1,0:T(8,128)(2,1)S(1)}, u32[]{:S(2)}, u32[]{:S(2)}) collective-permute-start(bf16[272,512]{1,0:T(8,128)(2,1)S(1)} %get-tuple-element.34), channel_id=1, source_target_pairs={{0,2},{1,3},{2,0},{3,1},{4,6},{5,7},{6,4},{7,5},{8,10},{9,11},{10,... | collective-permute-start | bytes 835592 | tf_op jit(solution)/shard_map/ppermute | solution.py:25
  5.9 12.1 %collective-permute-done.refs_0_ = bf16[256,512]{1,0:T(8,128)(2,1)S(1)} collective-permute-done((bf16[256,512]{1,0:T(8,128)(2,1)S(1)}, bf16[256,512]{1,0:T(8,128)(2,1)S(1)}, u32[]{:S(2)}, u32[]{:S(2)}) %collective-permute-start) | collective-permute-done | bytes 262176 | tf_op jit(solution)/shard_map/ppermute | solution.py:25
  18.0 0.5 collective-permute-start.4
  18.6 1.9 %prepare.1 = (f32[3,520,512]{2,1,0:T(8,128)S(1)}, f32[1,2048]{1,0:T(1,128)S(1)}) custom-call(s32[1,512]{1,0:T(1,128)S(1)} %bitcast.22, f32[512,512]{1,0:T(8,128)S(1)} %copy-done, f32[3,256,512]{2,1,0:T(8,128)S(1)} %bitcast.21, f32[1,512]{1,0:T(1,128)S(1)} %bitcast.23), custom_call_target="tpu_custom_call" | custom-call | flops 4000000000 | bytes 2097152 | tf_op jit(solution)/shard_map/prepare/pallas_call | solution.py:395
  20.5 1.3 %collective-permute-start.5 = (f32[1,2048]{1,0:T(1,128)S(1)}, f32[1,2048]{1,0:T(1,128)S(1)}, u32[]{:S(2)}, u32[]{:S(2)}) collective-permute-start(f32[1,2048]{1,0:T(1,128)S(1)} %get-tuple-element.35), channel_id=1, source_target_pairs={{4,0},{8,4},{12,8},{16,12},{20,16},{24,20},{28,24},{5,1},{9,5},{13... | collective-permute-start | bytes 24584 | tf_op jit(solution)/shard_map/ppermute | solution.py:30
  21.9 2.0 %shard_map.86.refs_3_ = f32[3,528,512]{2,1,0:T(8,128)S(1)} custom-call(bf16[528,512]{1,0:T(8,128)(2,1)S(1)} %get-tuple-element.29.refs_0_, bf16[528,512]{1,0:T(8,128)(2,1)S(1)} %collective-permute-done.2.refs_1_, bf16[3,2048,512]{2,1,0:T(8,128)(2,1)S(1)} %bitcast.8, f32[3,520,512]{2,1,0:T(8,128)S(1)} %get-tuple-element.31.refs_3_.refs_4_, f32[1,512]{1,0:T(1,128)S(1)} %bitcast.19), custom_call_target="tpu_custom_call" | custom-call | flops 1660944384 | bytes 3145728 | tf_op jit(solution)/shard_map/pallas_call | solution.py:426
  23.9 2.1 %shard_map.87 = (f32[256,512]{1,0:T(8,128)S(1)}, f32[256,512]{1,0:T(8,128)S(1)}, f32[5,512]{1,0:T(8,128)S(1)}, f32[24,512]{1,0:T(8,128)S(1)}) custom-call(bf16[256,512]{1,0:T(8,128)(2,1)S(1)} %collective-permute-done.refs_0_, bf16[256,512]{1,0:T(8,128)(2,1)S(1)} %collective-permute-done.1.refs_1_, bf16[3,2048,512]{2,1,0:T(8,128)(2,1)S(1)} %bitcast.9, ...), custom_call_target="tpu_custom_call" | custom-call | flops 805306368 | bytes 3145728 | tf_op jit(solution)/shard_map/pallas_call | solution.py:455
  26.1 2.2 %shard_map.88 = (f32[256,512]{1,0:T(8,128)S(1)}, f32[256,512]{1,0:T(8,128)S(1)}, f32[5,512]{1,0:T(8,128)S(1)}, f32[8,8,128]{2,1,0:T(8,128)S(1)}) custom-call(bf16[272,512]{1,0:T(8,128)(2,1)S(1)} %collective-permute-done.3.refs_0_, bf16[272,512]{1,0:T(8,128)(2,1)S(1)} %collective-permute-done.4.refs_1_, bf16[3,2048,512]{2,1,0:T(8,128)(2,1)S(1)} %bitcast.10, ...), custom_call_target="tpu_custom_call" | custom-call | flops 855638016 | bytes 3145728 | tf_op jit(solution)/shard_map/pallas_call | solution.py:455
  28.3 13.6 %all_to_all.10.refs_5_ = f32[8,8,128]{2,1,0:T(8,128)S(1)} all-to-all(f32[8,8,128]{2,1,0:T(8,128)S(1)} %get-tuple-element.41), channel_id=1, replica_groups=mesh['tm'=8,'hid'=4] {'tm'}, dimensions={0} | all-to-all | bytes 65536 | tf_op jit(solution)/shard_map/all_to_all | solution.py:468
  42.3 1.6 %collective-permute-start.6 = (bf16[256,512]{1,0:T(8,128)(2,1)S(1)}, bf16[256,512]{1,0:T(8,128)(2,1)S(1)}, u32[]{:S(2)}, u32[]{:S(2)}) collective-permute-start(bf16[256,512]{1,0:T(8,128)(2,1)S(1)} %get-tuple-element.42), channel_id=1, source_target_pairs={{0,2},{1,3},{2,0},{3,1},{4,6},{5,7},{6,4},{7,5},{8,10},{9,11},{10,... | collective-permute-start | bytes 786440 | tf_op jit(solution)/shard_map/ppermute | solution.py:25
  43.9 0.5 collective-permute-start.9
  44.4 7.2 %collective-permute-done.6.refs_0_ = bf16[256,512]{1,0:T(8,128)(2,1)S(1)} collective-permute-done((bf16[256,512]{1,0:T(8,128)(2,1)S(1)}, bf16[256,512]{1,0:T(8,128)(2,1)S(1)}, u32[]{:S(2)}, u32[]{:S(2)}) %collective-permute-start.6) | collective-permute-done | bytes 262176 | tf_op jit(solution)/shard_map/ppermute | solution.py:25
  51.6 5.1 %collective-permute-done.9.refs_0_ = bf16[256,512]{1,0:T(8,128)(2,1)S(1)} collective-permute-done((bf16[256,512]{1,0:T(8,128)(2,1)S(1)}, bf16[256,512]{1,0:T(8,128)(2,1)S(1)}, u32[]{:S(2)}, u32[]{:S(2)}) %collective-permute-start.9) | collective-permute-done | bytes 262176 | tf_op jit(solution)/shard_map/ppermute | solution.py:25
  56.6 1.9 %shard_map.90.refs_3_ = f32[3,512,512]{2,1,0:T(8,128)S(1)} custom-call(bf16[512,512]{1,0:T(8,128)(2,1)S(1)} %get-tuple-element.43.refs_0_, bf16[512,512]{1,0:T(8,128)(2,1)S(1)} %collective-permute-done.8.refs_1_, bf16[3,2048,512]{2,1,0:T(8,128)(2,1)S(1)} %bitcast.11, f32[3,520,512]{2,1,0:T(8,128)S(1)} %get-tuple-element.31.refs_3_.refs_4_, f32[1,512]{1,0:T(1,128)S(1)} %bitcast.20), custom_call_target="tpu_custom_call" | custom-call | flops 1610612736 | bytes 3145728 | tf_op jit(solution)/shard_map/pallas_call | solution.py:426
  58.6 2.1 %shard_map.91 = (f32[256,512]{1,0:T(8,128)S(1)}, f32[256,512]{1,0:T(8,128)S(1)}, f32[5,512]{1,0:T(8,128)S(1)}) custom-call(bf16[256,512]{1,0:T(8,128)(2,1)S(1)} %collective-permute-done.6.refs_0_, bf16[256,512]{1,0:T(8,128)(2,1)S(1)} %collective-permute-done.7.refs_1_, bf16[3,2048,512]{2,1,0:T(8,128)(2,1)S(1)} %bitcast.12, ...), custom_call_target="tpu_custom_call" | custom-call | flops 805306368 | bytes 3145728 | tf_op jit(solution)/shard_map/pallas_call | solution.py:455
  60.7 2.2 %shard_map.92 = (f32[256,512]{1,0:T(8,128)S(1)}, f32[256,512]{1,0:T(8,128)S(1)}, f32[5,512]{1,0:T(8,128)S(1)}, f32[8,9,128]{2,1,0:T(8,128)S(1)}) custom-call(bf16[256,512]{1,0:T(8,128)(2,1)S(1)} %collective-permute-done.9.refs_0_, bf16[256,512]{1,0:T(8,128)(2,1)S(1)} %collective-permute-done.10.refs_1_, bf16[3,2048,512]{2,1,0:T(8,128)(2,1)S(1)} %bitcast.13, ...), custom_call_target="tpu_custom_call" | custom-call | flops 805306368 | bytes 3145728 | tf_op jit(solution)/shard_map/pallas_call | solution.py:455
  62.9 9.3 %all_to_all.11.refs_5_.all_ref = f32[8,9,128]{2,1,0:T(8,128)S(1)} all-to-all(f32[8,9,128]{2,1,0:T(8,128)S(1)} %get-tuple-element.53), channel_id=1, replica_groups=mesh['tm'=8,'hid'=4] {'tm'}, dimensions={0} | all-to-all | bytes 73728 | tf_op jit(solution)/shard_map/all_to_all | solution.py:468
  72.3 1.6 %collective-permute-start.12 = (f32[1,128]{1,0:T(1,128)S(1)}, f32[1,128]{1,0:T(1,128)S(1)}, u32[]{:S(2)}, u32[]{:S(2)}) collective-permute-start(f32[1,128]{1,0:T(1,128)S(1)} %sums.1.refs_0_), channel_id=1, source_target_pairs={{0,2},{1,3},{2,0},{3,1},{4,6},{5,7},{6,4},{7,5},{8,10},{9,11},{10,... | collective-permute-start | bytes 1544 | tf_op jit(solution)/shard_map/ppermute | solution.py:25
  74.2 1.2 %shard_map.93 = f32[512,512]{1,0:T(8,128)} custom-call(f32[256,512]{1,0:T(8,128)S(1)} %get-tuple-element.45.refs_0_, f32[256,512]{1,0:T(8,128)S(1)} %get-tuple-element.46.refs_1_, f32[256,512]{1,0:T(8,128)S(1)} %get-tuple-element.50.refs_2_, f32[256,512]{1,0:T(8,128)S(1)} %get-tuple-element.51.refs_3_, f32[5,512]{1,0:T(8,128)S(1)} %get-tuple-element.52.refs_4_, ...), custom_call_target="tpu_custom_call" | custom-call | flops 524288 | bytes 4194304 | tf_op jit(solution)/shard_map/pallas_call | solution.py:486
  75.4 0.5 collective-permute-done.12.refs_2_
  75.9 0.9 %collective-permute-done.13.refs_3_ = f32[1,128]{1,0:T(1,128)S(1)} collective-permute-done((f32[1,128]{1,0:T(1,128)S(1)}, f32[1,128]{1,0:T(1,128)S(1)}, u32[]{:S(2)}, u32[]{:S(2)}) %collective-permute-start.13) | collective-permute-done | bytes 544 | tf_op jit(solution)/shard_map/ppermute | solution.py:25
  76.9 0.7 norm.1
  (39 shorter events, 1.1 us)
Async XLA Ops:
  1.9 0.7 copy-start.1
  2.6 15.9 %copy-start = (f32[512,512]{1,0:T(8,128)S(1)}, f32[512,512]{1,0:T(8,128)}, u32[]{:S(2)}) copy-start(f32[512,512]{1,0:T(8,128)} %refs_5_.1) | copy-start | bytes 3145732
  2.6 15.9 %copy-start.4 = (f32[256,3,512]{2,0,1:T(8,128)S(1)}, f32[256,3,512]{2,0,1:T(8,128)}, u32[]{:S(2)}) copy-start(f32[256,3,512]{2,0,1:T(8,128)} %param.8) | copy-start | bytes 4718596
  2.6 15.9 %copy-start.5 = (s32[512]{0:T(512)S(1)}, s32[512]{0:T(512)}, u32[]{:S(2)}) copy-start(s32[512]{0:T(512)} %param.7) | copy-start | bytes 6148
  2.6 15.9 %copy-start.6 = (f32[512]{0:T(512)S(1)}, f32[512]{0:T(512)}, u32[]{:S(2)}) copy-start(f32[512]{0:T(512)} %param.10) | copy-start | bytes 6148
  2.7 15.3 %collective-permute-start.3 = (bf16[272,512]{1,0:T(8,128)(2,1)S(1)}, bf16[272,512]{1,0:T(8,128)(2,1)S(1)}, u32[]{:S(2)}, u32[]{:S(2)}) collective-permute-start(bf16[272,512]{1,0:T(8,128)(2,1)S(1)} %get-tuple-element.34), channel_id=1, source_target_pairs={{0,2},{1,3},{2,0},{3,1},{4,6},{5,7},{6,4},{7,5},{8,10},{9,11},{10,... | collective-permute-start | bytes 835592 | tf_op jit(solution)/shard_map/ppermute | solution.py:25
  5.8 12.3 %collective-permute-start = (bf16[256,512]{1,0:T(8,128)(2,1)S(1)}, bf16[256,512]{1,0:T(8,128)(2,1)S(1)}, u32[]{:S(2)}, u32[]{:S(2)}) collective-permute-start(bf16[256,512]{1,0:T(8,128)(2,1)S(1)} %slice.3), channel_id=1, source_target_pairs={{0,2},{1,3},{2,0},{3,1},{4,6},{5,7},{6,4},{7,5},{8,10},{9,11},{10,... | collective-permute-start | bytes 786440 | tf_op jit(solution)/shard_map/ppermute | solution.py:25
  5.9 16.0 %collective-permute-start.2 = (bf16[528,512]{1,0:T(8,128)(2,1)S(1)}, bf16[528,512]{1,0:T(8,128)(2,1)S(1)}, u32[]{:S(2)}, u32[]{:S(2)}) collective-permute-start(bf16[528,512]{1,0:T(8,128)(2,1)S(1)} %get-tuple-element.29.refs_0_), channel_id=1, source_target_pairs={{0,1},{1,0},{2,3},{3,2},{4,5},{5,4},{6,7},{7,6},{8,9},{9,8},{10,11... | collective-permute-start | bytes 1622024 | tf_op jit(solution)/shard_map/ppermute | solution.py:25
  18.0 5.9 %collective-permute-start.1 = (bf16[256,512]{1,0:T(8,128)(2,1)S(1)}, bf16[256,512]{1,0:T(8,128)(2,1)S(1)}, u32[]{:S(2)}, u32[]{:S(2)}) collective-permute-start(bf16[256,512]{1,0:T(8,128)(2,1)S(1)} %collective-permute-done.refs_0_), channel_id=1, source_target_pairs={{0,1},{1,0},{2,3},{3,2},{4,5},{5,4},{6,7},{7,6},{8,9},{9,8},{10,11... | collective-permute-start | bytes 786440 | tf_op jit(solution)/shard_map/ppermute | solution.py:25
  18.0 8.1 %collective-permute-start.4 = (bf16[272,512]{1,0:T(8,128)(2,1)S(1)}, bf16[272,512]{1,0:T(8,128)(2,1)S(1)}, u32[]{:S(2)}, u32[]{:S(2)}) collective-permute-start(bf16[272,512]{1,0:T(8,128)(2,1)S(1)} %collective-permute-done.3.refs_0_), channel_id=1, source_target_pairs={{0,1},{1,0},{2,3},{3,2},{4,5},{5,4},{6,7},{7,6},{8,9},{9,8},{10,11... | collective-permute-start | bytes 835592 | tf_op jit(solution)/shard_map/ppermute | solution.py:25
  18.5 3.3 %slice-start = ((s8[6291456]{0:T(1024)(128)(4,1)}), s8[4194304]{0:T(1024)(128)(4,1)S(1)}, s32[]{:S(2)}) async-start(s8[6291456]{0:T(1024)(128)(4,1)} %bitcast.6), calls=%async_computation.2 | async-start | bytes 8388608
  18.6 3.3 %slice-start.1 = ((s8[6291456]{0:T(1024)(128)(4,1)}), s8[2097152]{0:T(1024)(128)(4,1)S(1)}, s32[]{:S(2)}) async-start(s8[6291456]{0:T(1024)(128)(4,1)} %bitcast.6), calls=%async_computation.3 | async-start | bytes 4194304
  18.6 3.3 %copy-start.3 = (f32[512]{0:T(512)S(1)}, f32[512]{0:T(512)}, u32[]{:S(2)}) copy-start(f32[512]{0:T(512)} %param.11) | copy-start | bytes 6148
  20.5 5.5 %collective-permute-start.5 = (f32[1,2048]{1,0:T(1,128)S(1)}, f32[1,2048]{1,0:T(1,128)S(1)}, u32[]{:S(2)}, u32[]{:S(2)}) collective-permute-start(f32[1,2048]{1,0:T(1,128)S(1)} %get-tuple-element.35), channel_id=1, source_target_pairs={{4,0},{8,4},{12,8},{16,12},{20,16},{24,20},{28,24},{5,1},{9,5},{13... | collective-permute-start | bytes 24584 | tf_op jit(solution)/shard_map/ppermute | solution.py:30
  21.9 2.0 %copy-start.2 = (f32[512]{0:T(512)S(1)}, f32[512]{0:T(512)}, u32[]{:S(2)}) copy-start(f32[512]{0:T(512)} %param.12) | copy-start | bytes 6148
  42.2 14.4 %collective-permute-start.8 = (bf16[512,512]{1,0:T(8,128)(2,1)S(1)}, bf16[512,512]{1,0:T(8,128)(2,1)S(1)}, u32[]{:S(2)}, u32[]{:S(2)}) collective-permute-start(bf16[512,512]{1,0:T(8,128)(2,1)S(1)} %get-tuple-element.43.refs_0_), channel_id=1, source_target_pairs={{0,1},{1,0},{2,3},{3,2},{4,5},{5,4},{6,7},{7,6},{8,9},{9,8},{10,11... | collective-permute-start | bytes 1572872 | tf_op jit(solution)/shard_map/ppermute | solution.py:25
  42.3 9.2 %collective-permute-start.6 = (bf16[256,512]{1,0:T(8,128)(2,1)S(1)}, bf16[256,512]{1,0:T(8,128)(2,1)S(1)}, u32[]{:S(2)}, u32[]{:S(2)}) collective-permute-start(bf16[256,512]{1,0:T(8,128)(2,1)S(1)} %get-tuple-element.42), channel_id=1, source_target_pairs={{0,2},{1,3},{2,0},{3,1},{4,6},{5,7},{6,4},{7,5},{8,10},{9,11},{10,... | collective-permute-start | bytes 786440 | tf_op jit(solution)/shard_map/ppermute | solution.py:25
  43.9 12.7 %collective-permute-start.9 = (bf16[256,512]{1,0:T(8,128)(2,1)S(1)}, bf16[256,512]{1,0:T(8,128)(2,1)S(1)}, u32[]{:S(2)}, u32[]{:S(2)}) collective-permute-start(bf16[256,512]{1,0:T(8,128)(2,1)S(1)} %get-tuple-element.47), channel_id=1, source_target_pairs={{0,2},{1,3},{2,0},{3,1},{4,6},{5,7},{6,4},{7,5},{8,10},{9,11},{10,... | collective-permute-start | bytes 786440 | tf_op jit(solution)/shard_map/ppermute | solution.py:25
  51.6 7.0 %collective-permute-start.7 = (bf16[256,512]{1,0:T(8,128)(2,1)S(1)}, bf16[256,512]{1,0:T(8,128)(2,1)S(1)}, u32[]{:S(2)}, u32[]{:S(2)}) collective-permute-start(bf16[256,512]{1,0:T(8,128)(2,1)S(1)} %collective-permute-done.6.refs_0_), channel_id=1, source_target_pairs={{0,1},{1,0},{2,3},{3,2},{4,5},{5,4},{6,7},{7,6},{8,9},{9,8},{10,11... | collective-permute-start | bytes 786440 | tf_op jit(solution)/shard_map/ppermute | solution.py:25
  56.6 4.0 %collective-permute-start.10 = (bf16[256,512]{1,0:T(8,128)(2,1)S(1)}, bf16[256,512]{1,0:T(8,128)(2,1)S(1)}, u32[]{:S(2)}, u32[]{:S(2)}) collective-permute-start(bf16[256,512]{1,0:T(8,128)(2,1)S(1)} %collective-permute-done.9.refs_0_), channel_id=1, source_target_pairs={{0,1},{1,0},{2,3},{3,2},{4,5},{5,4},{6,7},{7,6},{8,9},{9,8},{10,11... | collective-permute-start | bytes 786440 | tf_op jit(solution)/shard_map/ppermute | solution.py:25
  72.2 3.2 %collective-permute-start.11 = (f32[1,128]{1,0:T(1,128)S(1)}, f32[1,128]{1,0:T(1,128)S(1)}, u32[]{:S(2)}, u32[]{:S(2)}) collective-permute-start(f32[1,128]{1,0:T(1,128)S(1)} %sums.1.refs_0_), channel_id=1, source_target_pairs={{0,1},{1,0},{2,3},{3,2},{4,5},{5,4},{6,7},{7,6},{8,9},{9,8},{10,11... | collective-permute-start | bytes 1544 | tf_op jit(solution)/shard_map/ppermute | solution.py:25
  72.3 3.6 %collective-permute-start.12 = (f32[1,128]{1,0:T(1,128)S(1)}, f32[1,128]{1,0:T(1,128)S(1)}, u32[]{:S(2)}, u32[]{:S(2)}) collective-permute-start(f32[1,128]{1,0:T(1,128)S(1)} %sums.1.refs_0_), channel_id=1, source_target_pairs={{0,2},{1,3},{2,0},{3,1},{4,6},{5,7},{6,4},{7,5},{8,10},{9,11},{10,... | collective-permute-start | bytes 1544 | tf_op jit(solution)/shard_map/ppermute | solution.py:25
  73.9 3.0 %collective-permute-start.13 = (f32[1,128]{1,0:T(1,128)S(1)}, f32[1,128]{1,0:T(1,128)S(1)}, u32[]{:S(2)}, u32[]{:S(2)}) collective-permute-start(f32[1,128]{1,0:T(1,128)S(1)} %sums.1.refs_0_), channel_id=1, source_target_pairs={{0,3},{1,2},{2,1},{3,0},{4,7},{5,6},{6,5},{7,4},{8,11},{9,10},{10,... | collective-permute-start | bytes 1544 | tf_op jit(solution)/shard_map/ppermute | solution.py:25

commit v8 on v7

--- a/solution.py
+++ b/solution.py
@@ -9,10 +9,11 @@
 
 
 ITERS = 2
-SHARES = ((8, 8), (8, 8))
+SHARES = ((10, 6), (10, 6))
 CHUNKS = len(SHARES[0])
 GROUP = 8
-EXTRA = 16
+EXTRA = 8
+SPLIT = ((1, 1), (1, 1))
 TILE = 256
 LANES = 128
 COVER = 2_000_000_000
@@ -32,6 +33,10 @@
 
 def sigmoid(x):
     return 0.5 * jnp.tanh(0.5 * x) + 0.5
+
+
+def splits(step, index, count):
+    return SPLIT[step][index] if count == 4 else 0
 
 
 def spans(step, rows):
@@ -170,9 +175,20 @@
                     )
 
 
+def direct_kernel(start, count, far_ref, weight_ref, base_ref, out_ref):
+    height, width = far_ref.shape
+    first = (lax.axis_index("hid") ^ (count // 2)) * width
+    for tile in range(width // TILE):
+        lanes = pl.ds(tile * TILE, TILE)
+        for gate in range(3):
+            found = tile_dot(far_ref, weight_ref, first, gate, lanes)
+            out_ref[gate, :, lanes] = base_ref[gate, pl.ds(start, height), lanes] + found
+
+
 def step_kernel(count, index, start, chunk, step, copies, *refs):
     refs = list(refs)
-    far = [refs.pop(0) for _ in range(count // 2)]
+    split = splits(step, index, count)
+    far = [refs.pop(0) for _ in range(split, count // 2)]
     weight_ref, base_ref, inputs_ref, state_ref, init_ref = [refs.pop(0) for _ in range(5)]
     last = index == CHUNKS - 1
     next_ref, edge_ref = [refs.pop(0) for _ in range(2)] if last else (None, None)
@@ -184,7 +200,7 @@
     begins = last and step == 0
     send_ref = refs.pop(0) if last else None
     lhs, *products = refs
-    height = lhs.shape[0]
+    height = products[0].shape[1]
     rows, width = state_ref.shape
     lead = height - chunk
     hid = lax.axis_index("hid")
@@ -196,9 +212,15 @@
     if opens:
         diagonals(weight_ref, hid, diag_ref)
     own = hid % (count // 2)
-    for offset in range(count // 2):
-        lhs[:, pl.ds(pl.multiple_of((own ^ offset) * width, width), width)] = far[offset][...]
-    first = ((hid - own) ^ (count // 2)) * width
+    if split:
+        lhs = far[0]
+        first = (hid ^ (count // 2) ^ 1) * width
+        begin_row = 0
+    else:
+        for offset in range(count // 2):
+            lhs[:, pl.ds(pl.multiple_of((own ^ offset) * width, width), width)] = far[offset][...]
+        first = ((hid - own) ^ (count // 2)) * width
+        begin_row = start
     row = lax.broadcasted_iota(jnp.int32, (GROUP, TILE), 0)
     zeros = jnp.zeros((GROUP, TILE), F32)
 
@@ -230,7 +252,7 @@
             state = jnp.where(row == GROUP - 1, turned_next, turned)
             turned = turned_next
             place = lead + group * GROUP
-            bases = [base_ref[gate, pl.ds(start + place, GROUP), lanes] for gate in range(3)]
+            bases = [base_ref[gate, pl.ds(begin_row + place, GROUP), lanes] for gate in range(3)]
             inputs = inputs_ref[2, token, lanes]
             if last and group == groups - 1:
                 edges = [edge_ref[:, pl.ds((gate + 1) * width + tile * TILE, TILE)] for gate in range(3)]
@@ -261,7 +283,7 @@
             run_a, run_b = last_a * run_a, last_a * run_b + last_b
         if begins:
             begin = gates(
-                [base_ref[gate, pl.ds(start, GROUP), lanes] for gate in range(3)],
+                [base_ref[gate, pl.ds(begin_row, GROUP), lanes] for gate in range(3)],
                 [products[tile][gate, pl.ds(0, GROUP), :] for gate in range(3)],
                 inputs_ref[2, pl.ds(rows, GROUP), lanes],
                 jnp.broadcast_to(init_ref[:, lanes], (GROUP, TILE)),
@@ -436,8 +458,19 @@
         for index, (start, chunk) in enumerate(spans(step, rows)):
             last = index == CHUNKS - 1
             height = moved[index].shape[0]
-            operands = [far[index][offset] for offset in range(count // 2, count)]
-            operands += [weight, base, inputs, state, init_state[None]]
+            split = splits(step, index, count)
+            sums = base
+            if split:
+                sums = pl.pallas_call(
+                    functools.partial(direct_kernel, start, count),
+                    out_shape=jax.ShapeDtypeStruct((3, height, width), F32),
+                    in_specs=vmem(3),
+                    out_specs=vmem(1)[0],
+                    compiler_params=params(16),
+                    cost_estimate=cost(3 * height * full * width // 2, 3 * full * width),
+                )(far[index][count // 2], weight, base)
+            operands = [far[index][offset] for offset in range(count // 2 + split, count)]
+            operands += [weight, sums, inputs, state, init_state[None]]
             if last:
                 operands += [following, edge]
             if diag is not None:

time: 78 us -> 73.9 us (0.947)
  waiting for transfers between devices: 25.9 us -> 22.3 us
    ppermute x13, waiting for transfers between devices: 25.8 us -> 22.3 us  [swapped(): return lax.ppermute(block, axis, route)]
    pallas_call x0 -> x4, Pallas kernels: none -> 2.44 us  [newton(): pl.pallas_call(functools.partial(direct_kernel, start, count), out_shape=...]
    pallas_call x4, Pallas kernels: 8.57 us -> 6.38 us  [newton(): pl.pallas_call(functools.partial(step_kernel, count, index, start, chunk,...]
  transfers between devices with their start and end apart: 14 -> 14, of which waited for: 6 -> 6; matrix products, arithmetic and copies ran while one was open for 0% -> 0% of each run, Pallas kernels for 15% -> 18%
where the time goes in v8:
time: 73.9 us; the launch traced here: 73.6 us
  blocking collectives  23 us (31%)
  waiting for transfers between devices  22.3 us (30%)
  Pallas kernels  17 us (23%)
  starting transfers between devices  8.95 us (12%)
  other arithmetic  1.3 us (2%)
  between operations  1.05 us (1%)
    all_to_all x2, blocking collectives, newton(): every = lax.all_to_all(found[-1], 'tm', 0, 0)  23 us
    ppermute x13, waiting for transfers between devices, swapped(): return lax.ppermute(block, axis, route)  22.3 us
    ppermute x13, starting transfers between devices, swapped(): return lax.ppermute(block, axis, route)  7.65 us
    pallas_call x4, Pallas kernels, newton(): pl.pallas_call(functools.partial(step_kernel, count, index, start, chunk,...  6.38 us
    pallas_call x2, Pallas kernels, newton(): pl.pallas_call(functools.partial(base_kernel, step, count), out_shape=jax...  3.89 us
    pallas_call x4, Pallas kernels, newton(): pl.pallas_call(functools.partial(direct_kernel, start, count), out_shape=...  2.44 us
    pallas_call x1, Pallas kernels, newton(): pl.pallas_call(prepare_kernel, out_shape=[jax.ShapeDtypeStruct((3, rows +...  1.93 us
    pallas_call x2, Pallas kernels, newton(): pl.pallas_call(functools.partial(apply_kernel, step), out_shape=outs, in_...  1.57 us
  transfers between devices with their start and end apart: 14, of which 6 were waited for; matrix products, arithmetic and copies ran while one was open for 0% of the time, Pallas kernels for 18%

profile of v8, /device:TPU:0, one launch (start us, length us, event | category | flops | bytes accessed | tf_op | source)
XLA Modules:
  0.0 73.6 jit_solution(2341730745239698467)
XLA Ops:
  0.6 1.3 %convert_element_type.3.rounded_ref = bf16[512,512]{1,0:T(8,128)(2,1)S(1)} convert(f32[512,512]{1,0:T(8,128)} %refs_4_.1) | non-fusion elementwise | flops 262144 | bytes 1572864 | tf_op jit(solution)/shard_map/convert_element_type | solution.py:401
  2.0 3.1 %collective-permute-start = (bf16[320,512]{1,0:T(8,128)(2,1)S(1)}, bf16[320,512]{1,0:T(8,128)(2,1)S(1)}, u32[]{:S(2)}, u32[]{:S(2)}) collective-permute-start(bf16[320,512]{1,0:T(8,128)(2,1)S(1)} %slice.3), channel_id=1, source_target_pairs={{0,2},{1,3},{2,0},{3,1},{4,6},{5,7},{6,4},{7,5},{8,10},{9,11},{10,... | collective-permute-start | bytes 983048 | tf_op jit(solution)/shard_map/ppermute | solution.py:26
  5.3 8.3 %collective-permute-done.far_ref = bf16[320,512]{1,0:T(8,128)(2,1)S(1)} collective-permute-done((bf16[320,512]{1,0:T(8,128)(2,1)S(1)}, bf16[320,512]{1,0:T(8,128)(2,1)S(1)}, u32[]{:S(2)}, u32[]{:S(2)}) %collective-permute-start) | collective-permute-done | bytes 327712 | tf_op jit(solution)/shard_map/ppermute | solution.py:26
  13.7 1.9 %prepare.1 = (f32[3,520,512]{2,1,0:T(8,128)S(1)}, f32[1,2048]{1,0:T(1,128)S(1)}) custom-call(s32[1,512]{1,0:T(1,128)S(1)} %bitcast.26, f32[512,512]{1,0:T(8,128)S(1)} %copy-done, f32[3,256,512]{2,1,0:T(8,128)S(1)} %bitcast.25, f32[1,512]{1,0:T(1,128)S(1)} %bitcast.27), custom_call_target="tpu_custom_call" | custom-call | flops 4000000000 | bytes 2097152 | tf_op jit(solution)/shard_map/prepare/pallas_call | solution.py:417
  15.6 1.3 %collective-permute-start.5 = (f32[1,2048]{1,0:T(1,128)S(1)}, f32[1,2048]{1,0:T(1,128)S(1)}, u32[]{:S(2)}, u32[]{:S(2)}) collective-permute-start(f32[1,2048]{1,0:T(1,128)S(1)} %get-tuple-element.35), channel_id=1, source_target_pairs={{4,0},{8,4},{12,8},{16,12},{20,16},{24,20},{28,24},{5,1},{9,5},{13... | collective-permute-start | bytes 24584 | tf_op jit(solution)/shard_map/ppermute | solution.py:31
  17.5 2.0 %shard_map.86.base_ref = f32[3,520,512]{2,1,0:T(8,128)S(1)} custom-call(bf16[520,512]{1,0:T(8,128)(2,1)S(1)} %get-tuple-element.29.refs_0_, bf16[520,512]{1,0:T(8,128)(2,1)S(1)} %collective-permute-done.2.refs_1_, bf16[3,2048,512]{2,1,0:T(8,128)(2,1)S(1)} %bitcast.8, f32[3,520,512]{2,1,0:T(8,128)S(1)} %get-tuple-element.31.refs_3_, f32[1,512]{1,0:T(1,128)S(1)} %bitcast.23), custom_call_target="tpu_custom_call" | custom-call | flops 1635778560 | bytes 3145728 | tf_op jit(solution)/shard_map/pallas_call | solution.py:448
  19.5 0.5 shard_map.89.refs_2_
  20.0 0.7 shard_map.87.refs_2_
  20.7 1.9 %shard_map.88 = (f32[320,512]{1,0:T(8,128)S(1)}, f32[320,512]{1,0:T(8,128)S(1)}, f32[5,512]{1,0:T(8,128)S(1)}, f32[24,512]{1,0:T(8,128)S(1)}) custom-call(bf16[320,512]{1,0:T(8,128)(2,1)S(1)} %collective-permute-done.1.refs_0_, bf16[3,2048,512]{2,1,0:T(8,128)(2,1)S(1)} %bitcast.11, f32[3,320,512]{2,1,0:T(8,128)S(1)} %shard_map.87.refs_2_, ...), custom_call_target="tpu_custom_call" | custom-call | flops 1006632960 | bytes 3145728 | tf_op jit(solution)/shard_map/pallas_call | solution.py:488
  22.7 1.3 %shard_map.90 = (f32[192,512]{1,0:T(8,128)S(1)}, f32[192,512]{1,0:T(8,128)S(1)}, f32[5,512]{1,0:T(8,128)S(1)}, f32[8,8,128]{2,1,0:T(8,128)S(1)}) custom-call(bf16[200,512]{1,0:T(8,128)(2,1)S(1)} %collective-permute-done.4.refs_0_, bf16[3,2048,512]{2,1,0:T(8,128)(2,1)S(1)} %bitcast.12, f32[3,200,512]{2,1,0:T(8,128)S(1)} %shard_map.89.refs_2_, ...), custom_call_target="tpu_custom_call" | custom-call | flops 629145600 | bytes 3145728 | tf_op jit(solution)/shard_map/pallas_call | solution.py:488
  23.9 13.7 %all_to_all.10.refs_5_ = f32[8,8,128]{2,1,0:T(8,128)S(1)} all-to-all(f32[8,8,128]{2,1,0:T(8,128)S(1)} %get-tuple-element.41), channel_id=1, replica_groups=mesh['tm'=8,'hid'=4] {'tm'}, dimensions={0} | all-to-all | bytes 65536 | tf_op jit(solution)/shard_map/all_to_all | solution.py:501
  38.0 1.6 %collective-permute-start.6 = (bf16[320,512]{1,0:T(8,128)(2,1)S(1)}, bf16[320,512]{1,0:T(8,128)(2,1)S(1)}, u32[]{:S(2)}, u32[]{:S(2)}) collective-permute-start(bf16[320,512]{1,0:T(8,128)(2,1)S(1)} %get-tuple-element.42), channel_id=1, source_target_pairs={{0,2},{1,3},{2,0},{3,1},{4,6},{5,7},{6,4},{7,5},{8,10},{9,11},{10,... | collective-permute-start | bytes 983048 | tf_op jit(solution)/shard_map/ppermute | solution.py:26
  40.1 8.6 %collective-permute-done.6.far_ref = bf16[320,512]{1,0:T(8,128)(2,1)S(1)} collective-permute-done((bf16[320,512]{1,0:T(8,128)(2,1)S(1)}, bf16[320,512]{1,0:T(8,128)(2,1)S(1)}, u32[]{:S(2)}, u32[]{:S(2)}) %collective-permute-start.6) | collective-permute-done | bytes 327712 | tf_op jit(solution)/shard_map/ppermute | solution.py:26
  48.7 3.7 %collective-permute-done.9.far_ref = bf16[192,512]{1,0:T(8,128)(2,1)S(1)} collective-permute-done((bf16[192,512]{1,0:T(8,128)(2,1)S(1)}, bf16[192,512]{1,0:T(8,128)(2,1)S(1)}, u32[]{:S(2)}, u32[]{:S(2)}) %collective-permute-start.9) | collective-permute-done | bytes 196640 | tf_op jit(solution)/shard_map/ppermute | solution.py:26
  52.4 1.9 %shard_map.92.base_ref = f32[3,512,512]{2,1,0:T(8,128)S(1)} custom-call(bf16[512,512]{1,0:T(8,128)(2,1)S(1)} %get-tuple-element.43.refs_0_, bf16[512,512]{1,0:T(8,128)(2,1)S(1)} %collective-permute-done.8.refs_1_, bf16[3,2048,512]{2,1,0:T(8,128)(2,1)S(1)} %bitcast.13, f32[3,520,512]{2,1,0:T(8,128)S(1)} %get-tuple-element.31.refs_3_, f32[1,512]{1,0:T(1,128)S(1)} %bitcast.24), custom_call_target="tpu_custom_call" | custom-call | flops 1610612736 | bytes 3145728 | tf_op jit(solution)/shard_map/pallas_call | solution.py:448
  54.8 0.7 shard_map.93.refs_2_
  55.5 1.9 %shard_map.94 = (f32[320,512]{1,0:T(8,128)S(1)}, f32[320,512]{1,0:T(8,128)S(1)}, f32[5,512]{1,0:T(8,128)S(1)}) custom-call(bf16[320,512]{1,0:T(8,128)(2,1)S(1)} %collective-permute-done.7.refs_0_, bf16[3,2048,512]{2,1,0:T(8,128)(2,1)S(1)} %bitcast.16, f32[3,320,512]{2,1,0:T(8,128)S(1)} %shard_map.93.refs_2_, f32[3,520,512]{2,1,0:T(8,128)S(1)} %get-tuple-element.31.refs_3_, ...), custom_call_target="tpu_custom_call" | custom-call | flops 1006632960 | bytes 3145728 | tf_op jit(solution)/shard_map/pallas_call | solution.py:488
  57.4 1.3 %shard_map.96 = (f32[192,512]{1,0:T(8,128)S(1)}, f32[192,512]{1,0:T(8,128)S(1)}, f32[5,512]{1,0:T(8,128)S(1)}, f32[8,9,128]{2,1,0:T(8,128)S(1)}) custom-call(bf16[192,512]{1,0:T(8,128)(2,1)S(1)} %collective-permute-done.10.refs_0_, bf16[3,2048,512]{2,1,0:T(8,128)(2,1)S(1)} %bitcast.17, f32[3,192,512]{2,1,0:T(8,128)S(1)} %shard_map.95.refs_2_, ...), custom_call_target="tpu_custom_call" | custom-call | flops 603979776 | bytes 3145728 | tf_op jit(solution)/shard_map/pallas_call | solution.py:488
  58.7 9.3 %all_to_all.11.refs_5_.all_ref = f32[8,9,128]{2,1,0:T(8,128)S(1)} all-to-all(f32[8,9,128]{2,1,0:T(8,128)S(1)} %get-tuple-element.53), channel_id=1, replica_groups=mesh['tm'=8,'hid'=4] {'tm'}, dimensions={0} | all-to-all | bytes 73728 | tf_op jit(solution)/shard_map/all_to_all | solution.py:501
  68.2 1.6 %collective-permute-start.12 = (f32[1,128]{1,0:T(1,128)S(1)}, f32[1,128]{1,0:T(1,128)S(1)}, u32[]{:S(2)}, u32[]{:S(2)}) collective-permute-start(f32[1,128]{1,0:T(1,128)S(1)} %sums.1.refs_0_), channel_id=1, source_target_pairs={{0,2},{1,3},{2,0},{3,1},{4,6},{5,7},{6,4},{7,5},{8,10},{9,11},{10,... | collective-permute-start | bytes 1544 | tf_op jit(solution)/shard_map/ppermute | solution.py:26
  70.0 1.2 %shard_map.97 = f32[512,512]{1,0:T(8,128)} custom-call(f32[320,512]{1,0:T(8,128)S(1)} %get-tuple-element.45.refs_0_, f32[320,512]{1,0:T(8,128)S(1)} %get-tuple-element.46.refs_1_, f32[192,512]{1,0:T(8,128)S(1)} %get-tuple-element.50.refs_2_, f32[192,512]{1,0:T(8,128)S(1)} %get-tuple-element.51.refs_3_, f32[5,512]{1,0:T(8,128)S(1)} %get-tuple-element.52.refs_4_, ...), custom_call_target="tpu_custom_call" | custom-call | flops 524288 | bytes 4194304 | tf_op jit(solution)/shard_map/pallas_call | solution.py:519
  71.2 0.5 collective-permute-done.12.refs_2_
  71.8 0.9 %collective-permute-done.13.refs_3_ = f32[1,128]{1,0:T(1,128)S(1)} collective-permute-done((f32[1,128]{1,0:T(1,128)S(1)}, f32[1,128]{1,0:T(1,128)S(1)}, u32[]{:S(2)}, u32[]{:S(2)}) %collective-permute-start.13) | collective-permute-done | bytes 544 | tf_op jit(solution)/shard_map/ppermute | solution.py:26
  72.7 0.7 norm.1
  (41 shorter events, 2.7 us)
Async XLA Ops:
  0.6 4.4 %copy-start.1 = (f32[512]{0:T(512)S(1)}, f32[512]{0:T(512)}, u32[]{:S(2)}) copy-start(f32[512]{0:T(512)} %param.12) | copy-start | bytes 6148
  2.0 11.6 %collective-permute-start = (bf16[320,512]{1,0:T(8,128)(2,1)S(1)}, bf16[320,512]{1,0:T(8,128)(2,1)S(1)}, u32[]{:S(2)}, u32[]{:S(2)}) collective-permute-start(bf16[320,512]{1,0:T(8,128)(2,1)S(1)} %slice.3), channel_id=1, source_target_pairs={{0,2},{1,3},{2,0},{3,1},{4,6},{5,7},{6,4},{7,5},{8,10},{9,11},{10,... | collective-permute-start | bytes 983048 | tf_op jit(solution)/shard_map/ppermute | solution.py:26
  5.0 8.6 %copy-start = (f32[512,512]{1,0:T(8,128)S(1)}, f32[512,512]{1,0:T(8,128)}, u32[]{:S(2)}) copy-start(f32[512,512]{1,0:T(8,128)} %refs_4_.1) | copy-start | bytes 3145732
  5.0 8.6 %copy-start.3 = (f32[256,3,512]{2,0,1:T(8,128)S(1)}, f32[256,3,512]{2,0,1:T(8,128)}, u32[]{:S(2)}) copy-start(f32[256,3,512]{2,0,1:T(8,128)} %param.8) | copy-start | bytes 4718596
  5.0 8.6 %copy-start.4 = (s32[512]{0:T(512)S(1)}, s32[512]{0:T(512)}, u32[]{:S(2)}) copy-start(s32[512]{0:T(512)} %param.7) | copy-start | bytes 6148
  5.0 8.6 %copy-start.5 = (f32[512]{0:T(512)S(1)}, f32[512]{0:T(512)}, u32[]{:S(2)}) copy-start(f32[512]{0:T(512)} %param.10) | copy-start | bytes 6148
  5.1 12.3 %collective-permute-start.2 = (bf16[520,512]{1,0:T(8,128)(2,1)S(1)}, bf16[520,512]{1,0:T(8,128)(2,1)S(1)}, u32[]{:S(2)}, u32[]{:S(2)}) collective-permute-start(bf16[520,512]{1,0:T(8,128)(2,1)S(1)} %get-tuple-element.29.refs_0_), channel_id=1, source_target_pairs={{0,1},{1,0},{2,3},{3,2},{4,5},{5,4},{6,7},{7,6},{8,9},{9,8},{10,11... | collective-permute-start | bytes 1597448 | tf_op jit(solution)/shard_map/ppermute | solution.py:26
  5.2 11.9 %collective-permute-start.3 = (bf16[200,512]{1,0:T(8,128)(2,1)S(1)}, bf16[200,512]{1,0:T(8,128)(2,1)S(1)}, u32[]{:S(2)}, u32[]{:S(2)}) collective-permute-start(bf16[200,512]{1,0:T(8,128)(2,1)S(1)} %get-tuple-element.34), channel_id=1, source_target_pairs={{0,2},{1,3},{2,0},{3,1},{4,6},{5,7},{6,4},{7,5},{8,10},{9,11},{10,... | collective-permute-start | bytes 614408 | tf_op jit(solution)/shard_map/ppermute | solution.py:26
  13.6 7.1 %collective-permute-start.1 = (bf16[320,512]{1,0:T(8,128)(2,1)S(1)}, bf16[320,512]{1,0:T(8,128)(2,1)S(1)}, u32[]{:S(2)}, u32[]{:S(2)}) collective-permute-start(bf16[320,512]{1,0:T(8,128)(2,1)S(1)} %collective-permute-done.far_ref), channel_id=1, source_target_pairs={{0,1},{1,0},{2,3},{3,2},{4,5},{5,4},{6,7},{7,6},{8,9},{9,8},{10,11... | collective-permute-start | bytes 983048 | tf_op jit(solution)/shard_map/ppermute | solution.py:26
  13.6 3.9 %slice-start = ((s8[6291456]{0:T(1024)(128)(4,1)}), s8[4194304]{0:T(1024)(128)(4,1)S(1)}, s32[]{:S(2)}) async-start(s8[6291456]{0:T(1024)(128)(4,1)} %bitcast.6), calls=%async_computation.2 | async-start | bytes 8388608
  13.6 3.8 %slice-start.1 = ((s8[6291456]{0:T(1024)(128)(4,1)}), s8[2097152]{0:T(1024)(128)(4,1)S(1)}, s32[]{:S(2)}) async-start(s8[6291456]{0:T(1024)(128)(4,1)} %bitcast.6), calls=%async_computation.3 | async-start | bytes 4194304
  13.6 3.8 %copy-start.2 = (f32[512]{0:T(512)S(1)}, f32[512]{0:T(512)}, u32[]{:S(2)}) copy-start(f32[512]{0:T(512)} %param.11) | copy-start | bytes 6148
  15.6 7.1 %collective-permute-start.5 = (f32[1,2048]{1,0:T(1,128)S(1)}, f32[1,2048]{1,0:T(1,128)S(1)}, u32[]{:S(2)}, u32[]{:S(2)}) collective-permute-start(f32[1,2048]{1,0:T(1,128)S(1)} %get-tuple-element.35), channel_id=1, source_target_pairs={{4,0},{8,4},{12,8},{16,12},{20,16},{24,20},{28,24},{5,1},{9,5},{13... | collective-permute-start | bytes 24584 | tf_op jit(solution)/shard_map/ppermute | solution.py:31
  17.1 5.5 %collective-permute-start.4 = (bf16[200,512]{1,0:T(8,128)(2,1)S(1)}, bf16[200,512]{1,0:T(8,128)(2,1)S(1)}, u32[]{:S(2)}, u32[]{:S(2)}) collective-permute-start(bf16[200,512]{1,0:T(8,128)(2,1)S(1)} %collective-permute-done.3.far_ref), channel_id=1, source_target_pairs={{0,1},{1,0},{2,3},{3,2},{4,5},{5,4},{6,7},{7,6},{8,9},{9,8},{10,11... | collective-permute-start | bytes 614408 | tf_op jit(solution)/shard_map/ppermute | solution.py:26
  37.9 14.4 %collective-permute-start.8 = (bf16[512,512]{1,0:T(8,128)(2,1)S(1)}, bf16[512,512]{1,0:T(8,128)(2,1)S(1)}, u32[]{:S(2)}, u32[]{:S(2)}) collective-permute-start(bf16[512,512]{1,0:T(8,128)(2,1)S(1)} %get-tuple-element.43.refs_0_), channel_id=1, source_target_pairs={{0,1},{1,0},{2,3},{3,2},{4,5},{5,4},{6,7},{7,6},{8,9},{9,8},{10,11... | collective-permute-start | bytes 1572872 | tf_op jit(solution)/shard_map/ppermute | solution.py:26
  38.0 10.7 %collective-permute-start.6 = (bf16[320,512]{1,0:T(8,128)(2,1)S(1)}, bf16[320,512]{1,0:T(8,128)(2,1)S(1)}, u32[]{:S(2)}, u32[]{:S(2)}) collective-permute-start(bf16[320,512]{1,0:T(8,128)(2,1)S(1)} %get-tuple-element.42), channel_id=1, source_target_pairs={{0,2},{1,3},{2,0},{3,1},{4,6},{5,7},{6,4},{7,5},{8,10},{9,11},{10,... | collective-permute-start | bytes 983048 | tf_op jit(solution)/shard_map/ppermute | solution.py:26
  39.6 12.7 %collective-permute-start.9 = (bf16[192,512]{1,0:T(8,128)(2,1)S(1)}, bf16[192,512]{1,0:T(8,128)(2,1)S(1)}, u32[]{:S(2)}, u32[]{:S(2)}) collective-permute-start(bf16[192,512]{1,0:T(8,128)(2,1)S(1)} %get-tuple-element.47), channel_id=1, source_target_pairs={{0,2},{1,3},{2,0},{3,1},{4,6},{5,7},{6,4},{7,5},{8,10},{9,11},{10,... | collective-permute-start | bytes 589832 | tf_op jit(solution)/shard_map/ppermute | solution.py:26
  48.7 6.8 %collective-permute-start.7 = (bf16[320,512]{1,0:T(8,128)(2,1)S(1)}, bf16[320,512]{1,0:T(8,128)(2,1)S(1)}, u32[]{:S(2)}, u32[]{:S(2)}) collective-permute-start(bf16[320,512]{1,0:T(8,128)(2,1)S(1)} %collective-permute-done.6.far_ref), channel_id=1, source_target_pairs={{0,1},{1,0},{2,3},{3,2},{4,5},{5,4},{6,7},{7,6},{8,9},{9,8},{10,11... | collective-permute-start | bytes 983048 | tf_op jit(solution)/shard_map/ppermute | solution.py:26
  52.4 5.1 %collective-permute-start.10 = (bf16[192,512]{1,0:T(8,128)(2,1)S(1)}, bf16[192,512]{1,0:T(8,128)(2,1)S(1)}, u32[]{:S(2)}, u32[]{:S(2)}) collective-permute-start(bf16[192,512]{1,0:T(8,128)(2,1)S(1)} %collective-permute-done.9.far_ref), channel_id=1, source_target_pairs={{0,1},{1,0},{2,3},{3,2},{4,5},{5,4},{6,7},{7,6},{8,9},{9,8},{10,11... | collective-permute-start | bytes 589832 | tf_op jit(solution)/shard_map/ppermute | solution.py:26
  68.1 3.2 %collective-permute-start.11 = (f32[1,128]{1,0:T(1,128)S(1)}, f32[1,128]{1,0:T(1,128)S(1)}, u32[]{:S(2)}, u32[]{:S(2)}) collective-permute-start(f32[1,128]{1,0:T(1,128)S(1)} %sums.1.refs_0_), channel_id=1, source_target_pairs={{0,1},{1,0},{2,3},{3,2},{4,5},{5,4},{6,7},{7,6},{8,9},{9,8},{10,11... | collective-permute-start | bytes 1544 | tf_op jit(solution)/shard_map/ppermute | solution.py:26
  68.2 3.6 %collective-permute-start.12 = (f32[1,128]{1,0:T(1,128)S(1)}, f32[1,128]{1,0:T(1,128)S(1)}, u32[]{:S(2)}, u32[]{:S(2)}) collective-permute-start(f32[1,128]{1,0:T(1,128)S(1)} %sums.1.refs_0_), channel_id=1, source_target_pairs={{0,2},{1,3},{2,0},{3,1},{4,6},{5,7},{6,4},{7,5},{8,10},{9,11},{10,... | collective-permute-start | bytes 1544 | tf_op jit(solution)/shard_map/ppermute | solution.py:26
  69.7 3.0 %collective-permute-start.13 = (f32[1,128]{1,0:T(1,128)S(1)}, f32[1,128]{1,0:T(1,128)S(1)}, u32[]{:S(2)}, u32[]{:S(2)}) collective-permute-start(f32[1,128]{1,0:T(1,128)S(1)} %sums.1.refs_0_), channel_id=1, source_target_pairs={{0,3},{1,2},{2,1},{3,0},{4,7},{5,6},{6,5},{7,4},{8,11},{9,10},{10,... | collective-permute-start | bytes 1544 | tf_op jit(solution)/shard_map/ppermute | solution.py:26

commit v9 on v8

--- a/solution.py
+++ b/solution.py
@@ -9,7 +9,7 @@
 
 
 ITERS = 2
-SHARES = ((10, 6), (10, 6))
+SHARES = ((10, 6), (19, 13))
 CHUNKS = len(SHARES[0])
 GROUP = 8
 EXTRA = 8
@@ -83,18 +83,9 @@
 def prepare_kernel(ids_ref, guess_ref, table_ref, bias_ref, out_ref, line_ref):
     vocab, width = table_ref.shape[1:]
     rows = ids_ref.shape[1]
-    ids = ids_ref[...]
-
-    def spread(line):
-        entry = lax.broadcasted_iota(jnp.int32, (vocab, line.shape[1]), 0)
-        return (entry == line).astype(F32).astype(BF16)
-
-    def pick(hot, part):
-        return lax.dot_general(hot, part, (((0,), (0,)), ((), ())), preferred_element_type=F32)
-
-    lane = lax.broadcasted_iota(jnp.int32, (1, rows), 1)
-    hot = spread(jnp.where(lane == rows - 1, vocab, pltpu.roll(ids, rows - 1, 1)))
-    hot_begin = spread(jnp.broadcast_to(ids[:, 0:1], (1, LANES)))
+    entry = lax.broadcasted_iota(jnp.int32, (vocab, rows), 0)
+    hot = (entry == pltpu.roll(ids_ref[...], rows - 1, 1)).astype(F32).astype(BF16)
+    row = lax.broadcasted_iota(jnp.int32, (GROUP, width), 0)
     line_ref[:, pl.ds(0, width)] = guess_ref[0:1, :]
     for gate in range(3):
         table = table_ref[gate]
@@ -104,11 +95,14 @@
         for _ in range(3):
             part = table.astype(BF16)
             table = table - part.astype(F32)
-            picked = (pick(hot, part), pick(hot_begin, part))
-            total = picked if total is None else (total[0] + picked[0], total[1] + picked[1])
-        out_ref[gate, pl.ds(0, rows), :] = total[0]
-        out_ref[gate, pl.ds(rows, GROUP), :] = total[1][0:GROUP]
-        line_ref[:, pl.ds((gate + 1) * width, width)] = total[1][0:1]
+            picked = lax.dot_general(hot, part, (((0,), (0,)), ((), ())), preferred_element_type=F32)
+            total = picked if total is None else total + picked
+        ending = total[rows - GROUP :]
+        begin = ending[GROUP - 1 :]
+        out_ref[gate, pl.ds(0, rows - GROUP), :] = total[: rows - GROUP]
+        out_ref[gate, pl.ds(rows - GROUP, GROUP), :] = jnp.where(row == GROUP - 1, 0.0, ending)
+        out_ref[gate, pl.ds(rows, GROUP), :] = jnp.broadcast_to(begin, (GROUP, width))
+        line_ref[:, pl.ds((gate + 1) * width, width)] = begin
 
 
 def diagonals(weight_ref, hid, diag_ref):

time: 73.9 us -> 73.6 us (level)
  no operation moved by 1% of the time
where the time goes in v9:
time: 73.6 us; the launch traced here: 73.4 us
  blocking collectives  23 us (31%)
  waiting for transfers between devices  22.5 us (31%)
  Pallas kernels  16.6 us (23%)
  starting transfers between devices  8.83 us (12%)
  other arithmetic  1.3 us (2%)
  between operations  1.05 us (1%)
    all_to_all x2, blocking collectives, newton(): every = lax.all_to_all(found[-1], 'tm', 0, 0)  23 us
    ppermute x13, waiting for transfers between devices, swapped(): return lax.ppermute(block, axis, route)  22.5 us
    ppermute x13, starting transfers between devices, swapped(): return lax.ppermute(block, axis, route)  7.41 us
    pallas_call x4, Pallas kernels, newton(): pl.pallas_call(functools.partial(step_kernel, count, index, start, chunk,...  6.38 us
    pallas_call x2, Pallas kernels, newton(): pl.pallas_call(functools.partial(base_kernel, step, count), out_shape=jax...  3.9 us
    pallas_call x4, Pallas kernels, newton(): pl.pallas_call(functools.partial(direct_kernel, start, count), out_shape=...  2.44 us
    pallas_call x2, Pallas kernels, newton(): pl.pallas_call(functools.partial(apply_kernel, step), out_shape=outs, in_...  1.55 us
    pallas_call x1, Pallas kernels, newton(): pl.pallas_call(prepare_kernel, out_shape=[jax.ShapeDtypeStruct((3, rows +...  1.55 us
  transfers between devices with their start and end apart: 14, of which 6 were waited for; matrix products, arithmetic and copies ran while one was open for 0% of the time, Pallas kernels for 18%

profile of v9, /device:TPU:0, one launch (start us, length us, event | category | flops | bytes accessed | tf_op | source)
XLA Modules:
  0.0 73.4 jit_solution(15923824526149195705)
XLA Ops:
  0.6 1.3 %convert_element_type.3.rounded_ref = bf16[512,512]{1,0:T(8,128)(2,1)S(1)} convert(f32[512,512]{1,0:T(8,128)} %refs_4_.1) | non-fusion elementwise | flops 262144 | bytes 1572864 | tf_op jit(solution)/shard_map/convert_element_type | solution.py:395
  2.0 3.1 %collective-permute-start = (bf16[320,512]{1,0:T(8,128)(2,1)S(1)}, bf16[320,512]{1,0:T(8,128)(2,1)S(1)}, u32[]{:S(2)}, u32[]{:S(2)}) collective-permute-start(bf16[320,512]{1,0:T(8,128)(2,1)S(1)} %slice.3), channel_id=1, source_target_pairs={{0,2},{1,3},{2,0},{3,1},{4,6},{5,7},{6,4},{7,5},{8,10},{9,11},{10,... | collective-permute-start | bytes 983048 | tf_op jit(solution)/shard_map/ppermute | solution.py:26
  5.3 8.3 %collective-permute-done.far_ref = bf16[320,512]{1,0:T(8,128)(2,1)S(1)} collective-permute-done((bf16[320,512]{1,0:T(8,128)(2,1)S(1)}, bf16[320,512]{1,0:T(8,128)(2,1)S(1)}, u32[]{:S(2)}, u32[]{:S(2)}) %collective-permute-start) | collective-permute-done | bytes 327712 | tf_op jit(solution)/shard_map/ppermute | solution.py:26
  13.7 1.6 %prepare.1 = (f32[3,520,512]{2,1,0:T(8,128)S(1)}, f32[1,2048]{1,0:T(1,128)S(1)}) custom-call(s32[1,512]{1,0:T(1,128)S(1)} %bitcast.26, f32[512,512]{1,0:T(8,128)S(1)} %copy-done, f32[3,256,512]{2,1,0:T(8,128)S(1)} %bitcast.25, f32[1,512]{1,0:T(1,128)S(1)} %bitcast.27), custom_call_target="tpu_custom_call" | custom-call | flops 4000000000 | bytes 2097152 | tf_op jit(solution)/shard_map/prepare/pallas_call | solution.py:411
  15.2 1.4 %collective-permute-start.5 = (f32[1,2048]{1,0:T(1,128)S(1)}, f32[1,2048]{1,0:T(1,128)S(1)}, u32[]{:S(2)}, u32[]{:S(2)}) collective-permute-start(f32[1,2048]{1,0:T(1,128)S(1)} %get-tuple-element.35), channel_id=1, source_target_pairs={{4,0},{8,4},{12,8},{16,12},{20,16},{24,20},{28,24},{5,1},{9,5},{13... | collective-permute-start | bytes 24584 | tf_op jit(solution)/shard_map/ppermute | solution.py:31
  17.2 2.0 %shard_map.86.base_ref = f32[3,520,512]{2,1,0:T(8,128)S(1)} custom-call(bf16[520,512]{1,0:T(8,128)(2,1)S(1)} %get-tuple-element.29.refs_0_, bf16[520,512]{1,0:T(8,128)(2,1)S(1)} %collective-permute-done.2.refs_1_, bf16[3,2048,512]{2,1,0:T(8,128)(2,1)S(1)} %bitcast.8, f32[3,520,512]{2,1,0:T(8,128)S(1)} %get-tuple-element.31.refs_3_, f32[1,512]{1,0:T(1,128)S(1)} %bitcast.23), custom_call_target="tpu_custom_call" | custom-call | flops 1635778560 | bytes 3145728 | tf_op jit(solution)/shard_map/pallas_call | solution.py:442
  19.2 0.5 shard_map.89.refs_2_
  19.8 0.7 shard_map.87.refs_2_
  20.5 1.9 %shard_map.88 = (f32[320,512]{1,0:T(8,128)S(1)}, f32[320,512]{1,0:T(8,128)S(1)}, f32[5,512]{1,0:T(8,128)S(1)}, f32[24,512]{1,0:T(8,128)S(1)}) custom-call(bf16[320,512]{1,0:T(8,128)(2,1)S(1)} %collective-permute-done.1.refs_0_, bf16[3,2048,512]{2,1,0:T(8,128)(2,1)S(1)} %bitcast.11, f32[3,320,512]{2,1,0:T(8,128)S(1)} %shard_map.87.refs_2_, ...), custom_call_target="tpu_custom_call" | custom-call | flops 1006632960 | bytes 3145728 | tf_op jit(solution)/shard_map/pallas_call | solution.py:482
  22.4 1.3 %shard_map.90 = (f32[192,512]{1,0:T(8,128)S(1)}, f32[192,512]{1,0:T(8,128)S(1)}, f32[5,512]{1,0:T(8,128)S(1)}, f32[8,8,128]{2,1,0:T(8,128)S(1)}) custom-call(bf16[200,512]{1,0:T(8,128)(2,1)S(1)} %collective-permute-done.4.refs_0_, bf16[3,2048,512]{2,1,0:T(8,128)(2,1)S(1)} %bitcast.12, f32[3,200,512]{2,1,0:T(8,128)S(1)} %shard_map.89.refs_2_, ...), custom_call_target="tpu_custom_call" | custom-call | flops 629145600 | bytes 3145728 | tf_op jit(solution)/shard_map/pallas_call | solution.py:482
  23.7 13.7 %all_to_all.10.refs_5_ = f32[8,8,128]{2,1,0:T(8,128)S(1)} all-to-all(f32[8,8,128]{2,1,0:T(8,128)S(1)} %get-tuple-element.41), channel_id=1, replica_groups=mesh['tm'=8,'hid'=4] {'tm'}, dimensions={0} | all-to-all | bytes 65536 | tf_op jit(solution)/shard_map/all_to_all | solution.py:495
  37.8 1.6 %collective-permute-start.6 = (bf16[304,512]{1,0:T(8,128)(2,1)S(1)}, bf16[304,512]{1,0:T(8,128)(2,1)S(1)}, u32[]{:S(2)}, u32[]{:S(2)}) collective-permute-start(bf16[304,512]{1,0:T(8,128)(2,1)S(1)} %get-tuple-element.42), channel_id=1, source_target_pairs={{0,2},{1,3},{2,0},{3,1},{4,6},{5,7},{6,4},{7,5},{8,10},{9,11},{10,... | collective-permute-start | bytes 933896 | tf_op jit(solution)/shard_map/ppermute | solution.py:26
  39.9 8.2 %collective-permute-done.6.far_ref = bf16[304,512]{1,0:T(8,128)(2,1)S(1)} collective-permute-done((bf16[304,512]{1,0:T(8,128)(2,1)S(1)}, bf16[304,512]{1,0:T(8,128)(2,1)S(1)}, u32[]{:S(2)}, u32[]{:S(2)}) %collective-permute-start.6) | collective-permute-done | bytes 311328 | tf_op jit(solution)/shard_map/ppermute | solution.py:26
  48.1 4.0 %collective-permute-done.9.far_ref = bf16[208,512]{1,0:T(8,128)(2,1)S(1)} collective-permute-done((bf16[208,512]{1,0:T(8,128)(2,1)S(1)}, bf16[208,512]{1,0:T(8,128)(2,1)S(1)}, u32[]{:S(2)}, u32[]{:S(2)}) %collective-permute-start.9) | collective-permute-done | bytes 213024 | tf_op jit(solution)/shard_map/ppermute | solution.py:26
  52.1 1.9 %shard_map.92.base_ref = f32[3,512,512]{2,1,0:T(8,128)S(1)} custom-call(bf16[512,512]{1,0:T(8,128)(2,1)S(1)} %get-tuple-element.43.refs_0_, bf16[512,512]{1,0:T(8,128)(2,1)S(1)} %collective-permute-done.8.refs_1_, bf16[3,2048,512]{2,1,0:T(8,128)(2,1)S(1)} %bitcast.13, f32[3,520,512]{2,1,0:T(8,128)S(1)} %get-tuple-element.31.refs_3_, f32[1,512]{1,0:T(1,128)S(1)} %bitcast.24), custom_call_target="tpu_custom_call" | custom-call | flops 1610612736 | bytes 3145728 | tf_op jit(solution)/shard_map/pallas_call | solution.py:442
  54.6 0.7 shard_map.93.refs_2_
  55.3 1.8 %shard_map.94 = (f32[304,512]{1,0:T(8,128)S(1)}, f32[304,512]{1,0:T(8,128)S(1)}, f32[5,512]{1,0:T(8,128)S(1)}) custom-call(bf16[304,512]{1,0:T(8,128)(2,1)S(1)} %collective-permute-done.7.refs_0_, bf16[3,2048,512]{2,1,0:T(8,128)(2,1)S(1)} %bitcast.16, f32[3,304,512]{2,1,0:T(8,128)S(1)} %shard_map.93.refs_2_, f32[3,520,512]{2,1,0:T(8,128)S(1)} %get-tuple-element.31.refs_3_, ...), custom_call_target="tpu_custom_call" | custom-call | flops 956301312 | bytes 3145728 | tf_op jit(solution)/shard_map/pallas_call | solution.py:482
  57.1 1.4 %shard_map.96 = (f32[208,512]{1,0:T(8,128)S(1)}, f32[208,512]{1,0:T(8,128)S(1)}, f32[5,512]{1,0:T(8,128)S(1)}, f32[8,9,128]{2,1,0:T(8,128)S(1)}) custom-call(bf16[208,512]{1,0:T(8,128)(2,1)S(1)} %collective-permute-done.10.refs_0_, bf16[3,2048,512]{2,1,0:T(8,128)(2,1)S(1)} %bitcast.17, f32[3,208,512]{2,1,0:T(8,128)S(1)} %shard_map.95.refs_2_, ...), custom_call_target="tpu_custom_call" | custom-call | flops 654311424 | bytes 3145728 | tf_op jit(solution)/shard_map/pallas_call | solution.py:482
  58.5 9.3 %all_to_all.11.refs_5_.all_ref = f32[8,9,128]{2,1,0:T(8,128)S(1)} all-to-all(f32[8,9,128]{2,1,0:T(8,128)S(1)} %get-tuple-element.53), channel_id=1, replica_groups=mesh['tm'=8,'hid'=4] {'tm'}, dimensions={0} | all-to-all | bytes 73728 | tf_op jit(solution)/shard_map/all_to_all | solution.py:495
  67.9 1.6 %collective-permute-start.12 = (f32[1,128]{1,0:T(1,128)S(1)}, f32[1,128]{1,0:T(1,128)S(1)}, u32[]{:S(2)}, u32[]{:S(2)}) collective-permute-start(f32[1,128]{1,0:T(1,128)S(1)} %sums.1.refs_0_), channel_id=1, source_target_pairs={{0,2},{1,3},{2,0},{3,1},{4,6},{5,7},{6,4},{7,5},{8,10},{9,11},{10,... | collective-permute-start | bytes 1544 | tf_op jit(solution)/shard_map/ppermute | solution.py:26
  69.7 1.2 %shard_map.97 = f32[512,512]{1,0:T(8,128)} custom-call(f32[304,512]{1,0:T(8,128)S(1)} %get-tuple-element.45.refs_0_, f32[304,512]{1,0:T(8,128)S(1)} %get-tuple-element.46.refs_1_, f32[208,512]{1,0:T(8,128)S(1)} %get-tuple-element.50.refs_2_, f32[208,512]{1,0:T(8,128)S(1)} %get-tuple-element.51.refs_3_, f32[5,512]{1,0:T(8,128)S(1)} %get-tuple-element.52.refs_4_, ...), custom_call_target="tpu_custom_call" | custom-call | flops 524288 | bytes 4194304 | tf_op jit(solution)/shard_map/pallas_call | solution.py:513
  71.0 0.6 collective-permute-done.12.refs_2_
  71.5 0.9 %collective-permute-done.13.refs_3_ = f32[1,128]{1,0:T(1,128)S(1)} collective-permute-done((f32[1,128]{1,0:T(1,128)S(1)}, f32[1,128]{1,0:T(1,128)S(1)}, u32[]{:S(2)}, u32[]{:S(2)}) %collective-permute-start.13) | collective-permute-done | bytes 544 | tf_op jit(solution)/shard_map/ppermute | solution.py:26
  72.5 0.7 norm.1
  (41 shorter events, 2.7 us)
Async XLA Ops:
  0.6 4.4 %copy-start.1 = (f32[512]{0:T(512)S(1)}, f32[512]{0:T(512)}, u32[]{:S(2)}) copy-start(f32[512]{0:T(512)} %param.12) | copy-start | bytes 6148
  2.0 11.6 %collective-permute-start = (bf16[320,512]{1,0:T(8,128)(2,1)S(1)}, bf16[320,512]{1,0:T(8,128)(2,1)S(1)}, u32[]{:S(2)}, u32[]{:S(2)}) collective-permute-start(bf16[320,512]{1,0:T(8,128)(2,1)S(1)} %slice.3), channel_id=1, source_target_pairs={{0,2},{1,3},{2,0},{3,1},{4,6},{5,7},{6,4},{7,5},{8,10},{9,11},{10,... | collective-permute-start | bytes 983048 | tf_op jit(solution)/shard_map/ppermute | solution.py:26
  5.0 8.6 %copy-start = (f32[512,512]{1,0:T(8,128)S(1)}, f32[512,512]{1,0:T(8,128)}, u32[]{:S(2)}) copy-start(f32[512,512]{1,0:T(8,128)} %refs_4_.1) | copy-start | bytes 3145732
  5.0 8.6 %copy-start.3 = (f32[256,3,512]{2,0,1:T(8,128)S(1)}, f32[256,3,512]{2,0,1:T(8,128)}, u32[]{:S(2)}) copy-start(f32[256,3,512]{2,0,1:T(8,128)} %param.8) | copy-start | bytes 4718596
  5.0 8.6 %copy-start.4 = (s32[512]{0:T(512)S(1)}, s32[512]{0:T(512)}, u32[]{:S(2)}) copy-start(s32[512]{0:T(512)} %param.7) | copy-start | bytes 6148
  5.0 8.6 %copy-start.5 = (f32[512]{0:T(512)S(1)}, f32[512]{0:T(512)}, u32[]{:S(2)}) copy-start(f32[512]{0:T(512)} %param.10) | copy-start | bytes 6148
  5.1 12.1 %collective-permute-start.2 = (bf16[520,512]{1,0:T(8,128)(2,1)S(1)}, bf16[520,512]{1,0:T(8,128)(2,1)S(1)}, u32[]{:S(2)}, u32[]{:S(2)}) collective-permute-start(bf16[520,512]{1,0:T(8,128)(2,1)S(1)} %get-tuple-element.29.refs_0_), channel_id=1, source_target_pairs={{0,1},{1,0},{2,3},{3,2},{4,5},{5,4},{6,7},{7,6},{8,9},{9,8},{10,11... | collective-permute-start | bytes 1597448 | tf_op jit(solution)/shard_map/ppermute | solution.py:26
  5.2 11.9 %collective-permute-start.3 = (bf16[200,512]{1,0:T(8,128)(2,1)S(1)}, bf16[200,512]{1,0:T(8,128)(2,1)S(1)}, u32[]{:S(2)}, u32[]{:S(2)}) collective-permute-start(bf16[200,512]{1,0:T(8,128)(2,1)S(1)} %get-tuple-element.34), channel_id=1, source_target_pairs={{0,2},{1,3},{2,0},{3,1},{4,6},{5,7},{6,4},{7,5},{8,10},{9,11},{10,... | collective-permute-start | bytes 614408 | tf_op jit(solution)/shard_map/ppermute | solution.py:26
  13.6 6.9 %collective-permute-start.1 = (bf16[320,512]{1,0:T(8,128)(2,1)S(1)}, bf16[320,512]{1,0:T(8,128)(2,1)S(1)}, u32[]{:S(2)}, u32[]{:S(2)}) collective-permute-start(bf16[320,512]{1,0:T(8,128)(2,1)S(1)} %collective-permute-done.far_ref), channel_id=1, source_target_pairs={{0,1},{1,0},{2,3},{3,2},{4,5},{5,4},{6,7},{7,6},{8,9},{9,8},{10,11... | collective-permute-start | bytes 983048 | tf_op jit(solution)/shard_map/ppermute | solution.py:26
  13.6 3.6 %slice-start = ((s8[6291456]{0:T(1024)(128)(4,1)}), s8[4194304]{0:T(1024)(128)(4,1)S(1)}, s32[]{:S(2)}) async-start(s8[6291456]{0:T(1024)(128)(4,1)} %bitcast.6), calls=%async_computation.2 | async-start | bytes 8388608
  13.6 3.6 %slice-start.1 = ((s8[6291456]{0:T(1024)(128)(4,1)}), s8[2097152]{0:T(1024)(128)(4,1)S(1)}, s32[]{:S(2)}) async-start(s8[6291456]{0:T(1024)(128)(4,1)} %bitcast.6), calls=%async_computation.3 | async-start | bytes 4194304
  13.6 3.6 %copy-start.2 = (f32[512]{0:T(512)S(1)}, f32[512]{0:T(512)}, u32[]{:S(2)}) copy-start(f32[512]{0:T(512)} %param.11) | copy-start | bytes 6148
  15.2 7.2 %collective-permute-start.5 = (f32[1,2048]{1,0:T(1,128)S(1)}, f32[1,2048]{1,0:T(1,128)S(1)}, u32[]{:S(2)}, u32[]{:S(2)}) collective-permute-start(f32[1,2048]{1,0:T(1,128)S(1)} %get-tuple-element.35), channel_id=1, source_target_pairs={{4,0},{8,4},{12,8},{16,12},{20,16},{24,20},{28,24},{5,1},{9,5},{13... | collective-permute-start | bytes 24584 | tf_op jit(solution)/shard_map/ppermute | solution.py:31
  17.1 5.3 %collective-permute-start.4 = (bf16[200,512]{1,0:T(8,128)(2,1)S(1)}, bf16[200,512]{1,0:T(8,128)(2,1)S(1)}, u32[]{:S(2)}, u32[]{:S(2)}) collective-permute-start(bf16[200,512]{1,0:T(8,128)(2,1)S(1)} %collective-permute-done.3.far_ref), channel_id=1, source_target_pairs={{0,1},{1,0},{2,3},{3,2},{4,5},{5,4},{6,7},{7,6},{8,9},{9,8},{10,11... | collective-permute-start | bytes 614408 | tf_op jit(solution)/shard_map/ppermute | solution.py:26
  37.7 14.4 %collective-permute-start.8 = (bf16[512,512]{1,0:T(8,128)(2,1)S(1)}, bf16[512,512]{1,0:T(8,128)(2,1)S(1)}, u32[]{:S(2)}, u32[]{:S(2)}) collective-permute-start(bf16[512,512]{1,0:T(8,128)(2,1)S(1)} %get-tuple-element.43.refs_0_), channel_id=1, source_target_pairs={{0,1},{1,0},{2,3},{3,2},{4,5},{5,4},{6,7},{7,6},{8,9},{9,8},{10,11... | collective-permute-start | bytes 1572872 | tf_op jit(solution)/shard_map/ppermute | solution.py:26
  37.8 10.3 %collective-permute-start.6 = (bf16[304,512]{1,0:T(8,128)(2,1)S(1)}, bf16[304,512]{1,0:T(8,128)(2,1)S(1)}, u32[]{:S(2)}, u32[]{:S(2)}) collective-permute-start(bf16[304,512]{1,0:T(8,128)(2,1)S(1)} %get-tuple-element.42), channel_id=1, source_target_pairs={{0,2},{1,3},{2,0},{3,1},{4,6},{5,7},{6,4},{7,5},{8,10},{9,11},{10,... | collective-permute-start | bytes 933896 | tf_op jit(solution)/shard_map/ppermute | solution.py:26
  39.4 12.7 %collective-permute-start.9 = (bf16[208,512]{1,0:T(8,128)(2,1)S(1)}, bf16[208,512]{1,0:T(8,128)(2,1)S(1)}, u32[]{:S(2)}, u32[]{:S(2)}) collective-permute-start(bf16[208,512]{1,0:T(8,128)(2,1)S(1)} %get-tuple-element.47), channel_id=1, source_target_pairs={{0,2},{1,3},{2,0},{3,1},{4,6},{5,7},{6,4},{7,5},{8,10},{9,11},{10,... | collective-permute-start | bytes 638984 | tf_op jit(solution)/shard_map/ppermute | solution.py:26
  48.1 7.2 %collective-permute-start.7 = (bf16[304,512]{1,0:T(8,128)(2,1)S(1)}, bf16[304,512]{1,0:T(8,128)(2,1)S(1)}, u32[]{:S(2)}, u32[]{:S(2)}) collective-permute-start(bf16[304,512]{1,0:T(8,128)(2,1)S(1)} %collective-permute-done.6.far_ref), channel_id=1, source_target_pairs={{0,1},{1,0},{2,3},{3,2},{4,5},{5,4},{6,7},{7,6},{8,9},{9,8},{10,11... | collective-permute-start | bytes 933896 | tf_op jit(solution)/shard_map/ppermute | solution.py:26
  52.1 5.0 %collective-permute-start.10 = (bf16[208,512]{1,0:T(8,128)(2,1)S(1)}, bf16[208,512]{1,0:T(8,128)(2,1)S(1)}, u32[]{:S(2)}, u32[]{:S(2)}) collective-permute-start(bf16[208,512]{1,0:T(8,128)(2,1)S(1)} %collective-permute-done.9.far_ref), channel_id=1, source_target_pairs={{0,1},{1,0},{2,3},{3,2},{4,5},{5,4},{6,7},{7,6},{8,9},{9,8},{10,11... | collective-permute-start | bytes 638984 | tf_op jit(solution)/shard_map/ppermute | solution.py:26
  67.8 3.1 %collective-permute-start.11 = (f32[1,128]{1,0:T(1,128)S(1)}, f32[1,128]{1,0:T(1,128)S(1)}, u32[]{:S(2)}, u32[]{:S(2)}) collective-permute-start(f32[1,128]{1,0:T(1,128)S(1)} %sums.1.refs_0_), channel_id=1, source_target_pairs={{0,1},{1,0},{2,3},{3,2},{4,5},{5,4},{6,7},{7,6},{8,9},{9,8},{10,11... | collective-permute-start | bytes 1544 | tf_op jit(solution)/shard_map/ppermute | solution.py:26
  67.9 3.6 %collective-permute-start.12 = (f32[1,128]{1,0:T(1,128)S(1)}, f32[1,128]{1,0:T(1,128)S(1)}, u32[]{:S(2)}, u32[]{:S(2)}) collective-permute-start(f32[1,128]{1,0:T(1,128)S(1)} %sums.1.refs_0_), channel_id=1, source_target_pairs={{0,2},{1,3},{2,0},{3,1},{4,6},{5,7},{6,4},{7,5},{8,10},{9,11},{10,... | collective-permute-start | bytes 1544 | tf_op jit(solution)/shard_map/ppermute | solution.py:26
  69.5 3.0 %collective-permute-start.13 = (f32[1,128]{1,0:T(1,128)S(1)}, f32[1,128]{1,0:T(1,128)S(1)}, u32[]{:S(2)}, u32[]{:S(2)}) collective-permute-start(f32[1,128]{1,0:T(1,128)S(1)} %sums.1.refs_0_), channel_id=1, source_target_pairs={{0,3},{1,2},{2,1},{3,0},{4,7},{5,6},{6,5},{7,4},{8,11},{9,10},{10,... | collective-permute-start | bytes 1544 | tf_op jit(solution)/shard_map/ppermute | solution.py:26

commit v10 on v9

--- a/solution.py
+++ b/solution.py
@@ -80,13 +80,12 @@
         whole_ref[pl.ds(at + lead, chunk), :] = block
 
 
-def prepare_kernel(ids_ref, guess_ref, table_ref, bias_ref, out_ref, line_ref):
+def prepare_kernel(ids_ref, table_ref, bias_ref, out_ref):
     vocab, width = table_ref.shape[1:]
     rows = ids_ref.shape[1]
     entry = lax.broadcasted_iota(jnp.int32, (vocab, rows), 0)
     hot = (entry == pltpu.roll(ids_ref[...], rows - 1, 1)).astype(F32).astype(BF16)
     row = lax.broadcasted_iota(jnp.int32, (GROUP, width), 0)
-    line_ref[:, pl.ds(0, width)] = guess_ref[0:1, :]
     for gate in range(3):
         table = table_ref[gate]
         if gate == 0:
@@ -102,7 +101,6 @@
         out_ref[gate, pl.ds(0, rows - GROUP), :] = total[: rows - GROUP]
         out_ref[gate, pl.ds(rows - GROUP, GROUP), :] = jnp.where(row == GROUP - 1, 0.0, ending)
         out_ref[gate, pl.ds(rows, GROUP), :] = jnp.broadcast_to(begin, (GROUP, width))
-        line_ref[:, pl.ds((gate + 1) * width, width)] = begin
 
 
 def diagonals(weight_ref, hid, diag_ref):
@@ -141,10 +139,16 @@
 
 
 def base_kernel(step, count, *refs):
-    near, (weight_ref, inputs_ref, bias_ref, base_ref, lhs) = refs[: count // 2], refs[count // 2 :]
+    near, (weight_ref, inputs_ref, bias_ref, *lines, lhs) = refs[: count // 2], refs[count // 2 :]
+    base_ref = lines[0] if step else lines[1]
     height, _ = lhs.shape
     width = base_ref.shape[2]
     rows = inputs_ref.shape[1] - GROUP
+    if step == 0:
+        guess_ref, _, line_ref = lines
+        line_ref[:, pl.ds(0, width)] = guess_ref[0:1, :]
+        for gate in range(3):
+            line_ref[:, pl.ds((gate + 1) * width, width)] = inputs_ref[gate, pl.ds(rows, 1), :]
     hid = lax.axis_index("hid")
     own = hid % (count // 2)
     for offset in range(count // 2):
@@ -408,20 +412,16 @@
         name="merge",
     )(rounded, init_state[None])
     moved = [opening, *moved]
-    inputs, line = pl.pallas_call(
+    inputs = pl.pallas_call(
         prepare_kernel,
-        out_shape=[
-            jax.ShapeDtypeStruct((3, rows + GROUP, width), F32),
-            jax.ShapeDtypeStruct((1, 4 * width), F32),
-        ],
-        in_specs=vmem(4),
-        out_specs=vmem(2),
+        out_shape=jax.ShapeDtypeStruct((3, rows + GROUP, width), F32),
+        in_specs=vmem(3),
+        out_specs=vmem(1)[0],
         compiler_params=params(32),
         cost_estimate=cost(2 * COVER, 8 * rows * width),
         name="prepare",
-    )(token_ids[None], rest, table, z_bias[None])
-    edge = from_next(line, "tm")
-    state, following = rest, edge
+    )(token_ids[None], table, z_bias[None])
+    state = rest
 
     ends, diag = None, None
     for step in range(ITERS):
@@ -439,15 +439,23 @@
                     far[index][offset | bit] = swapped(far[index][offset], "hid", bit)
             bit //= 2
         height = whole.shape[0]
-        base = pl.pallas_call(
+        operands = [*[near[offset] for offset in range(count // 2)], weight, inputs, hn_bias[None]]
+        outs = [jax.ShapeDtypeStruct((3, height, width), F32)]
+        if step == 0:
+            operands.append(state)
+            outs.append(jax.ShapeDtypeStruct((1, 4 * width), F32))
+        base, *line = pl.pallas_call(
             functools.partial(base_kernel, step, count),
-            out_shape=jax.ShapeDtypeStruct((3, height, width), F32),
-            in_specs=vmem(count // 2 + 3),
-            out_specs=vmem(1)[0],
+            out_shape=outs,
+            in_specs=vmem(len(operands)),
+            out_specs=vmem(len(outs)),
             scratch_shapes=[pltpu.VMEM((height, full // 2), BF16)],
             compiler_params=params(16),
             cost_estimate=cost(3 * height * full * width, 3 * full * width),
-        )(*[near[offset] for offset in range(count // 2)], weight, inputs, hn_bias[None])
+        )(*operands)
+        if step == 0:
+            edge = from_next(line[0], "tm")
+            following = edge
         maps = []
         for index, (start, chunk) in enumerate(spans(step, rows)):
             last = index == CHUNKS - 1

time: 73.6 us -> 74.9 us (1.018)
  waiting for transfers between devices: 22.5 us -> 25 us
  blocking collectives: 23 us -> 22 us
    ppermute x13, waiting for transfers between devices: 22.5 us -> 24 us  [swapped(): return lax.ppermute(block, axis, route)]
    ppermute x1, waiting for transfers between devices: 0.01 us -> 1 us  [from_next(): return lax.ppermute(block, axis, route)]
    all_to_all x2, blocking collectives: 23 us -> 22 us  [newton(): every = lax.all_to_all(found[-1], 'tm', 0, 0)]
  transfers between devices with their start and end apart: 14 -> 14, of which waited for: 6 -> 7; matrix products, arithmetic and copies ran while one was open for 0% -> 0% of each run, Pallas kernels for 18% -> 17%
where the time goes in v10:
time: 74.9 us; the launch traced here: 74.6 us
  waiting for transfers between devices  25 us (33%)
  blocking collectives  22 us (29%)
  Pallas kernels  16.6 us (22%)
  starting transfers between devices  8.62 us (12%)
  other arithmetic  1.3 us (2%)
  between operations  1.05 us (1%)
    ppermute x13, waiting for transfers between devices, swapped(): return lax.ppermute(block, axis, route)  24 us
    all_to_all x2, blocking collectives, newton(): every = lax.all_to_all(found[-1], 'tm', 0, 0)  22 us
    ppermute x13, starting transfers between devices, swapped(): return lax.ppermute(block, axis, route)  7.33 us
    pallas_call x4, Pallas kernels, newton(): pl.pallas_call(functools.partial(step_kernel, count, index, start, chunk,...  6.38 us
    pallas_call x2, Pallas kernels, newton(): pl.pallas_call(functools.partial(base_kernel, step, count), out_shape=out...  3.89 us
    pallas_call x4, Pallas kernels, newton(): pl.pallas_call(functools.partial(direct_kernel, start, count), out_shape=...  2.47 us
    pallas_call x2, Pallas kernels, newton(): pl.pallas_call(functools.partial(apply_kernel, step), out_shape=outs, in_...  1.55 us
    pallas_call x1, Pallas kernels, newton(): pl.pallas_call(prepare_kernel, out_shape=jax.ShapeDtypeStruct((3, rows +...  1.55 us
  transfers between devices with their start and end apart: 14, of which 7 were waited for; matrix products, arithmetic and copies ran while one was open for 0% of the time, Pallas kernels for 17%

profile of v10, /device:TPU:0, one launch (start us, length us, event | category | flops | bytes accessed | tf_op | source)
XLA Modules:
  0.0 74.6 jit_solution(15371697163260804744)
XLA Ops:
  0.6 1.3 %convert_element_type.3.rounded_ref = bf16[512,512]{1,0:T(8,128)(2,1)S(1)} convert(f32[512,512]{1,0:T(8,128)} %refs_4_.1) | non-fusion elementwise | flops 262144 | bytes 1572864 | tf_op jit(solution)/shard_map/convert_element_type | solution.py:399
  2.0 3.1 %collective-permute-start = (bf16[320,512]{1,0:T(8,128)(2,1)S(1)}, bf16[320,512]{1,0:T(8,128)(2,1)S(1)}, u32[]{:S(2)}, u32[]{:S(2)}) collective-permute-start(bf16[320,512]{1,0:T(8,128)(2,1)S(1)} %slice.3), channel_id=1, source_target_pairs={{0,2},{1,3},{2,0},{3,1},{4,6},{5,7},{6,4},{7,5},{8,10},{9,11},{10,... | collective-permute-start | bytes 983048 | tf_op jit(solution)/shard_map/ppermute | solution.py:26
  5.3 8.3 %collective-permute-done.far_ref = bf16[320,512]{1,0:T(8,128)(2,1)S(1)} collective-permute-done((bf16[320,512]{1,0:T(8,128)(2,1)S(1)}, bf16[320,512]{1,0:T(8,128)(2,1)S(1)}, u32[]{:S(2)}, u32[]{:S(2)}) %collective-permute-start) | collective-permute-done | bytes 327712 | tf_op jit(solution)/shard_map/ppermute | solution.py:26
  13.7 1.5 %prepare.1.refs_3_ = f32[3,520,512]{2,1,0:T(8,128)S(1)} custom-call(s32[1,512]{1,0:T(1,128)S(1)} %bitcast.26, f32[3,256,512]{2,1,0:T(8,128)S(1)} %bitcast.25, f32[1,512]{1,0:T(1,128)S(1)} %bitcast.27), custom_call_target="tpu_custom_call" | custom-call | flops 4000000000 | bytes 2097152 | tf_op jit(solution)/shard_map/prepare/pallas_call | solution.py:415
  15.2 1.9 %collective-permute-done.3.far_ref = bf16[200,512]{1,0:T(8,128)(2,1)S(1)} collective-permute-done((bf16[200,512]{1,0:T(8,128)(2,1)S(1)}, bf16[200,512]{1,0:T(8,128)(2,1)S(1)}, u32[]{:S(2)}, u32[]{:S(2)}) %collective-permute-start.3) | collective-permute-done | bytes 204832 | tf_op jit(solution)/shard_map/ppermute | solution.py:26
  17.2 2.0 %shard_map.86 = (f32[3,520,512]{2,1,0:T(8,128)S(1)}, f32[1,2048]{1,0:T(1,128)S(1)}) custom-call(bf16[520,512]{1,0:T(8,128)(2,1)S(1)} %get-tuple-element.29.refs_0_, bf16[520,512]{1,0:T(8,128)(2,1)S(1)} %collective-permute-done.2.refs_1_, bf16[3,2048,512]{2,1,0:T(8,128)(2,1)S(1)} %bitcast.8, f32[3,520,512]{2,1,0:T(8,128)S(1)} %prepare.1.refs_3_, ...), custom_call_target="tpu_custom_call" | custom-call | flops 1635778560 | bytes 3145728 | tf_op jit(solution)/shard_map/pallas_call | solution.py:447
  19.2 1.3 %collective-permute-start.5 = (f32[1,2048]{1,0:T(1,128)S(1)}, f32[1,2048]{1,0:T(1,128)S(1)}, u32[]{:S(2)}, u32[]{:S(2)}) collective-permute-start(f32[1,2048]{1,0:T(1,128)S(1)} %get-tuple-element.35), channel_id=1, source_target_pairs={{4,0},{8,4},{12,8},{16,12},{20,16},{24,20},{28,24},{5,1},{9,5},{13... | collective-permute-start | bytes 24584 | tf_op jit(solution)/shard_map/ppermute | solution.py:31
  21.0 0.7 shard_map.87.refs_2_
  21.7 2.0 %shard_map.88 = (f32[320,512]{1,0:T(8,128)S(1)}, f32[320,512]{1,0:T(8,128)S(1)}, f32[5,512]{1,0:T(8,128)S(1)}, f32[24,512]{1,0:T(8,128)S(1)}) custom-call(bf16[320,512]{1,0:T(8,128)(2,1)S(1)} %collective-permute-done.1.refs_0_, bf16[3,2048,512]{2,1,0:T(8,128)(2,1)S(1)} %bitcast.11, f32[3,320,512]{2,1,0:T(8,128)S(1)} %shard_map.87.refs_2_, ...), custom_call_target="tpu_custom_call" | custom-call | flops 1006632960 | bytes 3145728 | tf_op jit(solution)/shard_map/pallas_call | solution.py:490
  23.7 1.0 %collective-permute-done.5.refs_6_.refs_7_ = f32[1,2048]{1,0:T(1,128)S(1)} collective-permute-done((f32[1,2048]{1,0:T(1,128)S(1)}, f32[1,2048]{1,0:T(1,128)S(1)}, u32[]{:S(2)}, u32[]{:S(2)}) %collective-permute-start.5) | collective-permute-done | bytes 8224 | tf_op jit(solution)/shard_map/ppermute | solution.py:31
  24.7 1.2 %shard_map.90 = (f32[192,512]{1,0:T(8,128)S(1)}, f32[192,512]{1,0:T(8,128)S(1)}, f32[5,512]{1,0:T(8,128)S(1)}, f32[8,8,128]{2,1,0:T(8,128)S(1)}) custom-call(bf16[200,512]{1,0:T(8,128)(2,1)S(1)} %collective-permute-done.4.refs_0_, bf16[3,2048,512]{2,1,0:T(8,128)(2,1)S(1)} %bitcast.12, f32[3,200,512]{2,1,0:T(8,128)S(1)} %shard_map.89.refs_2_, ...), custom_call_target="tpu_custom_call" | custom-call | flops 629145600 | bytes 3145728 | tf_op jit(solution)/shard_map/pallas_call | solution.py:490
  26.0 12.7 %all_to_all.10.refs_5_ = f32[8,8,128]{2,1,0:T(8,128)S(1)} all-to-all(f32[8,8,128]{2,1,0:T(8,128)S(1)} %get-tuple-element.41), channel_id=1, replica_groups=mesh['tm'=8,'hid'=4] {'tm'}, dimensions={0} | all-to-all | bytes 65536 | tf_op jit(solution)/shard_map/all_to_all | solution.py:503
  39.1 1.6 %collective-permute-start.6 = (bf16[304,512]{1,0:T(8,128)(2,1)S(1)}, bf16[304,512]{1,0:T(8,128)(2,1)S(1)}, u32[]{:S(2)}, u32[]{:S(2)}) collective-permute-start(bf16[304,512]{1,0:T(8,128)(2,1)S(1)} %get-tuple-element.42), channel_id=1, source_target_pairs={{0,2},{1,3},{2,0},{3,1},{4,6},{5,7},{6,4},{7,5},{8,10},{9,11},{10,... | collective-permute-start | bytes 933896 | tf_op jit(solution)/shard_map/ppermute | solution.py:26
  41.1 8.2 %collective-permute-done.6.far_ref = bf16[304,512]{1,0:T(8,128)(2,1)S(1)} collective-permute-done((bf16[304,512]{1,0:T(8,128)(2,1)S(1)}, bf16[304,512]{1,0:T(8,128)(2,1)S(1)}, u32[]{:S(2)}, u32[]{:S(2)}) %collective-permute-start.6) | collective-permute-done | bytes 311328 | tf_op jit(solution)/shard_map/ppermute | solution.py:26
  49.4 4.0 %collective-permute-done.9.far_ref = bf16[208,512]{1,0:T(8,128)(2,1)S(1)} collective-permute-done((bf16[208,512]{1,0:T(8,128)(2,1)S(1)}, bf16[208,512]{1,0:T(8,128)(2,1)S(1)}, u32[]{:S(2)}, u32[]{:S(2)}) %collective-permute-start.9) | collective-permute-done | bytes 213024 | tf_op jit(solution)/shard_map/ppermute | solution.py:26
  53.4 1.9 %shard_map.92.base_ref = f32[3,512,512]{2,1,0:T(8,128)S(1)} custom-call(bf16[512,512]{1,0:T(8,128)(2,1)S(1)} %get-tuple-element.43.refs_0_, bf16[512,512]{1,0:T(8,128)(2,1)S(1)} %collective-permute-done.8.refs_1_, bf16[3,2048,512]{2,1,0:T(8,128)(2,1)S(1)} %bitcast.13, f32[3,520,512]{2,1,0:T(8,128)S(1)} %prepare.1.refs_3_, f32[1,512]{1,0:T(1,128)S(1)} %bitcast.24), custom_call_target="tpu_custom_call" | custom-call | flops 1610612736 | bytes 3145728 | tf_op jit(solution)/shard_map/pallas_call | solution.py:447
  55.8 0.7 shard_map.93.refs_2_
  56.6 1.8 %shard_map.94 = (f32[304,512]{1,0:T(8,128)S(1)}, f32[304,512]{1,0:T(8,128)S(1)}, f32[5,512]{1,0:T(8,128)S(1)}) custom-call(bf16[304,512]{1,0:T(8,128)(2,1)S(1)} %collective-permute-done.7.refs_0_, bf16[3,2048,512]{2,1,0:T(8,128)(2,1)S(1)} %bitcast.16, f32[3,304,512]{2,1,0:T(8,128)S(1)} %shard_map.93.refs_2_, f32[3,520,512]{2,1,0:T(8,128)S(1)} %prepare.1.refs_3_, ...), custom_call_target="tpu_custom_call" | custom-call | flops 956301312 | bytes 3145728 | tf_op jit(solution)/shard_map/pallas_call | solution.py:490
  58.4 1.4 %shard_map.96 = (f32[208,512]{1,0:T(8,128)S(1)}, f32[208,512]{1,0:T(8,128)S(1)}, f32[5,512]{1,0:T(8,128)S(1)}, f32[8,9,128]{2,1,0:T(8,128)S(1)}) custom-call(bf16[208,512]{1,0:T(8,128)(2,1)S(1)} %collective-permute-done.10.refs_0_, bf16[3,2048,512]{2,1,0:T(8,128)(2,1)S(1)} %bitcast.17, f32[3,208,512]{2,1,0:T(8,128)S(1)} %shard_map.95.refs_2_, ...), custom_call_target="tpu_custom_call" | custom-call | flops 654311424 | bytes 3145728 | tf_op jit(solution)/shard_map/pallas_call | solution.py:490
  59.7 9.3 %all_to_all.11.refs_5_.all_ref = f32[8,9,128]{2,1,0:T(8,128)S(1)} all-to-all(f32[8,9,128]{2,1,0:T(8,128)S(1)} %get-tuple-element.53), channel_id=1, replica_groups=mesh['tm'=8,'hid'=4] {'tm'}, dimensions={0} | all-to-all | bytes 73728 | tf_op jit(solution)/shard_map/all_to_all | solution.py:503
  69.2 1.6 %collective-permute-start.12 = (f32[1,128]{1,0:T(1,128)S(1)}, f32[1,128]{1,0:T(1,128)S(1)}, u32[]{:S(2)}, u32[]{:S(2)}) collective-permute-start(f32[1,128]{1,0:T(1,128)S(1)} %sums.1.refs_0_), channel_id=1, source_target_pairs={{0,2},{1,3},{2,0},{3,1},{4,6},{5,7},{6,4},{7,5},{8,10},{9,11},{10,... | collective-permute-start | bytes 1544 | tf_op jit(solution)/shard_map/ppermute | solution.py:26
  71.0 1.2 %shard_map.97 = f32[512,512]{1,0:T(8,128)} custom-call(f32[304,512]{1,0:T(8,128)S(1)} %get-tuple-element.45.refs_0_, f32[304,512]{1,0:T(8,128)S(1)} %get-tuple-element.46.refs_1_, f32[208,512]{1,0:T(8,128)S(1)} %get-tuple-element.50.refs_2_, f32[208,512]{1,0:T(8,128)S(1)} %get-tuple-element.51.refs_3_, f32[5,512]{1,0:T(8,128)S(1)} %get-tuple-element.52.refs_4_, ...), custom_call_target="tpu_custom_call" | custom-call | flops 524288 | bytes 4194304 | tf_op jit(solution)/shard_map/pallas_call | solution.py:521
  72.8 0.9 %collective-permute-done.13.refs_3_ = f32[1,128]{1,0:T(1,128)S(1)} collective-permute-done((f32[1,128]{1,0:T(1,128)S(1)}, f32[1,128]{1,0:T(1,128)S(1)}, u32[]{:S(2)}, u32[]{:S(2)}) %collective-permute-start.13) | collective-permute-done | bytes 544 | tf_op jit(solution)/shard_map/ppermute | solution.py:26
  73.8 0.7 norm.1
  (41 shorter events, 3.2 us)
Async XLA Ops:
  0.6 4.4 %copy-start.1 = (f32[512]{0:T(512)S(1)}, f32[512]{0:T(512)}, u32[]{:S(2)}) copy-start(f32[512]{0:T(512)} %param.12) | copy-start | bytes 6148
  2.0 11.6 %collective-permute-start = (bf16[320,512]{1,0:T(8,128)(2,1)S(1)}, bf16[320,512]{1,0:T(8,128)(2,1)S(1)}, u32[]{:S(2)}, u32[]{:S(2)}) collective-permute-start(bf16[320,512]{1,0:T(8,128)(2,1)S(1)} %slice.3), channel_id=1, source_target_pairs={{0,2},{1,3},{2,0},{3,1},{4,6},{5,7},{6,4},{7,5},{8,10},{9,11},{10,... | collective-permute-start | bytes 983048 | tf_op jit(solution)/shard_map/ppermute | solution.py:26
  5.0 8.6 %copy-start.3 = (f32[256,3,512]{2,0,1:T(8,128)S(1)}, f32[256,3,512]{2,0,1:T(8,128)}, u32[]{:S(2)}) copy-start(f32[256,3,512]{2,0,1:T(8,128)} %param.8) | copy-start | bytes 4718596
  5.0 8.6 %copy-start.4 = (s32[512]{0:T(512)S(1)}, s32[512]{0:T(512)}, u32[]{:S(2)}) copy-start(s32[512]{0:T(512)} %param.7) | copy-start | bytes 6148
  5.0 8.6 %copy-start.5 = (f32[512]{0:T(512)S(1)}, f32[512]{0:T(512)}, u32[]{:S(2)}) copy-start(f32[512]{0:T(512)} %param.10) | copy-start | bytes 6148
  5.1 12.0 %collective-permute-start.2 = (bf16[520,512]{1,0:T(8,128)(2,1)S(1)}, bf16[520,512]{1,0:T(8,128)(2,1)S(1)}, u32[]{:S(2)}, u32[]{:S(2)}) collective-permute-start(bf16[520,512]{1,0:T(8,128)(2,1)S(1)} %get-tuple-element.29.refs_0_), channel_id=1, source_target_pairs={{0,1},{1,0},{2,3},{3,2},{4,5},{5,4},{6,7},{7,6},{8,9},{9,8},{10,11... | collective-permute-start | bytes 1597448 | tf_op jit(solution)/shard_map/ppermute | solution.py:26
  5.2 11.9 %collective-permute-start.3 = (bf16[200,512]{1,0:T(8,128)(2,1)S(1)}, bf16[200,512]{1,0:T(8,128)(2,1)S(1)}, u32[]{:S(2)}, u32[]{:S(2)}) collective-permute-start(bf16[200,512]{1,0:T(8,128)(2,1)S(1)} %get-tuple-element.34), channel_id=1, source_target_pairs={{0,2},{1,3},{2,0},{3,1},{4,6},{5,7},{6,4},{7,5},{8,10},{9,11},{10,... | collective-permute-start | bytes 614408 | tf_op jit(solution)/shard_map/ppermute | solution.py:26
  13.6 8.1 %collective-permute-start.1 = (bf16[320,512]{1,0:T(8,128)(2,1)S(1)}, bf16[320,512]{1,0:T(8,128)(2,1)S(1)}, u32[]{:S(2)}, u32[]{:S(2)}) collective-permute-start(bf16[320,512]{1,0:T(8,128)(2,1)S(1)} %collective-permute-done.far_ref), channel_id=1, source_target_pairs={{0,1},{1,0},{2,3},{3,2},{4,5},{5,4},{6,7},{7,6},{8,9},{9,8},{10,11... | collective-permute-start | bytes 983048 | tf_op jit(solution)/shard_map/ppermute | solution.py:26
  13.6 3.5 %slice-start = ((s8[6291456]{0:T(1024)(128)(4,1)}), s8[4194304]{0:T(1024)(128)(4,1)S(1)}, s32[]{:S(2)}) async-start(s8[6291456]{0:T(1024)(128)(4,1)} %bitcast.6), calls=%async_computation.2 | async-start | bytes 8388608
  13.6 3.5 %slice-start.1 = ((s8[6291456]{0:T(1024)(128)(4,1)}), s8[2097152]{0:T(1024)(128)(4,1)S(1)}, s32[]{:S(2)}) async-start(s8[6291456]{0:T(1024)(128)(4,1)} %bitcast.6), calls=%async_computation.3 | async-start | bytes 4194304
  13.6 3.5 %copy-start = (f32[512,512]{1,0:T(8,128)S(1)}, f32[512,512]{1,0:T(8,128)}, u32[]{:S(2)}) copy-start(f32[512,512]{1,0:T(8,128)} %refs_4_.1) | copy-start | bytes 3145732
  13.6 3.5 %copy-start.2 = (f32[512]{0:T(512)S(1)}, f32[512]{0:T(512)}, u32[]{:S(2)}) copy-start(f32[512]{0:T(512)} %param.11) | copy-start | bytes 6148
  17.1 6.6 %collective-permute-start.4 = (bf16[200,512]{1,0:T(8,128)(2,1)S(1)}, bf16[200,512]{1,0:T(8,128)(2,1)S(1)}, u32[]{:S(2)}, u32[]{:S(2)}) collective-permute-start(bf16[200,512]{1,0:T(8,128)(2,1)S(1)} %collective-permute-done.3.far_ref), channel_id=1, source_target_pairs={{0,1},{1,0},{2,3},{3,2},{4,5},{5,4},{6,7},{7,6},{8,9},{9,8},{10,11... | collective-permute-start | bytes 614408 | tf_op jit(solution)/shard_map/ppermute | solution.py:26
  19.2 5.5 %collective-permute-start.5 = (f32[1,2048]{1,0:T(1,128)S(1)}, f32[1,2048]{1,0:T(1,128)S(1)}, u32[]{:S(2)}, u32[]{:S(2)}) collective-permute-start(f32[1,2048]{1,0:T(1,128)S(1)} %get-tuple-element.35), channel_id=1, source_target_pairs={{4,0},{8,4},{12,8},{16,12},{20,16},{24,20},{28,24},{5,1},{9,5},{13... | collective-permute-start | bytes 24584 | tf_op jit(solution)/shard_map/ppermute | solution.py:31
  39.0 14.4 %collective-permute-start.8 = (bf16[512,512]{1,0:T(8,128)(2,1)S(1)}, bf16[512,512]{1,0:T(8,128)(2,1)S(1)}, u32[]{:S(2)}, u32[]{:S(2)}) collective-permute-start(bf16[512,512]{1,0:T(8,128)(2,1)S(1)} %get-tuple-element.43.refs_0_), channel_id=1, source_target_pairs={{0,1},{1,0},{2,3},{3,2},{4,5},{5,4},{6,7},{7,6},{8,9},{9,8},{10,11... | collective-permute-start | bytes 1572872 | tf_op jit(solution)/shard_map/ppermute | solution.py:26
  39.1 10.3 %collective-permute-start.6 = (bf16[304,512]{1,0:T(8,128)(2,1)S(1)}, bf16[304,512]{1,0:T(8,128)(2,1)S(1)}, u32[]{:S(2)}, u32[]{:S(2)}) collective-permute-start(bf16[304,512]{1,0:T(8,128)(2,1)S(1)} %get-tuple-element.42), channel_id=1, source_target_pairs={{0,2},{1,3},{2,0},{3,1},{4,6},{5,7},{6,4},{7,5},{8,10},{9,11},{10,... | collective-permute-start | bytes 933896 | tf_op jit(solution)/shard_map/ppermute | solution.py:26
  40.6 12.7 %collective-permute-start.9 = (bf16[208,512]{1,0:T(8,128)(2,1)S(1)}, bf16[208,512]{1,0:T(8,128)(2,1)S(1)}, u32[]{:S(2)}, u32[]{:S(2)}) collective-permute-start(bf16[208,512]{1,0:T(8,128)(2,1)S(1)} %get-tuple-element.47), channel_id=1, source_target_pairs={{0,2},{1,3},{2,0},{3,1},{4,6},{5,7},{6,4},{7,5},{8,10},{9,11},{10,... | collective-permute-start | bytes 638984 | tf_op jit(solution)/shard_map/ppermute | solution.py:26
  49.4 7.2 %collective-permute-start.7 = (bf16[304,512]{1,0:T(8,128)(2,1)S(1)}, bf16[304,512]{1,0:T(8,128)(2,1)S(1)}, u32[]{:S(2)}, u32[]{:S(2)}) collective-permute-start(bf16[304,512]{1,0:T(8,128)(2,1)S(1)} %collective-permute-done.6.far_ref), channel_id=1, source_target_pairs={{0,1},{1,0},{2,3},{3,2},{4,5},{5,4},{6,7},{7,6},{8,9},{9,8},{10,11... | collective-permute-start | bytes 933896 | tf_op jit(solution)/shard_map/ppermute | solution.py:26
  53.4 5.0 %collective-permute-start.10 = (bf16[208,512]{1,0:T(8,128)(2,1)S(1)}, bf16[208,512]{1,0:T(8,128)(2,1)S(1)}, u32[]{:S(2)}, u32[]{:S(2)}) collective-permute-start(bf16[208,512]{1,0:T(8,128)(2,1)S(1)} %collective-permute-done.9.far_ref), channel_id=1, source_target_pairs={{0,1},{1,0},{2,3},{3,2},{4,5},{5,4},{6,7},{7,6},{8,9},{9,8},{10,11... | collective-permute-start | bytes 638984 | tf_op jit(solution)/shard_map/ppermute | solution.py:26
  69.1 3.1 %collective-permute-start.11 = (f32[1,128]{1,0:T(1,128)S(1)}, f32[1,128]{1,0:T(1,128)S(1)}, u32[]{:S(2)}, u32[]{:S(2)}) collective-permute-start(f32[1,128]{1,0:T(1,128)S(1)} %sums.1.refs_0_), channel_id=1, source_target_pairs={{0,1},{1,0},{2,3},{3,2},{4,5},{5,4},{6,7},{7,6},{8,9},{9,8},{10,11... | collective-permute-start | bytes 1544 | tf_op jit(solution)/shard_map/ppermute | solution.py:26
  69.2 3.6 %collective-permute-start.12 = (f32[1,128]{1,0:T(1,128)S(1)}, f32[1,128]{1,0:T(1,128)S(1)}, u32[]{:S(2)}, u32[]{:S(2)}) collective-permute-start(f32[1,128]{1,0:T(1,128)S(1)} %sums.1.refs_0_), channel_id=1, source_target_pairs={{0,2},{1,3},{2,0},{3,1},{4,6},{5,7},{6,4},{7,5},{8,10},{9,11},{10,... | collective-permute-start | bytes 1544 | tf_op jit(solution)/shard_map/ppermute | solution.py:26
  70.8 3.0 %collective-permute-start.13 = (f32[1,128]{1,0:T(1,128)S(1)}, f32[1,128]{1,0:T(1,128)S(1)}, u32[]{:S(2)}, u32[]{:S(2)}) collective-permute-start(f32[1,128]{1,0:T(1,128)S(1)} %sums.1.refs_0_), channel_id=1, source_target_pairs={{0,3},{1,2},{2,1},{3,0},{4,7},{5,6},{6,5},{7,4},{8,11},{9,10},{10,... | collective-permute-start | bytes 1544 | tf_op jit(solution)/shard_map/ppermute | solution.py:26

commit v11 on v10

--- a/solution.py
+++ b/solution.py
@@ -9,7 +9,7 @@
 
 
 ITERS = 2
-SHARES = ((10, 6), (19, 13))
+SHARES = ((9, 7), (19, 13))
 CHUNKS = len(SHARES[0])
 GROUP = 8
 EXTRA = 8
@@ -306,11 +306,8 @@
         if last:
             send_a = jnp.where(is_first, 0.0, run_a[0:1])
             send_b = jnp.where(is_first, run_a[0:1] * begin + run_b[0:1], run_b[0:1])
-            for part in range(TILE // LANES):
-                at = tile * (TILE // LANES) + part
-                for line, sent in ((at, send_a), (width // LANES + at, send_b)):
-                    picked = sent[:, part * LANES : (part + 1) * LANES]
-                    send_ref[:, pl.ds(line, 1), :] = jnp.broadcast_to(picked[None], (copies, 1, LANES))
+            for at, sent in ((0, send_a), (width, send_b)):
+                send_ref[:, :, pl.ds(at + tile * TILE, TILE)] = jnp.broadcast_to(sent[None], (copies, 1, TILE))
 
     dots(0)
     for tile in range(1, tiles):
@@ -324,7 +321,7 @@
             part = sum(ends_ref[pl.ds(line, 1), pl.ds(at, LANES)] for at in range(0, width, LANES))
             part = part + pltpu.roll(part, LANES // 2, 1)
             sums = jnp.where(lane // (LANES // 2) == half, part, sums)
-        send_ref[:, pl.ds(2 * width // LANES, 1), :] = jnp.broadcast_to(sums[None], (copies, 1, LANES))
+        send_ref[:, :, pl.ds(2 * width, LANES)] = jnp.broadcast_to(sums[None], (copies, 1, LANES))
 
 
 def apply_kernel(step, *refs):
@@ -333,17 +330,14 @@
     begin_ref, all_ref, state_ref = refs[:3]
     outs = refs[3:]
     rows, width = state_ref.shape
-    lines = width // LANES
     place = lax.axis_index("tm")
     peers = all_ref.shape[0]
 
     def compose(peer, enter):
-        moved = all_ref[peer, pl.ds(0, lines), :] * enter + all_ref[peer, pl.ds(lines, lines), :]
+        moved = all_ref[peer, :, pl.ds(0, width)] * enter + all_ref[peer, :, pl.ds(width, width)]
         return jnp.where(peer < place, moved, enter)
 
-    begin = jnp.concatenate([begin_ref[3:4, pl.ds(at * LANES, LANES)] for at in range(lines)], axis=0)
-    found = lax.fori_loop(0, peers, compose, begin, unroll=min(peers, 8))
-    enter = jnp.concatenate([found[at : at + 1] for at in range(lines)], axis=1)
+    enter = lax.fori_loop(0, peers, compose, begin_ref[3:4, :], unroll=min(peers, 8))
     height = 2 * GROUP
     row = lax.broadcasted_iota(jnp.int32, (height, width), 0)
     enter = jnp.broadcast_to(enter, (height, width))
@@ -375,7 +369,7 @@
 
 
 def sums_kernel(all_ref, out_ref):
-    out_ref[...] = jnp.sum(all_ref[:, pl.ds(all_ref.shape[1] - 1, 1), :], axis=0)
+    out_ref[...] = jnp.sum(all_ref[:, :, pl.ds(all_ref.shape[2] - LANES, LANES)], axis=0)
 
 
 def norm_kernel(size, *refs):
@@ -393,7 +387,6 @@
     blocks_tm = lax.axis_size("tm")
     weight = jnp.transpose(recur_weight, (1, 0, 2))
     table = jnp.transpose(input_table, (1, 0, 2))
-    lines = width // LANES
 
     first = spans(0, rows)[0][1]
     rounded, rest = lax.optimization_barrier((guess.astype(BF16), guess))
@@ -486,7 +479,7 @@
                 outs.append(jax.ShapeDtypeStruct((3 * GROUP, width), F32))
             copies = blocks_tm
             if last:
-                outs.append(jax.ShapeDtypeStruct((copies, 2 * lines + final, LANES), F32))
+                outs.append(jax.ShapeDtypeStruct((copies, 1, 2 * width + final * LANES), F32))
             found = pl.pallas_call(
                 functools.partial(step_kernel, count, index, start, chunk, step, copies),
                 out_shape=outs,

time: 74.9 us -> 74.6 us (level)
  no operation moved by 1% of the time
where the time goes in v11:
time: 74.6 us; the launch traced here: 74.4 us
  waiting for transfers between devices  25.1 us (34%)
  blocking collectives  21.6 us (29%)
  Pallas kernels  16.6 us (22%)
  starting transfers between devices  8.62 us (12%)
  other arithmetic  1.3 us (2%)
  between operations  1.05 us (1%)
    ppermute x13, waiting for transfers between devices, swapped(): return lax.ppermute(block, axis, route)  24 us
    all_to_all x2, blocking collectives, newton(): every = lax.all_to_all(found[-1], 'tm', 0, 0)  21.6 us
    ppermute x13, starting transfers between devices, swapped(): return lax.ppermute(block, axis, route)  7.33 us
    pallas_call x4, Pallas kernels, newton(): pl.pallas_call(functools.partial(step_kernel, count, index, start, chunk,...  6.39 us
    pallas_call x2, Pallas kernels, newton(): pl.pallas_call(functools.partial(base_kernel, step, count), out_shape=out...  3.89 us
    pallas_call x4, Pallas kernels, newton(): pl.pallas_call(functools.partial(direct_kernel, start, count), out_shape=...  2.47 us
    pallas_call x2, Pallas kernels, newton(): pl.pallas_call(functools.partial(apply_kernel, step), out_shape=outs, in_...  1.56 us
    pallas_call x1, Pallas kernels, newton(): pl.pallas_call(prepare_kernel, out_shape=jax.ShapeDtypeStruct((3, rows +...  1.55 us
  transfers between devices with their start and end apart: 14, of which 7 were waited for; matrix products, arithmetic and copies ran while one was open for 0% of the time, Pallas kernels for 17%

profile of v11, /device:TPU:0, one launch (start us, length us, event | category | flops | bytes accessed | tf_op | source)
XLA Modules:
  0.0 74.4 jit_solution(10837731168993997902)
XLA Ops:
  0.6 1.3 %convert_element_type.3.rounded_ref = bf16[512,512]{1,0:T(8,128)(2,1)S(1)} convert(f32[512,512]{1,0:T(8,128)} %refs_4_.1) | non-fusion elementwise | flops 262144 | bytes 1572864 | tf_op jit(solution)/shard_map/convert_element_type | solution.py:392
  2.0 3.1 %collective-permute-start = (bf16[288,512]{1,0:T(8,128)(2,1)S(1)}, bf16[288,512]{1,0:T(8,128)(2,1)S(1)}, u32[]{:S(2)}, u32[]{:S(2)}) collective-permute-start(bf16[288,512]{1,0:T(8,128)(2,1)S(1)} %slice.3), channel_id=1, source_target_pairs={{0,2},{1,3},{2,0},{3,1},{4,6},{5,7},{6,4},{7,5},{8,10},{9,11},{10,... | collective-permute-start | bytes 884744 | tf_op jit(solution)/shard_map/ppermute | solution.py:26
  5.3 7.6 %collective-permute-done.far_ref = bf16[288,512]{1,0:T(8,128)(2,1)S(1)} collective-permute-done((bf16[288,512]{1,0:T(8,128)(2,1)S(1)}, bf16[288,512]{1,0:T(8,128)(2,1)S(1)}, u32[]{:S(2)}, u32[]{:S(2)}) %collective-permute-start) | collective-permute-done | bytes 294944 | tf_op jit(solution)/shard_map/ppermute | solution.py:26
  13.0 1.6 %prepare.1.refs_3_ = f32[3,520,512]{2,1,0:T(8,128)S(1)} custom-call(s32[1,512]{1,0:T(1,128)S(1)} %bitcast.26, f32[3,256,512]{2,1,0:T(8,128)S(1)} %bitcast.25, f32[1,512]{1,0:T(1,128)S(1)} %bitcast.27), custom_call_target="tpu_custom_call" | custom-call | flops 4000000000 | bytes 2097152 | tf_op jit(solution)/shard_map/prepare/pallas_call | solution.py:408
  14.5 2.6 %collective-permute-done.3.far_ref = bf16[232,512]{1,0:T(8,128)(2,1)S(1)} collective-permute-done((bf16[232,512]{1,0:T(8,128)(2,1)S(1)}, bf16[232,512]{1,0:T(8,128)(2,1)S(1)}, u32[]{:S(2)}, u32[]{:S(2)}) %collective-permute-start.3) | collective-permute-done | bytes 237600 | tf_op jit(solution)/shard_map/ppermute | solution.py:26
  17.2 2.0 %shard_map.86 = (f32[3,520,512]{2,1,0:T(8,128)S(1)}, f32[1,2048]{1,0:T(1,128)S(1)}) custom-call(bf16[520,512]{1,0:T(8,128)(2,1)S(1)} %get-tuple-element.29.refs_0_, bf16[520,512]{1,0:T(8,128)(2,1)S(1)} %collective-permute-done.2.refs_1_, bf16[3,2048,512]{2,1,0:T(8,128)(2,1)S(1)} %bitcast.8, f32[3,520,512]{2,1,0:T(8,128)S(1)} %prepare.1.refs_3_, ...), custom_call_target="tpu_custom_call" | custom-call | flops 1635778560 | bytes 3145728 | tf_op jit(solution)/shard_map/pallas_call | solution.py:440
  19.2 1.3 %collective-permute-start.5 = (f32[1,2048]{1,0:T(1,128)S(1)}, f32[1,2048]{1,0:T(1,128)S(1)}, u32[]{:S(2)}, u32[]{:S(2)}) collective-permute-start(f32[1,2048]{1,0:T(1,128)S(1)} %get-tuple-element.35), channel_id=1, source_target_pairs={{4,0},{8,4},{12,8},{16,12},{20,16},{24,20},{28,24},{5,1},{9,5},{13... | collective-permute-start | bytes 24584 | tf_op jit(solution)/shard_map/ppermute | solution.py:31
  21.1 0.7 shard_map.87.refs_2_
  21.7 1.8 %shard_map.88 = (f32[288,512]{1,0:T(8,128)S(1)}, f32[288,512]{1,0:T(8,128)S(1)}, f32[5,512]{1,0:T(8,128)S(1)}, f32[24,512]{1,0:T(8,128)S(1)}) custom-call(bf16[288,512]{1,0:T(8,128)(2,1)S(1)} %collective-permute-done.1.refs_0_, bf16[3,2048,512]{2,1,0:T(8,128)(2,1)S(1)} %bitcast.11, f32[3,288,512]{2,1,0:T(8,128)S(1)} %shard_map.87.refs_2_, ...), custom_call_target="tpu_custom_call" | custom-call | flops 905969664 | bytes 3145728 | tf_op jit(solution)/shard_map/pallas_call | solution.py:483
  23.5 1.2 %collective-permute-done.5.refs_6_.refs_7_ = f32[1,2048]{1,0:T(1,128)S(1)} collective-permute-done((f32[1,2048]{1,0:T(1,128)S(1)}, f32[1,2048]{1,0:T(1,128)S(1)}, u32[]{:S(2)}, u32[]{:S(2)}) %collective-permute-start.5) | collective-permute-done | bytes 8224 | tf_op jit(solution)/shard_map/ppermute | solution.py:31
  24.7 1.4 %shard_map.90 = (f32[224,512]{1,0:T(8,128)S(1)}, f32[224,512]{1,0:T(8,128)S(1)}, f32[5,512]{1,0:T(8,128)S(1)}, f32[8,1,1024]{2,1,0:T(1,128)S(1)}) custom-call(bf16[232,512]{1,0:T(8,128)(2,1)S(1)} %collective-permute-done.4.refs_0_, bf16[3,2048,512]{2,1,0:T(8,128)(2,1)S(1)} %bitcast.12, f32[3,232,512]{2,1,0:T(8,128)S(1)} %shard_map.89.refs_2_, ...), custom_call_target="tpu_custom_call" | custom-call | flops 729808896 | bytes 3145728 | tf_op jit(solution)/shard_map/pallas_call | solution.py:483
  26.1 12.5 %all_to_all.10.refs_5_ = f32[8,1,1024]{2,1,0:T(1,128)S(1)} all-to-all(f32[8,1,1024]{2,1,0:T(1,128)S(1)} %get-tuple-element.41), channel_id=1, replica_groups=mesh['tm'=8,'hid'=4] {'tm'}, dimensions={0} | all-to-all | bytes 65536 | tf_op jit(solution)/shard_map/all_to_all | solution.py:496
  39.1 1.6 %collective-permute-start.6 = (bf16[304,512]{1,0:T(8,128)(2,1)S(1)}, bf16[304,512]{1,0:T(8,128)(2,1)S(1)}, u32[]{:S(2)}, u32[]{:S(2)}) collective-permute-start(bf16[304,512]{1,0:T(8,128)(2,1)S(1)} %get-tuple-element.42), channel_id=1, source_target_pairs={{0,2},{1,3},{2,0},{3,1},{4,6},{5,7},{6,4},{7,5},{8,10},{9,11},{10,... | collective-permute-start | bytes 933896 | tf_op jit(solution)/shard_map/ppermute | solution.py:26
  41.2 8.2 %collective-permute-done.6.far_ref = bf16[304,512]{1,0:T(8,128)(2,1)S(1)} collective-permute-done((bf16[304,512]{1,0:T(8,128)(2,1)S(1)}, bf16[304,512]{1,0:T(8,128)(2,1)S(1)}, u32[]{:S(2)}, u32[]{:S(2)}) %collective-permute-start.6) | collective-permute-done | bytes 311328 | tf_op jit(solution)/shard_map/ppermute | solution.py:26
  49.4 4.0 %collective-permute-done.9.far_ref = bf16[208,512]{1,0:T(8,128)(2,1)S(1)} collective-permute-done((bf16[208,512]{1,0:T(8,128)(2,1)S(1)}, bf16[208,512]{1,0:T(8,128)(2,1)S(1)}, u32[]{:S(2)}, u32[]{:S(2)}) %collective-permute-start.9) | collective-permute-done | bytes 213024 | tf_op jit(solution)/shard_map/ppermute | solution.py:26
  53.4 1.9 %shard_map.92.base_ref = f32[3,512,512]{2,1,0:T(8,128)S(1)} custom-call(bf16[512,512]{1,0:T(8,128)(2,1)S(1)} %get-tuple-element.43.refs_0_, bf16[512,512]{1,0:T(8,128)(2,1)S(1)} %collective-permute-done.8.refs_1_, bf16[3,2048,512]{2,1,0:T(8,128)(2,1)S(1)} %bitcast.13, f32[3,520,512]{2,1,0:T(8,128)S(1)} %prepare.1.refs_3_, f32[1,512]{1,0:T(1,128)S(1)} %bitcast.24), custom_call_target="tpu_custom_call" | custom-call | flops 1610612736 | bytes 3145728 | tf_op jit(solution)/shard_map/pallas_call | solution.py:440
  55.9 0.7 shard_map.93.refs_2_
  56.6 1.8 %shard_map.94 = (f32[304,512]{1,0:T(8,128)S(1)}, f32[304,512]{1,0:T(8,128)S(1)}, f32[5,512]{1,0:T(8,128)S(1)}) custom-call(bf16[304,512]{1,0:T(8,128)(2,1)S(1)} %collective-permute-done.7.refs_0_, bf16[3,2048,512]{2,1,0:T(8,128)(2,1)S(1)} %bitcast.16, f32[3,304,512]{2,1,0:T(8,128)S(1)} %shard_map.93.refs_2_, f32[3,520,512]{2,1,0:T(8,128)S(1)} %prepare.1.refs_3_, ...), custom_call_target="tpu_custom_call" | custom-call | flops 956301312 | bytes 3145728 | tf_op jit(solution)/shard_map/pallas_call | solution.py:483
  58.4 1.4 %shard_map.96 = (f32[208,512]{1,0:T(8,128)S(1)}, f32[208,512]{1,0:T(8,128)S(1)}, f32[5,512]{1,0:T(8,128)S(1)}, f32[8,1,1152]{2,1,0:T(1,128)S(1)}) custom-call(bf16[208,512]{1,0:T(8,128)(2,1)S(1)} %collective-permute-done.10.refs_0_, bf16[3,2048,512]{2,1,0:T(8,128)(2,1)S(1)} %bitcast.17, f32[3,208,512]{2,1,0:T(8,128)S(1)} %shard_map.95.refs_2_, ...), custom_call_target="tpu_custom_call" | custom-call | flops 654311424 | bytes 3145728 | tf_op jit(solution)/shard_map/pallas_call | solution.py:483
  59.8 9.1 %all_to_all.11.refs_5_.all_ref = f32[8,1,1152]{2,1,0:T(1,128)S(1)} all-to-all(f32[8,1,1152]{2,1,0:T(1,128)S(1)} %get-tuple-element.53), channel_id=1, replica_groups=mesh['tm'=8,'hid'=4] {'tm'}, dimensions={0} | all-to-all | bytes 73728 | tf_op jit(solution)/shard_map/all_to_all | solution.py:496
  68.9 1.6 %collective-permute-start.12 = (f32[1,128]{1,0:T(1,128)S(1)}, f32[1,128]{1,0:T(1,128)S(1)}, u32[]{:S(2)}, u32[]{:S(2)}) collective-permute-start(f32[1,128]{1,0:T(1,128)S(1)} %sums.1.refs_0_), channel_id=1, source_target_pairs={{0,2},{1,3},{2,0},{3,1},{4,6},{5,7},{6,4},{7,5},{8,10},{9,11},{10,... | collective-permute-start | bytes 1544 | tf_op jit(solution)/shard_map/ppermute | solution.py:26
  70.8 1.2 %shard_map.97 = f32[512,512]{1,0:T(8,128)} custom-call(f32[304,512]{1,0:T(8,128)S(1)} %get-tuple-element.45.refs_0_, f32[304,512]{1,0:T(8,128)S(1)} %get-tuple-element.46.refs_1_, f32[208,512]{1,0:T(8,128)S(1)} %get-tuple-element.50.refs_2_, f32[208,512]{1,0:T(8,128)S(1)} %get-tuple-element.51.refs_3_, f32[5,512]{1,0:T(8,128)S(1)} %get-tuple-element.52.refs_4_, ...), custom_call_target="tpu_custom_call" | custom-call | flops 524288 | bytes 4194304 | tf_op jit(solution)/shard_map/pallas_call | solution.py:514
  72.6 0.9 %collective-permute-done.13.refs_3_ = f32[1,128]{1,0:T(1,128)S(1)} collective-permute-done((f32[1,128]{1,0:T(1,128)S(1)}, f32[1,128]{1,0:T(1,128)S(1)}, u32[]{:S(2)}, u32[]{:S(2)}) %collective-permute-start.13) | collective-permute-done | bytes 544 | tf_op jit(solution)/shard_map/ppermute | solution.py:26
  73.5 0.7 norm.1
  (41 shorter events, 3.2 us)
Async XLA Ops:
  0.6 4.4 %copy-start.1 = (f32[512]{0:T(512)S(1)}, f32[512]{0:T(512)}, u32[]{:S(2)}) copy-start(f32[512]{0:T(512)} %param.12) | copy-start | bytes 6148
  2.0 10.9 %collective-permute-start = (bf16[288,512]{1,0:T(8,128)(2,1)S(1)}, bf16[288,512]{1,0:T(8,128)(2,1)S(1)}, u32[]{:S(2)}, u32[]{:S(2)}) collective-permute-start(bf16[288,512]{1,0:T(8,128)(2,1)S(1)} %slice.3), channel_id=1, source_target_pairs={{0,2},{1,3},{2,0},{3,1},{4,6},{5,7},{6,4},{7,5},{8,10},{9,11},{10,... | collective-permute-start | bytes 884744 | tf_op jit(solution)/shard_map/ppermute | solution.py:26
  5.0 7.9 %copy-start.3 = (f32[256,3,512]{2,0,1:T(8,128)S(1)}, f32[256,3,512]{2,0,1:T(8,128)}, u32[]{:S(2)}) copy-start(f32[256,3,512]{2,0,1:T(8,128)} %param.8) | copy-start | bytes 4718596
  5.0 7.9 %copy-start.4 = (s32[512]{0:T(512)S(1)}, s32[512]{0:T(512)}, u32[]{:S(2)}) copy-start(s32[512]{0:T(512)} %param.7) | copy-start | bytes 6148
  5.0 7.9 %copy-start.5 = (f32[512]{0:T(512)S(1)}, f32[512]{0:T(512)}, u32[]{:S(2)}) copy-start(f32[512]{0:T(512)} %param.10) | copy-start | bytes 6148
  5.1 12.0 %collective-permute-start.2 = (bf16[520,512]{1,0:T(8,128)(2,1)S(1)}, bf16[520,512]{1,0:T(8,128)(2,1)S(1)}, u32[]{:S(2)}, u32[]{:S(2)}) collective-permute-start(bf16[520,512]{1,0:T(8,128)(2,1)S(1)} %get-tuple-element.29.refs_0_), channel_id=1, source_target_pairs={{0,1},{1,0},{2,3},{3,2},{4,5},{5,4},{6,7},{7,6},{8,9},{9,8},{10,11... | collective-permute-start | bytes 1597448 | tf_op jit(solution)/shard_map/ppermute | solution.py:26
  5.2 11.9 %collective-permute-start.3 = (bf16[232,512]{1,0:T(8,128)(2,1)S(1)}, bf16[232,512]{1,0:T(8,128)(2,1)S(1)}, u32[]{:S(2)}, u32[]{:S(2)}) collective-permute-start(bf16[232,512]{1,0:T(8,128)(2,1)S(1)} %get-tuple-element.34), channel_id=1, source_target_pairs={{0,2},{1,3},{2,0},{3,1},{4,6},{5,7},{6,4},{7,5},{8,10},{9,11},{10,... | collective-permute-start | bytes 712712 | tf_op jit(solution)/shard_map/ppermute | solution.py:26
  12.9 8.8 %collective-permute-start.1 = (bf16[288,512]{1,0:T(8,128)(2,1)S(1)}, bf16[288,512]{1,0:T(8,128)(2,1)S(1)}, u32[]{:S(2)}, u32[]{:S(2)}) collective-permute-start(bf16[288,512]{1,0:T(8,128)(2,1)S(1)} %collective-permute-done.far_ref), channel_id=1, source_target_pairs={{0,1},{1,0},{2,3},{3,2},{4,5},{5,4},{6,7},{7,6},{8,9},{9,8},{10,11... | collective-permute-start | bytes 884744 | tf_op jit(solution)/shard_map/ppermute | solution.py:26
  12.9 4.2 %slice-start = ((s8[6291456]{0:T(1024)(128)(4,1)}), s8[4194304]{0:T(1024)(128)(4,1)S(1)}, s32[]{:S(2)}) async-start(s8[6291456]{0:T(1024)(128)(4,1)} %bitcast.6), calls=%async_computation.2 | async-start | bytes 8388608
  12.9 4.2 %slice-start.1 = ((s8[6291456]{0:T(1024)(128)(4,1)}), s8[2097152]{0:T(1024)(128)(4,1)S(1)}, s32[]{:S(2)}) async-start(s8[6291456]{0:T(1024)(128)(4,1)} %bitcast.6), calls=%async_computation.3 | async-start | bytes 4194304
  12.9 4.2 %copy-start = (f32[512,512]{1,0:T(8,128)S(1)}, f32[512,512]{1,0:T(8,128)}, u32[]{:S(2)}) copy-start(f32[512,512]{1,0:T(8,128)} %refs_4_.1) | copy-start | bytes 3145732
  12.9 4.2 %copy-start.2 = (f32[512]{0:T(512)S(1)}, f32[512]{0:T(512)}, u32[]{:S(2)}) copy-start(f32[512]{0:T(512)} %param.11) | copy-start | bytes 6148
  17.1 6.4 %collective-permute-start.4 = (bf16[232,512]{1,0:T(8,128)(2,1)S(1)}, bf16[232,512]{1,0:T(8,128)(2,1)S(1)}, u32[]{:S(2)}, u32[]{:S(2)}) collective-permute-start(bf16[232,512]{1,0:T(8,128)(2,1)S(1)} %collective-permute-done.3.far_ref), channel_id=1, source_target_pairs={{0,1},{1,0},{2,3},{3,2},{4,5},{5,4},{6,7},{7,6},{8,9},{9,8},{10,11... | collective-permute-start | bytes 712712 | tf_op jit(solution)/shard_map/ppermute | solution.py:26
  19.2 5.5 %collective-permute-start.5 = (f32[1,2048]{1,0:T(1,128)S(1)}, f32[1,2048]{1,0:T(1,128)S(1)}, u32[]{:S(2)}, u32[]{:S(2)}) collective-permute-start(f32[1,2048]{1,0:T(1,128)S(1)} %get-tuple-element.35), channel_id=1, source_target_pairs={{4,0},{8,4},{12,8},{16,12},{20,16},{24,20},{28,24},{5,1},{9,5},{13... | collective-permute-start | bytes 24584 | tf_op jit(solution)/shard_map/ppermute | solution.py:31
  39.0 14.4 %collective-permute-start.8 = (bf16[512,512]{1,0:T(8,128)(2,1)S(1)}, bf16[512,512]{1,0:T(8,128)(2,1)S(1)}, u32[]{:S(2)}, u32[]{:S(2)}) collective-permute-start(bf16[512,512]{1,0:T(8,128)(2,1)S(1)} %get-tuple-element.43.refs_0_), channel_id=1, source_target_pairs={{0,1},{1,0},{2,3},{3,2},{4,5},{5,4},{6,7},{7,6},{8,9},{9,8},{10,11... | collective-permute-start | bytes 1572872 | tf_op jit(solution)/shard_map/ppermute | solution.py:26
  39.1 10.3 %collective-permute-start.6 = (bf16[304,512]{1,0:T(8,128)(2,1)S(1)}, bf16[304,512]{1,0:T(8,128)(2,1)S(1)}, u32[]{:S(2)}, u32[]{:S(2)}) collective-permute-start(bf16[304,512]{1,0:T(8,128)(2,1)S(1)} %get-tuple-element.42), channel_id=1, source_target_pairs={{0,2},{1,3},{2,0},{3,1},{4,6},{5,7},{6,4},{7,5},{8,10},{9,11},{10,... | collective-permute-start | bytes 933896 | tf_op jit(solution)/shard_map/ppermute | solution.py:26
  40.7 12.7 %collective-permute-start.9 = (bf16[208,512]{1,0:T(8,128)(2,1)S(1)}, bf16[208,512]{1,0:T(8,128)(2,1)S(1)}, u32[]{:S(2)}, u32[]{:S(2)}) collective-permute-start(bf16[208,512]{1,0:T(8,128)(2,1)S(1)} %get-tuple-element.47), channel_id=1, source_target_pairs={{0,2},{1,3},{2,0},{3,1},{4,6},{5,7},{6,4},{7,5},{8,10},{9,11},{10,... | collective-permute-start | bytes 638984 | tf_op jit(solution)/shard_map/ppermute | solution.py:26
  49.4 7.2 %collective-permute-start.7 = (bf16[304,512]{1,0:T(8,128)(2,1)S(1)}, bf16[304,512]{1,0:T(8,128)(2,1)S(1)}, u32[]{:S(2)}, u32[]{:S(2)}) collective-permute-start(bf16[304,512]{1,0:T(8,128)(2,1)S(1)} %collective-permute-done.6.far_ref), channel_id=1, source_target_pairs={{0,1},{1,0},{2,3},{3,2},{4,5},{5,4},{6,7},{7,6},{8,9},{9,8},{10,11... | collective-permute-start | bytes 933896 | tf_op jit(solution)/shard_map/ppermute | solution.py:26
  53.4 5.0 %collective-permute-start.10 = (bf16[208,512]{1,0:T(8,128)(2,1)S(1)}, bf16[208,512]{1,0:T(8,128)(2,1)S(1)}, u32[]{:S(2)}, u32[]{:S(2)}) collective-permute-start(bf16[208,512]{1,0:T(8,128)(2,1)S(1)} %collective-permute-done.9.far_ref), channel_id=1, source_target_pairs={{0,1},{1,0},{2,3},{3,2},{4,5},{5,4},{6,7},{7,6},{8,9},{9,8},{10,11... | collective-permute-start | bytes 638984 | tf_op jit(solution)/shard_map/ppermute | solution.py:26
  68.8 3.1 %collective-permute-start.11 = (f32[1,128]{1,0:T(1,128)S(1)}, f32[1,128]{1,0:T(1,128)S(1)}, u32[]{:S(2)}, u32[]{:S(2)}) collective-permute-start(f32[1,128]{1,0:T(1,128)S(1)} %sums.1.refs_0_), channel_id=1, source_target_pairs={{0,1},{1,0},{2,3},{3,2},{4,5},{5,4},{6,7},{7,6},{8,9},{9,8},{10,11... | collective-permute-start | bytes 1544 | tf_op jit(solution)/shard_map/ppermute | solution.py:26
  68.9 3.6 %collective-permute-start.12 = (f32[1,128]{1,0:T(1,128)S(1)}, f32[1,128]{1,0:T(1,128)S(1)}, u32[]{:S(2)}, u32[]{:S(2)}) collective-permute-start(f32[1,128]{1,0:T(1,128)S(1)} %sums.1.refs_0_), channel_id=1, source_target_pairs={{0,2},{1,3},{2,0},{3,1},{4,6},{5,7},{6,4},{7,5},{8,10},{9,11},{10,... | collective-permute-start | bytes 1544 | tf_op jit(solution)/shard_map/ppermute | solution.py:26
  70.5 3.0 %collective-permute-start.13 = (f32[1,128]{1,0:T(1,128)S(1)}, f32[1,128]{1,0:T(1,128)S(1)}, u32[]{:S(2)}, u32[]{:S(2)}) collective-permute-start(f32[1,128]{1,0:T(1,128)S(1)} %sums.1.refs_0_), channel_id=1, source_target_pairs={{0,3},{1,2},{2,1},{3,0},{4,7},{5,6},{6,5},{7,4},{8,11},{9,10},{10,... | collective-permute-start | bytes 1544 | tf_op jit(solution)/shard_map/ppermute | solution.py:26
